TPU v7x, 32 devices: a whole 2x2x4 slice. The times are simulated.
32 devices in a mesh: group: 2 (over y), seq: 8 (over z, x), head: 2 (over core).
Axes of the slice: x: 2, y: 2, z: 4, core: 2. Of those that a mesh axis runs over, the one named last changes fastest.
Arguments:
- response_query: bfloat16 [16, 128, 4096], P('group', 'seq', 'head'), parts along dimension 0, may hold values from -6 to 6, as said below
- response_key: bfloat16 [16, 128, 512], P('group', 'seq', 'head'), parts along dimension 0, may hold values from -8 to 8, as said below
- response_value: bfloat16 [16, 128, 512], P('group', 'seq', 'head'), parts along dimension 0, may hold values from -6 to 6
- response_grad: bfloat16 [16, 128, 4096], P('group', 'seq', 'head'), parts along dimension 0, may hold values from -6 to 6
- prompt_key: bfloat16 [192, 512], P(('group', 'seq'), 'head'), parts along dimension 0, may hold values from -8 to 8, as said below
- prompt_value: bfloat16 [192, 512], P(('group', 'seq'), 'head'), parts along dimension 0, may hold values from -6 to 6
- lengths: int32 [16], P('group'), parts along dimension 0, may hold values from 1 to 128, 512 in all
- home_rank: int32 [16], P('group'), parts along dimension 0, may hold values from 0 to 7, each once
- prompt_seen: int32 [16], P('group'), parts along dimension 0, may hold values from 24 to 96
Outputs:
- response_output: bfloat16 [16, 128, 4096], P(('group', 'seq'), None, 'head'), parts along dimension 0
- response_query_grad: bfloat16 [16, 128, 4096], P('group', 'seq', 'head'), parts along dimension 0
- response_key_grad: bfloat16 [16, 128, 512], P('group', 'seq', 'head'), parts along dimension 0
- response_value_grad: bfloat16 [16, 128, 512], P('group', 'seq', 'head'), parts along dimension 0
- prompt_key_grad: bfloat16 [192, 512], P(('group', 'seq'), 'head'), parts along dimension 0
- prompt_value_grad: bfloat16 [192, 512], P(('group', 'seq'), 'head'), parts along dimension 0
There are 2 independent parts, one for each index of `group`. A program takes and returns all parts, laid end to end along the dimension named above; each array names one. Nothing has to cross between parts.
Inputs may be any that keep to these rules, and one draw needn't show every extreme that they name: `response_query`: queries are finite. `response_key`: keys are finite. `prompt_key`: keys are finite. `lengths`: some response has exactly 128 tokens. `home_rank`: every index of seq is the home of exactly one response.
All inputs are finite; a program needn't handle non-finite values.
Results may differ from a plain program's by a relative error of at most 0.017.
The roundings to bfloat16 on the way count: a program that leaves them out, or rounds other values in their place, can miss the bound.
Values may be sent and summed in bfloat16 or wider, within the bound.
No kernel may reach another device: no remote copies, remote signals or barrier semaphores. Data moves between devices by JAX's collectives and lax.ppermute only.
A program may use at most 128 MiB of HBM per device.

v0:
```python
import jax
import jax.numpy as jnp
from jax import lax
from jax.sharding import PartitionSpec as P

HEAD_DIM = 128


NEG_FILL = -1e30


def head_logits(queries, all_keys, allowed, head_index, group_size, scale_factor):
    row_count = queries.shape[0]
    low = head_index * group_size * HEAD_DIM
    high = (head_index + 1) * group_size * HEAD_DIM
    query_head = queries[:, low:high].reshape(row_count, group_size, HEAD_DIM)
    key_head = all_keys[:, head_index * HEAD_DIM : (head_index + 1) * HEAD_DIM]
    logits = (
        jnp.einsum("rhd,kd->rhk", query_head, key_head, preferred_element_type=jnp.float32)
        * scale_factor
    )
    return (query_head, key_head, jnp.where(allowed[:, None, :], logits, NEG_FILL))


def forward(queries, all_keys, all_values, allowed, live_rows, scale_factor):
    row_count = queries.shape[0]
    kv_count = all_keys.shape[1] // HEAD_DIM
    group_size = queries.shape[1] // all_keys.shape[1]
    outputs = []
    totals = []
    for head_index in range(kv_count):
        query_head, key_head, logits = head_logits(
            queries, all_keys, allowed, head_index, group_size, scale_factor
        )
        value_head = all_values[:, head_index * HEAD_DIM : (head_index + 1) * HEAD_DIM]
        row_max = jnp.max(logits, axis=2, keepdims=True)
        log_total = row_max + jnp.log(jnp.sum(jnp.exp(logits - row_max), axis=2, keepdims=True))
        weights = jnp.exp(logits - log_total).astype(jnp.bfloat16)
        mixed = jnp.einsum("rhk,kd->rhd", weights, value_head, preferred_element_type=jnp.float32)
        output_head = jnp.where(live_rows[:, None, None], mixed, 0.0).astype(jnp.bfloat16)
        outputs.append(output_head.reshape(row_count, group_size * HEAD_DIM))
        totals.append(log_total)
    return (jnp.concatenate(outputs, axis=1), totals)


def head_terms(grad_rows, live_rows, output, head_index, group_size):
    row_count = grad_rows.shape[0]
    low = head_index * group_size * HEAD_DIM
    high = (head_index + 1) * group_size * HEAD_DIM
    grad_head = jnp.where(live_rows[:, None], grad_rows[:, low:high], jnp.zeros((), jnp.bfloat16))
    grad_head = grad_head.reshape(row_count, group_size, HEAD_DIM)
    output_head = lax.optimization_barrier(output[:, low:high]).reshape(
        row_count, group_size, HEAD_DIM
    )
    row_dot = jnp.sum(
        grad_head.astype(jnp.float32) * output_head.astype(jnp.float32), axis=2, keepdims=True
    )
    return (grad_head, row_dot)


def backward(
    queries, all_keys, all_values, grad_rows, allowed, live_rows, output, totals, scale_factor
):
    row_count = queries.shape[0]
    kv_count = all_keys.shape[1] // HEAD_DIM
    group_size = queries.shape[1] // all_keys.shape[1]
    query_grads = []
    key_grads = []
    value_grads = []
    for head_index in range(kv_count):
        query_head, key_head, logits = head_logits(
            queries, all_keys, allowed, head_index, group_size, scale_factor
        )
        value_head = all_values[:, head_index * HEAD_DIM : (head_index + 1) * HEAD_DIM]
        prob = jnp.exp(logits - totals[head_index])
        weights = prob.astype(jnp.bfloat16)
        grad_head, row_dot = head_terms(grad_rows, live_rows, output, head_index, group_size)
        spread = jnp.einsum(
            "rhd,kd->rhk", grad_head, value_head, preferred_element_type=jnp.float32
        )
        dlogit = (prob * (spread - row_dot)).astype(jnp.bfloat16)
        query_part = (
            jnp.einsum("rhk,kd->rhd", dlogit, key_head, preferred_element_type=jnp.float32)
            * scale_factor
        )
        query_grads.append(query_part.reshape(row_count, group_size * HEAD_DIM))
        key_grads.append(
            jnp.einsum("rhk,rhd->kd", dlogit, query_head, preferred_element_type=jnp.float32)
            * scale_factor
        )
        value_grads.append(
            jnp.einsum("rhk,rhd->kd", weights, grad_head, preferred_element_type=jnp.float32)
        )
    return (
        jnp.concatenate(query_grads, axis=1),
        jnp.concatenate(key_grads, axis=1),
        jnp.concatenate(value_grads, axis=1),
    )


def body(
    response_query,
    response_key,
    response_value,
    response_grad,
    prompt_key,
    prompt_value,
    lengths,
    home_rank,
    prompt_seen,
):
    rank_count = home_rank.shape[0]
    rank_ids = jnp.arange(rank_count, dtype=jnp.int32)
    resident = jnp.sum(
        jnp.where(home_rank[None, :] == rank_ids[:, None], rank_ids[None, :], 0), axis=1
    )
    own_rank = lax.axis_index("seq")
    scale_factor = 1.0 / HEAD_DIM**0.5
    arrived = (
        lax.all_to_all(response_query[resident], "seq", split_axis=0, concat_axis=1, tiled=True),
        lax.all_to_all(response_key[resident], "seq", split_axis=0, concat_axis=1, tiled=True),
        lax.all_to_all(response_value[resident], "seq", split_axis=0, concat_axis=1, tiled=True),
        lax.all_to_all(response_grad[resident], "seq", split_axis=0, concat_axis=1, tiled=True),
    )
    queries = arrived[0][0]
    own_keys = arrived[1][0]
    own_values = arrived[2][0]
    grad_rows = arrived[3][0]
    own_response = resident[own_rank]
    length = lengths[own_response]
    visible = prompt_seen[own_response]
    max_length = queries.shape[0]
    prompt_rows = prompt_key.shape[0]
    prompt_total = prompt_rows * lax.axis_size("seq")
    positions = jnp.arange(max_length, dtype=jnp.int32)
    prompt_cols = jnp.arange(prompt_total, dtype=jnp.int32)
    seen_part = jnp.broadcast_to(prompt_cols[None, :] < visible, (max_length, prompt_total))
    allowed = jnp.concatenate([seen_part, positions[None, :] <= positions[:, None]], axis=1)
    live_rows = positions < length
    gathered_keys, gathered_values = (
        lax.all_gather(prompt_key, "seq", axis=0, tiled=True),
        lax.all_gather(prompt_value, "seq", axis=0, tiled=True),
    )
    all_keys = jnp.concatenate([gathered_keys, own_keys], axis=0)
    all_values = jnp.concatenate([gathered_values, own_values], axis=0)
    response_out, response_totals = forward(
        queries, all_keys, all_values, allowed, live_rows, scale_factor
    )
    query_grad, key_grad, value_grad = backward(
        queries,
        all_keys,
        all_values,
        grad_rows,
        allowed,
        live_rows,
        response_out,
        response_totals,
        scale_factor,
    )
    key_summed, value_summed = (
        lax.psum_scatter(key_grad[:prompt_total], "seq", scatter_dimension=0, tiled=True),
        lax.psum_scatter(value_grad[:prompt_total], "seq", scatter_dimension=0, tiled=True),
    )
    returned = (
        lax.all_to_all(
            query_grad.astype(jnp.bfloat16)[None], "seq", split_axis=1, concat_axis=0, tiled=True
        ),
        lax.all_to_all(
            key_grad[prompt_total:].astype(jnp.bfloat16)[None],
            "seq",
            split_axis=1,
            concat_axis=0,
            tiled=True,
        ),
        lax.all_to_all(
            value_grad[prompt_total:].astype(jnp.bfloat16)[None],
            "seq",
            split_axis=1,
            concat_axis=0,
            tiled=True,
        ),
    )
    return (
        response_out[None],
        returned[0][home_rank],
        returned[1][home_rank],
        returned[2][home_rank],
        key_summed.astype(jnp.bfloat16),
        value_summed.astype(jnp.bfloat16),
    )


def solution(mesh):
    placed = (
        P("group", "seq", "head"),
        P("group", "seq", "head"),
        P("group", "seq", "head"),
        P("group", "seq", "head"),
        P(("group", "seq"), "head"),
        P(("group", "seq"), "head"),
        P("group"),
        P("group"),
        P("group"),
    )
    return jax.shard_map(
        body,
        mesh=mesh,
        in_specs=placed,
        out_specs=(
            P(("group", "seq"), None, "head"),
            P("group", "seq", "head"),
            P("group", "seq", "head"),
            P("group", "seq", "head"),
            P(("group", "seq"), "head"),
            P(("group", "seq"), "head"),
        ),
        check_vma=False,
    )
```

profile of v0, /device:TPU:8, one launch (start us, length us, event | category | flops | bytes accessed | tf_op | source)
XLA Modules:
  0.0 196.0 jit_solution(3605869147865452374)
XLA Ops:
  0.6 0.8 select_reduce_fusion
  1.7 1.4 gather_fusion.3
  3.1 6.4 %all-to-all-start.3 = ((bf16[8,16,2048]{2,1,0:T(8,128)(2,1)}), bf16[8,16,2048]{2,1,0:T(8,128)(2,1)S(1)}, u32[]{:S(2)}, u32[]{:S(2)}) async-start(bf16[8,16,2048]{2,1,0:T(8,128)(2,1)} %gather_fusion.3), calls=%async_computation.3 | async-start | bytes 1048576 | tf_op jit(solution)/shard_map/all_to_all | solution.py:123
  9.5 1.4 gather_fusion
  10.8 11.9 %all-to-all-done.3 = bf16[8,16,2048]{2,1,0:T(8,128)(2,1)S(1)} async-done(((bf16[8,16,2048]{2,1,0:T(8,128)(2,1)}), bf16[8,16,2048]{2,1,0:T(8,128)(2,1)S(1)}, u32[]{:S(2)}, u32[]{:S(2)}) %all-to-all-start.3) | async-done | bytes 524320 | tf_op jit(solution)/shard_map/all_to_all | solution.py:123
  22.7 5.0 %all-to-all-start = ((bf16[8,16,2048]{2,1,0:T(8,128)(2,1)}), bf16[8,16,2048]{2,1,0:T(8,128)(2,1)S(1)}, u32[]{:S(2)}, u32[]{:S(2)}) async-start(bf16[8,16,2048]{2,1,0:T(8,128)(2,1)} %gather_fusion), calls=%async_computation | async-start | bytes 1048576 | tf_op jit(solution)/shard_map/all_to_all | solution.py:120
  27.7 0.6 dynamic_slice.9
  30.3 0.6 dynamic_slice.11
  30.9 0.6 dynamic_slice.10
  31.5 1.2 gather_fusion.2
  32.7 1.2 gather_fusion.1
  33.9 28.0 %all-gather = bf16[8,12,256]{2,1,0:T(8,128)(2,1)S(1)} all-gather(bf16[1,12,256]{2,1,0:T(8,128)(2,1)S(1)} %bitcast.131), channel_id=1, replica_groups=mesh['group'=2,'seq'=8,'head'=2] {'seq'}, dimensions={0}, use_global_device_ids=true | all-gather | bytes 55296 | tf_op jit(solution)/shard_map/all_gather | solution.py:141
  61.9 0.7 copy-done.11
  62.5 30.5 %all-gather.1 = bf16[8,12,256]{2,1,0:T(8,128)(2,1)S(1)} all-gather(bf16[1,12,256]{2,1,0:T(8,128)(2,1)S(1)} %bitcast.132), channel_id=1, replica_groups=mesh['group'=2,'seq'=8,'head'=2] {'seq'}, dimensions={0}, use_global_device_ids=true | all-gather | bytes 55296 | tf_op jit(solution)/shard_map/all_gather | solution.py:142
  93.1 0.6 copy-done.12
  93.7 0.6 dynamic-slice.6
  95.0 0.7 iota_compare_fusion.2
  95.6 0.7 iota_compare_fusion.3
  96.5 8.6 %all-to-all-start.1 = ((bf16[8,16,256]{2,1,0:T(8,128)(2,1)}), bf16[8,16,256]{2,1,0:T(8,128)(2,1)S(1)}, u32[]{:S(2)}, u32[]{:S(2)}) async-start(bf16[8,16,256]{2,1,0:T(8,128)(2,1)} %gather_fusion.1), calls=%async_computation.1 | async-start | bytes 131072 | tf_op jit(solution)/shard_map/all_to_all | solution.py:121
  105.5 4.7 %all-to-all-done.1 = bf16[8,16,256]{2,1,0:T(8,128)(2,1)S(1)} async-done(((bf16[8,16,256]{2,1,0:T(8,128)(2,1)}), bf16[8,16,256]{2,1,0:T(8,128)(2,1)S(1)}, u32[]{:S(2)}, u32[]{:S(2)}) %all-to-all-start.1) | async-done | bytes 65568 | tf_op jit(solution)/shard_map/all_to_all | solution.py:121
  110.2 5.1 %all-to-all-start.2 = ((bf16[8,16,256]{2,1,0:T(8,128)(2,1)}), bf16[8,16,256]{2,1,0:T(8,128)(2,1)S(1)}, u32[]{:S(2)}, u32[]{:S(2)}) async-start(bf16[8,16,256]{2,1,0:T(8,128)(2,1)} %gather_fusion.2), calls=%async_computation.2 | async-start | bytes 131072 | tf_op jit(solution)/shard_map/all_to_all | solution.py:122
  115.3 0.3 fusion.53
  115.7 0.3 convolution_bitcast_fusion
  116.0 4.5 %all-to-all-done.2 = bf16[8,16,256]{2,1,0:T(8,128)(2,1)S(1)} async-done(((bf16[8,16,256]{2,1,0:T(8,128)(2,1)}), bf16[8,16,256]{2,1,0:T(8,128)(2,1)S(1)}, u32[]{:S(2)}, u32[]{:S(2)}) %all-to-all-start.2) | async-done | bytes 65568 | tf_op jit(solution)/shard_map/all_to_all | solution.py:122
  120.5 0.3 fusion.9
  120.9 0.3 fusion.7
  121.2 0.3 fusion.12
  121.5 0.3 fusion.11
  122.1 0.3 fusion.54
  122.6 0.3 fusion.8
  122.9 0.3 convolution_bitcast_fusion.1
  123.2 0.6 copy-done.3
  123.9 0.5 broadcast.89
  124.5 1.0 reduce.2
  125.5 0.6 reshape.232
  126.1 5.8 %all-to-all-start.6 = ((bf16[8,2,2048]{2,1,0:T(2,128)(2,1)}), bf16[8,2,2048]{2,1,0:T(2,128)(2,1)}, u32[]{:S(2)}, u32[]{:S(2)}) async-start(bf16[8,2,2048]{2,1,0:T(2,128)(2,1)} %reshape.232), calls=%async_computation.6 | async-start | bytes 131072 | tf_op jit(solution)/shard_map/all_to_all | solution.py:175
  132.0 0.3 fusion.6
  132.3 0.3 fusion.13
  132.6 0.3 fusion.10
  132.9 0.5 copy.88
  133.5 1.0 reduce.1
  134.5 0.6 reshape.230
  135.2 0.5 copy.87
  135.7 1.5 all-to-all-done.6
  137.2 5.1 %all-to-all-start.5 = ((bf16[8,2,2048]{2,1,0:T(2,128)(2,1)}), bf16[8,2,2048]{2,1,0:T(2,128)(2,1)S(1)}, u32[]{:S(2)}, u32[]{:S(2)}) async-start(bf16[8,2,2048]{2,1,0:T(2,128)(2,1)} %reshape.230), calls=%async_computation.5 | async-start | bytes 131072 | tf_op jit(solution)/shard_map/all_to_all | solution.py:168
  142.2 1.1 fusion.55
  143.3 3.7 %reduce = bf16[128,2048]{1,0:T(8,128)(2,1)S(1)} reduce(bf16[128,1,2048]{2,1,0:T(2,128)(2,1)S(1)} %fusion.55, bf16[]{:T(256)} %broadcast.89), dimensions={1}, to_apply=%fusion.55.reduce_sub_computation | reduce | bytes 1048578
  147.0 1.2 reshape.228
  148.2 6.2 %all-to-all-start.4 = ((bf16[8,2,16384]{2,1,0:T(2,128)(2,1)}), bf16[8,2,16384]{2,1,0:T(2,128)(2,1)S(1)}, u32[]{:S(2)}, u32[]{:S(2)}) async-start(bf16[8,2,16384]{2,1,0:T(2,128)(2,1)} %reshape.228), calls=%async_computation.4 | async-start | bytes 1048576 | tf_op jit(solution)/shard_map/all_to_all | solution.py:165
  154.5 20.2 %fusion.51 = (f32[16,256]{1,0:T(8,128)S(1)}, f32[16,256]{1,0:T(8,128)S(1)}) fusion(f32[96,256]{1,0:T(8,128)S(1)} %get-tuple-element.49, f32[96,256]{1,0:T(8,128)S(1)} %get-tuple-element.48), kind=kCustom, calls=%all-reduce-scatter.2 | all-reduce-scatter fusion | flops 65537 | bytes 229888
  174.7 2.1 %collective-permute-start.2 = (bf16[16,256]{1,0:T(8,128)(2,1)S(1)}, bf16[16,256]{1,0:T(8,128)(2,1)S(1)}, u32[]{:S(2)}, u32[]{:S(2)}) collective-permute-start(bf16[16,256]{1,0:T(8,128)(2,1)S(1)} %convert.44), channel_id=1, source_target_pairs={{0,2},{2,4},{4,6},{6,8},{8,10},{10,12},{12,14},{1,3},{3,5},{5,7},{... | collective-permute-start | bytes 24584
  176.9 3.0 %collective-permute-start.3 = (bf16[12,256]{1,0:T(8,128)(2,1)S(1)}, bf16[12,256]{1,0:T(8,128)(2,1)S(1)}, u32[]{:S(2)}, u32[]{:S(2)}) collective-permute-start(bf16[12,256]{1,0:T(8,128)(2,1)S(1)} %slice.83), channel_id=1, source_target_pairs={{0,4},{2,6},{4,8},{6,10},{8,12},{10,14},{1,5},{3,7},{5,9},{7,11},{... | collective-permute-start | bytes 18440
  179.9 3.5 %collective-permute-start = (bf16[16,256]{1,0:T(8,128)(2,1)S(1)}, bf16[16,256]{1,0:T(8,128)(2,1)S(1)}, u32[]{:S(2)}, u32[]{:S(2)}) collective-permute-start(bf16[16,256]{1,0:T(8,128)(2,1)S(1)} %convert.43), channel_id=1, source_target_pairs={{0,2},{2,4},{4,6},{6,8},{8,10},{10,12},{12,14},{1,3},{3,5},{5,7},{... | collective-permute-start | bytes 24584
  183.4 2.1 %collective-permute-start.1 = (bf16[12,256]{1,0:T(8,128)(2,1)S(1)}, bf16[12,256]{1,0:T(8,128)(2,1)S(1)}, u32[]{:S(2)}, u32[]{:S(2)}) collective-permute-start(bf16[12,256]{1,0:T(8,128)(2,1)S(1)} %slice.82), channel_id=1, source_target_pairs={{0,4},{2,6},{4,8},{6,10},{8,12},{10,14},{1,5},{3,7},{5,9},{7,11},{... | collective-permute-start | bytes 18440
  185.5 1.0 copy.95
  186.8 2.2 %collective-permute-done.1 = bf16[12,256]{1,0:T(8,128)(2,1)S(1)} collective-permute-done((bf16[12,256]{1,0:T(8,128)(2,1)S(1)}, bf16[12,256]{1,0:T(8,128)(2,1)S(1)}, u32[]{:S(2)}, u32[]{:S(2)}) %collective-permute-start.1) | collective-permute-done | bytes 6176
  189.2 0.6 dynamic-slice_convert_fusion
  189.8 0.6 dynamic-slice_convert_fusion.1
  190.4 0.9 reshape.233
  191.4 1.2 gather_fusion.6
  192.6 1.2 gather_fusion.5
  193.8 0.5 reshape.229
  194.3 0.3 copy.104
  194.6 1.4 gather_fusion.4
  (71 shorter events, 2.6 us)
Async XLA Ops:
  0.6 1.1 copy-start
  3.1 6.4 %copy-start.7 = (bf16[8,16,2048]{2,1,0:T(8,128)(2,1)S(1)}, bf16[8,16,2048]{2,1,0:T(8,128)(2,1)}, u32[]{:S(2)}) copy-start(bf16[8,16,2048]{2,1,0:T(8,128)(2,1)} %param.9) | copy-start | bytes 1572868
  3.1 19.6 %all-to-all-start.3 = ((bf16[8,16,2048]{2,1,0:T(8,128)(2,1)}), bf16[8,16,2048]{2,1,0:T(8,128)(2,1)S(1)}, u32[]{:S(2)}, u32[]{:S(2)}) async-start(bf16[8,16,2048]{2,1,0:T(8,128)(2,1)} %gather_fusion.3), calls=%async_computation.3 | async-start | bytes 1048576 | tf_op jit(solution)/shard_map/all_to_all | solution.py:123
  22.7 8.8 %copy-start.8 = (bf16[8,16,256]{2,1,0:T(8,128)(2,1)S(1)}, bf16[8,16,256]{2,1,0:T(8,128)(2,1)}, u32[]{:S(2)}) copy-start(bf16[8,16,256]{2,1,0:T(8,128)(2,1)} %param.11) | copy-start | bytes 196612
  22.7 73.8 %all-to-all-start = ((bf16[8,16,2048]{2,1,0:T(8,128)(2,1)}), bf16[8,16,2048]{2,1,0:T(8,128)(2,1)S(1)}, u32[]{:S(2)}, u32[]{:S(2)}) async-start(bf16[8,16,2048]{2,1,0:T(8,128)(2,1)} %gather_fusion), calls=%async_computation | async-start | bytes 1048576 | tf_op jit(solution)/shard_map/all_to_all | solution.py:120
  29.6 0.7 copy-start.13
  30.3 0.7 copy-start.14
  31.5 1.2 copy-start.9
  32.7 1.2 copy-start.10
  61.8 0.7 copy-start.11
  93.1 0.7 copy-start.12
  96.5 13.7 %all-to-all-start.1 = ((bf16[8,16,256]{2,1,0:T(8,128)(2,1)}), bf16[8,16,256]{2,1,0:T(8,128)(2,1)S(1)}, u32[]{:S(2)}, u32[]{:S(2)}) async-start(bf16[8,16,256]{2,1,0:T(8,128)(2,1)} %gather_fusion.1), calls=%async_computation.1 | async-start | bytes 131072 | tf_op jit(solution)/shard_map/all_to_all | solution.py:121
  110.2 10.3 %all-to-all-start.2 = ((bf16[8,16,256]{2,1,0:T(8,128)(2,1)}), bf16[8,16,256]{2,1,0:T(8,128)(2,1)S(1)}, u32[]{:S(2)}, u32[]{:S(2)}) async-start(bf16[8,16,256]{2,1,0:T(8,128)(2,1)} %gather_fusion.2), calls=%async_computation.2 | async-start | bytes 131072 | tf_op jit(solution)/shard_map/all_to_all | solution.py:122
  116.0 7.2 %copy-start.1 = (f32[224,128]{1,0:T(8,128)}, f32[224,128]{1,0:T(8,128)S(1)}, u32[]{:S(2)}) copy-start(f32[224,128]{1,0:T(8,128)S(1)} %convolution_bitcast_fusion) | copy-start | bytes 344068
  121.5 11.9 %copy-start.5 = (f32[224,128]{1,0:T(8,128)}, f32[224,128]{1,0:T(8,128)S(1)}, u32[]{:S(2)}) copy-start(f32[224,128]{1,0:T(8,128)S(1)} %fusion.12) | copy-start | bytes 344068
  123.2 0.6 copy-start.3
  126.1 11.0 %all-to-all-start.6 = ((bf16[8,2,2048]{2,1,0:T(2,128)(2,1)}), bf16[8,2,2048]{2,1,0:T(2,128)(2,1)}, u32[]{:S(2)}, u32[]{:S(2)}) async-start(bf16[8,2,2048]{2,1,0:T(2,128)(2,1)} %reshape.232), calls=%async_computation.6 | async-start | bytes 131072 | tf_op jit(solution)/shard_map/all_to_all | solution.py:175
  137.2 11.1 %all-to-all-start.5 = ((bf16[8,2,2048]{2,1,0:T(2,128)(2,1)}), bf16[8,2,2048]{2,1,0:T(2,128)(2,1)S(1)}, u32[]{:S(2)}, u32[]{:S(2)}) async-start(bf16[8,2,2048]{2,1,0:T(2,128)(2,1)} %reshape.230), calls=%async_computation.5 | async-start | bytes 131072 | tf_op jit(solution)/shard_map/all_to_all | solution.py:168
  148.2 6.2 %copy-start.15 = (s32[8]{0:T(128)S(1)}, s32[8]{0:T(128)}, u32[]{:S(2)}) copy-start(s32[8]{0:T(128)} %param.16) | copy-start | bytes 100
  148.2 6.2 %copy-start.2 = (f32[224,128]{1,0:T(8,128)S(1)}, f32[224,128]{1,0:T(8,128)}, u32[]{:S(2)}) copy-start(f32[224,128]{1,0:T(8,128)} %copy-done.1) | copy-start | bytes 344068
  148.2 6.2 %copy-start.4 = (f32[224,128]{1,0:T(8,128)S(1)}, f32[224,128]{1,0:T(8,128)}, u32[]{:S(2)}) copy-start(f32[224,128]{1,0:T(8,128)} %copy-done.3) | copy-start | bytes 344068
  148.2 6.2 %copy-start.6 = (f32[224,128]{1,0:T(8,128)S(1)}, f32[224,128]{1,0:T(8,128)}, u32[]{:S(2)}) copy-start(f32[224,128]{1,0:T(8,128)} %copy-done.5) | copy-start | bytes 344068
  148.2 45.5 %all-to-all-start.4 = ((bf16[8,2,16384]{2,1,0:T(2,128)(2,1)}), bf16[8,2,16384]{2,1,0:T(2,128)(2,1)S(1)}, u32[]{:S(2)}, u32[]{:S(2)}) async-start(bf16[8,2,16384]{2,1,0:T(2,128)(2,1)} %reshape.228), calls=%async_computation.4 | async-start | bytes 1048576 | tf_op jit(solution)/shard_map/all_to_all | solution.py:165
  174.7 11.8 %collective-permute-start.2 = (bf16[16,256]{1,0:T(8,128)(2,1)S(1)}, bf16[16,256]{1,0:T(8,128)(2,1)S(1)}, u32[]{:S(2)}, u32[]{:S(2)}) collective-permute-start(bf16[16,256]{1,0:T(8,128)(2,1)S(1)} %convert.44), channel_id=1, source_target_pairs={{0,2},{2,4},{4,6},{6,8},{8,10},{10,12},{12,14},{1,3},{3,5},{5,7},{... | collective-permute-start | bytes 24584
  176.9 9.7 %collective-permute-start.3 = (bf16[12,256]{1,0:T(8,128)(2,1)S(1)}, bf16[12,256]{1,0:T(8,128)(2,1)S(1)}, u32[]{:S(2)}, u32[]{:S(2)}) collective-permute-start(bf16[12,256]{1,0:T(8,128)(2,1)S(1)} %slice.83), channel_id=1, source_target_pairs={{0,4},{2,6},{4,8},{6,10},{8,12},{10,14},{1,5},{3,7},{5,9},{7,11},{... | collective-permute-start | bytes 18440
  179.9 9.1 %collective-permute-start = (bf16[16,256]{1,0:T(8,128)(2,1)S(1)}, bf16[16,256]{1,0:T(8,128)(2,1)S(1)}, u32[]{:S(2)}, u32[]{:S(2)}) collective-permute-start(bf16[16,256]{1,0:T(8,128)(2,1)S(1)} %convert.43), channel_id=1, source_target_pairs={{0,2},{2,4},{4,6},{6,8},{8,10},{10,12},{12,14},{1,3},{3,5},{5,7},{... | collective-permute-start | bytes 24584
  183.4 5.5 %collective-permute-start.1 = (bf16[12,256]{1,0:T(8,128)(2,1)S(1)}, bf16[12,256]{1,0:T(8,128)(2,1)S(1)}, u32[]{:S(2)}, u32[]{:S(2)}) collective-permute-start(bf16[12,256]{1,0:T(8,128)(2,1)S(1)} %slice.82), channel_id=1, source_target_pairs={{0,4},{2,6},{4,8},{6,10},{8,12},{10,14},{1,5},{3,7},{5,9},{7,11},{... | collective-permute-start | bytes 18440
where the time goes:
time: 198 us; the launch traced here: 196 us
  blocking collectives  78.7 us (40%)
  starting transfers between devices  52.8 us (27%)
  waiting for transfers between devices  24.7 us (12%)
  local copies, waits for them, and re-layouts  22.9 us (12%)
  other arithmetic  9.71 us (5%)
  between operations  3.81 us (2%)
  matrix products  3.43 us (2%)
    all_gather x1, blocking collectives, body(): lax.all_gather(prompt_value, 'seq', axis=0, tiled=True)  30.5 us
    all_gather x1, blocking collectives, body(): lax.all_gather(prompt_key, 'seq', axis=0, tiled=True)  28 us
    unnamed x1, blocking collectives  20.2 us
    all_to_all x1, waiting for transfers between devices, body(): lax.all_to_all(response_grad[resident], 'seq', split_axis=0, concat_axis=...  11.9 us
    unnamed x4, starting transfers between devices  10.7 us
    unnamed x50, local copies, waits for them, and re-layouts  9.16 us
    all_to_all x1, starting transfers between devices, body(): lax.all_to_all(response_key[resident], 'seq', split_axis=0, concat_axis=1...  8.57 us
    unnamed x6, other arithmetic  6.82 us
  transfers between devices with their start and end apart: 11, of which 5 were waited for; matrix products, arithmetic and copies ran while one was open for 23% of the time, Pallas kernels for 0%

commit v1 on v0

--- a/solution.py
+++ b/solution.py
@@ -1,12 +1,256 @@
+import functools
+
 import jax
 import jax.numpy as jnp
 from jax import lax
+from jax.experimental import pallas as pl
+from jax.experimental.pallas import tpu as pltpu
 from jax.sharding import PartitionSpec as P
 
 HEAD_DIM = 128
 
 
 NEG_FILL = -1e30
+BF16 = jnp.bfloat16
+F32 = jnp.float32
+
+
+def resident_of(home_ref, rank, count):
+    found = jnp.int32(0)
+    for index in range(count):
+        found = jnp.where(home_ref[index] == rank, jnp.int32(index), found)
+    return found
+
+
+def dot(left, right, contract):
+    return lax.dot_general(left, right, ((contract[0], contract[1]), ((), ())), preferred_element_type=F32)
+
+
+def pack_kernel(home_ref, q_ref, k_ref, v_ref, g_ref, pk_ref, pv_ref, *rest, count):
+    blocks, prompt, sems = rest[:count], rest[count], rest[count + 1]
+    rank = lax.axis_index("seq")
+    prompt_rows, kv_width = pk_ref.shape
+    q_width = q_ref.shape[2]
+    starts = []
+    for distance in range(count):
+        index = resident_of(home_ref, rank ^ distance, count)
+        block = blocks[distance]
+        low = 0
+        for part, ref in enumerate((q_ref, g_ref, k_ref, v_ref)):
+            width = ref.shape[2]
+            starts.append(
+                pltpu.make_async_copy(
+                    ref.at[index], block.at[:, pl.ds(low, width)], sems.at[distance, part]
+                )
+            )
+            starts[-1].start()
+            low += width
+    prompt[...] = jnp.zeros(prompt.shape, BF16)
+    prompt[:prompt_rows, :kv_width] = pk_ref[...]
+    prompt[:prompt_rows, kv_width:] = pv_ref[...]
+    low = 2 * q_width + 2 * kv_width
+    for distance in range(count):
+        starts.append(
+            pltpu.make_async_copy(
+                prompt, blocks[distance].at[:, pl.ds(low, 2 * kv_width)], sems.at[distance, 4]
+            )
+        )
+        starts[-1].start()
+    for copy in starts:
+        copy.wait()
+
+
+def attend_kernel(lengths_ref, home_ref, seen_ref, *rest, count, prompt_rows, q_width, kv_width):
+    blocks = rest[:count]
+    out_ref = rest[count]
+    returns = rest[count + 1 : 2 * count + 1]
+    x, y, o, in_sems, out_sems = rest[2 * count + 1 :]
+    rank = lax.axis_index("seq")
+    rows = blocks[0].shape[0]
+    total = rows * count
+    kv_count = kv_width // HEAD_DIM
+    group_size = q_width // kv_width
+    scale = 1.0 / HEAD_DIM**0.5
+    arrivals = []
+    for distance in range(count):
+        arrivals.append(
+            pltpu.make_async_copy(
+                blocks[distance], x.at[pl.ds((rank ^ distance) * rows, rows), :], in_sems.at[distance]
+            )
+        )
+        arrivals[-1].start()
+    own = resident_of(home_ref, rank, count)
+    length = lengths_ref[own]
+    visible = seen_ref[own]
+    column = lax.broadcasted_iota(jnp.int32, (total, total), 1)
+    position = lax.broadcasted_iota(jnp.int32, (total, total), 0)
+    shard_row = column % rows
+    prompt_index = column // rows * prompt_rows + shard_row
+    allowed = jnp.concatenate(
+        [(shard_row < prompt_rows) & (prompt_index < visible), column <= position], axis=1
+    )
+    live = lax.broadcasted_iota(jnp.int32, (total, HEAD_DIM), 0) < length
+    for copy in arrivals:
+        copy.wait()
+    leaving = []
+    for kv in range(kv_count):
+        low = 2 * q_width + kv * HEAD_DIM
+        keys = jnp.concatenate(
+            [x[:, low + 2 * kv_width : low + 2 * kv_width + HEAD_DIM], x[:, low : low + HEAD_DIM]], axis=0
+        )
+        low += kv_width
+        values = jnp.concatenate(
+            [x[:, low + 2 * kv_width : low + 2 * kv_width + HEAD_DIM], x[:, low : low + HEAD_DIM]], axis=0
+        )
+        key_grad = jnp.zeros((2 * total, HEAD_DIM), F32)
+        value_grad = jnp.zeros((2 * total, HEAD_DIM), F32)
+        for member in range(group_size):
+            head = (kv * group_size + member) * HEAD_DIM
+            query = x[:, head : head + HEAD_DIM]
+            grad = jnp.where(live, x[:, q_width + head : q_width + head + HEAD_DIM], jnp.zeros((), BF16))
+            logits = jnp.where(allowed, dot(query, keys, ((1,), (1,))) * scale, NEG_FILL)
+            spread = dot(grad, values, ((1,), (1,)))
+            raised = jnp.exp(logits - jnp.max(logits, axis=1, keepdims=True))
+            prob = raised * (1.0 / jnp.sum(raised, axis=1, keepdims=True))
+            weights = prob.astype(BF16)
+            output = jnp.where(live, dot(weights, values, ((1,), (0,))), 0.0).astype(BF16)
+            o[:, head : head + HEAD_DIM] = output
+            row_dot = jnp.sum(grad.astype(F32) * output.astype(F32), axis=1, keepdims=True)
+            dlogit = (prob * (spread - row_dot)).astype(BF16)
+            y[:, head : head + HEAD_DIM] = (dot(dlogit, keys, ((1,), (0,))) * scale).astype(BF16)
+            key_grad += dot(dlogit, query, ((0,), (0,)))
+            value_grad += dot(weights, grad, ((0,), (0,)))
+        low = q_width + kv * HEAD_DIM
+        for part, summed in enumerate((key_grad * scale, value_grad)):
+            at = low + part * kv_width
+            y[:, at : at + HEAD_DIM] = summed[total:].astype(BF16)
+            at += 2 * kv_width
+            y[:, at : at + HEAD_DIM] = summed[:total].astype(BF16)
+    for distance in range(count):
+        leaving.append(
+            pltpu.make_async_copy(
+                y.at[pl.ds((rank ^ distance) * rows, rows), :], returns[distance], out_sems.at[distance]
+            )
+        )
+        leaving[-1].start()
+    leaving.append(pltpu.make_async_copy(o, out_ref.at[0], out_sems.at[count]))
+    leaving[-1].start()
+    for copy in leaving:
+        copy.wait()
+
+
+def unpack_kernel(home_ref, *rest, count, q_width, kv_width):
+    blocks = rest[:count]
+    qg_ref, kg_ref, vg_ref, pkg_ref, pvg_ref, parts, sems = rest[count:]
+    rank = lax.axis_index("seq")
+    prompt_rows = pkg_ref.shape[0]
+    copies = []
+    for distance in range(count):
+        low = q_width + 2 * kv_width
+        copies.append(
+            pltpu.make_async_copy(
+                blocks[distance].at[:, pl.ds(low, 2 * kv_width)], parts.at[distance], sems.at[distance, 0]
+            )
+        )
+        copies[-1].start()
+    moves = []
+    for distance in range(count):
+        index = resident_of(home_ref, rank ^ distance, count)
+        low = 0
+        for part, ref in enumerate((qg_ref, kg_ref, vg_ref)):
+            width = ref.shape[2]
+            moves.append(
+                pltpu.make_async_copy(
+                    blocks[distance].at[:, pl.ds(low, width)], ref.at[index], sems.at[distance, part + 1]
+                )
+            )
+            moves[-1].start()
+            low += width
+    for copy in copies:
+        copy.wait()
+    summed = parts[0].astype(F32)
+    for distance in range(1, count):
+        summed += parts[distance].astype(F32)
+    pkg_ref[...] = summed[:prompt_rows, :kv_width].astype(BF16)
+    pvg_ref[...] = summed[:prompt_rows, kv_width:].astype(BF16)
+    for copy in moves:
+        copy.wait()
+
+
+def exchange(blocks):
+    count = len(blocks)
+    return [blocks[0]] + [
+        lax.ppermute(blocks[d], "seq", [(i, i ^ d) for i in range(count)]) for d in range(1, count)
+    ]
+
+
+ANY = pl.BlockSpec(memory_space=pl.ANY)
+SMEM = pl.BlockSpec(memory_space=pltpu.SMEM)
+VMEM = pl.BlockSpec(memory_space=pltpu.VMEM)
+
+
+def packed_body(
+    response_query,
+    response_key,
+    response_value,
+    response_grad,
+    prompt_key,
+    prompt_value,
+    lengths,
+    home_rank,
+    prompt_seen,
+):
+    count = home_rank.shape[0]
+    rows, q_width = response_query.shape[1:]
+    prompt_rows, kv_width = prompt_key.shape
+    total = rows * count
+    in_width = 2 * q_width + 4 * kv_width
+    back_width = q_width + 4 * kv_width
+    blocks = pl.pallas_call(
+        functools.partial(pack_kernel, count=count),
+        name="pack",
+        out_shape=[jax.ShapeDtypeStruct((rows, in_width), BF16)] * count,
+        in_specs=[SMEM, ANY, ANY, ANY, ANY, VMEM, VMEM],
+        out_specs=[ANY] * count,
+        scratch_shapes=[pltpu.VMEM((rows, 2 * kv_width), BF16), pltpu.SemaphoreType.DMA((count, 5))],
+    )(home_rank, response_query, response_key, response_value, response_grad, prompt_key, prompt_value)
+    arrived = exchange(blocks)
+    output, *returns = pl.pallas_call(
+        functools.partial(
+            attend_kernel, count=count, prompt_rows=prompt_rows, q_width=q_width, kv_width=kv_width
+        ),
+        name="attend",
+        out_shape=[jax.ShapeDtypeStruct((1, total, q_width), BF16)]
+        + [jax.ShapeDtypeStruct((rows, back_width), BF16)] * count,
+        in_specs=[SMEM] * 3 + [ANY] * count,
+        out_specs=[ANY] * (count + 1),
+        scratch_shapes=[
+            pltpu.VMEM((total, in_width), BF16),
+            pltpu.VMEM((total, back_width), BF16),
+            pltpu.VMEM((total, q_width), BF16),
+            pltpu.SemaphoreType.DMA((count,)),
+            pltpu.SemaphoreType.DMA((count + 1,)),
+        ],
+    )(lengths, home_rank, prompt_seen, *arrived)
+    returned = exchange(returns)
+    grads = pl.pallas_call(
+        functools.partial(unpack_kernel, count=count, q_width=q_width, kv_width=kv_width),
+        name="unpack",
+        out_shape=[
+            jax.ShapeDtypeStruct((count, rows, q_width), BF16),
+            jax.ShapeDtypeStruct((count, rows, kv_width), BF16),
+            jax.ShapeDtypeStruct((count, rows, kv_width), BF16),
+            jax.ShapeDtypeStruct((prompt_rows, kv_width), BF16),
+            jax.ShapeDtypeStruct((prompt_rows, kv_width), BF16),
+        ],
+        in_specs=[SMEM] + [ANY] * count,
+        out_specs=[ANY, ANY, ANY, VMEM, VMEM],
+        scratch_shapes=[
+            pltpu.VMEM((count, rows, 2 * kv_width), BF16),
+            pltpu.SemaphoreType.DMA((count, 4)),
+        ],
+    )(home_rank, *returned)
+    return (output, *grads)
 
 
 def head_logits(queries, all_keys, allowed, head_index, group_size, scale_factor):
@@ -190,6 +434,15 @@
     )
 
 
+def choose_body(response_query, *others):
+    count, rows = response_query.shape[:2]
+    prompt_rows = others[3].shape[0]
+    fits = rows % 16 == 0 and prompt_rows <= rows and rows * count == HEAD_DIM
+    if fits and count & (count - 1) == 0 and count <= 16:
+        return packed_body(response_query, *others)
+    return body(response_query, *others)
+
+
 def solution(mesh):
     placed = (
         P("group", "seq", "head"),
@@ -203,7 +456,7 @@
         P("group"),
     )
     return jax.shard_map(
-        body,
+        choose_body,
         mesh=mesh,
         in_specs=placed,
         out_specs=(

time: 198 us -> 132 us (0.67)
  blocking collectives: 78.7 us -> 0 us
  Pallas kernels: 0 us -> 73.1 us
  starting transfers between devices: 52.8 us -> 19 us
  local copies, waits for them, and re-layouts: 22.9 us -> 1.25 us
  waiting for transfers between devices: 24.7 us -> 37.5 us
  other arithmetic: 9.71 us -> 0 us
  matrix products: 3.43 us -> 0 us
  between operations: 3.81 us -> 0.73 us
    pallas_call x0 -> x3, Pallas kernels: none -> 73.1 us  [the longest x1 38 us: packed_body(): pl.pallas_call(functools.partial(pack_kernel, count=count), name='pack',...]
    all_gather x2 -> x0, blocking collectives: 58.5 us -> none  [the longest x1 30.5 us: body(): lax.all_gather(prompt_value, 'seq', axis=0, tiled=True)]
    all_to_all x7 -> x0, starting transfers between devices: 42.1 us -> none  [the longest x1 8.57 us: body(): lax.all_to_all(response_key[resident], 'seq', split_axis=0, concat_axis=1...]
    ppermute x0 -> x14, waiting for transfers between devices: none -> 37.5 us  [exchange(): lax.ppermute(blocks[d], 'seq', [(i, i ^ d) for i in range(count)])]
    all_to_all x7 -> x0, waiting for transfers between devices: 22.5 us -> none  [the longest x1 11.9 us: body(): lax.all_to_all(response_grad[resident], 'seq', split_axis=0, concat_axis=...]
    unnamed x1 -> x0, blocking collectives: 20.2 us -> none
    ppermute x0 -> x14, starting transfers between devices: none -> 19 us  [exchange(): lax.ppermute(blocks[d], 'seq', [(i, i ^ d) for i in range(count)])]
    unnamed x4 -> x0, starting transfers between devices: 10.7 us -> none
  transfers between devices with their start and end apart: 11 -> 14, of which waited for: 5 -> 10; matrix products, arithmetic and copies ran while one was open for 23% -> 0% of each run, Pallas kernels for 0% -> 0%
where the time goes in v1:
time: 132 us
  Pallas kernels  73.1 us (55%)
  waiting for transfers between devices  37.5 us (28%)
  starting transfers between devices  19 us (14%)
    pallas_call x1, Pallas kernels, packed_body(): pl.pallas_call(functools.partial(pack_kernel, count=count), name='pack',...  38 us
    ppermute x14, waiting for transfers between devices, exchange(): lax.ppermute(blocks[d], 'seq', [(i, i ^ d) for i in range(count)])  37.5 us
    pallas_call x1, Pallas kernels, packed_body(): pl.pallas_call(functools.partial(unpack_kernel, count=count, q_width=q_wi...  22.5 us
    ppermute x14, starting transfers between devices, exchange(): lax.ppermute(blocks[d], 'seq', [(i, i ^ d) for i in range(count)])  19 us
    pallas_call x1, Pallas kernels, packed_body(): pl.pallas_call(functools.partial(attend_kernel, count=count, prompt_rows=...  12.6 us
  transfers between devices with their start and end apart: 14, of which 10 were waited for; matrix products, arithmetic and copies ran while one was open for 0% of the time, Pallas kernels for 0%

profile of v1, /device:TPU:8, one launch (start us, length us, event | category | flops | bytes accessed | tf_op | source)
XLA Modules:
  0.0 131.5 jit_solution(10606981403328918785)
XLA Ops:
  0.6 38.0 %pack.1 = (bf16[16,5120]{1,0:T(8,128)(2,1)}, bf16[16,5120]{1,0:T(8,128)(2,1)}, bf16[16,5120]{1,0:T(8,128)(2,1)}, bf16[16,5120]{1,0:T(8,128)(2,1)}, bf16[16,5120]...) custom-call(s32[8]{0:T(128)} %home_ref.5, ...), custom_call_target="tpu_custom_call" | custom-call | tf_op jit(solution)/shard_map/pack/pallas_call | solution.py:209
  38.6 1.6 %collective-permute-start = (bf16[16,5120]{1,0:T(8,128)(2,1)}, bf16[16,5120]{1,0:T(8,128)(2,1)S(1)}, u32[]{:S(2)}, u32[]{:S(2)}) collective-permute-start(bf16[16,5120]{1,0:T(8,128)(2,1)} %get-tuple-element.29), channel_id=1, source_target_pairs={{0,2},{2,0},{4,6},{6,4},{8,10},{10,8},{12,14},{14,12},{1,3},{3,1},... | collective-permute-start | bytes 491528 | tf_op jit(solution)/shard_map/ppermute | solution.py:183
  40.2 0.4 collective-permute-start.1
  40.6 1.5 %collective-permute-start.2 = (bf16[16,5120]{1,0:T(8,128)(2,1)}, bf16[16,5120]{1,0:T(8,128)(2,1)S(1)}, u32[]{:S(2)}, u32[]{:S(2)}) collective-permute-start(bf16[16,5120]{1,0:T(8,128)(2,1)} %get-tuple-element.31), channel_id=1, source_target_pairs={{0,6},{2,4},{4,2},{6,0},{8,14},{10,12},{12,10},{14,8},{1,7},{3,5},... | collective-permute-start | bytes 491528 | tf_op jit(solution)/shard_map/ppermute | solution.py:183
  42.1 2.6 %collective-permute-start.3 = (bf16[16,5120]{1,0:T(8,128)(2,1)}, bf16[16,5120]{1,0:T(8,128)(2,1)S(1)}, u32[]{:S(2)}, u32[]{:S(2)}) collective-permute-start(bf16[16,5120]{1,0:T(8,128)(2,1)} %get-tuple-element.32), channel_id=1, source_target_pairs={{0,8},{2,10},{4,12},{6,14},{8,0},{10,2},{12,4},{14,6},{1,9},{3,11}... | collective-permute-start | bytes 491528 | tf_op jit(solution)/shard_map/ppermute | solution.py:183
  44.7 1.3 collective-permute-start.4
  46.0 0.0 collective-permute-done.rest_1_
  46.0 0.0 copy-start
  46.0 1.6 %collective-permute-start.5 = (bf16[16,5120]{1,0:T(8,128)(2,1)}, bf16[16,5120]{1,0:T(8,128)(2,1)S(1)}, u32[]{:S(2)}, u32[]{:S(2)}) collective-permute-start(bf16[16,5120]{1,0:T(8,128)(2,1)} %get-tuple-element.34), channel_id=1, source_target_pairs={{0,12},{2,14},{4,8},{6,10},{8,4},{10,6},{12,0},{14,2},{1,13},{3,15... | collective-permute-start | bytes 491528 | tf_op jit(solution)/shard_map/ppermute | solution.py:183
  47.6 3.7 %collective-permute-done.1.rest_2_ = bf16[16,5120]{1,0:T(8,128)(2,1)S(1)} collective-permute-done((bf16[16,5120]{1,0:T(8,128)(2,1)}, bf16[16,5120]{1,0:T(8,128)(2,1)S(1)}, u32[]{:S(2)}, u32[]{:S(2)}) %collective-permute-start.1) | collective-permute-done | bytes 163872 | tf_op jit(solution)/shard_map/ppermute | solution.py:183
  51.3 0.0 copy-start.1
  51.3 0.0 collective-permute-start.6
  51.3 2.3 %collective-permute-done.2.rest_3_ = bf16[16,5120]{1,0:T(8,128)(2,1)S(1)} collective-permute-done((bf16[16,5120]{1,0:T(8,128)(2,1)}, bf16[16,5120]{1,0:T(8,128)(2,1)S(1)}, u32[]{:S(2)}, u32[]{:S(2)}) %collective-permute-start.2) | collective-permute-done | bytes 163872 | tf_op jit(solution)/shard_map/ppermute | solution.py:183
  53.6 0.0 copy-start.2
  53.6 10.1 %collective-permute-done.3.rest_4_ = bf16[16,5120]{1,0:T(8,128)(2,1)S(1)} collective-permute-done((bf16[16,5120]{1,0:T(8,128)(2,1)}, bf16[16,5120]{1,0:T(8,128)(2,1)S(1)}, u32[]{:S(2)}, u32[]{:S(2)}) %collective-permute-start.3) | collective-permute-done | bytes 163872 | tf_op jit(solution)/shard_map/ppermute | solution.py:183
  63.7 0.0 copy-start.3
  63.7 3.5 %collective-permute-done.4.rest_5_ = bf16[16,5120]{1,0:T(8,128)(2,1)S(1)} collective-permute-done((bf16[16,5120]{1,0:T(8,128)(2,1)}, bf16[16,5120]{1,0:T(8,128)(2,1)S(1)}, u32[]{:S(2)}, u32[]{:S(2)}) %collective-permute-start.4) | collective-permute-done | bytes 163872 | tf_op jit(solution)/shard_map/ppermute | solution.py:183
  67.2 0.0 copy-start.4
  67.2 3.3 %collective-permute-done.5.rest_6_ = bf16[16,5120]{1,0:T(8,128)(2,1)S(1)} collective-permute-done((bf16[16,5120]{1,0:T(8,128)(2,1)}, bf16[16,5120]{1,0:T(8,128)(2,1)S(1)}, u32[]{:S(2)}, u32[]{:S(2)}) %collective-permute-start.5) | collective-permute-done | bytes 163872 | tf_op jit(solution)/shard_map/ppermute | solution.py:183
  70.5 0.0 copy-start.5
  70.5 2.5 %collective-permute-done.6.rest_7_ = bf16[16,5120]{1,0:T(8,128)(2,1)S(1)} collective-permute-done((bf16[16,5120]{1,0:T(8,128)(2,1)}, bf16[16,5120]{1,0:T(8,128)(2,1)S(1)}, u32[]{:S(2)}, u32[]{:S(2)}) %collective-permute-start.6) | collective-permute-done | bytes 163872 | tf_op jit(solution)/shard_map/ppermute | solution.py:183
  73.1 0.0 copy-start.6
  73.1 0.0 copy-done
  73.1 0.0 copy-done.1
  73.1 0.0 copy-done.2
  73.1 0.0 copy-done.3
  73.1 0.0 copy-done.4
  73.1 0.0 copy-done.5
  73.1 0.6 copy-done.6
  73.7 12.6 %attend.1 = (bf16[1,128,2048]{2,1,0:T(8,128)(2,1)}, bf16[16,3072]{1,0:T(8,128)(2,1)}, bf16[16,3072]{1,0:T(8,128)(2,1)}, bf16[16,3072]{1,0:T(8,128)(2,1)}, bf16[1...) custom-call(s32[8]{0:T(128)} %lengths_ref.1, ...), custom_call_target="tpu_custom_call" | custom-call | tf_op jit(solution)/shard_map/attend/pallas_call | solution.py:218
  86.3 0.8 collective-permute-start.7
  87.1 0.0 collective-permute-start.8
  87.1 2.8 %collective-permute-start.9 = (bf16[16,3072]{1,0:T(8,128)(2,1)}, bf16[16,3072]{1,0:T(8,128)(2,1)S(1)}, u32[]{:S(2)}, u32[]{:S(2)}) collective-permute-start(bf16[16,3072]{1,0:T(8,128)(2,1)} %get-tuple-element.40), channel_id=1, source_target_pairs={{0,6},{2,4},{4,2},{6,0},{8,14},{10,12},{12,10},{14,8},{1,7},{3,5},... | collective-permute-start | bytes 294920 | tf_op jit(solution)/shard_map/ppermute | solution.py:183
  89.9 2.0 %collective-permute-start.10 = (bf16[16,3072]{1,0:T(8,128)(2,1)}, bf16[16,3072]{1,0:T(8,128)(2,1)S(1)}, u32[]{:S(2)}, u32[]{:S(2)}) collective-permute-start(bf16[16,3072]{1,0:T(8,128)(2,1)} %get-tuple-element.41), channel_id=1, source_target_pairs={{0,8},{2,10},{4,12},{6,14},{8,0},{10,2},{12,4},{14,6},{1,9},{3,11}... | collective-permute-start | bytes 294920 | tf_op jit(solution)/shard_map/ppermute | solution.py:183
  91.9 1.1 collective-permute-start.11
  93.0 0.0 collective-permute-done.7.rest_1_
  93.0 0.0 copy-start.7
  93.0 2.3 %collective-permute-start.12 = (bf16[16,3072]{1,0:T(8,128)(2,1)}, bf16[16,3072]{1,0:T(8,128)(2,1)S(1)}, u32[]{:S(2)}, u32[]{:S(2)}) collective-permute-start(bf16[16,3072]{1,0:T(8,128)(2,1)} %get-tuple-element.43), channel_id=1, source_target_pairs={{0,12},{2,14},{4,8},{6,10},{8,4},{10,6},{12,0},{14,2},{1,13},{3,15... | collective-permute-start | bytes 294920 | tf_op jit(solution)/shard_map/ppermute | solution.py:183
  95.3 0.0 collective-permute-done.8.rest_2_
  95.3 0.0 copy-start.8
  95.3 1.0 collective-permute-start.13
  96.4 0.0 collective-permute-done.9.rest_3_
  96.4 0.0 copy-start.9
  96.4 6.2 %collective-permute-done.10.rest_4_ = bf16[16,3072]{1,0:T(8,128)(2,1)S(1)} collective-permute-done((bf16[16,3072]{1,0:T(8,128)(2,1)}, bf16[16,3072]{1,0:T(8,128)(2,1)S(1)}, u32[]{:S(2)}, u32[]{:S(2)}) %collective-permute-start.10) | collective-permute-done | bytes 98336 | tf_op jit(solution)/shard_map/ppermute | solution.py:183
  102.6 0.0 copy-start.10
  102.6 1.9 %collective-permute-done.11.rest_5_ = bf16[16,3072]{1,0:T(8,128)(2,1)S(1)} collective-permute-done((bf16[16,3072]{1,0:T(8,128)(2,1)}, bf16[16,3072]{1,0:T(8,128)(2,1)S(1)}, u32[]{:S(2)}, u32[]{:S(2)}) %collective-permute-start.11) | collective-permute-done | bytes 98336 | tf_op jit(solution)/shard_map/ppermute | solution.py:183
  104.4 0.0 copy-start.11
  104.4 2.0 %collective-permute-done.12.rest_6_ = bf16[16,3072]{1,0:T(8,128)(2,1)S(1)} collective-permute-done((bf16[16,3072]{1,0:T(8,128)(2,1)}, bf16[16,3072]{1,0:T(8,128)(2,1)S(1)}, u32[]{:S(2)}, u32[]{:S(2)}) %collective-permute-start.12) | collective-permute-done | bytes 98336 | tf_op jit(solution)/shard_map/ppermute | solution.py:183
  106.4 0.0 copy-start.12
  106.4 2.0 %collective-permute-done.13.rest_7_ = bf16[16,3072]{1,0:T(8,128)(2,1)S(1)} collective-permute-done((bf16[16,3072]{1,0:T(8,128)(2,1)}, bf16[16,3072]{1,0:T(8,128)(2,1)S(1)}, u32[]{:S(2)}, u32[]{:S(2)}) %collective-permute-start.13) | collective-permute-done | bytes 98336 | tf_op jit(solution)/shard_map/ppermute | solution.py:183
  108.4 0.0 copy-start.13
  108.4 0.0 copy-done.7
  108.4 0.0 copy-done.8
  108.4 0.0 copy-done.9
  108.4 0.0 copy-done.10
  108.4 0.0 copy-done.11
  108.4 0.0 copy-done.12
  108.4 0.6 copy-done.13
  109.0 22.5 %unpack.1 = (bf16[8,16,2048]{2,1,0:T(8,128)(2,1)}, bf16[8,16,256]{2,1,0:T(8,128)(2,1)}, bf16[8,16,256]{2,1,0:T(8,128)(2,1)}, bf16[12,256]{1,0:T(8,128)(2,1)}, bf16[12,256]{1,0:T(8,128)(2,1)}) custom-call(s32[8]{0:T(128)} %home_ref.5, bf16[16,3072]{1,0:T(8,128)(2,1)} %get-tuple-element.37.rest_0_, bf16[16,3072]{1,0:T(8,128)(2,1)} %copy-done.7, ...), custom_call_target="tpu_custom_call" | custom-call | tf_op jit(solution)/shard_map/unpack/pallas_call | solution.py:236
Async XLA Ops:
  38.6 7.4 %collective-permute-start = (bf16[16,5120]{1,0:T(8,128)(2,1)}, bf16[16,5120]{1,0:T(8,128)(2,1)S(1)}, u32[]{:S(2)}, u32[]{:S(2)}) collective-permute-start(bf16[16,5120]{1,0:T(8,128)(2,1)} %get-tuple-element.29), channel_id=1, source_target_pairs={{0,2},{2,0},{4,6},{6,4},{8,10},{10,8},{12,14},{14,12},{1,3},{3,1},... | collective-permute-start | bytes 491528 | tf_op jit(solution)/shard_map/ppermute | solution.py:183
  40.2 11.2 %collective-permute-start.1 = (bf16[16,5120]{1,0:T(8,128)(2,1)}, bf16[16,5120]{1,0:T(8,128)(2,1)S(1)}, u32[]{:S(2)}, u32[]{:S(2)}) collective-permute-start(bf16[16,5120]{1,0:T(8,128)(2,1)} %get-tuple-element.30), channel_id=1, source_target_pairs={{0,4},{2,6},{4,0},{6,2},{8,12},{10,14},{12,8},{14,10},{1,5},{3,7},... | collective-permute-start | bytes 491528 | tf_op jit(solution)/shard_map/ppermute | solution.py:183
  40.6 13.0 %collective-permute-start.2 = (bf16[16,5120]{1,0:T(8,128)(2,1)}, bf16[16,5120]{1,0:T(8,128)(2,1)S(1)}, u32[]{:S(2)}, u32[]{:S(2)}) collective-permute-start(bf16[16,5120]{1,0:T(8,128)(2,1)} %get-tuple-element.31), channel_id=1, source_target_pairs={{0,6},{2,4},{4,2},{6,0},{8,14},{10,12},{12,10},{14,8},{1,7},{3,5},... | collective-permute-start | bytes 491528 | tf_op jit(solution)/shard_map/ppermute | solution.py:183
  42.1 21.5 %collective-permute-start.3 = (bf16[16,5120]{1,0:T(8,128)(2,1)}, bf16[16,5120]{1,0:T(8,128)(2,1)S(1)}, u32[]{:S(2)}, u32[]{:S(2)}) collective-permute-start(bf16[16,5120]{1,0:T(8,128)(2,1)} %get-tuple-element.32), channel_id=1, source_target_pairs={{0,8},{2,10},{4,12},{6,14},{8,0},{10,2},{12,4},{14,6},{1,9},{3,11}... | collective-permute-start | bytes 491528 | tf_op jit(solution)/shard_map/ppermute | solution.py:183
  44.7 22.5 %collective-permute-start.4 = (bf16[16,5120]{1,0:T(8,128)(2,1)}, bf16[16,5120]{1,0:T(8,128)(2,1)S(1)}, u32[]{:S(2)}, u32[]{:S(2)}) collective-permute-start(bf16[16,5120]{1,0:T(8,128)(2,1)} %get-tuple-element.33), channel_id=1, source_target_pairs={{0,10},{2,8},{4,14},{6,12},{8,2},{10,0},{12,6},{14,4},{1,11},{3,9}... | collective-permute-start | bytes 491528 | tf_op jit(solution)/shard_map/ppermute | solution.py:183
  46.0 27.1 %copy-start = (bf16[16,5120]{1,0:T(8,128)(2,1)}, bf16[16,5120]{1,0:T(8,128)(2,1)S(1)}, u32[]{:S(2)}) copy-start(bf16[16,5120]{1,0:T(8,128)(2,1)S(1)} %collective-permute-done.rest_1_) | copy-start | bytes 491524
  46.0 24.5 %collective-permute-start.5 = (bf16[16,5120]{1,0:T(8,128)(2,1)}, bf16[16,5120]{1,0:T(8,128)(2,1)S(1)}, u32[]{:S(2)}, u32[]{:S(2)}) collective-permute-start(bf16[16,5120]{1,0:T(8,128)(2,1)} %get-tuple-element.34), channel_id=1, source_target_pairs={{0,12},{2,14},{4,8},{6,10},{8,4},{10,6},{12,0},{14,2},{1,13},{3,15... | collective-permute-start | bytes 491528 | tf_op jit(solution)/shard_map/ppermute | solution.py:183
  51.3 21.8 %copy-start.1 = (bf16[16,5120]{1,0:T(8,128)(2,1)}, bf16[16,5120]{1,0:T(8,128)(2,1)S(1)}, u32[]{:S(2)}) copy-start(bf16[16,5120]{1,0:T(8,128)(2,1)S(1)} %collective-permute-done.1.rest_2_) | copy-start | bytes 491524
  51.3 21.8 %collective-permute-start.6 = (bf16[16,5120]{1,0:T(8,128)(2,1)}, bf16[16,5120]{1,0:T(8,128)(2,1)S(1)}, u32[]{:S(2)}, u32[]{:S(2)}) collective-permute-start(bf16[16,5120]{1,0:T(8,128)(2,1)} %get-tuple-element.35), channel_id=1, source_target_pairs={{0,14},{2,12},{4,10},{6,8},{8,6},{10,4},{12,2},{14,0},{1,15},{3,13... | collective-permute-start | bytes 491528 | tf_op jit(solution)/shard_map/ppermute | solution.py:183
  53.6 19.5 %copy-start.2 = (bf16[16,5120]{1,0:T(8,128)(2,1)}, bf16[16,5120]{1,0:T(8,128)(2,1)S(1)}, u32[]{:S(2)}) copy-start(bf16[16,5120]{1,0:T(8,128)(2,1)S(1)} %collective-permute-done.2.rest_3_) | copy-start | bytes 491524
  63.7 9.4 %copy-start.3 = (bf16[16,5120]{1,0:T(8,128)(2,1)}, bf16[16,5120]{1,0:T(8,128)(2,1)S(1)}, u32[]{:S(2)}) copy-start(bf16[16,5120]{1,0:T(8,128)(2,1)S(1)} %collective-permute-done.3.rest_4_) | copy-start | bytes 491524
  67.2 5.9 %copy-start.4 = (bf16[16,5120]{1,0:T(8,128)(2,1)}, bf16[16,5120]{1,0:T(8,128)(2,1)S(1)}, u32[]{:S(2)}) copy-start(bf16[16,5120]{1,0:T(8,128)(2,1)S(1)} %collective-permute-done.4.rest_5_) | copy-start | bytes 491524
  70.5 2.6 %copy-start.5 = (bf16[16,5120]{1,0:T(8,128)(2,1)}, bf16[16,5120]{1,0:T(8,128)(2,1)S(1)}, u32[]{:S(2)}) copy-start(bf16[16,5120]{1,0:T(8,128)(2,1)S(1)} %collective-permute-done.5.rest_6_) | copy-start | bytes 491524
  73.1 0.7 copy-start.6
  86.3 6.6 %collective-permute-start.7 = (bf16[16,3072]{1,0:T(8,128)(2,1)}, bf16[16,3072]{1,0:T(8,128)(2,1)S(1)}, u32[]{:S(2)}, u32[]{:S(2)}) collective-permute-start(bf16[16,3072]{1,0:T(8,128)(2,1)} %get-tuple-element.38), channel_id=1, source_target_pairs={{0,2},{2,0},{4,6},{6,4},{8,10},{10,8},{12,14},{14,12},{1,3},{3,1},... | collective-permute-start | bytes 294920 | tf_op jit(solution)/shard_map/ppermute | solution.py:183
  87.1 8.2 %collective-permute-start.8 = (bf16[16,3072]{1,0:T(8,128)(2,1)}, bf16[16,3072]{1,0:T(8,128)(2,1)S(1)}, u32[]{:S(2)}, u32[]{:S(2)}) collective-permute-start(bf16[16,3072]{1,0:T(8,128)(2,1)} %get-tuple-element.39), channel_id=1, source_target_pairs={{0,4},{2,6},{4,0},{6,2},{8,12},{10,14},{12,8},{14,10},{1,5},{3,7},... | collective-permute-start | bytes 294920 | tf_op jit(solution)/shard_map/ppermute | solution.py:183
  87.1 9.2 %collective-permute-start.9 = (bf16[16,3072]{1,0:T(8,128)(2,1)}, bf16[16,3072]{1,0:T(8,128)(2,1)S(1)}, u32[]{:S(2)}, u32[]{:S(2)}) collective-permute-start(bf16[16,3072]{1,0:T(8,128)(2,1)} %get-tuple-element.40), channel_id=1, source_target_pairs={{0,6},{2,4},{4,2},{6,0},{8,14},{10,12},{12,10},{14,8},{1,7},{3,5},... | collective-permute-start | bytes 294920 | tf_op jit(solution)/shard_map/ppermute | solution.py:183
  89.9 12.7 %collective-permute-start.10 = (bf16[16,3072]{1,0:T(8,128)(2,1)}, bf16[16,3072]{1,0:T(8,128)(2,1)S(1)}, u32[]{:S(2)}, u32[]{:S(2)}) collective-permute-start(bf16[16,3072]{1,0:T(8,128)(2,1)} %get-tuple-element.41), channel_id=1, source_target_pairs={{0,8},{2,10},{4,12},{6,14},{8,0},{10,2},{12,4},{14,6},{1,9},{3,11}... | collective-permute-start | bytes 294920 | tf_op jit(solution)/shard_map/ppermute | solution.py:183
  91.9 12.6 %collective-permute-start.11 = (bf16[16,3072]{1,0:T(8,128)(2,1)}, bf16[16,3072]{1,0:T(8,128)(2,1)S(1)}, u32[]{:S(2)}, u32[]{:S(2)}) collective-permute-start(bf16[16,3072]{1,0:T(8,128)(2,1)} %get-tuple-element.42), channel_id=1, source_target_pairs={{0,10},{2,8},{4,14},{6,12},{8,2},{10,0},{12,6},{14,4},{1,11},{3,9}... | collective-permute-start | bytes 294920 | tf_op jit(solution)/shard_map/ppermute | solution.py:183
  93.0 15.4 %copy-start.7 = (bf16[16,3072]{1,0:T(8,128)(2,1)}, bf16[16,3072]{1,0:T(8,128)(2,1)S(1)}, u32[]{:S(2)}) copy-start(bf16[16,3072]{1,0:T(8,128)(2,1)S(1)} %collective-permute-done.7.rest_1_) | copy-start | bytes 294916
  93.0 13.4 %collective-permute-start.12 = (bf16[16,3072]{1,0:T(8,128)(2,1)}, bf16[16,3072]{1,0:T(8,128)(2,1)S(1)}, u32[]{:S(2)}, u32[]{:S(2)}) collective-permute-start(bf16[16,3072]{1,0:T(8,128)(2,1)} %get-tuple-element.43), channel_id=1, source_target_pairs={{0,12},{2,14},{4,8},{6,10},{8,4},{10,6},{12,0},{14,2},{1,13},{3,15... | collective-permute-start | bytes 294920 | tf_op jit(solution)/shard_map/ppermute | solution.py:183
  95.3 13.0 %copy-start.8 = (bf16[16,3072]{1,0:T(8,128)(2,1)}, bf16[16,3072]{1,0:T(8,128)(2,1)S(1)}, u32[]{:S(2)}) copy-start(bf16[16,3072]{1,0:T(8,128)(2,1)S(1)} %collective-permute-done.8.rest_2_) | copy-start | bytes 294916
  95.3 13.0 %collective-permute-start.13 = (bf16[16,3072]{1,0:T(8,128)(2,1)}, bf16[16,3072]{1,0:T(8,128)(2,1)S(1)}, u32[]{:S(2)}, u32[]{:S(2)}) collective-permute-start(bf16[16,3072]{1,0:T(8,128)(2,1)} %get-tuple-element.44), channel_id=1, source_target_pairs={{0,14},{2,12},{4,10},{6,8},{8,6},{10,4},{12,2},{14,0},{1,15},{3,13... | collective-permute-start | bytes 294920 | tf_op jit(solution)/shard_map/ppermute | solution.py:183
  96.4 12.0 %copy-start.9 = (bf16[16,3072]{1,0:T(8,128)(2,1)}, bf16[16,3072]{1,0:T(8,128)(2,1)S(1)}, u32[]{:S(2)}) copy-start(bf16[16,3072]{1,0:T(8,128)(2,1)S(1)} %collective-permute-done.9.rest_3_) | copy-start | bytes 294916
  102.6 5.8 %copy-start.10 = (bf16[16,3072]{1,0:T(8,128)(2,1)}, bf16[16,3072]{1,0:T(8,128)(2,1)S(1)}, u32[]{:S(2)}) copy-start(bf16[16,3072]{1,0:T(8,128)(2,1)S(1)} %collective-permute-done.10.rest_4_) | copy-start | bytes 294916
  104.4 4.0 %copy-start.11 = (bf16[16,3072]{1,0:T(8,128)(2,1)}, bf16[16,3072]{1,0:T(8,128)(2,1)S(1)}, u32[]{:S(2)}) copy-start(bf16[16,3072]{1,0:T(8,128)(2,1)S(1)} %collective-permute-done.11.rest_5_) | copy-start | bytes 294916
  106.4 2.0 %copy-start.12 = (bf16[16,3072]{1,0:T(8,128)(2,1)}, bf16[16,3072]{1,0:T(8,128)(2,1)S(1)}, u32[]{:S(2)}) copy-start(bf16[16,3072]{1,0:T(8,128)(2,1)S(1)} %collective-permute-done.12.rest_6_) | copy-start | bytes 294916
  108.4 0.6 copy-start.13

commit v2 on v1

--- a/solution.py
+++ b/solution.py
@@ -26,59 +26,36 @@
     return lax.dot_general(left, right, ((contract[0], contract[1]), ((), ())), preferred_element_type=F32)
 
 
-def pack_kernel(home_ref, q_ref, k_ref, v_ref, g_ref, pk_ref, pv_ref, *rest, count):
-    blocks, prompt, sems = rest[:count], rest[count], rest[count + 1]
+def pack_kernel(home_ref, q_ref, k_ref, v_ref, g_ref, pk_ref, pv_ref, *blocks, count):
     rank = lax.axis_index("seq")
     prompt_rows, kv_width = pk_ref.shape
-    q_width = q_ref.shape[2]
-    starts = []
+    rows = q_ref.shape[1]
+    spare = jnp.zeros((rows - prompt_rows, kv_width), BF16)
+    prompt = [jnp.concatenate([ref[...], spare], axis=0) for ref in (pk_ref, pv_ref)]
     for distance in range(count):
         index = resident_of(home_ref, rank ^ distance, count)
-        block = blocks[distance]
         low = 0
-        for part, ref in enumerate((q_ref, g_ref, k_ref, v_ref)):
-            width = ref.shape[2]
-            starts.append(
-                pltpu.make_async_copy(
-                    ref.at[index], block.at[:, pl.ds(low, width)], sems.at[distance, part]
-                )
-            )
-            starts[-1].start()
-            low += width
-    prompt[...] = jnp.zeros(prompt.shape, BF16)
-    prompt[:prompt_rows, :kv_width] = pk_ref[...]
-    prompt[:prompt_rows, kv_width:] = pv_ref[...]
-    low = 2 * q_width + 2 * kv_width
-    for distance in range(count):
-        starts.append(
-            pltpu.make_async_copy(
-                prompt, blocks[distance].at[:, pl.ds(low, 2 * kv_width)], sems.at[distance, 4]
-            )
-        )
-        starts[-1].start()
-    for copy in starts:
-        copy.wait()
+        for ref in (q_ref, g_ref, k_ref, v_ref):
+            blocks[distance][:, low : low + ref.shape[2]] = ref[index]
+            low += ref.shape[2]
+        for part in prompt:
+            blocks[distance][:, low : low + kv_width] = part
+            low += kv_width
 
 
 def attend_kernel(lengths_ref, home_ref, seen_ref, *rest, count, prompt_rows, q_width, kv_width):
     blocks = rest[:count]
     out_ref = rest[count]
     returns = rest[count + 1 : 2 * count + 1]
-    x, y, o, in_sems, out_sems = rest[2 * count + 1 :]
+    x, y = rest[2 * count + 1 :]
     rank = lax.axis_index("seq")
     rows = blocks[0].shape[0]
     total = rows * count
     kv_count = kv_width // HEAD_DIM
     group_size = q_width // kv_width
     scale = 1.0 / HEAD_DIM**0.5
-    arrivals = []
     for distance in range(count):
-        arrivals.append(
-            pltpu.make_async_copy(
-                blocks[distance], x.at[pl.ds((rank ^ distance) * rows, rows), :], in_sems.at[distance]
-            )
-        )
-        arrivals[-1].start()
+        x[pl.ds(pl.multiple_of((rank ^ distance) * rows, rows), rows), :] = blocks[distance][...]
     own = resident_of(home_ref, rank, count)
     length = lengths_ref[own]
     visible = seen_ref[own]
@@ -90,9 +67,6 @@
         [(shard_row < prompt_rows) & (prompt_index < visible), column <= position], axis=1
     )
     live = lax.broadcasted_iota(jnp.int32, (total, HEAD_DIM), 0) < length
-    for copy in arrivals:
-        copy.wait()
-    leaving = []
     for kv in range(kv_count):
         low = 2 * q_width + kv * HEAD_DIM
         keys = jnp.concatenate(
@@ -114,7 +88,7 @@
             prob = raised * (1.0 / jnp.sum(raised, axis=1, keepdims=True))
             weights = prob.astype(BF16)
             output = jnp.where(live, dot(weights, values, ((1,), (0,))), 0.0).astype(BF16)
-            o[:, head : head + HEAD_DIM] = output
+            out_ref[0, :, head : head + HEAD_DIM] = output
             row_dot = jnp.sum(grad.astype(F32) * output.astype(F32), axis=1, keepdims=True)
             dlogit = (prob * (spread - row_dot)).astype(BF16)
             y[:, head : head + HEAD_DIM] = (dot(dlogit, keys, ((1,), (0,))) * scale).astype(BF16)
@@ -127,54 +101,26 @@
             at += 2 * kv_width
             y[:, at : at + HEAD_DIM] = summed[:total].astype(BF16)
     for distance in range(count):
-        leaving.append(
-            pltpu.make_async_copy(
-                y.at[pl.ds((rank ^ distance) * rows, rows), :], returns[distance], out_sems.at[distance]
-            )
-        )
-        leaving[-1].start()
-    leaving.append(pltpu.make_async_copy(o, out_ref.at[0], out_sems.at[count]))
-    leaving[-1].start()
-    for copy in leaving:
-        copy.wait()
-
-
-def unpack_kernel(home_ref, *rest, count, q_width, kv_width):
+        returns[distance][...] = y[pl.ds(pl.multiple_of((rank ^ distance) * rows, rows), rows), :]
+
+
+def unpack_kernel(home_ref, *rest, count, kv_width):
     blocks = rest[:count]
-    qg_ref, kg_ref, vg_ref, pkg_ref, pvg_ref, parts, sems = rest[count:]
+    qg_ref, kg_ref, vg_ref, pkg_ref, pvg_ref = rest[count:]
     rank = lax.axis_index("seq")
     prompt_rows = pkg_ref.shape[0]
-    copies = []
-    for distance in range(count):
-        low = q_width + 2 * kv_width
-        copies.append(
-            pltpu.make_async_copy(
-                blocks[distance].at[:, pl.ds(low, 2 * kv_width)], parts.at[distance], sems.at[distance, 0]
-            )
-        )
-        copies[-1].start()
-    moves = []
+    summed = [jnp.zeros((blocks[0].shape[0], kv_width), F32)] * 2
     for distance in range(count):
         index = resident_of(home_ref, rank ^ distance, count)
         low = 0
-        for part, ref in enumerate((qg_ref, kg_ref, vg_ref)):
-            width = ref.shape[2]
-            moves.append(
-                pltpu.make_async_copy(
-                    blocks[distance].at[:, pl.ds(low, width)], ref.at[index], sems.at[distance, part + 1]
-                )
-            )
-            moves[-1].start()
-            low += width
-    for copy in copies:
-        copy.wait()
-    summed = parts[0].astype(F32)
-    for distance in range(1, count):
-        summed += parts[distance].astype(F32)
-    pkg_ref[...] = summed[:prompt_rows, :kv_width].astype(BF16)
-    pvg_ref[...] = summed[:prompt_rows, kv_width:].astype(BF16)
-    for copy in moves:
-        copy.wait()
+        for ref in (qg_ref, kg_ref, vg_ref):
+            ref[index] = blocks[distance][:, low : low + ref.shape[2]]
+            low += ref.shape[2]
+        for part in range(2):
+            summed[part] = summed[part] + blocks[distance][:, low : low + kv_width].astype(F32)
+            low += kv_width
+    pkg_ref[...] = summed[0][:prompt_rows].astype(BF16)
+    pvg_ref[...] = summed[1][:prompt_rows].astype(BF16)
 
 
 def exchange(blocks):
@@ -184,7 +130,6 @@
     ]
 
 
-ANY = pl.BlockSpec(memory_space=pl.ANY)
 SMEM = pl.BlockSpec(memory_space=pltpu.SMEM)
 VMEM = pl.BlockSpec(memory_space=pltpu.VMEM)
 
@@ -210,9 +155,8 @@
         functools.partial(pack_kernel, count=count),
         name="pack",
         out_shape=[jax.ShapeDtypeStruct((rows, in_width), BF16)] * count,
-        in_specs=[SMEM, ANY, ANY, ANY, ANY, VMEM, VMEM],
-        out_specs=[ANY] * count,
-        scratch_shapes=[pltpu.VMEM((rows, 2 * kv_width), BF16), pltpu.SemaphoreType.DMA((count, 5))],
+        in_specs=[SMEM] + [VMEM] * 6,
+        out_specs=[VMEM] * count,
     )(home_rank, response_query, response_key, response_value, response_grad, prompt_key, prompt_value)
     arrived = exchange(blocks)
     output, *returns = pl.pallas_call(
@@ -222,19 +166,16 @@
         name="attend",
         out_shape=[jax.ShapeDtypeStruct((1, total, q_width), BF16)]
         + [jax.ShapeDtypeStruct((rows, back_width), BF16)] * count,
-        in_specs=[SMEM] * 3 + [ANY] * count,
-        out_specs=[ANY] * (count + 1),
+        in_specs=[SMEM] * 3 + [VMEM] * count,
+        out_specs=[VMEM] * (count + 1),
         scratch_shapes=[
             pltpu.VMEM((total, in_width), BF16),
             pltpu.VMEM((total, back_width), BF16),
-            pltpu.VMEM((total, q_width), BF16),
-            pltpu.SemaphoreType.DMA((count,)),
-            pltpu.SemaphoreType.DMA((count + 1,)),
         ],
     )(lengths, home_rank, prompt_seen, *arrived)
     returned = exchange(returns)
     grads = pl.pallas_call(
-        functools.partial(unpack_kernel, count=count, q_width=q_width, kv_width=kv_width),
+        functools.partial(unpack_kernel, count=count, kv_width=kv_width),
         name="unpack",
         out_shape=[
             jax.ShapeDtypeStruct((count, rows, q_width), BF16),
@@ -243,12 +184,8 @@
             jax.ShapeDtypeStruct((prompt_rows, kv_width), BF16),
             jax.ShapeDtypeStruct((prompt_rows, kv_width), BF16),
         ],
-        in_specs=[SMEM] + [ANY] * count,
-        out_specs=[ANY, ANY, ANY, VMEM, VMEM],
-        scratch_shapes=[
-            pltpu.VMEM((count, rows, 2 * kv_width), BF16),
-            pltpu.SemaphoreType.DMA((count, 4)),
-        ],
+        in_specs=[SMEM] + [VMEM] * count,
+        out_specs=[VMEM] * 5,
     )(home_rank, *returned)
     return (output, *grads)
 

time: 132 us -> 74.7 us (0.57)
  Pallas kernels: 73.1 us -> 16.2 us
    pallas_call x1, Pallas kernels: 38 us -> 2.39 us  [packed_body(): pl.pallas_call(functools.partial(pack_kernel, count=count), name='pack',...]
    pallas_call x1, Pallas kernels: 22.5 us -> 2.11 us  [packed_body(): pl.pallas_call(functools.partial(unpack_kernel, count=count, kv_width=kv_...]
where the time goes in v2:
time: 74.7 us; the launch traced here: 74.5 us
  waiting for transfers between devices  37.5 us (50%)
  starting transfers between devices  18.9 us (25%)
  Pallas kernels  16.2 us (22%)
  local copies, waits for them, and re-layouts  1.25 us (2%)
    ppermute x14, waiting for transfers between devices, exchange(): lax.ppermute(blocks[d], 'seq', [(i, i ^ d) for i in range(count)])  37.5 us
    ppermute x14, starting transfers between devices, exchange(): lax.ppermute(blocks[d], 'seq', [(i, i ^ d) for i in range(count)])  18.9 us
    pallas_call x1, Pallas kernels, packed_body(): pl.pallas_call(functools.partial(attend_kernel, count=count, prompt_rows=...  11.7 us
    pallas_call x1, Pallas kernels, packed_body(): pl.pallas_call(functools.partial(pack_kernel, count=count), name='pack',...  2.39 us
    pallas_call x1, Pallas kernels, packed_body(): pl.pallas_call(functools.partial(unpack_kernel, count=count, kv_width=kv_...  2.11 us
  transfers between devices with their start and end apart: 14, of which 10 were waited for; matrix products, arithmetic and copies ran while one was open for 0% of the time, Pallas kernels for 0%

profile of v2, /device:TPU:8, one launch (start us, length us, event | category | flops | bytes accessed | tf_op | source)
XLA Modules:
  0.0 74.5 jit_solution(18221310590919634683)
XLA Ops:
  0.6 2.4 %pack.1 = (bf16[16,5120]{1,0:T(8,128)(2,1)}, bf16[16,5120]{1,0:T(8,128)(2,1)}, bf16[16,5120]{1,0:T(8,128)(2,1)}, bf16[16,5120]{1,0:T(8,128)(2,1)}, bf16[16,5120]...) custom-call(s32[8]{0:T(128)} %home_ref.5, ...), custom_call_target="tpu_custom_call" | custom-call | tf_op jit(solution)/shard_map/pack/pallas_call | solution.py:154
  3.0 1.5 %collective-permute-start = (bf16[16,5120]{1,0:T(8,128)(2,1)}, bf16[16,5120]{1,0:T(8,128)(2,1)S(1)}, u32[]{:S(2)}, u32[]{:S(2)}) collective-permute-start(bf16[16,5120]{1,0:T(8,128)(2,1)} %get-tuple-element.29), channel_id=1, source_target_pairs={{0,2},{2,0},{4,6},{6,4},{8,10},{10,8},{12,14},{14,12},{1,3},{3,1},... | collective-permute-start | bytes 491528 | tf_op jit(solution)/shard_map/ppermute | solution.py:129
  4.5 0.4 collective-permute-start.1
  5.0 1.5 %collective-permute-start.2 = (bf16[16,5120]{1,0:T(8,128)(2,1)}, bf16[16,5120]{1,0:T(8,128)(2,1)S(1)}, u32[]{:S(2)}, u32[]{:S(2)}) collective-permute-start(bf16[16,5120]{1,0:T(8,128)(2,1)} %get-tuple-element.31), channel_id=1, source_target_pairs={{0,6},{2,4},{4,2},{6,0},{8,14},{10,12},{12,10},{14,8},{1,7},{3,5},... | collective-permute-start | bytes 491528 | tf_op jit(solution)/shard_map/ppermute | solution.py:129
  6.5 2.6 %collective-permute-start.3 = (bf16[16,5120]{1,0:T(8,128)(2,1)}, bf16[16,5120]{1,0:T(8,128)(2,1)S(1)}, u32[]{:S(2)}, u32[]{:S(2)}) collective-permute-start(bf16[16,5120]{1,0:T(8,128)(2,1)} %get-tuple-element.32), channel_id=1, source_target_pairs={{0,8},{2,10},{4,12},{6,14},{8,0},{10,2},{12,4},{14,6},{1,9},{3,11}... | collective-permute-start | bytes 491528 | tf_op jit(solution)/shard_map/ppermute | solution.py:129
  9.1 1.3 %collective-permute-start.4 = (bf16[16,5120]{1,0:T(8,128)(2,1)}, bf16[16,5120]{1,0:T(8,128)(2,1)S(1)}, u32[]{:S(2)}, u32[]{:S(2)}) collective-permute-start(bf16[16,5120]{1,0:T(8,128)(2,1)} %get-tuple-element.33), channel_id=1, source_target_pairs={{0,10},{2,8},{4,14},{6,12},{8,2},{10,0},{12,6},{14,4},{1,11},{3,9}... | collective-permute-start | bytes 491528 | tf_op jit(solution)/shard_map/ppermute | solution.py:129
  10.4 0.0 collective-permute-done.rest_1_
  10.4 0.0 copy-start
  10.4 1.6 %collective-permute-start.5 = (bf16[16,5120]{1,0:T(8,128)(2,1)}, bf16[16,5120]{1,0:T(8,128)(2,1)S(1)}, u32[]{:S(2)}, u32[]{:S(2)}) collective-permute-start(bf16[16,5120]{1,0:T(8,128)(2,1)} %get-tuple-element.34), channel_id=1, source_target_pairs={{0,12},{2,14},{4,8},{6,10},{8,4},{10,6},{12,0},{14,2},{1,13},{3,15... | collective-permute-start | bytes 491528 | tf_op jit(solution)/shard_map/ppermute | solution.py:129
  11.9 3.7 %collective-permute-done.1.rest_2_ = bf16[16,5120]{1,0:T(8,128)(2,1)S(1)} collective-permute-done((bf16[16,5120]{1,0:T(8,128)(2,1)}, bf16[16,5120]{1,0:T(8,128)(2,1)S(1)}, u32[]{:S(2)}, u32[]{:S(2)}) %collective-permute-start.1) | collective-permute-done | bytes 163872 | tf_op jit(solution)/shard_map/ppermute | solution.py:129
  15.7 0.0 copy-start.1
  15.7 0.0 collective-permute-start.6
  15.7 2.3 %collective-permute-done.2.rest_3_ = bf16[16,5120]{1,0:T(8,128)(2,1)S(1)} collective-permute-done((bf16[16,5120]{1,0:T(8,128)(2,1)}, bf16[16,5120]{1,0:T(8,128)(2,1)S(1)}, u32[]{:S(2)}, u32[]{:S(2)}) %collective-permute-start.2) | collective-permute-done | bytes 163872 | tf_op jit(solution)/shard_map/ppermute | solution.py:129
  17.9 0.0 copy-start.2
  17.9 10.1 %collective-permute-done.3.rest_4_ = bf16[16,5120]{1,0:T(8,128)(2,1)S(1)} collective-permute-done((bf16[16,5120]{1,0:T(8,128)(2,1)}, bf16[16,5120]{1,0:T(8,128)(2,1)S(1)}, u32[]{:S(2)}, u32[]{:S(2)}) %collective-permute-start.3) | collective-permute-done | bytes 163872 | tf_op jit(solution)/shard_map/ppermute | solution.py:129
  28.1 0.0 copy-start.3
  28.1 3.5 %collective-permute-done.4.rest_5_ = bf16[16,5120]{1,0:T(8,128)(2,1)S(1)} collective-permute-done((bf16[16,5120]{1,0:T(8,128)(2,1)}, bf16[16,5120]{1,0:T(8,128)(2,1)S(1)}, u32[]{:S(2)}, u32[]{:S(2)}) %collective-permute-start.4) | collective-permute-done | bytes 163872 | tf_op jit(solution)/shard_map/ppermute | solution.py:129
  31.6 0.0 copy-start.4
  31.6 3.3 %collective-permute-done.5.rest_6_ = bf16[16,5120]{1,0:T(8,128)(2,1)S(1)} collective-permute-done((bf16[16,5120]{1,0:T(8,128)(2,1)}, bf16[16,5120]{1,0:T(8,128)(2,1)S(1)}, u32[]{:S(2)}, u32[]{:S(2)}) %collective-permute-start.5) | collective-permute-done | bytes 163872 | tf_op jit(solution)/shard_map/ppermute | solution.py:129
  34.9 0.0 copy-start.5
  34.9 2.5 %collective-permute-done.6.rest_7_ = bf16[16,5120]{1,0:T(8,128)(2,1)S(1)} collective-permute-done((bf16[16,5120]{1,0:T(8,128)(2,1)}, bf16[16,5120]{1,0:T(8,128)(2,1)S(1)}, u32[]{:S(2)}, u32[]{:S(2)}) %collective-permute-start.6) | collective-permute-done | bytes 163872 | tf_op jit(solution)/shard_map/ppermute | solution.py:129
  37.4 0.0 copy-start.6
  37.4 0.0 copy-done
  37.4 0.0 copy-done.1
  37.4 0.0 copy-done.2
  37.4 0.0 copy-done.3
  37.5 0.0 copy-done.4
  37.5 0.0 copy-done.5
  37.5 0.6 copy-done.6
  38.1 11.7 %attend.1 = (bf16[1,128,2048]{2,1,0:T(8,128)(2,1)}, bf16[16,3072]{1,0:T(8,128)(2,1)}, bf16[16,3072]{1,0:T(8,128)(2,1)}, bf16[16,3072]{1,0:T(8,128)(2,1)}, bf16[1...) custom-call(s32[8]{0:T(128)} %lengths_ref.1, ...), custom_call_target="tpu_custom_call" | custom-call | tf_op jit(solution)/shard_map/attend/pallas_call | solution.py:162
  49.8 0.7 collective-permute-start.7
  50.5 0.0 collective-permute-start.8
  50.5 2.8 %collective-permute-start.9 = (bf16[16,3072]{1,0:T(8,128)(2,1)}, bf16[16,3072]{1,0:T(8,128)(2,1)S(1)}, u32[]{:S(2)}, u32[]{:S(2)}) collective-permute-start(bf16[16,3072]{1,0:T(8,128)(2,1)} %get-tuple-element.40), channel_id=1, source_target_pairs={{0,6},{2,4},{4,2},{6,0},{8,14},{10,12},{12,10},{14,8},{1,7},{3,5},... | collective-permute-start | bytes 294920 | tf_op jit(solution)/shard_map/ppermute | solution.py:129
  53.3 2.0 %collective-permute-start.10 = (bf16[16,3072]{1,0:T(8,128)(2,1)}, bf16[16,3072]{1,0:T(8,128)(2,1)S(1)}, u32[]{:S(2)}, u32[]{:S(2)}) collective-permute-start(bf16[16,3072]{1,0:T(8,128)(2,1)} %get-tuple-element.41), channel_id=1, source_target_pairs={{0,8},{2,10},{4,12},{6,14},{8,0},{10,2},{12,4},{14,6},{1,9},{3,11}... | collective-permute-start | bytes 294920 | tf_op jit(solution)/shard_map/ppermute | solution.py:129
  55.3 1.1 %collective-permute-start.11 = (bf16[16,3072]{1,0:T(8,128)(2,1)}, bf16[16,3072]{1,0:T(8,128)(2,1)S(1)}, u32[]{:S(2)}, u32[]{:S(2)}) collective-permute-start(bf16[16,3072]{1,0:T(8,128)(2,1)} %get-tuple-element.42), channel_id=1, source_target_pairs={{0,10},{2,8},{4,14},{6,12},{8,2},{10,0},{12,6},{14,4},{1,11},{3,9}... | collective-permute-start | bytes 294920 | tf_op jit(solution)/shard_map/ppermute | solution.py:129
  56.4 0.0 collective-permute-done.7.rest_1_
  56.4 0.0 copy-start.7
  56.4 2.3 %collective-permute-start.12 = (bf16[16,3072]{1,0:T(8,128)(2,1)}, bf16[16,3072]{1,0:T(8,128)(2,1)S(1)}, u32[]{:S(2)}, u32[]{:S(2)}) collective-permute-start(bf16[16,3072]{1,0:T(8,128)(2,1)} %get-tuple-element.43), channel_id=1, source_target_pairs={{0,12},{2,14},{4,8},{6,10},{8,4},{10,6},{12,0},{14,2},{1,13},{3,15... | collective-permute-start | bytes 294920 | tf_op jit(solution)/shard_map/ppermute | solution.py:129
  58.7 0.0 collective-permute-done.8.rest_2_
  58.7 0.0 copy-start.8
  58.7 1.0 %collective-permute-start.13 = (bf16[16,3072]{1,0:T(8,128)(2,1)}, bf16[16,3072]{1,0:T(8,128)(2,1)S(1)}, u32[]{:S(2)}, u32[]{:S(2)}) collective-permute-start(bf16[16,3072]{1,0:T(8,128)(2,1)} %get-tuple-element.44), channel_id=1, source_target_pairs={{0,14},{2,12},{4,10},{6,8},{8,6},{10,4},{12,2},{14,0},{1,15},{3,13... | collective-permute-start | bytes 294920 | tf_op jit(solution)/shard_map/ppermute | solution.py:129
  59.8 0.0 collective-permute-done.9.rest_3_
  59.8 0.0 copy-start.9
  59.8 6.2 %collective-permute-done.10.rest_4_ = bf16[16,3072]{1,0:T(8,128)(2,1)S(1)} collective-permute-done((bf16[16,3072]{1,0:T(8,128)(2,1)}, bf16[16,3072]{1,0:T(8,128)(2,1)S(1)}, u32[]{:S(2)}, u32[]{:S(2)}) %collective-permute-start.10) | collective-permute-done | bytes 98336 | tf_op jit(solution)/shard_map/ppermute | solution.py:129
  66.0 0.0 copy-start.10
  66.0 1.9 %collective-permute-done.11.rest_5_ = bf16[16,3072]{1,0:T(8,128)(2,1)S(1)} collective-permute-done((bf16[16,3072]{1,0:T(8,128)(2,1)}, bf16[16,3072]{1,0:T(8,128)(2,1)S(1)}, u32[]{:S(2)}, u32[]{:S(2)}) %collective-permute-start.11) | collective-permute-done | bytes 98336 | tf_op jit(solution)/shard_map/ppermute | solution.py:129
  67.8 0.0 copy-start.11
  67.8 2.0 %collective-permute-done.12.rest_6_ = bf16[16,3072]{1,0:T(8,128)(2,1)S(1)} collective-permute-done((bf16[16,3072]{1,0:T(8,128)(2,1)}, bf16[16,3072]{1,0:T(8,128)(2,1)S(1)}, u32[]{:S(2)}, u32[]{:S(2)}) %collective-permute-start.12) | collective-permute-done | bytes 98336 | tf_op jit(solution)/shard_map/ppermute | solution.py:129
  69.8 0.0 copy-start.12
  69.8 2.0 %collective-permute-done.13.rest_7_ = bf16[16,3072]{1,0:T(8,128)(2,1)S(1)} collective-permute-done((bf16[16,3072]{1,0:T(8,128)(2,1)}, bf16[16,3072]{1,0:T(8,128)(2,1)S(1)}, u32[]{:S(2)}, u32[]{:S(2)}) %collective-permute-start.13) | collective-permute-done | bytes 98336 | tf_op jit(solution)/shard_map/ppermute | solution.py:129
  71.8 0.0 copy-start.13
  71.8 0.0 copy-done.7
  71.8 0.0 copy-done.8
  71.8 0.0 copy-done.9
  71.8 0.0 copy-done.10
  71.8 0.0 copy-done.11
  71.8 0.0 copy-done.12
  71.8 0.6 copy-done.13
  72.4 2.1 %unpack.1 = (bf16[8,16,2048]{2,1,0:T(8,128)(2,1)}, bf16[8,16,256]{2,1,0:T(8,128)(2,1)}, bf16[8,16,256]{2,1,0:T(8,128)(2,1)}, bf16[12,256]{1,0:T(8,128)(2,1)}, bf16[12,256]{1,0:T(8,128)(2,1)}) custom-call(s32[8]{0:T(128)} %home_ref.5, bf16[16,3072]{1,0:T(8,128)(2,1)} %get-tuple-element.37.rest_0_, bf16[16,3072]{1,0:T(8,128)(2,1)} %copy-done.7, ...), custom_call_target="tpu_custom_call" | custom-call | tf_op jit(solution)/shard_map/unpack/pallas_call | solution.py:177
Async XLA Ops:
  3.0 7.3 %collective-permute-start = (bf16[16,5120]{1,0:T(8,128)(2,1)}, bf16[16,5120]{1,0:T(8,128)(2,1)S(1)}, u32[]{:S(2)}, u32[]{:S(2)}) collective-permute-start(bf16[16,5120]{1,0:T(8,128)(2,1)} %get-tuple-element.29), channel_id=1, source_target_pairs={{0,2},{2,0},{4,6},{6,4},{8,10},{10,8},{12,14},{14,12},{1,3},{3,1},... | collective-permute-start | bytes 491528 | tf_op jit(solution)/shard_map/ppermute | solution.py:129
  4.5 11.2 %collective-permute-start.1 = (bf16[16,5120]{1,0:T(8,128)(2,1)}, bf16[16,5120]{1,0:T(8,128)(2,1)S(1)}, u32[]{:S(2)}, u32[]{:S(2)}) collective-permute-start(bf16[16,5120]{1,0:T(8,128)(2,1)} %get-tuple-element.30), channel_id=1, source_target_pairs={{0,4},{2,6},{4,0},{6,2},{8,12},{10,14},{12,8},{14,10},{1,5},{3,7},... | collective-permute-start | bytes 491528 | tf_op jit(solution)/shard_map/ppermute | solution.py:129
  5.0 13.0 %collective-permute-start.2 = (bf16[16,5120]{1,0:T(8,128)(2,1)}, bf16[16,5120]{1,0:T(8,128)(2,1)S(1)}, u32[]{:S(2)}, u32[]{:S(2)}) collective-permute-start(bf16[16,5120]{1,0:T(8,128)(2,1)} %get-tuple-element.31), channel_id=1, source_target_pairs={{0,6},{2,4},{4,2},{6,0},{8,14},{10,12},{12,10},{14,8},{1,7},{3,5},... | collective-permute-start | bytes 491528 | tf_op jit(solution)/shard_map/ppermute | solution.py:129
  6.5 21.5 %collective-permute-start.3 = (bf16[16,5120]{1,0:T(8,128)(2,1)}, bf16[16,5120]{1,0:T(8,128)(2,1)S(1)}, u32[]{:S(2)}, u32[]{:S(2)}) collective-permute-start(bf16[16,5120]{1,0:T(8,128)(2,1)} %get-tuple-element.32), channel_id=1, source_target_pairs={{0,8},{2,10},{4,12},{6,14},{8,0},{10,2},{12,4},{14,6},{1,9},{3,11}... | collective-permute-start | bytes 491528 | tf_op jit(solution)/shard_map/ppermute | solution.py:129
  9.1 22.5 %collective-permute-start.4 = (bf16[16,5120]{1,0:T(8,128)(2,1)}, bf16[16,5120]{1,0:T(8,128)(2,1)S(1)}, u32[]{:S(2)}, u32[]{:S(2)}) collective-permute-start(bf16[16,5120]{1,0:T(8,128)(2,1)} %get-tuple-element.33), channel_id=1, source_target_pairs={{0,10},{2,8},{4,14},{6,12},{8,2},{10,0},{12,6},{14,4},{1,11},{3,9}... | collective-permute-start | bytes 491528 | tf_op jit(solution)/shard_map/ppermute | solution.py:129
  10.4 27.1 %copy-start = (bf16[16,5120]{1,0:T(8,128)(2,1)}, bf16[16,5120]{1,0:T(8,128)(2,1)S(1)}, u32[]{:S(2)}) copy-start(bf16[16,5120]{1,0:T(8,128)(2,1)S(1)} %collective-permute-done.rest_1_) | copy-start | bytes 491524
  10.4 24.5 %collective-permute-start.5 = (bf16[16,5120]{1,0:T(8,128)(2,1)}, bf16[16,5120]{1,0:T(8,128)(2,1)S(1)}, u32[]{:S(2)}, u32[]{:S(2)}) collective-permute-start(bf16[16,5120]{1,0:T(8,128)(2,1)} %get-tuple-element.34), channel_id=1, source_target_pairs={{0,12},{2,14},{4,8},{6,10},{8,4},{10,6},{12,0},{14,2},{1,13},{3,15... | collective-permute-start | bytes 491528 | tf_op jit(solution)/shard_map/ppermute | solution.py:129
  15.7 21.8 %copy-start.1 = (bf16[16,5120]{1,0:T(8,128)(2,1)}, bf16[16,5120]{1,0:T(8,128)(2,1)S(1)}, u32[]{:S(2)}) copy-start(bf16[16,5120]{1,0:T(8,128)(2,1)S(1)} %collective-permute-done.1.rest_2_) | copy-start | bytes 491524
  15.7 21.8 %collective-permute-start.6 = (bf16[16,5120]{1,0:T(8,128)(2,1)}, bf16[16,5120]{1,0:T(8,128)(2,1)S(1)}, u32[]{:S(2)}, u32[]{:S(2)}) collective-permute-start(bf16[16,5120]{1,0:T(8,128)(2,1)} %get-tuple-element.35), channel_id=1, source_target_pairs={{0,14},{2,12},{4,10},{6,8},{8,6},{10,4},{12,2},{14,0},{1,15},{3,13... | collective-permute-start | bytes 491528 | tf_op jit(solution)/shard_map/ppermute | solution.py:129
  17.9 19.5 %copy-start.2 = (bf16[16,5120]{1,0:T(8,128)(2,1)}, bf16[16,5120]{1,0:T(8,128)(2,1)S(1)}, u32[]{:S(2)}) copy-start(bf16[16,5120]{1,0:T(8,128)(2,1)S(1)} %collective-permute-done.2.rest_3_) | copy-start | bytes 491524
  28.1 9.4 %copy-start.3 = (bf16[16,5120]{1,0:T(8,128)(2,1)}, bf16[16,5120]{1,0:T(8,128)(2,1)S(1)}, u32[]{:S(2)}) copy-start(bf16[16,5120]{1,0:T(8,128)(2,1)S(1)} %collective-permute-done.3.rest_4_) | copy-start | bytes 491524
  31.6 5.9 %copy-start.4 = (bf16[16,5120]{1,0:T(8,128)(2,1)}, bf16[16,5120]{1,0:T(8,128)(2,1)S(1)}, u32[]{:S(2)}) copy-start(bf16[16,5120]{1,0:T(8,128)(2,1)S(1)} %collective-permute-done.4.rest_5_) | copy-start | bytes 491524
  34.9 2.6 %copy-start.5 = (bf16[16,5120]{1,0:T(8,128)(2,1)}, bf16[16,5120]{1,0:T(8,128)(2,1)S(1)}, u32[]{:S(2)}) copy-start(bf16[16,5120]{1,0:T(8,128)(2,1)S(1)} %collective-permute-done.5.rest_6_) | copy-start | bytes 491524
  37.4 0.7 copy-start.6
  49.8 6.6 %collective-permute-start.7 = (bf16[16,3072]{1,0:T(8,128)(2,1)}, bf16[16,3072]{1,0:T(8,128)(2,1)S(1)}, u32[]{:S(2)}, u32[]{:S(2)}) collective-permute-start(bf16[16,3072]{1,0:T(8,128)(2,1)} %get-tuple-element.38), channel_id=1, source_target_pairs={{0,2},{2,0},{4,6},{6,4},{8,10},{10,8},{12,14},{14,12},{1,3},{3,1},... | collective-permute-start | bytes 294920 | tf_op jit(solution)/shard_map/ppermute | solution.py:129
  50.5 8.2 %collective-permute-start.8 = (bf16[16,3072]{1,0:T(8,128)(2,1)}, bf16[16,3072]{1,0:T(8,128)(2,1)S(1)}, u32[]{:S(2)}, u32[]{:S(2)}) collective-permute-start(bf16[16,3072]{1,0:T(8,128)(2,1)} %get-tuple-element.39), channel_id=1, source_target_pairs={{0,4},{2,6},{4,0},{6,2},{8,12},{10,14},{12,8},{14,10},{1,5},{3,7},... | collective-permute-start | bytes 294920 | tf_op jit(solution)/shard_map/ppermute | solution.py:129
  50.5 9.2 %collective-permute-start.9 = (bf16[16,3072]{1,0:T(8,128)(2,1)}, bf16[16,3072]{1,0:T(8,128)(2,1)S(1)}, u32[]{:S(2)}, u32[]{:S(2)}) collective-permute-start(bf16[16,3072]{1,0:T(8,128)(2,1)} %get-tuple-element.40), channel_id=1, source_target_pairs={{0,6},{2,4},{4,2},{6,0},{8,14},{10,12},{12,10},{14,8},{1,7},{3,5},... | collective-permute-start | bytes 294920 | tf_op jit(solution)/shard_map/ppermute | solution.py:129
  53.3 12.7 %collective-permute-start.10 = (bf16[16,3072]{1,0:T(8,128)(2,1)}, bf16[16,3072]{1,0:T(8,128)(2,1)S(1)}, u32[]{:S(2)}, u32[]{:S(2)}) collective-permute-start(bf16[16,3072]{1,0:T(8,128)(2,1)} %get-tuple-element.41), channel_id=1, source_target_pairs={{0,8},{2,10},{4,12},{6,14},{8,0},{10,2},{12,4},{14,6},{1,9},{3,11}... | collective-permute-start | bytes 294920 | tf_op jit(solution)/shard_map/ppermute | solution.py:129
  55.3 12.6 %collective-permute-start.11 = (bf16[16,3072]{1,0:T(8,128)(2,1)}, bf16[16,3072]{1,0:T(8,128)(2,1)S(1)}, u32[]{:S(2)}, u32[]{:S(2)}) collective-permute-start(bf16[16,3072]{1,0:T(8,128)(2,1)} %get-tuple-element.42), channel_id=1, source_target_pairs={{0,10},{2,8},{4,14},{6,12},{8,2},{10,0},{12,6},{14,4},{1,11},{3,9}... | collective-permute-start | bytes 294920 | tf_op jit(solution)/shard_map/ppermute | solution.py:129
  56.4 15.4 %copy-start.7 = (bf16[16,3072]{1,0:T(8,128)(2,1)}, bf16[16,3072]{1,0:T(8,128)(2,1)S(1)}, u32[]{:S(2)}) copy-start(bf16[16,3072]{1,0:T(8,128)(2,1)S(1)} %collective-permute-done.7.rest_1_) | copy-start | bytes 294916
  56.4 13.4 %collective-permute-start.12 = (bf16[16,3072]{1,0:T(8,128)(2,1)}, bf16[16,3072]{1,0:T(8,128)(2,1)S(1)}, u32[]{:S(2)}, u32[]{:S(2)}) collective-permute-start(bf16[16,3072]{1,0:T(8,128)(2,1)} %get-tuple-element.43), channel_id=1, source_target_pairs={{0,12},{2,14},{4,8},{6,10},{8,4},{10,6},{12,0},{14,2},{1,13},{3,15... | collective-permute-start | bytes 294920 | tf_op jit(solution)/shard_map/ppermute | solution.py:129
  58.7 13.0 %copy-start.8 = (bf16[16,3072]{1,0:T(8,128)(2,1)}, bf16[16,3072]{1,0:T(8,128)(2,1)S(1)}, u32[]{:S(2)}) copy-start(bf16[16,3072]{1,0:T(8,128)(2,1)S(1)} %collective-permute-done.8.rest_2_) | copy-start | bytes 294916
  58.7 13.0 %collective-permute-start.13 = (bf16[16,3072]{1,0:T(8,128)(2,1)}, bf16[16,3072]{1,0:T(8,128)(2,1)S(1)}, u32[]{:S(2)}, u32[]{:S(2)}) collective-permute-start(bf16[16,3072]{1,0:T(8,128)(2,1)} %get-tuple-element.44), channel_id=1, source_target_pairs={{0,14},{2,12},{4,10},{6,8},{8,6},{10,4},{12,2},{14,0},{1,15},{3,13... | collective-permute-start | bytes 294920 | tf_op jit(solution)/shard_map/ppermute | solution.py:129
  59.8 12.0 %copy-start.9 = (bf16[16,3072]{1,0:T(8,128)(2,1)}, bf16[16,3072]{1,0:T(8,128)(2,1)S(1)}, u32[]{:S(2)}) copy-start(bf16[16,3072]{1,0:T(8,128)(2,1)S(1)} %collective-permute-done.9.rest_3_) | copy-start | bytes 294916
  66.0 5.8 %copy-start.10 = (bf16[16,3072]{1,0:T(8,128)(2,1)}, bf16[16,3072]{1,0:T(8,128)(2,1)S(1)}, u32[]{:S(2)}) copy-start(bf16[16,3072]{1,0:T(8,128)(2,1)S(1)} %collective-permute-done.10.rest_4_) | copy-start | bytes 294916
  67.8 4.0 %copy-start.11 = (bf16[16,3072]{1,0:T(8,128)(2,1)}, bf16[16,3072]{1,0:T(8,128)(2,1)S(1)}, u32[]{:S(2)}) copy-start(bf16[16,3072]{1,0:T(8,128)(2,1)S(1)} %collective-permute-done.11.rest_5_) | copy-start | bytes 294916
  69.8 2.0 %copy-start.12 = (bf16[16,3072]{1,0:T(8,128)(2,1)}, bf16[16,3072]{1,0:T(8,128)(2,1)S(1)}, u32[]{:S(2)}) copy-start(bf16[16,3072]{1,0:T(8,128)(2,1)S(1)} %collective-permute-done.12.rest_6_) | copy-start | bytes 294916
  71.8 0.6 copy-start.13

commit v3 on v0

--- a/solution.py
+++ b/solution.py
@@ -1,12 +1,242 @@
+import functools
+
 import jax
 import jax.numpy as jnp
 from jax import lax
+from jax.experimental import pallas as pl
+from jax.experimental.pallas import tpu as pltpu
 from jax.sharding import PartitionSpec as P
 
 HEAD_DIM = 128
 
 
 NEG_FILL = -1e30
+BF16 = jnp.bfloat16
+F32 = jnp.float32
+
+
+def resident_of(home_ref, rank, count):
+    found = jnp.int32(0)
+    for index in range(count):
+        found = jnp.where(home_ref[index] == rank, jnp.int32(index), found)
+    return found
+
+
+def dot(left, right, contract):
+    return lax.dot_general(left, right, ((contract[0], contract[1]), ((), ())), preferred_element_type=F32)
+
+
+def pack_kernel(home_ref, q_ref, k_ref, v_ref, g_ref, pk_ref, pv_ref, *blocks, count, heads):
+    rank = lax.axis_index("seq")
+    prompt_rows = pk_ref.shape[0]
+    rows = q_ref.shape[1]
+    near = count // 2
+    q_part = q_ref.shape[2] // heads
+    spare = jnp.zeros((rows - prompt_rows, HEAD_DIM), BF16)
+    width = 2 * q_part + 4 * HEAD_DIM
+    for head in range(heads):
+        lanes = slice(head * HEAD_DIM, (head + 1) * HEAD_DIM)
+        wide = slice(head * q_part, (head + 1) * q_part)
+        prompt = [jnp.concatenate([ref[:, lanes], spare], axis=0) for ref in (pk_ref, pv_ref)]
+        for distance in [*range(near, count), *range(near)]:
+            index = resident_of(home_ref, rank ^ distance, count)
+            if distance < near:
+                block, low = blocks[distance], head * width
+            else:
+                block, low = blocks[near + head * (count - near) + distance - near], 0
+            for ref, part in ((q_ref, wide), (g_ref, wide), (k_ref, lanes), (v_ref, lanes)):
+                size = part.stop - part.start
+                block[:, low : low + size] = ref[index, :, part]
+                low += size
+            for rows_of in prompt:
+                block[:, low : low + HEAD_DIM] = rows_of
+                low += HEAD_DIM
+
+
+def attend_kernel(lengths_ref, home_ref, seen_ref, *rest, count, prompt_rows, head, heads):
+    near = count // 2
+    last = head == heads - 1
+    blocks, rest = rest[:count], rest[count:]
+    kept, rest = rest[: (head if last else 0) * (near + 1)], rest[(head if last else 0) * (near + 1) :]
+    out_ref, returns, (x, y) = rest[0], rest[1 : count + 1], rest[count + 1 :]
+    rank = lax.axis_index("seq")
+    rows, width = blocks[near].shape
+    total = rows * count
+    q_part = (width - 4 * HEAD_DIM) // 2
+    back = q_part + 4 * HEAD_DIM
+    scale = 1.0 / HEAD_DIM**0.5
+    for distance in range(count):
+        low = head * width if distance < near else 0
+        at = pl.ds(pl.multiple_of((rank ^ distance) * rows, rows), rows)
+        x[at, :] = blocks[distance][:, low : low + width]
+    own = resident_of(home_ref, rank, count)
+    length = lengths_ref[own]
+    visible = seen_ref[own]
+    column = lax.broadcasted_iota(jnp.int32, (total, total), 1)
+    position = lax.broadcasted_iota(jnp.int32, (total, total), 0)
+    shard_row = column % rows
+    prompt_index = column // rows * prompt_rows + shard_row
+    allowed = jnp.concatenate(
+        [(shard_row < prompt_rows) & (prompt_index < visible), column <= position], axis=1
+    )
+    live = lax.broadcasted_iota(jnp.int32, (total, HEAD_DIM), 0) < length
+    out_low = head * q_part if last else 0
+
+    def lanes(low):
+        return x[:, low : low + HEAD_DIM]
+
+    low = 2 * q_part
+    keys = jnp.concatenate([lanes(low + 2 * HEAD_DIM), lanes(low)], axis=0)
+    values = jnp.concatenate([lanes(low + 3 * HEAD_DIM), lanes(low + HEAD_DIM)], axis=0)
+    key_grad = jnp.zeros((2 * total, HEAD_DIM), F32)
+    value_grad = jnp.zeros((2 * total, HEAD_DIM), F32)
+    for low in range(0, q_part, HEAD_DIM):
+        query = lanes(low)
+        grad = jnp.where(live, lanes(q_part + low), jnp.zeros((), BF16))
+        logits = jnp.where(allowed, dot(query, keys, ((1,), (1,))) * scale, NEG_FILL)
+        spread = dot(grad, values, ((1,), (1,)))
+        raised = jnp.exp(logits - jnp.max(logits, axis=1, keepdims=True))
+        prob = raised * (1.0 / jnp.sum(raised, axis=1, keepdims=True))
+        weights = prob.astype(BF16)
+        output = jnp.where(live, dot(weights, values, ((1,), (0,))), 0.0).astype(BF16)
+        out_ref[0, :, out_low + low : out_low + low + HEAD_DIM] = output
+        row_dot = jnp.sum(grad.astype(F32) * output.astype(F32), axis=1, keepdims=True)
+        dlogit = (prob * (spread - row_dot)).astype(BF16)
+        y[:, low : low + HEAD_DIM] = (dot(dlogit, keys, ((1,), (0,))) * scale).astype(BF16)
+        key_grad += dot(dlogit, query, ((0,), (0,)))
+        value_grad += dot(weights, grad, ((0,), (0,)))
+    for part, summed in enumerate((key_grad * scale, value_grad)):
+        at = q_part + part * HEAD_DIM
+        y[:, at : at + HEAD_DIM] = summed[total:].astype(BF16)
+        at += 2 * HEAD_DIM
+        y[:, at : at + HEAD_DIM] = summed[:total].astype(BF16)
+    for distance in range(count):
+        low = head * back if last and distance < near else 0
+        at = pl.ds(pl.multiple_of((rank ^ distance) * rows, rows), rows)
+        returns[distance][:, low : low + back] = y[at, :]
+    for earlier in range(len(kept) // (near + 1)):
+        parts = kept[earlier * (near + 1) : (earlier + 1) * (near + 1)]
+        out_ref[0, :, earlier * q_part : (earlier + 1) * q_part] = parts[0][0]
+        for distance in range(near):
+            returns[distance][:, earlier * back : (earlier + 1) * back] = parts[1 + distance][...]
+
+
+def unpack_kernel(home_ref, *rest, count, heads):
+    near = count // 2
+    blocks = rest[:-5]
+    qg_ref, kg_ref, vg_ref, pkg_ref, pvg_ref = rest[-5:]
+    rank = lax.axis_index("seq")
+    prompt_rows = pkg_ref.shape[0]
+    q_part = qg_ref.shape[2] // heads
+    back = q_part + 4 * HEAD_DIM
+    for head in range(heads):
+        lanes = slice(head * HEAD_DIM, (head + 1) * HEAD_DIM)
+        wide = slice(head * q_part, (head + 1) * q_part)
+        summed = [jnp.zeros((qg_ref.shape[1], HEAD_DIM), F32)] * 2
+        for distance in range(count):
+            index = resident_of(home_ref, rank ^ distance, count)
+            if distance < near:
+                block, low = blocks[distance], head * back
+            else:
+                block, low = blocks[near + head * (count - near) + distance - near], 0
+            for ref, part in ((qg_ref, wide), (kg_ref, lanes), (vg_ref, lanes)):
+                size = part.stop - part.start
+                ref[index, :, part] = block[:, low : low + size]
+                low += size
+            for part in range(2):
+                summed[part] = summed[part] + block[:, low : low + HEAD_DIM].astype(F32)
+                low += HEAD_DIM
+        pkg_ref[:, lanes] = summed[0][:prompt_rows].astype(BF16)
+        pvg_ref[:, lanes] = summed[1][:prompt_rows].astype(BF16)
+
+
+def exchange(blocks, distances, count):
+    arrived = []
+    for block, distance in zip(blocks, distances):
+        if distance:
+            block = lax.ppermute(block, "seq", [(i, i ^ distance) for i in range(count)])
+        arrived.append(block)
+    return arrived
+
+
+SMEM = pl.BlockSpec(memory_space=pltpu.SMEM)
+VMEM = pl.BlockSpec(memory_space=pltpu.VMEM)
+PARAMS = pltpu.CompilerParams(vmem_limit_bytes=24 * 1024 * 1024)
+
+
+def packed_body(
+    response_query,
+    response_key,
+    response_value,
+    response_grad,
+    prompt_key,
+    prompt_value,
+    lengths,
+    home_rank,
+    prompt_seen,
+):
+    count = home_rank.shape[0]
+    rows, q_width = response_query.shape[1:]
+    prompt_rows, kv_width = prompt_key.shape
+    total = rows * count
+    heads = kv_width // HEAD_DIM
+    near, far = range(count // 2), range(count // 2, count)
+    q_part = q_width // heads
+    width = 2 * q_part + 4 * HEAD_DIM
+    back = q_part + 4 * HEAD_DIM
+
+    def shape(*dims):
+        return jax.ShapeDtypeStruct(dims, BF16)
+
+    packed = pl.pallas_call(
+        functools.partial(pack_kernel, count=count, heads=heads),
+        name="pack",
+        out_shape=[shape(rows, heads * width)] * len(near) + [shape(rows, width)] * (len(far) * heads),
+        in_specs=[SMEM] + [VMEM] * 6,
+        out_specs=[VMEM] * (len(near) + len(far) * heads),
+        compiler_params=PARAMS,
+    )(home_rank, response_query, response_key, response_value, response_grad, prompt_key, prompt_value)
+    far_in = [exchange(packed[len(near) :][: len(far)], far, count)]
+    near_in = exchange(packed[: len(near)], near, count)
+    for head in range(1, heads):
+        blocks = packed[len(near) + head * len(far) :][: len(far)]
+        far_in.append(exchange(blocks, far, count))
+    kept, far_back = [], []
+    for head in range(heads):
+        last = head == heads - 1
+        whole = heads if last else 1
+        operands = [lengths, home_rank, prompt_seen, *near_in, *far_in[head], *(kept if last else [])]
+        results = pl.pallas_call(
+            functools.partial(
+                attend_kernel, count=count, prompt_rows=prompt_rows, head=head, heads=heads
+            ),
+            out_shape=[shape(1, total, whole * q_part)]
+            + [shape(rows, whole * back)] * len(near)
+            + [shape(rows, back)] * len(far),
+            in_specs=[SMEM] * 3 + [VMEM] * (len(operands) - 3),
+            out_specs=[VMEM] * (count + 1),
+            scratch_shapes=[pltpu.VMEM((total, width), BF16), pltpu.VMEM((total, back), BF16)],
+            compiler_params=PARAMS,
+        )(*operands)
+        far_back += exchange(results[1 + len(near) :], far, count)
+        kept += results[: 1 + len(near)]
+    output, *near_back = kept[-1 - len(near) :]
+    near_back = exchange(near_back, near, count)
+    grads = pl.pallas_call(
+        functools.partial(unpack_kernel, count=count, heads=heads),
+        name="unpack",
+        out_shape=[
+            shape(count, rows, q_width),
+            shape(count, rows, kv_width),
+            shape(count, rows, kv_width),
+            shape(prompt_rows, kv_width),
+            shape(prompt_rows, kv_width),
+        ],
+        in_specs=[SMEM] + [VMEM] * (len(near) + len(far) * heads),
+        out_specs=[VMEM] * 5,
+        compiler_params=PARAMS,
+    )(home_rank, *near_back, *far_back)
+    return (output, *grads)
 
 
 def head_logits(queries, all_keys, allowed, head_index, group_size, scale_factor):
@@ -29,7 +259,7 @@
     outputs = []
     totals = []
     for head_index in range(kv_count):
-        query_head, key_head, logits = head_logits(
+        _, _, logits = head_logits(
             queries, all_keys, allowed, head_index, group_size, scale_factor
         )
         value_head = all_values[:, head_index * HEAD_DIM : (head_index + 1) * HEAD_DIM]
@@ -190,6 +420,15 @@
     )
 
 
+def choose_body(response_query, *others):
+    count, rows = response_query.shape[:2]
+    prompt_rows = others[3].shape[0]
+    fits = rows % 16 == 0 and prompt_rows <= rows and rows * count == HEAD_DIM
+    if fits and count & (count - 1) == 0 and count <= 16:
+        return packed_body(response_query, *others)
+    return body(response_query, *others)
+
+
 def solution(mesh):
     placed = (
         P("group", "seq", "head"),
@@ -203,7 +442,7 @@
         P("group"),
     )
     return jax.shard_map(
-        body,
+        choose_body,
         mesh=mesh,
         in_specs=placed,
         out_specs=(

time: 198 us -> 74.6 us (0.38)
  the two profiles are of different devices: /device:TPU:8 before, /device:TPU:0 now
where the time goes in v3:
time: 74.6 us; the launch traced here: 74.2 us
  starting transfers between devices  44.2 us (59%)
  Pallas kernels  13.6 us (18%)
  waiting for transfers between devices  9.78 us (13%)
  local copies, waits for them, and re-layouts  5.81 us (8%)
    ppermute x22, starting transfers between devices, exchange(): lax.ppermute(block, 'seq', [(i, i ^ distance) for i in range(count)])  44.2 us
    pallas_call x2, Pallas kernels, packed_body(): pl.pallas_call(functools.partial(attend_kernel, count=count, prompt_rows=...  11.5 us
    ppermute x22, waiting for transfers between devices, exchange(): lax.ppermute(block, 'seq', [(i, i ^ distance) for i in range(count)])  9.78 us
    unnamed x18, local copies, waits for them, and re-layouts  5.81 us
  transfers between devices with their start and end apart: 22, of which 5 were waited for; matrix products, arithmetic and copies ran while one was open for 0% of the time, Pallas kernels for 7%

profile of v3, /device:TPU:0, one launch (start us, length us, event | category | flops | bytes accessed | tf_op | source)
XLA Modules:
  0.0 74.2 jit_solution(5277012379753832972)
XLA Ops:
  0.6 0.0 copy-start
  0.6 1.0 %copy-done = bf16[8,16,2048]{2,1,0:T(8,128)(2,1)S(1)} copy-done((bf16[8,16,2048]{2,1,0:T(8,128)(2,1)S(1)}, bf16[8,16,2048]{2,1,0:T(8,128)(2,1)}, u32[]{:S(2)}) %copy-start) | copy-done | bytes 524312
  1.7 0.0 copy-start.1
  1.7 1.0 %copy-done.1 = bf16[8,16,2048]{2,1,0:T(8,128)(2,1)S(1)} copy-done((bf16[8,16,2048]{2,1,0:T(8,128)(2,1)S(1)}, bf16[8,16,2048]{2,1,0:T(8,128)(2,1)}, u32[]{:S(2)}) %copy-start.1) | copy-done | bytes 524312
  2.7 0.0 copy-start.2
  2.7 0.8 %copy-done.2 = bf16[8,16,256]{2,1,0:T(8,128)(2,1)S(1)} copy-done((bf16[8,16,256]{2,1,0:T(8,128)(2,1)S(1)}, bf16[8,16,256]{2,1,0:T(8,128)(2,1)}, u32[]{:S(2)}) %copy-start.2) | copy-done | bytes 65560
  3.6 0.8 %copy-done.3 = bf16[8,16,256]{2,1,0:T(8,128)(2,1)S(1)} copy-done((bf16[8,16,256]{2,1,0:T(8,128)(2,1)S(1)}, bf16[8,16,256]{2,1,0:T(8,128)(2,1)}, u32[]{:S(2)}) %copy-start.3) | copy-done | bytes 65560
  4.4 0.7 copy-done.4
  5.1 0.0 copy-start.5
  5.1 0.7 copy-done.5
  5.8 0.0 copy-start.6
  5.8 0.7 copy-done.6
  6.4 0.7 pack.1
  7.1 4.1 %collective-permute-start.7 = (bf16[16,2560]{1,0:T(8,128)(2,1)S(1)}, bf16[16,2560]{1,0:T(8,128)(2,1)S(1)}, u32[]{:S(2)}, u32[]{:S(2)}) collective-permute-start(bf16[16,2560]{1,0:T(8,128)(2,1)S(1)} %get-tuple-element.49), channel_id=1, source_target_pairs={{0,8},{2,10},{4,12},{6,14},{8,0},{10,2},{12,4},{14,6},{1,9},{3,11}... | collective-permute-start | bytes 245768 | tf_op jit(solution)/shard_map/ppermute | solution.py:157
  11.3 1.3 %collective-permute-start.8 = (bf16[16,2560]{1,0:T(8,128)(2,1)S(1)}, bf16[16,2560]{1,0:T(8,128)(2,1)S(1)}, u32[]{:S(2)}, u32[]{:S(2)}) collective-permute-start(bf16[16,2560]{1,0:T(8,128)(2,1)S(1)} %get-tuple-element.50), channel_id=1, source_target_pairs={{0,10},{2,8},{4,14},{6,12},{8,2},{10,0},{12,6},{14,4},{1,11},{3,9}... | collective-permute-start | bytes 245768 | tf_op jit(solution)/shard_map/ppermute | solution.py:157
  12.5 0.3 collective-permute-start
  12.8 1.8 %collective-permute-start.1 = (bf16[16,5120]{1,0:T(8,128)(2,1)S(1)}, bf16[16,5120]{1,0:T(8,128)(2,1)S(1)}, u32[]{:S(2)}, u32[]{:S(2)}) collective-permute-start(bf16[16,5120]{1,0:T(8,128)(2,1)S(1)} %get-tuple-element.43), channel_id=1, source_target_pairs={{0,4},{2,6},{4,0},{6,2},{8,12},{10,14},{12,8},{14,10},{1,5},{3,7},... | collective-permute-start | bytes 491528 | tf_op jit(solution)/shard_map/ppermute | solution.py:157
  14.6 2.5 %collective-permute-start.9 = (bf16[16,2560]{1,0:T(8,128)(2,1)S(1)}, bf16[16,2560]{1,0:T(8,128)(2,1)S(1)}, u32[]{:S(2)}, u32[]{:S(2)}) collective-permute-start(bf16[16,2560]{1,0:T(8,128)(2,1)S(1)} %get-tuple-element.51), channel_id=1, source_target_pairs={{0,12},{2,14},{4,8},{6,10},{8,4},{10,6},{12,0},{14,2},{1,13},{3,15... | collective-permute-start | bytes 245768 | tf_op jit(solution)/shard_map/ppermute | solution.py:157
  17.1 0.0 collective-permute-done.7.rest_4_
  17.1 4.8 %collective-permute-start.10 = (bf16[16,2560]{1,0:T(8,128)(2,1)S(1)}, bf16[16,2560]{1,0:T(8,128)(2,1)S(1)}, u32[]{:S(2)}, u32[]{:S(2)}) collective-permute-start(bf16[16,2560]{1,0:T(8,128)(2,1)S(1)} %get-tuple-element.52), channel_id=1, source_target_pairs={{0,14},{2,12},{4,10},{6,8},{8,6},{10,4},{12,2},{14,0},{1,15},{3,13... | collective-permute-start | bytes 245768 | tf_op jit(solution)/shard_map/ppermute | solution.py:157
  21.9 0.0 collective-permute-done.8.rest_5_
  21.9 0.0 collective-permute-start.2
  21.9 2.4 %collective-permute-done.9.rest_6_ = bf16[16,2560]{1,0:T(8,128)(2,1)S(1)} collective-permute-done((bf16[16,2560]{1,0:T(8,128)(2,1)S(1)}, bf16[16,2560]{1,0:T(8,128)(2,1)S(1)}, u32[]{:S(2)}, u32[]{:S(2)}) %collective-permute-start.9) | collective-permute-done | bytes 81952 | tf_op jit(solution)/shard_map/ppermute | solution.py:157
  24.2 1.1 %collective-permute-start.3 = (bf16[16,2560]{1,0:T(8,128)(2,1)S(1)}, bf16[16,2560]{1,0:T(8,128)(2,1)S(1)}, u32[]{:S(2)}, u32[]{:S(2)}) collective-permute-start(bf16[16,2560]{1,0:T(8,128)(2,1)S(1)} %get-tuple-element.45), channel_id=1, source_target_pairs={{0,8},{2,10},{4,12},{6,14},{8,0},{10,2},{12,4},{14,6},{1,9},{3,11}... | collective-permute-start | bytes 245768 | tf_op jit(solution)/shard_map/ppermute | solution.py:157
  25.3 0.7 collective-permute-done.10.rest_7_
  26.0 4.7 %collective-permute-start.4 = (bf16[16,2560]{1,0:T(8,128)(2,1)S(1)}, bf16[16,2560]{1,0:T(8,128)(2,1)S(1)}, u32[]{:S(2)}, u32[]{:S(2)}) collective-permute-start(bf16[16,2560]{1,0:T(8,128)(2,1)S(1)} %get-tuple-element.46), channel_id=1, source_target_pairs={{0,10},{2,8},{4,14},{6,12},{8,2},{10,0},{12,6},{14,4},{1,11},{3,9}... | collective-permute-start | bytes 245768 | tf_op jit(solution)/shard_map/ppermute | solution.py:157
  30.7 0.0 collective-permute-done.rest_1_
  30.7 0.0 collective-permute-start.5
  30.8 0.0 collective-permute-done.1.rest_2_
  30.8 0.0 copy-start.7
  30.8 0.0 copy-start.8
  30.8 5.3 %collective-permute-start.6 = (bf16[16,2560]{1,0:T(8,128)(2,1)S(1)}, bf16[16,2560]{1,0:T(8,128)(2,1)S(1)}, u32[]{:S(2)}, u32[]{:S(2)}) collective-permute-start(bf16[16,2560]{1,0:T(8,128)(2,1)S(1)} %get-tuple-element.48), channel_id=1, source_target_pairs={{0,14},{2,12},{4,10},{6,8},{8,6},{10,4},{12,2},{14,0},{1,15},{3,13... | collective-permute-start | bytes 245768 | tf_op jit(solution)/shard_map/ppermute | solution.py:157
  36.1 0.0 collective-permute-done.2.rest_3_
  36.1 0.0 copy-done.7
  36.1 0.0 copy-done.8
  36.1 5.4 %shard_map.136 = (bf16[1,128,1024]{2,1,0:T(8,128)(2,1)S(1)}, bf16[16,1536]{1,0:T(8,128)(2,1)S(1)}, bf16[16,1536]{1,0:T(8,128)(2,1)S(1)}, bf16[16,1536]{1,0:T(8,1...) custom-call(s32[8]{0:T(128)S(1)} %copy-done.7, ...), custom_call_target="tpu_custom_call" | custom-call | tf_op jit(solution)/shard_map/pallas_call | solution.py:209
  41.5 0.0 collective-permute-done.3.rest_4_
  41.5 0.0 collective-permute-done.4.rest_5_
  41.5 0.0 collective-permute-done.5.rest_6_
  41.5 0.0 collective-permute-done.6.rest_7_
  41.5 6.1 %shard_map.137 = (bf16[1,128,2048]{2,1,0:T(8,128)(2,1)}, bf16[16,3072]{1,0:T(8,128)(2,1)S(1)}, bf16[16,3072]{1,0:T(8,128)(2,1)S(1)}, bf16[16,3072]{1,0:T(8,128)(...) custom-call(s32[8]{0:T(128)S(1)} %copy-done.7, ...), custom_call_target="tpu_custom_call" | custom-call | tf_op jit(solution)/shard_map/pallas_call | solution.py:209
  47.7 2.8 %collective-permute-start.18 = (bf16[16,1536]{1,0:T(8,128)(2,1)S(1)}, bf16[16,1536]{1,0:T(8,128)(2,1)S(1)}, u32[]{:S(2)}, u32[]{:S(2)}) collective-permute-start(bf16[16,1536]{1,0:T(8,128)(2,1)S(1)} %get-tuple-element.67), channel_id=1, source_target_pairs={{0,8},{2,10},{4,12},{6,14},{8,0},{10,2},{12,4},{14,6},{1,9},{3,11}... | collective-permute-start | bytes 147464 | tf_op jit(solution)/shard_map/ppermute | solution.py:157
  50.5 0.0 collective-permute-start.19
  50.5 1.9 %collective-permute-start.20 = (bf16[16,1536]{1,0:T(8,128)(2,1)S(1)}, bf16[16,1536]{1,0:T(8,128)(2,1)S(1)}, u32[]{:S(2)}, u32[]{:S(2)}) collective-permute-start(bf16[16,1536]{1,0:T(8,128)(2,1)S(1)} %get-tuple-element.69), channel_id=1, source_target_pairs={{0,12},{2,14},{4,8},{6,10},{8,4},{10,6},{12,0},{14,2},{1,13},{3,15... | collective-permute-start | bytes 147464 | tf_op jit(solution)/shard_map/ppermute | solution.py:157
  52.4 2.9 %collective-permute-start.21 = (bf16[16,1536]{1,0:T(8,128)(2,1)S(1)}, bf16[16,1536]{1,0:T(8,128)(2,1)S(1)}, u32[]{:S(2)}, u32[]{:S(2)}) collective-permute-start(bf16[16,1536]{1,0:T(8,128)(2,1)S(1)} %get-tuple-element.70), channel_id=1, source_target_pairs={{0,14},{2,12},{4,10},{6,8},{8,6},{10,4},{12,2},{14,0},{1,15},{3,13... | collective-permute-start | bytes 147464 | tf_op jit(solution)/shard_map/ppermute | solution.py:157
  55.3 1.0 %collective-permute-start.14 = (bf16[16,1536]{1,0:T(8,128)(2,1)S(1)}, bf16[16,1536]{1,0:T(8,128)(2,1)S(1)}, u32[]{:S(2)}, u32[]{:S(2)}) collective-permute-start(bf16[16,1536]{1,0:T(8,128)(2,1)S(1)} %get-tuple-element.63), channel_id=1, source_target_pairs={{0,8},{2,10},{4,12},{6,14},{8,0},{10,2},{12,4},{14,6},{1,9},{3,11}... | collective-permute-start | bytes 147464 | tf_op jit(solution)/shard_map/ppermute | solution.py:157
  56.3 0.0 collective-permute-done.18.rest_8_
  56.3 1.8 %collective-permute-start.15 = (bf16[16,1536]{1,0:T(8,128)(2,1)S(1)}, bf16[16,1536]{1,0:T(8,128)(2,1)S(1)}, u32[]{:S(2)}, u32[]{:S(2)}) collective-permute-start(bf16[16,1536]{1,0:T(8,128)(2,1)S(1)} %get-tuple-element.64), channel_id=1, source_target_pairs={{0,10},{2,8},{4,14},{6,12},{8,2},{10,0},{12,6},{14,4},{1,11},{3,9}... | collective-permute-start | bytes 147464 | tf_op jit(solution)/shard_map/ppermute | solution.py:157
  58.1 2.2 %collective-permute-done.19.rest_9_ = bf16[16,1536]{1,0:T(8,128)(2,1)S(1)} collective-permute-done((bf16[16,1536]{1,0:T(8,128)(2,1)S(1)}, bf16[16,1536]{1,0:T(8,128)(2,1)S(1)}, u32[]{:S(2)}, u32[]{:S(2)}) %collective-permute-start.19) | collective-permute-done | bytes 49184 | tf_op jit(solution)/shard_map/ppermute | solution.py:157
  60.3 0.0 collective-permute-start.11
  60.3 0.0 collective-permute-done.20.rest_10_
  60.3 0.8 %collective-permute-start.12 = (bf16[16,3072]{1,0:T(8,128)(2,1)S(1)}, bf16[16,3072]{1,0:T(8,128)(2,1)S(1)}, u32[]{:S(2)}, u32[]{:S(2)}) collective-permute-start(bf16[16,3072]{1,0:T(8,128)(2,1)S(1)} %get-tuple-element.61), channel_id=1, source_target_pairs={{0,4},{2,6},{4,0},{6,2},{8,12},{10,14},{12,8},{14,10},{1,5},{3,7},... | collective-permute-start | bytes 294920 | tf_op jit(solution)/shard_map/ppermute | solution.py:157
  61.1 0.0 collective-permute-done.21.rest_11_
  61.1 2.7 %collective-permute-start.13 = (bf16[16,3072]{1,0:T(8,128)(2,1)S(1)}, bf16[16,3072]{1,0:T(8,128)(2,1)S(1)}, u32[]{:S(2)}, u32[]{:S(2)}) collective-permute-start(bf16[16,3072]{1,0:T(8,128)(2,1)S(1)} %get-tuple-element.62), channel_id=1, source_target_pairs={{0,6},{2,4},{4,2},{6,0},{8,14},{10,12},{12,10},{14,8},{1,7},{3,5},... | collective-permute-start | bytes 294920 | tf_op jit(solution)/shard_map/ppermute | solution.py:157
  63.8 0.0 collective-permute-done.14.rest_4_
  63.8 2.1 %collective-permute-start.16 = (bf16[16,1536]{1,0:T(8,128)(2,1)S(1)}, bf16[16,1536]{1,0:T(8,128)(2,1)S(1)}, u32[]{:S(2)}, u32[]{:S(2)}) collective-permute-start(bf16[16,1536]{1,0:T(8,128)(2,1)S(1)} %get-tuple-element.65), channel_id=1, source_target_pairs={{0,12},{2,14},{4,8},{6,10},{8,4},{10,6},{12,0},{14,2},{1,13},{3,15... | collective-permute-start | bytes 147464 | tf_op jit(solution)/shard_map/ppermute | solution.py:157
  65.9 0.0 collective-permute-done.15.rest_5_
  65.9 2.3 %collective-permute-start.17 = (bf16[16,1536]{1,0:T(8,128)(2,1)S(1)}, bf16[16,1536]{1,0:T(8,128)(2,1)S(1)}, u32[]{:S(2)}, u32[]{:S(2)}) collective-permute-start(bf16[16,1536]{1,0:T(8,128)(2,1)S(1)} %get-tuple-element.66), channel_id=1, source_target_pairs={{0,14},{2,12},{4,10},{6,8},{8,6},{10,4},{12,2},{14,0},{1,15},{3,13... | collective-permute-start | bytes 147464 | tf_op jit(solution)/shard_map/ppermute | solution.py:157
  68.2 1.9 %collective-permute-done.16.rest_6_ = bf16[16,1536]{1,0:T(8,128)(2,1)S(1)} collective-permute-done((bf16[16,1536]{1,0:T(8,128)(2,1)S(1)}, bf16[16,1536]{1,0:T(8,128)(2,1)S(1)}, u32[]{:S(2)}, u32[]{:S(2)}) %collective-permute-start.16) | collective-permute-done | bytes 49184 | tf_op jit(solution)/shard_map/ppermute | solution.py:157
  70.1 2.6 %collective-permute-done.17.rest_7_ = bf16[16,1536]{1,0:T(8,128)(2,1)S(1)} collective-permute-done((bf16[16,1536]{1,0:T(8,128)(2,1)S(1)}, bf16[16,1536]{1,0:T(8,128)(2,1)S(1)}, u32[]{:S(2)}, u32[]{:S(2)}) %collective-permute-start.17) | collective-permute-done | bytes 49184 | tf_op jit(solution)/shard_map/ppermute | solution.py:157
  72.7 0.0 collective-permute-done.11.rest_1_
  72.7 0.0 collective-permute-done.12.rest_2_
  72.7 0.0 collective-permute-done.13.rest_3_
  72.7 1.5 %unpack.1 = (bf16[8,16,2048]{2,1,0:T(8,128)(2,1)}, bf16[8,16,256]{2,1,0:T(8,128)(2,1)}, bf16[8,16,256]{2,1,0:T(8,128)(2,1)}, bf16[12,256]{1,0:T(8,128)(2,1)}, bf16[12,256]{1,0:T(8,128)(2,1)}) custom-call(s32[8]{0:T(128)S(1)} %copy-done.6, bf16[16,3072]{1,0:T(8,128)(2,1)S(1)} %get-tuple-element.59.rest_0_, ...), custom_call_target="tpu_custom_call" | custom-call | tf_op jit(solution)/shard_map/unpack/pallas_call | solution.py:225
  (2 shorter events, 0.0 us)
Async XLA Ops:
  0.6 1.0 %copy-start = (bf16[8,16,2048]{2,1,0:T(8,128)(2,1)S(1)}, bf16[8,16,2048]{2,1,0:T(8,128)(2,1)}, u32[]{:S(2)}) copy-start(bf16[8,16,2048]{2,1,0:T(8,128)(2,1)} %q_ref.1) | copy-start | bytes 1572868
  1.7 1.0 %copy-start.1 = (bf16[8,16,2048]{2,1,0:T(8,128)(2,1)S(1)}, bf16[8,16,2048]{2,1,0:T(8,128)(2,1)}, u32[]{:S(2)}) copy-start(bf16[8,16,2048]{2,1,0:T(8,128)(2,1)} %g_ref.1) | copy-start | bytes 1572868
  2.7 0.8 %copy-start.2 = (bf16[8,16,256]{2,1,0:T(8,128)(2,1)S(1)}, bf16[8,16,256]{2,1,0:T(8,128)(2,1)}, u32[]{:S(2)}) copy-start(bf16[8,16,256]{2,1,0:T(8,128)(2,1)} %k_ref.1) | copy-start | bytes 196612
  3.6 0.8 %copy-start.3 = (bf16[8,16,256]{2,1,0:T(8,128)(2,1)S(1)}, bf16[8,16,256]{2,1,0:T(8,128)(2,1)}, u32[]{:S(2)}) copy-start(bf16[8,16,256]{2,1,0:T(8,128)(2,1)} %v_ref.1) | copy-start | bytes 196612
  4.4 0.7 copy-start.4
  5.1 0.7 copy-start.5
  5.8 0.7 copy-start.6
  7.1 10.0 %collective-permute-start.7 = (bf16[16,2560]{1,0:T(8,128)(2,1)S(1)}, bf16[16,2560]{1,0:T(8,128)(2,1)S(1)}, u32[]{:S(2)}, u32[]{:S(2)}) collective-permute-start(bf16[16,2560]{1,0:T(8,128)(2,1)S(1)} %get-tuple-element.49), channel_id=1, source_target_pairs={{0,8},{2,10},{4,12},{6,14},{8,0},{10,2},{12,4},{14,6},{1,9},{3,11}... | collective-permute-start | bytes 245768 | tf_op jit(solution)/shard_map/ppermute | solution.py:157
  11.3 10.6 %collective-permute-start.8 = (bf16[16,2560]{1,0:T(8,128)(2,1)S(1)}, bf16[16,2560]{1,0:T(8,128)(2,1)S(1)}, u32[]{:S(2)}, u32[]{:S(2)}) collective-permute-start(bf16[16,2560]{1,0:T(8,128)(2,1)S(1)} %get-tuple-element.50), channel_id=1, source_target_pairs={{0,10},{2,8},{4,14},{6,12},{8,2},{10,0},{12,6},{14,4},{1,11},{3,9}... | collective-permute-start | bytes 245768 | tf_op jit(solution)/shard_map/ppermute | solution.py:157
  12.5 18.2 %collective-permute-start = (bf16[16,5120]{1,0:T(8,128)(2,1)S(1)}, bf16[16,5120]{1,0:T(8,128)(2,1)S(1)}, u32[]{:S(2)}, u32[]{:S(2)}) collective-permute-start(bf16[16,5120]{1,0:T(8,128)(2,1)S(1)} %get-tuple-element.42), channel_id=1, source_target_pairs={{0,2},{2,0},{4,6},{6,4},{8,10},{10,8},{12,14},{14,12},{1,3},{3,1},... | collective-permute-start | bytes 491528 | tf_op jit(solution)/shard_map/ppermute | solution.py:157
  12.8 18.0 %collective-permute-start.1 = (bf16[16,5120]{1,0:T(8,128)(2,1)S(1)}, bf16[16,5120]{1,0:T(8,128)(2,1)S(1)}, u32[]{:S(2)}, u32[]{:S(2)}) collective-permute-start(bf16[16,5120]{1,0:T(8,128)(2,1)S(1)} %get-tuple-element.43), channel_id=1, source_target_pairs={{0,4},{2,6},{4,0},{6,2},{8,12},{10,14},{12,8},{14,10},{1,5},{3,7},... | collective-permute-start | bytes 491528 | tf_op jit(solution)/shard_map/ppermute | solution.py:157
  14.6 9.6 %collective-permute-start.9 = (bf16[16,2560]{1,0:T(8,128)(2,1)S(1)}, bf16[16,2560]{1,0:T(8,128)(2,1)S(1)}, u32[]{:S(2)}, u32[]{:S(2)}) collective-permute-start(bf16[16,2560]{1,0:T(8,128)(2,1)S(1)} %get-tuple-element.51), channel_id=1, source_target_pairs={{0,12},{2,14},{4,8},{6,10},{8,4},{10,6},{12,0},{14,2},{1,13},{3,15... | collective-permute-start | bytes 245768 | tf_op jit(solution)/shard_map/ppermute | solution.py:157
  17.1 8.9 %collective-permute-start.10 = (bf16[16,2560]{1,0:T(8,128)(2,1)S(1)}, bf16[16,2560]{1,0:T(8,128)(2,1)S(1)}, u32[]{:S(2)}, u32[]{:S(2)}) collective-permute-start(bf16[16,2560]{1,0:T(8,128)(2,1)S(1)} %get-tuple-element.52), channel_id=1, source_target_pairs={{0,14},{2,12},{4,10},{6,8},{8,6},{10,4},{12,2},{14,0},{1,15},{3,13... | collective-permute-start | bytes 245768 | tf_op jit(solution)/shard_map/ppermute | solution.py:157
  21.9 14.2 %collective-permute-start.2 = (bf16[16,5120]{1,0:T(8,128)(2,1)S(1)}, bf16[16,5120]{1,0:T(8,128)(2,1)S(1)}, u32[]{:S(2)}, u32[]{:S(2)}) collective-permute-start(bf16[16,5120]{1,0:T(8,128)(2,1)S(1)} %get-tuple-element.44), channel_id=1, source_target_pairs={{0,6},{2,4},{4,2},{6,0},{8,14},{10,12},{12,10},{14,8},{1,7},{3,5},... | collective-permute-start | bytes 491528 | tf_op jit(solution)/shard_map/ppermute | solution.py:157
  24.2 17.2 %collective-permute-start.3 = (bf16[16,2560]{1,0:T(8,128)(2,1)S(1)}, bf16[16,2560]{1,0:T(8,128)(2,1)S(1)}, u32[]{:S(2)}, u32[]{:S(2)}) collective-permute-start(bf16[16,2560]{1,0:T(8,128)(2,1)S(1)} %get-tuple-element.45), channel_id=1, source_target_pairs={{0,8},{2,10},{4,12},{6,14},{8,0},{10,2},{12,4},{14,6},{1,9},{3,11}... | collective-permute-start | bytes 245768 | tf_op jit(solution)/shard_map/ppermute | solution.py:157
  26.0 15.5 %collective-permute-start.4 = (bf16[16,2560]{1,0:T(8,128)(2,1)S(1)}, bf16[16,2560]{1,0:T(8,128)(2,1)S(1)}, u32[]{:S(2)}, u32[]{:S(2)}) collective-permute-start(bf16[16,2560]{1,0:T(8,128)(2,1)S(1)} %get-tuple-element.46), channel_id=1, source_target_pairs={{0,10},{2,8},{4,14},{6,12},{8,2},{10,0},{12,6},{14,4},{1,11},{3,9}... | collective-permute-start | bytes 245768 | tf_op jit(solution)/shard_map/ppermute | solution.py:157
  30.7 10.8 %collective-permute-start.5 = (bf16[16,2560]{1,0:T(8,128)(2,1)S(1)}, bf16[16,2560]{1,0:T(8,128)(2,1)S(1)}, u32[]{:S(2)}, u32[]{:S(2)}) collective-permute-start(bf16[16,2560]{1,0:T(8,128)(2,1)S(1)} %get-tuple-element.47), channel_id=1, source_target_pairs={{0,12},{2,14},{4,8},{6,10},{8,4},{10,6},{12,0},{14,2},{1,13},{3,15... | collective-permute-start | bytes 245768 | tf_op jit(solution)/shard_map/ppermute | solution.py:157
  30.8 5.3 %copy-start.7 = (s32[8]{0:T(128)S(1)}, s32[8]{0:T(128)}, u32[]{:S(2)}) copy-start(s32[8]{0:T(128)} %lengths_ref.3) | copy-start | bytes 100
  30.8 5.3 %copy-start.8 = (s32[8]{0:T(128)S(1)}, s32[8]{0:T(128)}, u32[]{:S(2)}) copy-start(s32[8]{0:T(128)} %seen_ref.3) | copy-start | bytes 100
  30.8 10.7 %collective-permute-start.6 = (bf16[16,2560]{1,0:T(8,128)(2,1)S(1)}, bf16[16,2560]{1,0:T(8,128)(2,1)S(1)}, u32[]{:S(2)}, u32[]{:S(2)}) collective-permute-start(bf16[16,2560]{1,0:T(8,128)(2,1)S(1)} %get-tuple-element.48), channel_id=1, source_target_pairs={{0,14},{2,12},{4,10},{6,8},{8,6},{10,4},{12,2},{14,0},{1,15},{3,13... | collective-permute-start | bytes 245768 | tf_op jit(solution)/shard_map/ppermute | solution.py:157
  47.7 8.6 %collective-permute-start.18 = (bf16[16,1536]{1,0:T(8,128)(2,1)S(1)}, bf16[16,1536]{1,0:T(8,128)(2,1)S(1)}, u32[]{:S(2)}, u32[]{:S(2)}) collective-permute-start(bf16[16,1536]{1,0:T(8,128)(2,1)S(1)} %get-tuple-element.67), channel_id=1, source_target_pairs={{0,8},{2,10},{4,12},{6,14},{8,0},{10,2},{12,4},{14,6},{1,9},{3,11}... | collective-permute-start | bytes 147464 | tf_op jit(solution)/shard_map/ppermute | solution.py:157
  50.5 9.9 %collective-permute-start.19 = (bf16[16,1536]{1,0:T(8,128)(2,1)S(1)}, bf16[16,1536]{1,0:T(8,128)(2,1)S(1)}, u32[]{:S(2)}, u32[]{:S(2)}) collective-permute-start(bf16[16,1536]{1,0:T(8,128)(2,1)S(1)} %get-tuple-element.68), channel_id=1, source_target_pairs={{0,10},{2,8},{4,14},{6,12},{8,2},{10,0},{12,6},{14,4},{1,11},{3,9}... | collective-permute-start | bytes 147464 | tf_op jit(solution)/shard_map/ppermute | solution.py:157
  50.5 9.9 %collective-permute-start.20 = (bf16[16,1536]{1,0:T(8,128)(2,1)S(1)}, bf16[16,1536]{1,0:T(8,128)(2,1)S(1)}, u32[]{:S(2)}, u32[]{:S(2)}) collective-permute-start(bf16[16,1536]{1,0:T(8,128)(2,1)S(1)} %get-tuple-element.69), channel_id=1, source_target_pairs={{0,12},{2,14},{4,8},{6,10},{8,4},{10,6},{12,0},{14,2},{1,13},{3,15... | collective-permute-start | bytes 147464 | tf_op jit(solution)/shard_map/ppermute | solution.py:157
  52.4 8.8 %collective-permute-start.21 = (bf16[16,1536]{1,0:T(8,128)(2,1)S(1)}, bf16[16,1536]{1,0:T(8,128)(2,1)S(1)}, u32[]{:S(2)}, u32[]{:S(2)}) collective-permute-start(bf16[16,1536]{1,0:T(8,128)(2,1)S(1)} %get-tuple-element.70), channel_id=1, source_target_pairs={{0,14},{2,12},{4,10},{6,8},{8,6},{10,4},{12,2},{14,0},{1,15},{3,13... | collective-permute-start | bytes 147464 | tf_op jit(solution)/shard_map/ppermute | solution.py:157
  55.3 8.5 %collective-permute-start.14 = (bf16[16,1536]{1,0:T(8,128)(2,1)S(1)}, bf16[16,1536]{1,0:T(8,128)(2,1)S(1)}, u32[]{:S(2)}, u32[]{:S(2)}) collective-permute-start(bf16[16,1536]{1,0:T(8,128)(2,1)S(1)} %get-tuple-element.63), channel_id=1, source_target_pairs={{0,8},{2,10},{4,12},{6,14},{8,0},{10,2},{12,4},{14,6},{1,9},{3,11}... | collective-permute-start | bytes 147464 | tf_op jit(solution)/shard_map/ppermute | solution.py:157
  56.3 9.6 %collective-permute-start.15 = (bf16[16,1536]{1,0:T(8,128)(2,1)S(1)}, bf16[16,1536]{1,0:T(8,128)(2,1)S(1)}, u32[]{:S(2)}, u32[]{:S(2)}) collective-permute-start(bf16[16,1536]{1,0:T(8,128)(2,1)S(1)} %get-tuple-element.64), channel_id=1, source_target_pairs={{0,10},{2,8},{4,14},{6,12},{8,2},{10,0},{12,6},{14,4},{1,11},{3,9}... | collective-permute-start | bytes 147464 | tf_op jit(solution)/shard_map/ppermute | solution.py:157
  60.3 12.4 %collective-permute-start.11 = (bf16[16,3072]{1,0:T(8,128)(2,1)S(1)}, bf16[16,3072]{1,0:T(8,128)(2,1)S(1)}, u32[]{:S(2)}, u32[]{:S(2)}) collective-permute-start(bf16[16,3072]{1,0:T(8,128)(2,1)S(1)} %get-tuple-element.60), channel_id=1, source_target_pairs={{0,2},{2,0},{4,6},{6,4},{8,10},{10,8},{12,14},{14,12},{1,3},{3,1},... | collective-permute-start | bytes 294920 | tf_op jit(solution)/shard_map/ppermute | solution.py:157
  60.3 12.4 %collective-permute-start.12 = (bf16[16,3072]{1,0:T(8,128)(2,1)S(1)}, bf16[16,3072]{1,0:T(8,128)(2,1)S(1)}, u32[]{:S(2)}, u32[]{:S(2)}) collective-permute-start(bf16[16,3072]{1,0:T(8,128)(2,1)S(1)} %get-tuple-element.61), channel_id=1, source_target_pairs={{0,4},{2,6},{4,0},{6,2},{8,12},{10,14},{12,8},{14,10},{1,5},{3,7},... | collective-permute-start | bytes 294920 | tf_op jit(solution)/shard_map/ppermute | solution.py:157
  61.1 11.6 %collective-permute-start.13 = (bf16[16,3072]{1,0:T(8,128)(2,1)S(1)}, bf16[16,3072]{1,0:T(8,128)(2,1)S(1)}, u32[]{:S(2)}, u32[]{:S(2)}) collective-permute-start(bf16[16,3072]{1,0:T(8,128)(2,1)S(1)} %get-tuple-element.62), channel_id=1, source_target_pairs={{0,6},{2,4},{4,2},{6,0},{8,14},{10,12},{12,10},{14,8},{1,7},{3,5},... | collective-permute-start | bytes 294920 | tf_op jit(solution)/shard_map/ppermute | solution.py:157
  63.8 6.3 %collective-permute-start.16 = (bf16[16,1536]{1,0:T(8,128)(2,1)S(1)}, bf16[16,1536]{1,0:T(8,128)(2,1)S(1)}, u32[]{:S(2)}, u32[]{:S(2)}) collective-permute-start(bf16[16,1536]{1,0:T(8,128)(2,1)S(1)} %get-tuple-element.65), channel_id=1, source_target_pairs={{0,12},{2,14},{4,8},{6,10},{8,4},{10,6},{12,0},{14,2},{1,13},{3,15... | collective-permute-start | bytes 147464 | tf_op jit(solution)/shard_map/ppermute | solution.py:157
  65.9 6.8 %collective-permute-start.17 = (bf16[16,1536]{1,0:T(8,128)(2,1)S(1)}, bf16[16,1536]{1,0:T(8,128)(2,1)S(1)}, u32[]{:S(2)}, u32[]{:S(2)}) collective-permute-start(bf16[16,1536]{1,0:T(8,128)(2,1)S(1)} %get-tuple-element.66), channel_id=1, source_target_pairs={{0,14},{2,12},{4,10},{6,8},{8,6},{10,4},{12,2},{14,0},{1,15},{3,13... | collective-permute-start | bytes 147464 | tf_op jit(solution)/shard_map/ppermute | solution.py:157

commit v4 on v3

--- a/solution.py
+++ b/solution.py
@@ -26,49 +26,65 @@
     return lax.dot_general(left, right, ((contract[0], contract[1]), ((), ())), preferred_element_type=F32)
 
 
-def pack_kernel(home_ref, q_ref, k_ref, v_ref, g_ref, pk_ref, pv_ref, *blocks, count, heads):
+def pack_kernel(home_ref, q_ref, k_ref, v_ref, g_ref, pk_ref, pv_ref, *rest, count, head, heads, by_rank):
+    blocks, (home, q, g, k, v, prompt, sems) = rest[:-7], rest[-7:]
     rank = lax.axis_index("seq")
     prompt_rows = pk_ref.shape[0]
-    rows = q_ref.shape[1]
-    near = count // 2
-    q_part = q_ref.shape[2] // heads
+    q_part = q.shape[2]
+    lanes = pl.ds(head * HEAD_DIM, HEAD_DIM)
+    wide = pl.ds(head * q_part, q_part)
+    copies = [
+        pltpu.make_async_copy(source, target, sems.at[index])
+        for index, (source, target) in enumerate(
+            (
+                (home_ref, home),
+                (q_ref.at[:, :, wide], q),
+                (g_ref.at[:, :, wide], g),
+                (k_ref.at[:, :, lanes], k),
+                (v_ref.at[:, :, lanes], v),
+                (pk_ref.at[:, lanes], prompt.at[0]),
+                (pv_ref.at[:, lanes], prompt.at[1]),
+            )
+        )
+    ]
+    for copy in copies:
+        copy.start()
+    for copy in copies:
+        copy.wait()
+    rows = q.shape[1]
     spare = jnp.zeros((rows - prompt_rows, HEAD_DIM), BF16)
-    width = 2 * q_part + 4 * HEAD_DIM
-    for head in range(heads):
-        lanes = slice(head * HEAD_DIM, (head + 1) * HEAD_DIM)
-        wide = slice(head * q_part, (head + 1) * q_part)
-        prompt = [jnp.concatenate([ref[:, lanes], spare], axis=0) for ref in (pk_ref, pv_ref)]
-        for distance in [*range(near, count), *range(near)]:
-            index = resident_of(home_ref, rank ^ distance, count)
-            if distance < near:
-                block, low = blocks[distance], head * width
-            else:
-                block, low = blocks[near + head * (count - near) + distance - near], 0
-            for ref, part in ((q_ref, wide), (g_ref, wide), (k_ref, lanes), (v_ref, lanes)):
-                size = part.stop - part.start
-                block[:, low : low + size] = ref[index, :, part]
-                low += size
-            for rows_of in prompt:
-                block[:, low : low + HEAD_DIM] = rows_of
-                low += HEAD_DIM
-
-
-def attend_kernel(lengths_ref, home_ref, seen_ref, *rest, count, prompt_rows, head, heads):
-    near = count // 2
-    last = head == heads - 1
-    blocks, rest = rest[:count], rest[count:]
-    kept, rest = rest[: (head if last else 0) * (near + 1)], rest[(head if last else 0) * (near + 1) :]
-    out_ref, returns, (x, y) = rest[0], rest[1 : count + 1], rest[count + 1 :]
-    rank = lax.axis_index("seq")
-    rows, width = blocks[near].shape
+    padded = [jnp.concatenate([prompt[part], spare], axis=0) for part in range(2)]
+    for place in range(count):
+        index = resident_of(home, place if by_rank else rank ^ place, count)
+        block = blocks[0].at[place] if by_rank else blocks[place]
+        low = 0
+        for ref in (q, g, k, v):
+            block[:, low : low + ref.shape[2]] = ref[index]
+            low += ref.shape[2]
+        for part in padded:
+            block[:, low : low + HEAD_DIM] = part
+            low += HEAD_DIM
+
+
+def attend_kernel(lengths_ref, home_ref, seen_ref, *rest, count, prompt_rows, by_rank):
+    blocks, rest = (rest[:1], rest[1:]) if by_rank else (rest[:count], rest[count:])
+    if by_rank:
+        (out_ref, y) = rest
+        x = blocks[0]
+        rows, width = x.shape[1:]
+    else:
+        earlier_ref, out_ref, *returns, x, y = rest
+        rows, width = blocks[0].shape
     total = rows * count
     q_part = (width - 4 * HEAD_DIM) // 2
-    back = q_part + 4 * HEAD_DIM
     scale = 1.0 / HEAD_DIM**0.5
-    for distance in range(count):
-        low = head * width if distance < near else 0
-        at = pl.ds(pl.multiple_of((rank ^ distance) * rows, rows), rows)
-        x[at, :] = blocks[distance][:, low : low + width]
+    rank = lax.axis_index("seq")
+    out_low = 0
+    if not by_rank:
+        for distance in range(count):
+            x[rank ^ distance] = blocks[distance][...]
+        out_low = earlier_ref.shape[2]
+        out_ref[:, :, :out_low] = earlier_ref[...]
     own = resident_of(home_ref, rank, count)
     length = lengths_ref[own]
     visible = seen_ref[own]
@@ -80,10 +96,12 @@
         [(shard_row < prompt_rows) & (prompt_index < visible), column <= position], axis=1
     )
     live = lax.broadcasted_iota(jnp.int32, (total, HEAD_DIM), 0) < length
-    out_low = head * q_part if last else 0
 
     def lanes(low):
-        return x[:, low : low + HEAD_DIM]
+        return x[:, :, low : low + HEAD_DIM].reshape(total, HEAD_DIM)
+
+    def give(low, value):
+        y[:, :, low : low + HEAD_DIM] = value.astype(BF16).reshape(count, rows, HEAD_DIM)
 
     low = 2 * q_part
     keys = jnp.concatenate([lanes(low + 2 * HEAD_DIM), lanes(low)], axis=0)
@@ -102,43 +120,31 @@
         out_ref[0, :, out_low + low : out_low + low + HEAD_DIM] = output
         row_dot = jnp.sum(grad.astype(F32) * output.astype(F32), axis=1, keepdims=True)
         dlogit = (prob * (spread - row_dot)).astype(BF16)
-        y[:, low : low + HEAD_DIM] = (dot(dlogit, keys, ((1,), (0,))) * scale).astype(BF16)
+        give(low, dot(dlogit, keys, ((1,), (0,))) * scale)
         key_grad += dot(dlogit, query, ((0,), (0,)))
         value_grad += dot(weights, grad, ((0,), (0,)))
     for part, summed in enumerate((key_grad * scale, value_grad)):
-        at = q_part + part * HEAD_DIM
-        y[:, at : at + HEAD_DIM] = summed[total:].astype(BF16)
-        at += 2 * HEAD_DIM
-        y[:, at : at + HEAD_DIM] = summed[:total].astype(BF16)
-    for distance in range(count):
-        low = head * back if last and distance < near else 0
-        at = pl.ds(pl.multiple_of((rank ^ distance) * rows, rows), rows)
-        returns[distance][:, low : low + back] = y[at, :]
-    for earlier in range(len(kept) // (near + 1)):
-        parts = kept[earlier * (near + 1) : (earlier + 1) * (near + 1)]
-        out_ref[0, :, earlier * q_part : (earlier + 1) * q_part] = parts[0][0]
-        for distance in range(near):
-            returns[distance][:, earlier * back : (earlier + 1) * back] = parts[1 + distance][...]
+        give(q_part + part * HEAD_DIM, summed[total:])
+        give(q_part + (part + 2) * HEAD_DIM, summed[:total])
+    if not by_rank:
+        for distance in range(count):
+            returns[distance][...] = y[rank ^ distance]
 
 
 def unpack_kernel(home_ref, *rest, count, heads):
-    near = count // 2
     blocks = rest[:-5]
     qg_ref, kg_ref, vg_ref, pkg_ref, pvg_ref = rest[-5:]
     rank = lax.axis_index("seq")
     prompt_rows = pkg_ref.shape[0]
     q_part = qg_ref.shape[2] // heads
-    back = q_part + 4 * HEAD_DIM
     for head in range(heads):
         lanes = slice(head * HEAD_DIM, (head + 1) * HEAD_DIM)
         wide = slice(head * q_part, (head + 1) * q_part)
         summed = [jnp.zeros((qg_ref.shape[1], HEAD_DIM), F32)] * 2
-        for distance in range(count):
-            index = resident_of(home_ref, rank ^ distance, count)
-            if distance < near:
-                block, low = blocks[distance], head * back
-            else:
-                block, low = blocks[near + head * (count - near) + distance - near], 0
+        for place in range(count):
+            index = resident_of(home_ref, rank ^ place if head else place, count)
+            block = blocks[1 + (head - 1) * count + place] if head else blocks[0].at[place]
+            low = 0
             for ref, part in ((qg_ref, wide), (kg_ref, lanes), (vg_ref, lanes)):
                 size = part.stop - part.start
                 ref[index, :, part] = block[:, low : low + size]
@@ -150,17 +156,23 @@
         pvg_ref[:, lanes] = summed[1][:prompt_rows].astype(BF16)
 
 
-def exchange(blocks, distances, count):
-    arrived = []
-    for block, distance in zip(blocks, distances):
-        if distance:
-            block = lax.ppermute(block, "seq", [(i, i ^ distance) for i in range(count)])
-        arrived.append(block)
+def exchange(blocks):
+    count = len(blocks)
+    arrived = list(blocks)
+    for distance in range(1, count):
+        arrived[distance] = lax.ppermute(
+            blocks[distance], "seq", [(i, i ^ distance) for i in range(count)]
+        )
     return arrived
+
+
+def exchange_by_rank(blocks):
+    return lax.all_to_all(blocks, "seq", split_axis=0, concat_axis=0, tiled=True)
 
 
 SMEM = pl.BlockSpec(memory_space=pltpu.SMEM)
 VMEM = pl.BlockSpec(memory_space=pltpu.VMEM)
+HBM = pl.BlockSpec(memory_space=pltpu.HBM)
 PARAMS = pltpu.CompilerParams(vmem_limit_bytes=24 * 1024 * 1024)
 
 
@@ -180,63 +192,61 @@
     prompt_rows, kv_width = prompt_key.shape
     total = rows * count
     heads = kv_width // HEAD_DIM
-    near, far = range(count // 2), range(count // 2, count)
     q_part = q_width // heads
     width = 2 * q_part + 4 * HEAD_DIM
     back = q_part + 4 * HEAD_DIM
 
-    def shape(*dims):
-        return jax.ShapeDtypeStruct(dims, BF16)
-
-    packed = pl.pallas_call(
-        functools.partial(pack_kernel, count=count, heads=heads),
-        name="pack",
-        out_shape=[shape(rows, heads * width)] * len(near) + [shape(rows, width)] * (len(far) * heads),
-        in_specs=[SMEM] + [VMEM] * 6,
-        out_specs=[VMEM] * (len(near) + len(far) * heads),
-        compiler_params=PARAMS,
-    )(home_rank, response_query, response_key, response_value, response_grad, prompt_key, prompt_value)
-    far_in = [exchange(packed[len(near) :][: len(far)], far, count)]
-    near_in = exchange(packed[: len(near)], near, count)
-    for head in range(1, heads):
-        blocks = packed[len(near) + head * len(far) :][: len(far)]
-        far_in.append(exchange(blocks, far, count))
-    kept, far_back = [], []
+    def shapes(by_rank, lanes):
+        dims = [(count, rows, lanes)] if by_rank else [(rows, lanes)] * count
+        return [jax.ShapeDtypeStruct(each, BF16) for each in dims]
+
+    arrived = []
+    sources = [
+        pltpu.with_memory_space_constraint(source, pltpu.HBM)
+        for source in (home_rank, response_query, response_key, response_value, response_grad, prompt_key, prompt_value)
+    ]
     for head in range(heads):
-        last = head == heads - 1
-        whole = heads if last else 1
-        operands = [lengths, home_rank, prompt_seen, *near_in, *far_in[head], *(kept if last else [])]
-        results = pl.pallas_call(
-            functools.partial(
-                attend_kernel, count=count, prompt_rows=prompt_rows, head=head, heads=heads
-            ),
-            out_shape=[shape(1, total, whole * q_part)]
-            + [shape(rows, whole * back)] * len(near)
-            + [shape(rows, back)] * len(far),
+        by_rank = head == 0
+        results = shapes(by_rank, width)
+        blocks = pl.pallas_call(
+            functools.partial(pack_kernel, count=count, head=head, heads=heads, by_rank=by_rank),
+            out_shape=results,
+            in_specs=[HBM] * 7,
+            out_specs=[VMEM] * len(results),
+            scratch_shapes=[pltpu.SMEM((count,), jnp.int32)]
+            + [pltpu.VMEM((count, rows, lanes), BF16) for lanes in (q_part, q_part, HEAD_DIM, HEAD_DIM)]
+            + [pltpu.VMEM((2, prompt_rows, HEAD_DIM), BF16), pltpu.SemaphoreType.DMA((7,))],
+            compiler_params=PARAMS,
+        )(*sources)
+        arrived.append([exchange_by_rank(blocks[0])] if by_rank else exchange(blocks))
+    output, returned = [], []
+    for head in range(heads):
+        by_rank = head == 0
+        operands = [lengths, home_rank, prompt_seen, *arrived[head], *output]
+        results = [jax.ShapeDtypeStruct((1, total, (head + 1) * q_part), BF16)] + shapes(by_rank, back)
+        scratch = [] if by_rank else [pltpu.VMEM((count, rows, lanes), BF16) for lanes in (width, back)]
+        output, *blocks = pl.pallas_call(
+            functools.partial(attend_kernel, count=count, prompt_rows=prompt_rows, by_rank=by_rank),
+            out_shape=results,
             in_specs=[SMEM] * 3 + [VMEM] * (len(operands) - 3),
-            out_specs=[VMEM] * (count + 1),
-            scratch_shapes=[pltpu.VMEM((total, width), BF16), pltpu.VMEM((total, back), BF16)],
+            out_specs=[VMEM] * len(results),
+            scratch_shapes=scratch,
             compiler_params=PARAMS,
         )(*operands)
-        far_back += exchange(results[1 + len(near) :], far, count)
-        kept += results[: 1 + len(near)]
-    output, *near_back = kept[-1 - len(near) :]
-    near_back = exchange(near_back, near, count)
+        output = [output]
+        returned += [exchange_by_rank(blocks[0])] if by_rank else exchange(blocks)
     grads = pl.pallas_call(
         functools.partial(unpack_kernel, count=count, heads=heads),
         name="unpack",
         out_shape=[
-            shape(count, rows, q_width),
-            shape(count, rows, kv_width),
-            shape(count, rows, kv_width),
-            shape(prompt_rows, kv_width),
-            shape(prompt_rows, kv_width),
+            jax.ShapeDtypeStruct(dims, BF16)
+            for dims in ((count, rows, q_width), *[(count, rows, kv_width)] * 2, *[(prompt_rows, kv_width)] * 2)
         ],
-        in_specs=[SMEM] + [VMEM] * (len(near) + len(far) * heads),
+        in_specs=[SMEM] + [VMEM] * len(returned),
         out_specs=[VMEM] * 5,
         compiler_params=PARAMS,
-    )(home_rank, *near_back, *far_back)
-    return (output, *grads)
+    )(home_rank, *returned)
+    return (output[0], *grads)
 
 
 def head_logits(queries, all_keys, allowed, head_index, group_size, scale_factor):

time: 74.6 us -> 84.4 us (1.13)
  blocking collectives: 0 us -> 24.9 us
  starting transfers between devices: 44.2 us -> 28.3 us
  local copies, waits for them, and re-layouts: 5.81 us -> 0.67 us
  waiting for transfers between devices: 9.78 us -> 13.6 us
  Pallas kernels: 13.6 us -> 16 us
    all_to_all x0 -> x1, blocking collectives: none -> 24.9 us  [exchange_by_rank(): lax.all_to_all(blocks, 'seq', split_axis=0, concat_axis=0, tiled=True)]
    ppermute x22 -> x14, starting transfers between devices: 44.2 us -> 24.8 us  [exchange(): lax.ppermute(blocks[distance], 'seq', [(i, i ^ distance) for i in range(c...]
    unnamed x18 -> x8, local copies, waits for them, and re-layouts: 5.81 us -> 0.67 us
    ppermute x22 -> x14, waiting for transfers between devices: 9.78 us -> 13.6 us  [exchange(): lax.ppermute(blocks[distance], 'seq', [(i, i ^ distance) for i in range(c...]
    all_to_all x0 -> x1, starting transfers between devices: none -> 3.45 us  [exchange_by_rank(): lax.all_to_all(blocks, 'seq', split_axis=0, concat_axis=0, tiled=True)]
    pallas_call x1 -> x2, Pallas kernels: 0.67 us -> 2.33 us  [packed_body(): pl.pallas_call(functools.partial(pack_kernel, count=count, head=head, hea...]
  transfers between devices with their start and end apart: 22 -> 15, of which waited for: 5 -> 4; matrix products, arithmetic and copies ran while one was open for 0% -> 0% of each run, Pallas kernels for 7% -> 9%
where the time goes in v4:
time: 84.4 us; the launch traced here: 84.1 us
  starting transfers between devices  28.3 us (34%)
  blocking collectives  24.9 us (30%)
  Pallas kernels  16 us (19%)
  waiting for transfers between devices  13.6 us (16%)
    all_to_all x1, blocking collectives, exchange_by_rank(): lax.all_to_all(blocks, 'seq', split_axis=0, concat_axis=0, tiled=True)  24.9 us
    ppermute x14, starting transfers between devices, exchange(): lax.ppermute(blocks[distance], 'seq', [(i, i ^ distance) for i in range(c...  24.8 us
    ppermute x14, waiting for transfers between devices, exchange(): lax.ppermute(blocks[distance], 'seq', [(i, i ^ distance) for i in range(c...  13.6 us
    pallas_call x2, Pallas kernels, packed_body(): pl.pallas_call(functools.partial(attend_kernel, count=count, prompt_rows=...  12.2 us
    all_to_all x1, starting transfers between devices, exchange_by_rank(): lax.all_to_all(blocks, 'seq', split_axis=0, concat_axis=0, tiled=True)  3.45 us
    pallas_call x2, Pallas kernels, packed_body(): pl.pallas_call(functools.partial(pack_kernel, count=count, head=head, hea...  2.33 us
  transfers between devices with their start and end apart: 15, of which 4 were waited for; matrix products, arithmetic and copies ran while one was open for 0% of the time, Pallas kernels for 9%

profile of v4, /device:TPU:0, one launch (start us, length us, event | category | flops | bytes accessed | tf_op | source)
XLA Modules:
  0.0 84.1 jit_solution(15897696748312303581)
XLA Ops:
  0.6 1.2 %shard_map.137 = bf16[8,16,2560]{2,1,0:T(8,128)(2,1)S(1)} custom-call(s32[8]{0:T(128)} %home_ref.9, bf16[8,16,2048]{2,1,0:T(8,128)(2,1)} %q_ref.3, bf16[8,16,256]{2,1,0:T(8,128)(2,1)} %k_ref.3, bf16[8,16,256]{2,1,0:T(8,128)(2,1)} %v_ref.3, bf16[8,16,2048]{2,1,0:T(8,128)(2,1)} %g_ref.3, bf16[12,256]{1,0:T(8,128)(2,1)} %pk_ref.3, bf16[12,256]{1,0:T(8,128)(2,1)} %pv_ref.3), custom_call_target="tpu_custom_call" | custom-call | tf_op jit(solution)/shard_map/pallas_call | solution.py:211
  1.8 0.0 copy-start
  1.8 0.0 copy-start.2
  1.8 0.0 copy-start.3
  1.8 24.9 %all_to_all.10.rest_0_ = bf16[8,16,2560]{2,1,0:T(8,128)(2,1)S(1)} all-to-all(bf16[8,16,2560]{2,1,0:T(8,128)(2,1)S(1)} %shard_map.137), channel_id=1, replica_groups=mesh['group'=2,'seq'=8,'head'=2] {'seq'}, dimensions={0} | all-to-all | bytes 1310720 | tf_op jit(solution)/shard_map/all_to_all | solution.py:170
  26.7 0.0 copy-done
  26.7 0.0 copy-done.2
  26.7 0.0 copy-done.3
  26.7 6.1 %shard_map.138 = (bf16[1,128,1024]{2,1,0:T(8,128)(2,1)S(1)}, bf16[8,16,1536]{2,1,0:T(8,128)(2,1)}) custom-call(s32[8]{0:T(128)S(1)} %copy-done.2, s32[8]{0:T(128)S(1)} %copy-done, s32[8]{0:T(128)S(1)} %copy-done.3, bf16[8,16,2560]{2,1,0:T(8,128)(2,1)S(1)} %all_to_all.10.rest_0_), custom_call_target="tpu_custom_call" | custom-call | tf_op jit(solution)/shard_map/pallas_call | solution.py:228
  32.8 3.5 %all-to-all-start.1 = ((bf16[8,16,1536]{2,1,0:T(8,128)(2,1)}), bf16[8,16,1536]{2,1,0:T(8,128)(2,1)S(1)}, u32[]{:S(2)}, u32[]{:S(2)}) async-start(bf16[8,16,1536]{2,1,0:T(8,128)(2,1)} %get-tuple-element.40), calls=%async_computation.1 | async-start | bytes 786432 | tf_op jit(solution)/shard_map/all_to_all | solution.py:170
  36.2 1.2 %shard_map.136 = (bf16[16,2560]{1,0:T(8,128)(2,1)S(1)}, bf16[16,2560]{1,0:T(8,128)(2,1)S(1)}, bf16[16,2560]{1,0:T(8,128)(2,1)S(1)}, bf16[16,2560]{1,0:T(8,128)(2...) custom-call(s32[8]{0:T(128)} %home_ref.9, ...), custom_call_target="tpu_custom_call" | custom-call | tf_op jit(solution)/shard_map/pallas_call | solution.py:211
  37.4 2.0 %collective-permute-start = (bf16[16,2560]{1,0:T(8,128)(2,1)S(1)}, bf16[16,2560]{1,0:T(8,128)(2,1)S(1)}, u32[]{:S(2)}, u32[]{:S(2)}) collective-permute-start(bf16[16,2560]{1,0:T(8,128)(2,1)S(1)} %get-tuple-element.31), channel_id=1, source_target_pairs={{0,2},{2,0},{4,6},{6,4},{8,10},{10,8},{12,14},{14,12},{1,3},{3,1},... | collective-permute-start | bytes 245768 | tf_op jit(solution)/shard_map/ppermute | solution.py:163
  39.4 1.5 %collective-permute-start.1 = (bf16[16,2560]{1,0:T(8,128)(2,1)S(1)}, bf16[16,2560]{1,0:T(8,128)(2,1)S(1)}, u32[]{:S(2)}, u32[]{:S(2)}) collective-permute-start(bf16[16,2560]{1,0:T(8,128)(2,1)S(1)} %get-tuple-element.32), channel_id=1, source_target_pairs={{0,4},{2,6},{4,0},{6,2},{8,12},{10,14},{12,8},{14,10},{1,5},{3,7},... | collective-permute-start | bytes 245768 | tf_op jit(solution)/shard_map/ppermute | solution.py:163
  40.9 0.1 collective-permute-start.2
  41.0 2.8 %collective-permute-start.3 = (bf16[16,2560]{1,0:T(8,128)(2,1)S(1)}, bf16[16,2560]{1,0:T(8,128)(2,1)S(1)}, u32[]{:S(2)}, u32[]{:S(2)}) collective-permute-start(bf16[16,2560]{1,0:T(8,128)(2,1)S(1)} %get-tuple-element.34), channel_id=1, source_target_pairs={{0,8},{2,10},{4,12},{6,14},{8,0},{10,2},{12,4},{14,6},{1,9},{3,11}... | collective-permute-start | bytes 245768 | tf_op jit(solution)/shard_map/ppermute | solution.py:163
  43.8 1.4 %collective-permute-start.4 = (bf16[16,2560]{1,0:T(8,128)(2,1)S(1)}, bf16[16,2560]{1,0:T(8,128)(2,1)S(1)}, u32[]{:S(2)}, u32[]{:S(2)}) collective-permute-start(bf16[16,2560]{1,0:T(8,128)(2,1)S(1)} %get-tuple-element.35), channel_id=1, source_target_pairs={{0,10},{2,8},{4,14},{6,12},{8,2},{10,0},{12,6},{14,4},{1,11},{3,9}... | collective-permute-start | bytes 245768 | tf_op jit(solution)/shard_map/ppermute | solution.py:163
  45.2 0.0 collective-permute-done.rest_1_
  45.2 3.3 %collective-permute-start.5 = (bf16[16,2560]{1,0:T(8,128)(2,1)S(1)}, bf16[16,2560]{1,0:T(8,128)(2,1)S(1)}, u32[]{:S(2)}, u32[]{:S(2)}) collective-permute-start(bf16[16,2560]{1,0:T(8,128)(2,1)S(1)} %get-tuple-element.36), channel_id=1, source_target_pairs={{0,12},{2,14},{4,8},{6,10},{8,4},{10,6},{12,0},{14,2},{1,13},{3,15... | collective-permute-start | bytes 245768 | tf_op jit(solution)/shard_map/ppermute | solution.py:163
  48.5 0.0 collective-permute-done.1.rest_2_
  48.5 1.7 %collective-permute-start.6 = (bf16[16,2560]{1,0:T(8,128)(2,1)S(1)}, bf16[16,2560]{1,0:T(8,128)(2,1)S(1)}, u32[]{:S(2)}, u32[]{:S(2)}) collective-permute-start(bf16[16,2560]{1,0:T(8,128)(2,1)S(1)} %get-tuple-element.37), channel_id=1, source_target_pairs={{0,14},{2,12},{4,10},{6,8},{8,6},{10,4},{12,2},{14,0},{1,15},{3,13... | collective-permute-start | bytes 245768 | tf_op jit(solution)/shard_map/ppermute | solution.py:163
  50.3 0.0 collective-permute-done.2.rest_3_
  50.3 7.6 %collective-permute-done.3.rest_4_ = bf16[16,2560]{1,0:T(8,128)(2,1)S(1)} collective-permute-done((bf16[16,2560]{1,0:T(8,128)(2,1)S(1)}, bf16[16,2560]{1,0:T(8,128)(2,1)S(1)}, u32[]{:S(2)}, u32[]{:S(2)}) %collective-permute-start.3) | collective-permute-done | bytes 81952 | tf_op jit(solution)/shard_map/ppermute | solution.py:163
  57.9 2.3 %collective-permute-done.4.rest_5_ = bf16[16,2560]{1,0:T(8,128)(2,1)S(1)} collective-permute-done((bf16[16,2560]{1,0:T(8,128)(2,1)S(1)}, bf16[16,2560]{1,0:T(8,128)(2,1)S(1)}, u32[]{:S(2)}, u32[]{:S(2)}) %collective-permute-start.4) | collective-permute-done | bytes 81952 | tf_op jit(solution)/shard_map/ppermute | solution.py:163
  60.2 0.0 collective-permute-done.5.rest_6_
  60.2 0.0 collective-permute-done.6.rest_7_
  60.2 0.0 copy-start.1
  60.2 0.7 copy-done.1
  60.8 6.1 %shard_map.139 = (bf16[1,128,2048]{2,1,0:T(8,128)(2,1)}, bf16[16,1536]{1,0:T(8,128)(2,1)S(1)}, bf16[16,1536]{1,0:T(8,128)(2,1)S(1)}, bf16[16,1536]{1,0:T(8,128)(...) custom-call(s32[8]{0:T(128)S(1)} %copy-done.2, ...), custom_call_target="tpu_custom_call" | custom-call | tf_op jit(solution)/shard_map/pallas_call | solution.py:228
  66.9 0.9 %collective-permute-start.7 = (bf16[16,1536]{1,0:T(8,128)(2,1)S(1)}, bf16[16,1536]{1,0:T(8,128)(2,1)S(1)}, u32[]{:S(2)}, u32[]{:S(2)}) collective-permute-start(bf16[16,1536]{1,0:T(8,128)(2,1)S(1)} %get-tuple-element.42), channel_id=1, source_target_pairs={{0,2},{2,0},{4,6},{6,4},{8,10},{10,8},{12,14},{14,12},{1,3},{3,1},... | collective-permute-start | bytes 147464 | tf_op jit(solution)/shard_map/ppermute | solution.py:163
  67.9 2.5 %collective-permute-start.8 = (bf16[16,1536]{1,0:T(8,128)(2,1)S(1)}, bf16[16,1536]{1,0:T(8,128)(2,1)S(1)}, u32[]{:S(2)}, u32[]{:S(2)}) collective-permute-start(bf16[16,1536]{1,0:T(8,128)(2,1)S(1)} %get-tuple-element.43), channel_id=1, source_target_pairs={{0,4},{2,6},{4,0},{6,2},{8,12},{10,14},{12,8},{14,10},{1,5},{3,7},... | collective-permute-start | bytes 147464 | tf_op jit(solution)/shard_map/ppermute | solution.py:163
  70.4 0.9 %collective-permute-start.9 = (bf16[16,1536]{1,0:T(8,128)(2,1)S(1)}, bf16[16,1536]{1,0:T(8,128)(2,1)S(1)}, u32[]{:S(2)}, u32[]{:S(2)}) collective-permute-start(bf16[16,1536]{1,0:T(8,128)(2,1)S(1)} %get-tuple-element.44), channel_id=1, source_target_pairs={{0,6},{2,4},{4,2},{6,0},{8,14},{10,12},{12,10},{14,8},{1,7},{3,5},... | collective-permute-start | bytes 147464 | tf_op jit(solution)/shard_map/ppermute | solution.py:163
  71.3 2.1 %collective-permute-start.10 = (bf16[16,1536]{1,0:T(8,128)(2,1)S(1)}, bf16[16,1536]{1,0:T(8,128)(2,1)S(1)}, u32[]{:S(2)}, u32[]{:S(2)}) collective-permute-start(bf16[16,1536]{1,0:T(8,128)(2,1)S(1)} %get-tuple-element.45), channel_id=1, source_target_pairs={{0,8},{2,10},{4,12},{6,14},{8,0},{10,2},{12,4},{14,6},{1,9},{3,11}... | collective-permute-start | bytes 147464 | tf_op jit(solution)/shard_map/ppermute | solution.py:163
  73.4 0.9 %collective-permute-start.11 = (bf16[16,1536]{1,0:T(8,128)(2,1)S(1)}, bf16[16,1536]{1,0:T(8,128)(2,1)S(1)}, u32[]{:S(2)}, u32[]{:S(2)}) collective-permute-start(bf16[16,1536]{1,0:T(8,128)(2,1)S(1)} %get-tuple-element.46), channel_id=1, source_target_pairs={{0,10},{2,8},{4,14},{6,12},{8,2},{10,0},{12,6},{14,4},{1,11},{3,9}... | collective-permute-start | bytes 147464 | tf_op jit(solution)/shard_map/ppermute | solution.py:163
  74.2 0.0 collective-permute-done.7.rest_2_
  74.3 1.5 %collective-permute-start.12 = (bf16[16,1536]{1,0:T(8,128)(2,1)S(1)}, bf16[16,1536]{1,0:T(8,128)(2,1)S(1)}, u32[]{:S(2)}, u32[]{:S(2)}) collective-permute-start(bf16[16,1536]{1,0:T(8,128)(2,1)S(1)} %get-tuple-element.47), channel_id=1, source_target_pairs={{0,12},{2,14},{4,8},{6,10},{8,4},{10,6},{12,0},{14,2},{1,13},{3,15... | collective-permute-start | bytes 147464 | tf_op jit(solution)/shard_map/ppermute | solution.py:163
  75.7 0.0 collective-permute-done.8.rest_3_
  75.7 3.2 %collective-permute-start.13 = (bf16[16,1536]{1,0:T(8,128)(2,1)S(1)}, bf16[16,1536]{1,0:T(8,128)(2,1)S(1)}, u32[]{:S(2)}, u32[]{:S(2)}) collective-permute-start(bf16[16,1536]{1,0:T(8,128)(2,1)S(1)} %get-tuple-element.48), channel_id=1, source_target_pairs={{0,14},{2,12},{4,10},{6,8},{8,6},{10,4},{12,2},{14,0},{1,15},{3,13... | collective-permute-start | bytes 147464 | tf_op jit(solution)/shard_map/ppermute | solution.py:163
  78.9 0.0 collective-permute-done.9.rest_4_
  78.9 0.0 collective-permute-done.10.rest_5_
  78.9 1.5 %collective-permute-done.11.rest_6_ = bf16[16,1536]{1,0:T(8,128)(2,1)S(1)} collective-permute-done((bf16[16,1536]{1,0:T(8,128)(2,1)S(1)}, bf16[16,1536]{1,0:T(8,128)(2,1)S(1)}, u32[]{:S(2)}, u32[]{:S(2)}) %collective-permute-start.11) | collective-permute-done | bytes 49184 | tf_op jit(solution)/shard_map/ppermute | solution.py:163
  80.4 0.0 collective-permute-done.12.rest_7_
  80.4 2.2 %collective-permute-done.13.rest_8_ = bf16[16,1536]{1,0:T(8,128)(2,1)S(1)} collective-permute-done((bf16[16,1536]{1,0:T(8,128)(2,1)S(1)}, bf16[16,1536]{1,0:T(8,128)(2,1)S(1)}, u32[]{:S(2)}, u32[]{:S(2)}) %collective-permute-start.13) | collective-permute-done | bytes 49184 | tf_op jit(solution)/shard_map/ppermute | solution.py:163
  82.6 0.0 all-to-all-done.1.rest_0_
  82.6 1.5 %unpack.1 = (bf16[8,16,2048]{2,1,0:T(8,128)(2,1)}, bf16[8,16,256]{2,1,0:T(8,128)(2,1)}, bf16[8,16,256]{2,1,0:T(8,128)(2,1)}, bf16[12,256]{1,0:T(8,128)(2,1)}, bf16[12,256]{1,0:T(8,128)(2,1)}) custom-call(s32[8]{0:T(128)S(1)} %copy-done.1, bf16[8,16,1536]{2,1,0:T(8,128)(2,1)S(1)} %all-to-all-done.1.rest_0_, bf16[16,1536]{1,0:T(8,128)(2,1)S(1)} %get-tuple-element.41.rest_1_, ...), custom_call_target="tpu_custom_call" | custom-call | tf_op jit(solution)/shard_map/unpack/pallas_call | solution.py:238
Async XLA Ops:
  1.8 24.9 %copy-start = (s32[8]{0:T(128)S(1)}, s32[8]{0:T(128)}, u32[]{:S(2)}) copy-start(s32[8]{0:T(128)} %home_ref.9) | copy-start | bytes 100
  1.8 24.9 %copy-start.2 = (s32[8]{0:T(128)S(1)}, s32[8]{0:T(128)}, u32[]{:S(2)}) copy-start(s32[8]{0:T(128)} %lengths_ref.3) | copy-start | bytes 100
  1.8 24.9 %copy-start.3 = (s32[8]{0:T(128)S(1)}, s32[8]{0:T(128)}, u32[]{:S(2)}) copy-start(s32[8]{0:T(128)} %seen_ref.3) | copy-start | bytes 100
  32.8 49.8 %all-to-all-start.1 = ((bf16[8,16,1536]{2,1,0:T(8,128)(2,1)}), bf16[8,16,1536]{2,1,0:T(8,128)(2,1)S(1)}, u32[]{:S(2)}, u32[]{:S(2)}) async-start(bf16[8,16,1536]{2,1,0:T(8,128)(2,1)} %get-tuple-element.40), calls=%async_computation.1 | async-start | bytes 786432 | tf_op jit(solution)/shard_map/all_to_all | solution.py:170
  37.4 7.8 %collective-permute-start = (bf16[16,2560]{1,0:T(8,128)(2,1)S(1)}, bf16[16,2560]{1,0:T(8,128)(2,1)S(1)}, u32[]{:S(2)}, u32[]{:S(2)}) collective-permute-start(bf16[16,2560]{1,0:T(8,128)(2,1)S(1)} %get-tuple-element.31), channel_id=1, source_target_pairs={{0,2},{2,0},{4,6},{6,4},{8,10},{10,8},{12,14},{14,12},{1,3},{3,1},... | collective-permute-start | bytes 245768 | tf_op jit(solution)/shard_map/ppermute | solution.py:163
  39.4 9.2 %collective-permute-start.1 = (bf16[16,2560]{1,0:T(8,128)(2,1)S(1)}, bf16[16,2560]{1,0:T(8,128)(2,1)S(1)}, u32[]{:S(2)}, u32[]{:S(2)}) collective-permute-start(bf16[16,2560]{1,0:T(8,128)(2,1)S(1)} %get-tuple-element.32), channel_id=1, source_target_pairs={{0,4},{2,6},{4,0},{6,2},{8,12},{10,14},{12,8},{14,10},{1,5},{3,7},... | collective-permute-start | bytes 245768 | tf_op jit(solution)/shard_map/ppermute | solution.py:163
  40.9 9.4 %collective-permute-start.2 = (bf16[16,2560]{1,0:T(8,128)(2,1)S(1)}, bf16[16,2560]{1,0:T(8,128)(2,1)S(1)}, u32[]{:S(2)}, u32[]{:S(2)}) collective-permute-start(bf16[16,2560]{1,0:T(8,128)(2,1)S(1)} %get-tuple-element.33), channel_id=1, source_target_pairs={{0,6},{2,4},{4,2},{6,0},{8,14},{10,12},{12,10},{14,8},{1,7},{3,5},... | collective-permute-start | bytes 245768 | tf_op jit(solution)/shard_map/ppermute | solution.py:163
  41.0 16.9 %collective-permute-start.3 = (bf16[16,2560]{1,0:T(8,128)(2,1)S(1)}, bf16[16,2560]{1,0:T(8,128)(2,1)S(1)}, u32[]{:S(2)}, u32[]{:S(2)}) collective-permute-start(bf16[16,2560]{1,0:T(8,128)(2,1)S(1)} %get-tuple-element.34), channel_id=1, source_target_pairs={{0,8},{2,10},{4,12},{6,14},{8,0},{10,2},{12,4},{14,6},{1,9},{3,11}... | collective-permute-start | bytes 245768 | tf_op jit(solution)/shard_map/ppermute | solution.py:163
  43.8 16.4 %collective-permute-start.4 = (bf16[16,2560]{1,0:T(8,128)(2,1)S(1)}, bf16[16,2560]{1,0:T(8,128)(2,1)S(1)}, u32[]{:S(2)}, u32[]{:S(2)}) collective-permute-start(bf16[16,2560]{1,0:T(8,128)(2,1)S(1)} %get-tuple-element.35), channel_id=1, source_target_pairs={{0,10},{2,8},{4,14},{6,12},{8,2},{10,0},{12,6},{14,4},{1,11},{3,9}... | collective-permute-start | bytes 245768 | tf_op jit(solution)/shard_map/ppermute | solution.py:163
  45.2 14.9 %collective-permute-start.5 = (bf16[16,2560]{1,0:T(8,128)(2,1)S(1)}, bf16[16,2560]{1,0:T(8,128)(2,1)S(1)}, u32[]{:S(2)}, u32[]{:S(2)}) collective-permute-start(bf16[16,2560]{1,0:T(8,128)(2,1)S(1)} %get-tuple-element.36), channel_id=1, source_target_pairs={{0,12},{2,14},{4,8},{6,10},{8,4},{10,6},{12,0},{14,2},{1,13},{3,15... | collective-permute-start | bytes 245768 | tf_op jit(solution)/shard_map/ppermute | solution.py:163
  48.5 11.6 %collective-permute-start.6 = (bf16[16,2560]{1,0:T(8,128)(2,1)S(1)}, bf16[16,2560]{1,0:T(8,128)(2,1)S(1)}, u32[]{:S(2)}, u32[]{:S(2)}) collective-permute-start(bf16[16,2560]{1,0:T(8,128)(2,1)S(1)} %get-tuple-element.37), channel_id=1, source_target_pairs={{0,14},{2,12},{4,10},{6,8},{8,6},{10,4},{12,2},{14,0},{1,15},{3,13... | collective-permute-start | bytes 245768 | tf_op jit(solution)/shard_map/ppermute | solution.py:163
  60.2 0.7 copy-start.1
  66.9 7.3 %collective-permute-start.7 = (bf16[16,1536]{1,0:T(8,128)(2,1)S(1)}, bf16[16,1536]{1,0:T(8,128)(2,1)S(1)}, u32[]{:S(2)}, u32[]{:S(2)}) collective-permute-start(bf16[16,1536]{1,0:T(8,128)(2,1)S(1)} %get-tuple-element.42), channel_id=1, source_target_pairs={{0,2},{2,0},{4,6},{6,4},{8,10},{10,8},{12,14},{14,12},{1,3},{3,1},... | collective-permute-start | bytes 147464 | tf_op jit(solution)/shard_map/ppermute | solution.py:163
  67.9 7.8 %collective-permute-start.8 = (bf16[16,1536]{1,0:T(8,128)(2,1)S(1)}, bf16[16,1536]{1,0:T(8,128)(2,1)S(1)}, u32[]{:S(2)}, u32[]{:S(2)}) collective-permute-start(bf16[16,1536]{1,0:T(8,128)(2,1)S(1)} %get-tuple-element.43), channel_id=1, source_target_pairs={{0,4},{2,6},{4,0},{6,2},{8,12},{10,14},{12,8},{14,10},{1,5},{3,7},... | collective-permute-start | bytes 147464 | tf_op jit(solution)/shard_map/ppermute | solution.py:163
  70.4 8.5 %collective-permute-start.9 = (bf16[16,1536]{1,0:T(8,128)(2,1)S(1)}, bf16[16,1536]{1,0:T(8,128)(2,1)S(1)}, u32[]{:S(2)}, u32[]{:S(2)}) collective-permute-start(bf16[16,1536]{1,0:T(8,128)(2,1)S(1)} %get-tuple-element.44), channel_id=1, source_target_pairs={{0,6},{2,4},{4,2},{6,0},{8,14},{10,12},{12,10},{14,8},{1,7},{3,5},... | collective-permute-start | bytes 147464 | tf_op jit(solution)/shard_map/ppermute | solution.py:163
  71.3 7.7 %collective-permute-start.10 = (bf16[16,1536]{1,0:T(8,128)(2,1)S(1)}, bf16[16,1536]{1,0:T(8,128)(2,1)S(1)}, u32[]{:S(2)}, u32[]{:S(2)}) collective-permute-start(bf16[16,1536]{1,0:T(8,128)(2,1)S(1)} %get-tuple-element.45), channel_id=1, source_target_pairs={{0,8},{2,10},{4,12},{6,14},{8,0},{10,2},{12,4},{14,6},{1,9},{3,11}... | collective-permute-start | bytes 147464 | tf_op jit(solution)/shard_map/ppermute | solution.py:163
  73.4 7.0 %collective-permute-start.11 = (bf16[16,1536]{1,0:T(8,128)(2,1)S(1)}, bf16[16,1536]{1,0:T(8,128)(2,1)S(1)}, u32[]{:S(2)}, u32[]{:S(2)}) collective-permute-start(bf16[16,1536]{1,0:T(8,128)(2,1)S(1)} %get-tuple-element.46), channel_id=1, source_target_pairs={{0,10},{2,8},{4,14},{6,12},{8,2},{10,0},{12,6},{14,4},{1,11},{3,9}... | collective-permute-start | bytes 147464 | tf_op jit(solution)/shard_map/ppermute | solution.py:163
  74.3 6.2 %collective-permute-start.12 = (bf16[16,1536]{1,0:T(8,128)(2,1)S(1)}, bf16[16,1536]{1,0:T(8,128)(2,1)S(1)}, u32[]{:S(2)}, u32[]{:S(2)}) collective-permute-start(bf16[16,1536]{1,0:T(8,128)(2,1)S(1)} %get-tuple-element.47), channel_id=1, source_target_pairs={{0,12},{2,14},{4,8},{6,10},{8,4},{10,6},{12,0},{14,2},{1,13},{3,15... | collective-permute-start | bytes 147464 | tf_op jit(solution)/shard_map/ppermute | solution.py:163
  75.7 6.9 %collective-permute-start.13 = (bf16[16,1536]{1,0:T(8,128)(2,1)S(1)}, bf16[16,1536]{1,0:T(8,128)(2,1)S(1)}, u32[]{:S(2)}, u32[]{:S(2)}) collective-permute-start(bf16[16,1536]{1,0:T(8,128)(2,1)S(1)} %get-tuple-element.48), channel_id=1, source_target_pairs={{0,14},{2,12},{4,10},{6,8},{8,6},{10,4},{12,2},{14,0},{1,15},{3,13... | collective-permute-start | bytes 147464 | tf_op jit(solution)/shard_map/ppermute | solution.py:163

commit v5 on v4

--- a/solution.py
+++ b/solution.py
@@ -66,25 +66,26 @@
             low += HEAD_DIM
 
 
-def attend_kernel(lengths_ref, home_ref, seen_ref, *rest, count, prompt_rows, by_rank):
-    blocks, rest = (rest[:1], rest[1:]) if by_rank else (rest[:count], rest[count:])
+def attend_kernel(lengths_ref, home_ref, seen_ref, *rest, count, prompt_rows, head, heads):
+    near = count // 2
+    by_rank = head > 0
+    last = head == heads - 1
+    taken = 1 if by_rank else count
+    blocks, rest = rest[:taken], rest[taken:]
+    kept, rest = (rest[: head * (near + 1)], rest[head * (near + 1) :]) if last else ((), rest)
+    out_ref, returns, scratch = rest[0], rest[1 : count + 1], rest[count + 1 :]
+    rank = lax.axis_index("seq")
     if by_rank:
-        (out_ref, y) = rest
-        x = blocks[0]
-        rows, width = x.shape[1:]
+        x, y = blocks[0], scratch[0]
     else:
-        earlier_ref, out_ref, *returns, x, y = rest
-        rows, width = blocks[0].shape
+        x, y = scratch
+        for distance in range(count):
+            x[rank ^ distance] = blocks[distance][...]
+    rows, width = x.shape[1:]
     total = rows * count
     q_part = (width - 4 * HEAD_DIM) // 2
     scale = 1.0 / HEAD_DIM**0.5
-    rank = lax.axis_index("seq")
-    out_low = 0
-    if not by_rank:
-        for distance in range(count):
-            x[rank ^ distance] = blocks[distance][...]
-        out_low = earlier_ref.shape[2]
-        out_ref[:, :, :out_low] = earlier_ref[...]
+    out_low = head * q_part if last else 0
     own = resident_of(home_ref, rank, count)
     length = lengths_ref[own]
     visible = seen_ref[own]
@@ -126,25 +127,35 @@
     for part, summed in enumerate((key_grad * scale, value_grad)):
         give(q_part + part * HEAD_DIM, summed[total:])
         give(q_part + (part + 2) * HEAD_DIM, summed[:total])
-    if not by_rank:
-        for distance in range(count):
-            returns[distance][...] = y[rank ^ distance]
+    back = y.shape[2]
+    for distance in range(count):
+        low = head * back if last and distance < near else 0
+        returns[distance][:, low : low + back] = y[rank ^ distance]
+    for earlier in range(len(kept) // (near + 1)):
+        parts = kept[earlier * (near + 1) : (earlier + 1) * (near + 1)]
+        out_ref[:, :, earlier * q_part : (earlier + 1) * q_part] = parts[0][...]
+        for distance in range(near):
+            returns[distance][:, earlier * back : (earlier + 1) * back] = parts[1 + distance][...]
 
 
 def unpack_kernel(home_ref, *rest, count, heads):
+    near = count // 2
     blocks = rest[:-5]
     qg_ref, kg_ref, vg_ref, pkg_ref, pvg_ref = rest[-5:]
     rank = lax.axis_index("seq")
     prompt_rows = pkg_ref.shape[0]
     q_part = qg_ref.shape[2] // heads
+    back = q_part + 4 * HEAD_DIM
     for head in range(heads):
         lanes = slice(head * HEAD_DIM, (head + 1) * HEAD_DIM)
         wide = slice(head * q_part, (head + 1) * q_part)
         summed = [jnp.zeros((qg_ref.shape[1], HEAD_DIM), F32)] * 2
-        for place in range(count):
-            index = resident_of(home_ref, rank ^ place if head else place, count)
-            block = blocks[1 + (head - 1) * count + place] if head else blocks[0].at[place]
-            low = 0
+        for distance in range(count):
+            index = resident_of(home_ref, rank ^ distance, count)
+            if distance < near:
+                block, low = blocks[distance], head * back
+            else:
+                block, low = blocks[near + head * (count - near) + distance - near], 0
             for ref, part in ((qg_ref, wide), (kg_ref, lanes), (vg_ref, lanes)):
                 size = part.stop - part.start
                 ref[index, :, part] = block[:, low : low + size]
@@ -156,13 +167,12 @@
         pvg_ref[:, lanes] = summed[1][:prompt_rows].astype(BF16)
 
 
-def exchange(blocks):
-    count = len(blocks)
-    arrived = list(blocks)
-    for distance in range(1, count):
-        arrived[distance] = lax.ppermute(
-            blocks[distance], "seq", [(i, i ^ distance) for i in range(count)]
-        )
+def exchange(blocks, distances, count):
+    arrived = []
+    for block, distance in zip(blocks, distances):
+        if distance:
+            block = lax.ppermute(block, "seq", [(i, i ^ distance) for i in range(count)])
+        arrived.append(block)
     return arrived
 
 
@@ -206,7 +216,7 @@
         for source in (home_rank, response_query, response_key, response_value, response_grad, prompt_key, prompt_value)
     ]
     for head in range(heads):
-        by_rank = head == 0
+        by_rank = head > 0
         results = shapes(by_rank, width)
         blocks = pl.pallas_call(
             functools.partial(pack_kernel, count=count, head=head, heads=heads, by_rank=by_rank),
@@ -218,23 +228,32 @@
             + [pltpu.VMEM((2, prompt_rows, HEAD_DIM), BF16), pltpu.SemaphoreType.DMA((7,))],
             compiler_params=PARAMS,
         )(*sources)
-        arrived.append([exchange_by_rank(blocks[0])] if by_rank else exchange(blocks))
-    output, returned = [], []
+        if by_rank:
+            arrived.append([exchange_by_rank(blocks[0])])
+        else:
+            arrived.append(exchange(blocks, range(count), count))
+    near, far = range(count // 2), range(count // 2, count)
+    kept, far_back = [], []
     for head in range(heads):
-        by_rank = head == 0
-        operands = [lengths, home_rank, prompt_seen, *arrived[head], *output]
-        results = [jax.ShapeDtypeStruct((1, total, (head + 1) * q_part), BF16)] + shapes(by_rank, back)
-        scratch = [] if by_rank else [pltpu.VMEM((count, rows, lanes), BF16) for lanes in (width, back)]
-        output, *blocks = pl.pallas_call(
-            functools.partial(attend_kernel, count=count, prompt_rows=prompt_rows, by_rank=by_rank),
-            out_shape=results,
+        last = head == heads - 1
+        operands = [lengths, home_rank, prompt_seen, *arrived[head], *(kept if last else [])]
+        whole = heads if last else 1
+        results = [(1, total, whole * q_part)] + [(rows, whole * back)] * len(near) + [(rows, back)] * len(far)
+        scratch = [back] if head else [width, back]
+        results = pl.pallas_call(
+            functools.partial(
+                attend_kernel, count=count, prompt_rows=prompt_rows, head=head, heads=heads
+            ),
+            out_shape=[jax.ShapeDtypeStruct(dims, BF16) for dims in results],
             in_specs=[SMEM] * 3 + [VMEM] * (len(operands) - 3),
             out_specs=[VMEM] * len(results),
-            scratch_shapes=scratch,
+            scratch_shapes=[pltpu.VMEM((count, rows, lanes), BF16) for lanes in scratch],
             compiler_params=PARAMS,
         )(*operands)
-        output = [output]
-        returned += [exchange_by_rank(blocks[0])] if by_rank else exchange(blocks)
+        kept += results[: 1 + len(near)]
+        far_back += exchange(results[1 + len(near) :], far, count)
+    output, *near_back = kept[-1 - len(near) :]
+    returned = exchange(near_back, near, count) + far_back
     grads = pl.pallas_call(
         functools.partial(unpack_kernel, count=count, heads=heads),
         name="unpack",
@@ -246,7 +265,7 @@
         out_specs=[VMEM] * 5,
         compiler_params=PARAMS,
     )(home_rank, *returned)
-    return (output[0], *grads)
+    return (output, *grads)
 
 
 def head_logits(queries, all_keys, allowed, head_index, group_size, scale_factor):

time: 84.4 us -> 76.4 us (0.905)
  blocking collectives: 24.9 us -> 0 us
  starting transfers between devices: 28.3 us -> 43.5 us
  waiting for transfers between devices: 13.6 us -> 15.9 us
    all_to_all x1 -> x0, blocking collectives: 24.9 us -> none  [exchange_by_rank(): lax.all_to_all(blocks, 'seq', split_axis=0, concat_axis=0, tiled=True)]
    ppermute x14 -> x18, starting transfers between devices: 24.8 us -> 36.2 us  [exchange(): lax.ppermute(block, 'seq', [(i, i ^ distance) for i in range(count)])]
    all_to_all x1, starting transfers between devices: 3.45 us -> 7.29 us  [exchange_by_rank(): lax.all_to_all(blocks, 'seq', split_axis=0, concat_axis=0, tiled=True)]
    ppermute x14 -> x18, waiting for transfers between devices: 13.6 us -> 15.9 us  [exchange(): lax.ppermute(block, 'seq', [(i, i ^ distance) for i in range(count)])]
  transfers between devices with their start and end apart: 15 -> 19, of which waited for: 4 -> 4; matrix products, arithmetic and copies ran while one was open for 0% -> 0% of each run, Pallas kernels for 9% -> 17%
where the time goes in v5:
time: 76.4 us; the launch traced here: 76.2 us
  starting transfers between devices  43.5 us (57%)
  Pallas kernels  16.1 us (21%)
  waiting for transfers between devices  15.9 us (21%)
    ppermute x18, starting transfers between devices, exchange(): lax.ppermute(block, 'seq', [(i, i ^ distance) for i in range(count)])  36.2 us
    ppermute x18, waiting for transfers between devices, exchange(): lax.ppermute(block, 'seq', [(i, i ^ distance) for i in range(count)])  15.9 us
    pallas_call x2, Pallas kernels, packed_body(): pl.pallas_call(functools.partial(attend_kernel, count=count, prompt_rows=...  11.4 us
    all_to_all x1, starting transfers between devices, exchange_by_rank(): lax.all_to_all(blocks, 'seq', split_axis=0, concat_axis=0, tiled=True)  7.29 us
    pallas_call x2, Pallas kernels, packed_body(): pl.pallas_call(functools.partial(pack_kernel, count=count, head=head, hea...  3.17 us
  transfers between devices with their start and end apart: 19, of which 4 were waited for; matrix products, arithmetic and copies ran while one was open for 0% of the time, Pallas kernels for 17%

profile of v5, /device:TPU:0, one launch (start us, length us, event | category | flops | bytes accessed | tf_op | source)
XLA Modules:
  0.0 76.2 jit_solution(3303716289866729779)
XLA Ops:
  0.6 2.0 %shard_map.136 = bf16[8,16,2560]{2,1,0:T(8,128)(2,1)} custom-call(s32[8]{0:T(128)} %home_ref.9, bf16[8,16,2048]{2,1,0:T(8,128)(2,1)} %q_ref.3, bf16[8,16,256]{2,1,0:T(8,128)(2,1)} %k_ref.3, bf16[8,16,256]{2,1,0:T(8,128)(2,1)} %v_ref.3, bf16[8,16,2048]{2,1,0:T(8,128)(2,1)} %g_ref.3, bf16[12,256]{1,0:T(8,128)(2,1)} %pk_ref.3, bf16[12,256]{1,0:T(8,128)(2,1)} %pv_ref.3), custom_call_target="tpu_custom_call" | custom-call | tf_op jit(solution)/shard_map/pallas_call | solution.py:221
  2.7 7.3 %all-to-all-start = ((bf16[8,16,2560]{2,1,0:T(8,128)(2,1)}), bf16[8,16,2560]{2,1,0:T(8,128)(2,1)S(1)}, u32[]{:S(2)}, u32[]{:S(2)}) async-start(bf16[8,16,2560]{2,1,0:T(8,128)(2,1)} %shard_map.136), calls=%async_computation | async-start | bytes 1310720 | tf_op jit(solution)/shard_map/all_to_all | solution.py:180
  9.9 1.2 %shard_map.137 = (bf16[16,2560]{1,0:T(8,128)(2,1)S(1)}, bf16[16,2560]{1,0:T(8,128)(2,1)S(1)}, bf16[16,2560]{1,0:T(8,128)(2,1)S(1)}, bf16[16,2560]{1,0:T(8,128)(2...) custom-call(s32[8]{0:T(128)} %home_ref.9, ...), custom_call_target="tpu_custom_call" | custom-call | tf_op jit(solution)/shard_map/pallas_call | solution.py:221
  11.1 2.1 %collective-permute-start = (bf16[16,2560]{1,0:T(8,128)(2,1)S(1)}, bf16[16,2560]{1,0:T(8,128)(2,1)S(1)}, u32[]{:S(2)}, u32[]{:S(2)}) collective-permute-start(bf16[16,2560]{1,0:T(8,128)(2,1)S(1)} %get-tuple-element.38), channel_id=1, source_target_pairs={{0,2},{2,0},{4,6},{6,4},{8,10},{10,8},{12,14},{14,12},{1,3},{3,1},... | collective-permute-start | bytes 245768 | tf_op jit(solution)/shard_map/ppermute | solution.py:174
  13.2 1.5 %collective-permute-start.1 = (bf16[16,2560]{1,0:T(8,128)(2,1)S(1)}, bf16[16,2560]{1,0:T(8,128)(2,1)S(1)}, u32[]{:S(2)}, u32[]{:S(2)}) collective-permute-start(bf16[16,2560]{1,0:T(8,128)(2,1)S(1)} %get-tuple-element.39), channel_id=1, source_target_pairs={{0,4},{2,6},{4,0},{6,2},{8,12},{10,14},{12,8},{14,10},{1,5},{3,7},... | collective-permute-start | bytes 245768 | tf_op jit(solution)/shard_map/ppermute | solution.py:174
  14.7 0.1 collective-permute-start.2
  14.7 2.8 %collective-permute-start.3 = (bf16[16,2560]{1,0:T(8,128)(2,1)S(1)}, bf16[16,2560]{1,0:T(8,128)(2,1)S(1)}, u32[]{:S(2)}, u32[]{:S(2)}) collective-permute-start(bf16[16,2560]{1,0:T(8,128)(2,1)S(1)} %get-tuple-element.41), channel_id=1, source_target_pairs={{0,8},{2,10},{4,12},{6,14},{8,0},{10,2},{12,4},{14,6},{1,9},{3,11}... | collective-permute-start | bytes 245768 | tf_op jit(solution)/shard_map/ppermute | solution.py:174
  17.6 1.5 %collective-permute-start.4 = (bf16[16,2560]{1,0:T(8,128)(2,1)S(1)}, bf16[16,2560]{1,0:T(8,128)(2,1)S(1)}, u32[]{:S(2)}, u32[]{:S(2)}) collective-permute-start(bf16[16,2560]{1,0:T(8,128)(2,1)S(1)} %get-tuple-element.42), channel_id=1, source_target_pairs={{0,10},{2,8},{4,14},{6,12},{8,2},{10,0},{12,6},{14,4},{1,11},{3,9}... | collective-permute-start | bytes 245768 | tf_op jit(solution)/shard_map/ppermute | solution.py:174
  19.0 0.0 collective-permute-done.rest_1_
  19.1 4.4 %collective-permute-start.5 = (bf16[16,2560]{1,0:T(8,128)(2,1)S(1)}, bf16[16,2560]{1,0:T(8,128)(2,1)S(1)}, u32[]{:S(2)}, u32[]{:S(2)}) collective-permute-start(bf16[16,2560]{1,0:T(8,128)(2,1)S(1)} %get-tuple-element.43), channel_id=1, source_target_pairs={{0,12},{2,14},{4,8},{6,10},{8,4},{10,6},{12,0},{14,2},{1,13},{3,15... | collective-permute-start | bytes 245768 | tf_op jit(solution)/shard_map/ppermute | solution.py:174
  23.5 0.0 collective-permute-done.1.rest_2_
  23.5 0.0 copy-start
  23.5 0.0 copy-start.1
  23.5 0.0 copy-start.2
  23.5 4.8 %collective-permute-start.6 = (bf16[16,2560]{1,0:T(8,128)(2,1)S(1)}, bf16[16,2560]{1,0:T(8,128)(2,1)S(1)}, u32[]{:S(2)}, u32[]{:S(2)}) collective-permute-start(bf16[16,2560]{1,0:T(8,128)(2,1)S(1)} %get-tuple-element.44), channel_id=1, source_target_pairs={{0,14},{2,12},{4,10},{6,8},{8,6},{10,4},{12,2},{14,0},{1,15},{3,13... | collective-permute-start | bytes 245768 | tf_op jit(solution)/shard_map/ppermute | solution.py:174
  28.3 0.0 collective-permute-done.2.rest_3_
  28.3 9.1 %collective-permute-done.3.rest_4_ = bf16[16,2560]{1,0:T(8,128)(2,1)S(1)} collective-permute-done((bf16[16,2560]{1,0:T(8,128)(2,1)S(1)}, bf16[16,2560]{1,0:T(8,128)(2,1)S(1)}, u32[]{:S(2)}, u32[]{:S(2)}) %collective-permute-start.3) | collective-permute-done | bytes 81952 | tf_op jit(solution)/shard_map/ppermute | solution.py:174
  37.4 2.2 %collective-permute-done.4.rest_5_ = bf16[16,2560]{1,0:T(8,128)(2,1)S(1)} collective-permute-done((bf16[16,2560]{1,0:T(8,128)(2,1)S(1)}, bf16[16,2560]{1,0:T(8,128)(2,1)S(1)}, u32[]{:S(2)}, u32[]{:S(2)}) %collective-permute-start.4) | collective-permute-done | bytes 81952 | tf_op jit(solution)/shard_map/ppermute | solution.py:174
  39.7 0.0 collective-permute-done.5.rest_6_
  39.7 0.0 collective-permute-done.6.rest_7_
  39.7 0.0 copy-done
  39.7 0.0 copy-done.1
  39.7 0.0 copy-done.2
  39.7 5.4 %shard_map.138 = (bf16[1,128,1024]{2,1,0:T(8,128)(2,1)S(1)}, bf16[16,1536]{1,0:T(8,128)(2,1)S(1)}, bf16[16,1536]{1,0:T(8,128)(2,1)S(1)}, bf16[16,1536]{1,0:T(8,1...) custom-call(s32[8]{0:T(128)S(1)} %copy-done.1, ...), custom_call_target="tpu_custom_call" | custom-call | tf_op jit(solution)/shard_map/pallas_call | solution.py:243
  45.1 3.1 %collective-permute-start.10 = (bf16[16,1536]{1,0:T(8,128)(2,1)S(1)}, bf16[16,1536]{1,0:T(8,128)(2,1)S(1)}, u32[]{:S(2)}, u32[]{:S(2)}) collective-permute-start(bf16[16,1536]{1,0:T(8,128)(2,1)S(1)} %get-tuple-element.55), channel_id=1, source_target_pairs={{0,8},{2,10},{4,12},{6,14},{8,0},{10,2},{12,4},{14,6},{1,9},{3,11}... | collective-permute-start | bytes 147464 | tf_op jit(solution)/shard_map/ppermute | solution.py:174
  48.2 0.3 collective-permute-start.11
  48.5 2.2 %collective-permute-start.12 = (bf16[16,1536]{1,0:T(8,128)(2,1)S(1)}, bf16[16,1536]{1,0:T(8,128)(2,1)S(1)}, u32[]{:S(2)}, u32[]{:S(2)}) collective-permute-start(bf16[16,1536]{1,0:T(8,128)(2,1)S(1)} %get-tuple-element.57), channel_id=1, source_target_pairs={{0,12},{2,14},{4,8},{6,10},{8,4},{10,6},{12,0},{14,2},{1,13},{3,15... | collective-permute-start | bytes 147464 | tf_op jit(solution)/shard_map/ppermute | solution.py:174
  50.7 2.4 %collective-permute-start.13 = (bf16[16,1536]{1,0:T(8,128)(2,1)S(1)}, bf16[16,1536]{1,0:T(8,128)(2,1)S(1)}, u32[]{:S(2)}, u32[]{:S(2)}) collective-permute-start(bf16[16,1536]{1,0:T(8,128)(2,1)S(1)} %get-tuple-element.58), channel_id=1, source_target_pairs={{0,14},{2,12},{4,10},{6,8},{8,6},{10,4},{12,2},{14,0},{1,15},{3,13... | collective-permute-start | bytes 147464 | tf_op jit(solution)/shard_map/ppermute | solution.py:174
  53.0 0.0 all-to-all-done.rest_0_
  53.0 6.1 %shard_map.139 = (bf16[1,128,2048]{2,1,0:T(8,128)(2,1)}, bf16[16,3072]{1,0:T(8,128)(2,1)S(1)}, bf16[16,3072]{1,0:T(8,128)(2,1)S(1)}, bf16[16,3072]{1,0:T(8,128)(...) custom-call(s32[8]{0:T(128)S(1)} %copy-done.1, ...), custom_call_target="tpu_custom_call" | custom-call | tf_op jit(solution)/shard_map/pallas_call | solution.py:243
  59.1 1.1 %collective-permute-start.14 = (bf16[16,1536]{1,0:T(8,128)(2,1)S(1)}, bf16[16,1536]{1,0:T(8,128)(2,1)S(1)}, u32[]{:S(2)}, u32[]{:S(2)}) collective-permute-start(bf16[16,1536]{1,0:T(8,128)(2,1)S(1)} %get-tuple-element.59), channel_id=1, source_target_pairs={{0,8},{2,10},{4,12},{6,14},{8,0},{10,2},{12,4},{14,6},{1,9},{3,11}... | collective-permute-start | bytes 147464 | tf_op jit(solution)/shard_map/ppermute | solution.py:174
  60.1 0.0 collective-permute-done.10.rest_4_
  60.1 2.1 %collective-permute-start.15 = (bf16[16,1536]{1,0:T(8,128)(2,1)S(1)}, bf16[16,1536]{1,0:T(8,128)(2,1)S(1)}, u32[]{:S(2)}, u32[]{:S(2)}) collective-permute-start(bf16[16,1536]{1,0:T(8,128)(2,1)S(1)} %get-tuple-element.60), channel_id=1, source_target_pairs={{0,10},{2,8},{4,14},{6,12},{8,2},{10,0},{12,6},{14,4},{1,11},{3,9}... | collective-permute-start | bytes 147464 | tf_op jit(solution)/shard_map/ppermute | solution.py:174
  62.2 0.0 collective-permute-done.11.rest_5_
  62.2 1.3 %collective-permute-start.7 = (bf16[16,3072]{1,0:T(8,128)(2,1)S(1)}, bf16[16,3072]{1,0:T(8,128)(2,1)S(1)}, u32[]{:S(2)}, u32[]{:S(2)}) collective-permute-start(bf16[16,3072]{1,0:T(8,128)(2,1)S(1)} %get-tuple-element.52), channel_id=1, source_target_pairs={{0,2},{2,0},{4,6},{6,4},{8,10},{10,8},{12,14},{14,12},{1,3},{3,1},... | collective-permute-start | bytes 294920 | tf_op jit(solution)/shard_map/ppermute | solution.py:174
  63.5 0.0 collective-permute-done.12.rest_6_
  63.5 1.1 %collective-permute-start.8 = (bf16[16,3072]{1,0:T(8,128)(2,1)S(1)}, bf16[16,3072]{1,0:T(8,128)(2,1)S(1)}, u32[]{:S(2)}, u32[]{:S(2)}) collective-permute-start(bf16[16,3072]{1,0:T(8,128)(2,1)S(1)} %get-tuple-element.53), channel_id=1, source_target_pairs={{0,4},{2,6},{4,0},{6,2},{8,12},{10,14},{12,8},{14,10},{1,5},{3,7},... | collective-permute-start | bytes 294920 | tf_op jit(solution)/shard_map/ppermute | solution.py:174
  64.5 0.0 collective-permute-done.13.rest_7_
  64.5 1.2 %collective-permute-start.9 = (bf16[16,3072]{1,0:T(8,128)(2,1)S(1)}, bf16[16,3072]{1,0:T(8,128)(2,1)S(1)}, u32[]{:S(2)}, u32[]{:S(2)}) collective-permute-start(bf16[16,3072]{1,0:T(8,128)(2,1)S(1)} %get-tuple-element.54), channel_id=1, source_target_pairs={{0,6},{2,4},{4,2},{6,0},{8,14},{10,12},{12,10},{14,8},{1,7},{3,5},... | collective-permute-start | bytes 294920 | tf_op jit(solution)/shard_map/ppermute | solution.py:174
  65.7 0.0 collective-permute-done.14.rest_8_
  65.7 2.2 %collective-permute-start.16 = (bf16[16,1536]{1,0:T(8,128)(2,1)S(1)}, bf16[16,1536]{1,0:T(8,128)(2,1)S(1)}, u32[]{:S(2)}, u32[]{:S(2)}) collective-permute-start(bf16[16,1536]{1,0:T(8,128)(2,1)S(1)} %get-tuple-element.61), channel_id=1, source_target_pairs={{0,12},{2,14},{4,8},{6,10},{8,4},{10,6},{12,0},{14,2},{1,13},{3,15... | collective-permute-start | bytes 147464 | tf_op jit(solution)/shard_map/ppermute | solution.py:174
  67.9 0.0 collective-permute-done.15.rest_9_
  67.9 2.4 %collective-permute-start.17 = (bf16[16,1536]{1,0:T(8,128)(2,1)S(1)}, bf16[16,1536]{1,0:T(8,128)(2,1)S(1)}, u32[]{:S(2)}, u32[]{:S(2)}) collective-permute-start(bf16[16,1536]{1,0:T(8,128)(2,1)S(1)} %get-tuple-element.62), channel_id=1, source_target_pairs={{0,14},{2,12},{4,10},{6,8},{8,6},{10,4},{12,2},{14,0},{1,15},{3,13... | collective-permute-start | bytes 147464 | tf_op jit(solution)/shard_map/ppermute | solution.py:174
  70.2 1.4 %collective-permute-done.16.rest_10_ = bf16[16,1536]{1,0:T(8,128)(2,1)S(1)} collective-permute-done((bf16[16,1536]{1,0:T(8,128)(2,1)S(1)}, bf16[16,1536]{1,0:T(8,128)(2,1)S(1)}, u32[]{:S(2)}, u32[]{:S(2)}) %collective-permute-start.16) | collective-permute-done | bytes 49184 | tf_op jit(solution)/shard_map/ppermute | solution.py:174
  71.6 3.1 %collective-permute-done.17.rest_11_ = bf16[16,1536]{1,0:T(8,128)(2,1)S(1)} collective-permute-done((bf16[16,1536]{1,0:T(8,128)(2,1)S(1)}, bf16[16,1536]{1,0:T(8,128)(2,1)S(1)}, u32[]{:S(2)}, u32[]{:S(2)}) %collective-permute-start.17) | collective-permute-done | bytes 49184 | tf_op jit(solution)/shard_map/ppermute | solution.py:174
  74.7 0.0 collective-permute-done.7.rest_1_
  74.7 0.0 collective-permute-done.8.rest_2_
  74.7 0.0 collective-permute-done.9.rest_3_
  74.7 1.5 %unpack.1 = (bf16[8,16,2048]{2,1,0:T(8,128)(2,1)}, bf16[8,16,256]{2,1,0:T(8,128)(2,1)}, bf16[8,16,256]{2,1,0:T(8,128)(2,1)}, bf16[12,256]{1,0:T(8,128)(2,1)}, bf16[12,256]{1,0:T(8,128)(2,1)}) custom-call(s32[8]{0:T(128)S(1)} %copy-done, bf16[16,3072]{1,0:T(8,128)(2,1)S(1)} %get-tuple-element.51.rest_0_, bf16[16,3072]{1,0:T(8,128)(2,1)S(1)} %collective-permute-done.7.rest_1_, ...), custom_call_target="tpu_custom_call" | custom-call | tf_op jit(solution)/shard_map/unpack/pallas_call | solution.py:257
Async XLA Ops:
  2.7 50.4 %all-to-all-start = ((bf16[8,16,2560]{2,1,0:T(8,128)(2,1)}), bf16[8,16,2560]{2,1,0:T(8,128)(2,1)S(1)}, u32[]{:S(2)}, u32[]{:S(2)}) async-start(bf16[8,16,2560]{2,1,0:T(8,128)(2,1)} %shard_map.136), calls=%async_computation | async-start | bytes 1310720 | tf_op jit(solution)/shard_map/all_to_all | solution.py:180
  11.1 7.9 %collective-permute-start = (bf16[16,2560]{1,0:T(8,128)(2,1)S(1)}, bf16[16,2560]{1,0:T(8,128)(2,1)S(1)}, u32[]{:S(2)}, u32[]{:S(2)}) collective-permute-start(bf16[16,2560]{1,0:T(8,128)(2,1)S(1)} %get-tuple-element.38), channel_id=1, source_target_pairs={{0,2},{2,0},{4,6},{6,4},{8,10},{10,8},{12,14},{14,12},{1,3},{3,1},... | collective-permute-start | bytes 245768 | tf_op jit(solution)/shard_map/ppermute | solution.py:174
  13.2 10.3 %collective-permute-start.1 = (bf16[16,2560]{1,0:T(8,128)(2,1)S(1)}, bf16[16,2560]{1,0:T(8,128)(2,1)S(1)}, u32[]{:S(2)}, u32[]{:S(2)}) collective-permute-start(bf16[16,2560]{1,0:T(8,128)(2,1)S(1)} %get-tuple-element.39), channel_id=1, source_target_pairs={{0,4},{2,6},{4,0},{6,2},{8,12},{10,14},{12,8},{14,10},{1,5},{3,7},... | collective-permute-start | bytes 245768 | tf_op jit(solution)/shard_map/ppermute | solution.py:174
  14.7 13.6 %collective-permute-start.2 = (bf16[16,2560]{1,0:T(8,128)(2,1)S(1)}, bf16[16,2560]{1,0:T(8,128)(2,1)S(1)}, u32[]{:S(2)}, u32[]{:S(2)}) collective-permute-start(bf16[16,2560]{1,0:T(8,128)(2,1)S(1)} %get-tuple-element.40), channel_id=1, source_target_pairs={{0,6},{2,4},{4,2},{6,0},{8,14},{10,12},{12,10},{14,8},{1,7},{3,5},... | collective-permute-start | bytes 245768 | tf_op jit(solution)/shard_map/ppermute | solution.py:174
  14.7 22.7 %collective-permute-start.3 = (bf16[16,2560]{1,0:T(8,128)(2,1)S(1)}, bf16[16,2560]{1,0:T(8,128)(2,1)S(1)}, u32[]{:S(2)}, u32[]{:S(2)}) collective-permute-start(bf16[16,2560]{1,0:T(8,128)(2,1)S(1)} %get-tuple-element.41), channel_id=1, source_target_pairs={{0,8},{2,10},{4,12},{6,14},{8,0},{10,2},{12,4},{14,6},{1,9},{3,11}... | collective-permute-start | bytes 245768 | tf_op jit(solution)/shard_map/ppermute | solution.py:174
  17.6 22.1 %collective-permute-start.4 = (bf16[16,2560]{1,0:T(8,128)(2,1)S(1)}, bf16[16,2560]{1,0:T(8,128)(2,1)S(1)}, u32[]{:S(2)}, u32[]{:S(2)}) collective-permute-start(bf16[16,2560]{1,0:T(8,128)(2,1)S(1)} %get-tuple-element.42), channel_id=1, source_target_pairs={{0,10},{2,8},{4,14},{6,12},{8,2},{10,0},{12,6},{14,4},{1,11},{3,9}... | collective-permute-start | bytes 245768 | tf_op jit(solution)/shard_map/ppermute | solution.py:174
  19.1 20.6 %collective-permute-start.5 = (bf16[16,2560]{1,0:T(8,128)(2,1)S(1)}, bf16[16,2560]{1,0:T(8,128)(2,1)S(1)}, u32[]{:S(2)}, u32[]{:S(2)}) collective-permute-start(bf16[16,2560]{1,0:T(8,128)(2,1)S(1)} %get-tuple-element.43), channel_id=1, source_target_pairs={{0,12},{2,14},{4,8},{6,10},{8,4},{10,6},{12,0},{14,2},{1,13},{3,15... | collective-permute-start | bytes 245768 | tf_op jit(solution)/shard_map/ppermute | solution.py:174
  23.5 16.2 %copy-start = (s32[8]{0:T(128)S(1)}, s32[8]{0:T(128)}, u32[]{:S(2)}) copy-start(s32[8]{0:T(128)} %home_ref.9) | copy-start | bytes 100
  23.5 16.2 %copy-start.1 = (s32[8]{0:T(128)S(1)}, s32[8]{0:T(128)}, u32[]{:S(2)}) copy-start(s32[8]{0:T(128)} %lengths_ref.3) | copy-start | bytes 100
  23.5 16.2 %copy-start.2 = (s32[8]{0:T(128)S(1)}, s32[8]{0:T(128)}, u32[]{:S(2)}) copy-start(s32[8]{0:T(128)} %seen_ref.3) | copy-start | bytes 100
  23.5 16.2 %collective-permute-start.6 = (bf16[16,2560]{1,0:T(8,128)(2,1)S(1)}, bf16[16,2560]{1,0:T(8,128)(2,1)S(1)}, u32[]{:S(2)}, u32[]{:S(2)}) collective-permute-start(bf16[16,2560]{1,0:T(8,128)(2,1)S(1)} %get-tuple-element.44), channel_id=1, source_target_pairs={{0,14},{2,12},{4,10},{6,8},{8,6},{10,4},{12,2},{14,0},{1,15},{3,13... | collective-permute-start | bytes 245768 | tf_op jit(solution)/shard_map/ppermute | solution.py:174
  45.1 15.0 %collective-permute-start.10 = (bf16[16,1536]{1,0:T(8,128)(2,1)S(1)}, bf16[16,1536]{1,0:T(8,128)(2,1)S(1)}, u32[]{:S(2)}, u32[]{:S(2)}) collective-permute-start(bf16[16,1536]{1,0:T(8,128)(2,1)S(1)} %get-tuple-element.55), channel_id=1, source_target_pairs={{0,8},{2,10},{4,12},{6,14},{8,0},{10,2},{12,4},{14,6},{1,9},{3,11}... | collective-permute-start | bytes 147464 | tf_op jit(solution)/shard_map/ppermute | solution.py:174
  48.2 14.0 %collective-permute-start.11 = (bf16[16,1536]{1,0:T(8,128)(2,1)S(1)}, bf16[16,1536]{1,0:T(8,128)(2,1)S(1)}, u32[]{:S(2)}, u32[]{:S(2)}) collective-permute-start(bf16[16,1536]{1,0:T(8,128)(2,1)S(1)} %get-tuple-element.56), channel_id=1, source_target_pairs={{0,10},{2,8},{4,14},{6,12},{8,2},{10,0},{12,6},{14,4},{1,11},{3,9}... | collective-permute-start | bytes 147464 | tf_op jit(solution)/shard_map/ppermute | solution.py:174
  48.5 15.0 %collective-permute-start.12 = (bf16[16,1536]{1,0:T(8,128)(2,1)S(1)}, bf16[16,1536]{1,0:T(8,128)(2,1)S(1)}, u32[]{:S(2)}, u32[]{:S(2)}) collective-permute-start(bf16[16,1536]{1,0:T(8,128)(2,1)S(1)} %get-tuple-element.57), channel_id=1, source_target_pairs={{0,12},{2,14},{4,8},{6,10},{8,4},{10,6},{12,0},{14,2},{1,13},{3,15... | collective-permute-start | bytes 147464 | tf_op jit(solution)/shard_map/ppermute | solution.py:174
  50.7 13.9 %collective-permute-start.13 = (bf16[16,1536]{1,0:T(8,128)(2,1)S(1)}, bf16[16,1536]{1,0:T(8,128)(2,1)S(1)}, u32[]{:S(2)}, u32[]{:S(2)}) collective-permute-start(bf16[16,1536]{1,0:T(8,128)(2,1)S(1)} %get-tuple-element.58), channel_id=1, source_target_pairs={{0,14},{2,12},{4,10},{6,8},{8,6},{10,4},{12,2},{14,0},{1,15},{3,13... | collective-permute-start | bytes 147464 | tf_op jit(solution)/shard_map/ppermute | solution.py:174
  59.1 6.6 %collective-permute-start.14 = (bf16[16,1536]{1,0:T(8,128)(2,1)S(1)}, bf16[16,1536]{1,0:T(8,128)(2,1)S(1)}, u32[]{:S(2)}, u32[]{:S(2)}) collective-permute-start(bf16[16,1536]{1,0:T(8,128)(2,1)S(1)} %get-tuple-element.59), channel_id=1, source_target_pairs={{0,8},{2,10},{4,12},{6,14},{8,0},{10,2},{12,4},{14,6},{1,9},{3,11}... | collective-permute-start | bytes 147464 | tf_op jit(solution)/shard_map/ppermute | solution.py:174
  60.1 7.7 %collective-permute-start.15 = (bf16[16,1536]{1,0:T(8,128)(2,1)S(1)}, bf16[16,1536]{1,0:T(8,128)(2,1)S(1)}, u32[]{:S(2)}, u32[]{:S(2)}) collective-permute-start(bf16[16,1536]{1,0:T(8,128)(2,1)S(1)} %get-tuple-element.60), channel_id=1, source_target_pairs={{0,10},{2,8},{4,14},{6,12},{8,2},{10,0},{12,6},{14,4},{1,11},{3,9}... | collective-permute-start | bytes 147464 | tf_op jit(solution)/shard_map/ppermute | solution.py:174
  62.2 12.5 %collective-permute-start.7 = (bf16[16,3072]{1,0:T(8,128)(2,1)S(1)}, bf16[16,3072]{1,0:T(8,128)(2,1)S(1)}, u32[]{:S(2)}, u32[]{:S(2)}) collective-permute-start(bf16[16,3072]{1,0:T(8,128)(2,1)S(1)} %get-tuple-element.52), channel_id=1, source_target_pairs={{0,2},{2,0},{4,6},{6,4},{8,10},{10,8},{12,14},{14,12},{1,3},{3,1},... | collective-permute-start | bytes 294920 | tf_op jit(solution)/shard_map/ppermute | solution.py:174
  63.5 11.2 %collective-permute-start.8 = (bf16[16,3072]{1,0:T(8,128)(2,1)S(1)}, bf16[16,3072]{1,0:T(8,128)(2,1)S(1)}, u32[]{:S(2)}, u32[]{:S(2)}) collective-permute-start(bf16[16,3072]{1,0:T(8,128)(2,1)S(1)} %get-tuple-element.53), channel_id=1, source_target_pairs={{0,4},{2,6},{4,0},{6,2},{8,12},{10,14},{12,8},{14,10},{1,5},{3,7},... | collective-permute-start | bytes 294920 | tf_op jit(solution)/shard_map/ppermute | solution.py:174
  64.5 10.1 %collective-permute-start.9 = (bf16[16,3072]{1,0:T(8,128)(2,1)S(1)}, bf16[16,3072]{1,0:T(8,128)(2,1)S(1)}, u32[]{:S(2)}, u32[]{:S(2)}) collective-permute-start(bf16[16,3072]{1,0:T(8,128)(2,1)S(1)} %get-tuple-element.54), channel_id=1, source_target_pairs={{0,6},{2,4},{4,2},{6,0},{8,14},{10,12},{12,10},{14,8},{1,7},{3,5},... | collective-permute-start | bytes 294920 | tf_op jit(solution)/shard_map/ppermute | solution.py:174
  65.7 5.9 %collective-permute-start.16 = (bf16[16,1536]{1,0:T(8,128)(2,1)S(1)}, bf16[16,1536]{1,0:T(8,128)(2,1)S(1)}, u32[]{:S(2)}, u32[]{:S(2)}) collective-permute-start(bf16[16,1536]{1,0:T(8,128)(2,1)S(1)} %get-tuple-element.61), channel_id=1, source_target_pairs={{0,12},{2,14},{4,8},{6,10},{8,4},{10,6},{12,0},{14,2},{1,13},{3,15... | collective-permute-start | bytes 147464 | tf_op jit(solution)/shard_map/ppermute | solution.py:174
  67.9 6.8 %collective-permute-start.17 = (bf16[16,1536]{1,0:T(8,128)(2,1)S(1)}, bf16[16,1536]{1,0:T(8,128)(2,1)S(1)}, u32[]{:S(2)}, u32[]{:S(2)}) collective-permute-start(bf16[16,1536]{1,0:T(8,128)(2,1)S(1)} %get-tuple-element.62), channel_id=1, source_target_pairs={{0,14},{2,12},{4,10},{6,8},{8,6},{10,4},{12,2},{14,0},{1,15},{3,13... | collective-permute-start | bytes 147464 | tf_op jit(solution)/shard_map/ppermute | solution.py:174

commit v6 on v5

--- a/solution.py
+++ b/solution.py
@@ -67,12 +67,11 @@
 
 
 def attend_kernel(lengths_ref, home_ref, seen_ref, *rest, count, prompt_rows, head, heads):
-    near = count // 2
     by_rank = head > 0
     last = head == heads - 1
     taken = 1 if by_rank else count
     blocks, rest = rest[:taken], rest[taken:]
-    kept, rest = (rest[: head * (near + 1)], rest[head * (near + 1) :]) if last else ((), rest)
+    kept, rest = (rest[:head], rest[head:]) if last else ((), rest)
     out_ref, returns, scratch = rest[0], rest[1 : count + 1], rest[count + 1 :]
     rank = lax.axis_index("seq")
     if by_rank:
@@ -109,53 +108,51 @@
     values = jnp.concatenate([lanes(low + 3 * HEAD_DIM), lanes(low + HEAD_DIM)], axis=0)
     key_grad = jnp.zeros((2 * total, HEAD_DIM), F32)
     value_grad = jnp.zeros((2 * total, HEAD_DIM), F32)
-    for low in range(0, q_part, HEAD_DIM):
-        query = lanes(low)
-        grad = jnp.where(live, lanes(q_part + low), jnp.zeros((), BF16))
+    together = q_part // HEAD_DIM
+    allowed = jnp.concatenate([allowed] * together, axis=0)
+    live = jnp.concatenate([live] * together, axis=0)
+    for first in range(0, q_part, together * HEAD_DIM):
+        lows = range(first, min(q_part, first + together * HEAD_DIM), HEAD_DIM)
+        query = jnp.concatenate([lanes(low) for low in lows], axis=0)
+        grad = jnp.concatenate([lanes(q_part + low) for low in lows], axis=0)
+        grad = jnp.where(live, grad, jnp.zeros((), BF16))
         logits = jnp.where(allowed, dot(query, keys, ((1,), (1,))) * scale, NEG_FILL)
         spread = dot(grad, values, ((1,), (1,)))
         raised = jnp.exp(logits - jnp.max(logits, axis=1, keepdims=True))
         prob = raised * (1.0 / jnp.sum(raised, axis=1, keepdims=True))
         weights = prob.astype(BF16)
         output = jnp.where(live, dot(weights, values, ((1,), (0,))), 0.0).astype(BF16)
-        out_ref[0, :, out_low + low : out_low + low + HEAD_DIM] = output
         row_dot = jnp.sum(grad.astype(F32) * output.astype(F32), axis=1, keepdims=True)
         dlogit = (prob * (spread - row_dot)).astype(BF16)
-        give(low, dot(dlogit, keys, ((1,), (0,))) * scale)
+        query_grad = dot(dlogit, keys, ((1,), (0,))) * scale
+        for member, low in enumerate(lows):
+            at = slice(member * total, (member + 1) * total)
+            out_ref[0, :, out_low + low : out_low + low + HEAD_DIM] = output[at]
+            give(low, query_grad[at])
         key_grad += dot(dlogit, query, ((0,), (0,)))
         value_grad += dot(weights, grad, ((0,), (0,)))
     for part, summed in enumerate((key_grad * scale, value_grad)):
         give(q_part + part * HEAD_DIM, summed[total:])
         give(q_part + (part + 2) * HEAD_DIM, summed[:total])
-    back = y.shape[2]
     for distance in range(count):
-        low = head * back if last and distance < near else 0
-        returns[distance][:, low : low + back] = y[rank ^ distance]
-    for earlier in range(len(kept) // (near + 1)):
-        parts = kept[earlier * (near + 1) : (earlier + 1) * (near + 1)]
-        out_ref[:, :, earlier * q_part : (earlier + 1) * q_part] = parts[0][...]
-        for distance in range(near):
-            returns[distance][:, earlier * back : (earlier + 1) * back] = parts[1 + distance][...]
+        returns[distance][...] = y[rank ^ distance]
+    for earlier, part in enumerate(kept):
+        out_ref[:, :, earlier * q_part : (earlier + 1) * q_part] = part[...]
 
 
 def unpack_kernel(home_ref, *rest, count, heads):
-    near = count // 2
     blocks = rest[:-5]
     qg_ref, kg_ref, vg_ref, pkg_ref, pvg_ref = rest[-5:]
     rank = lax.axis_index("seq")
     prompt_rows = pkg_ref.shape[0]
     q_part = qg_ref.shape[2] // heads
-    back = q_part + 4 * HEAD_DIM
     for head in range(heads):
         lanes = slice(head * HEAD_DIM, (head + 1) * HEAD_DIM)
         wide = slice(head * q_part, (head + 1) * q_part)
         summed = [jnp.zeros((qg_ref.shape[1], HEAD_DIM), F32)] * 2
         for distance in range(count):
             index = resident_of(home_ref, rank ^ distance, count)
-            if distance < near:
-                block, low = blocks[distance], head * back
-            else:
-                block, low = blocks[near + head * (count - near) + distance - near], 0
+            block, low = blocks[head * count + distance], 0
             for ref, part in ((qg_ref, wide), (kg_ref, lanes), (vg_ref, lanes)):
                 size = part.stop - part.start
                 ref[index, :, part] = block[:, low : low + size]
@@ -232,13 +229,12 @@
             arrived.append([exchange_by_rank(blocks[0])])
         else:
             arrived.append(exchange(blocks, range(count), count))
-    near, far = range(count // 2), range(count // 2, count)
-    kept, far_back = [], []
+    kept, returned = [], []
     for head in range(heads):
         last = head == heads - 1
         operands = [lengths, home_rank, prompt_seen, *arrived[head], *(kept if last else [])]
         whole = heads if last else 1
-        results = [(1, total, whole * q_part)] + [(rows, whole * back)] * len(near) + [(rows, back)] * len(far)
+        results = [(1, total, whole * q_part)] + [(rows, back)] * count
         scratch = [back] if head else [width, back]
         results = pl.pallas_call(
             functools.partial(
@@ -250,10 +246,9 @@
             scratch_shapes=[pltpu.VMEM((count, rows, lanes), BF16) for lanes in scratch],
             compiler_params=PARAMS,
         )(*operands)
-        kept += results[: 1 + len(near)]
-        far_back += exchange(results[1 + len(near) :], far, count)
-    output, *near_back = kept[-1 - len(near) :]
-    returned = exchange(near_back, near, count) + far_back
+        kept.append(results[0])
+        returned += exchange(results[1:], range(count), count)
+    output = kept[-1]
     grads = pl.pallas_call(
         functools.partial(unpack_kernel, count=count, heads=heads),
         name="unpack",

time: 76.4 us -> 72.9 us (0.954)
  Pallas kernels: 16.1 us -> 9.21 us
  starting transfers between devices: 43.5 us -> 47.8 us
  waiting for transfers between devices: 15.9 us -> 15 us
    pallas_call x2, Pallas kernels: 11.4 us -> 4.6 us  [packed_body(): pl.pallas_call(functools.partial(attend_kernel, count=count, prompt_rows=...]
    ppermute x18 -> x21, starting transfers between devices: 36.2 us -> 40.5 us  [exchange(): lax.ppermute(block, 'seq', [(i, i ^ distance) for i in range(count)])]
    ppermute x18 -> x21, waiting for transfers between devices: 15.9 us -> 15 us  [exchange(): lax.ppermute(block, 'seq', [(i, i ^ distance) for i in range(count)])]
  transfers between devices with their start and end apart: 19 -> 22, of which waited for: 4 -> 5; matrix products, arithmetic and copies ran while one was open for 0% -> 0% of each run, Pallas kernels for 17% -> 8%
where the time goes in v6:
time: 72.9 us; the launch traced here: 72.7 us
  starting transfers between devices  47.8 us (66%)
  waiting for transfers between devices  15 us (21%)
  Pallas kernels  9.21 us (13%)
    ppermute x21, starting transfers between devices, exchange(): lax.ppermute(block, 'seq', [(i, i ^ distance) for i in range(count)])  40.5 us
    ppermute x21, waiting for transfers between devices, exchange(): lax.ppermute(block, 'seq', [(i, i ^ distance) for i in range(count)])  15 us
    all_to_all x1, starting transfers between devices, exchange_by_rank(): lax.all_to_all(blocks, 'seq', split_axis=0, concat_axis=0, tiled=True)  7.29 us
    pallas_call x2, Pallas kernels, packed_body(): pl.pallas_call(functools.partial(attend_kernel, count=count, prompt_rows=...  4.6 us
    pallas_call x2, Pallas kernels, packed_body(): pl.pallas_call(functools.partial(pack_kernel, count=count, head=head, hea...  3.15 us
  transfers between devices with their start and end apart: 22, of which 5 were waited for; matrix products, arithmetic and copies ran while one was open for 0% of the time, Pallas kernels for 8%

profile of v6, /device:TPU:0, one launch (start us, length us, event | category | flops | bytes accessed | tf_op | source)
XLA Modules:
  0.0 72.7 jit_solution(15818875153122201208)
XLA Ops:
  0.6 2.0 %shard_map.136 = bf16[8,16,2560]{2,1,0:T(8,128)(2,1)} custom-call(s32[8]{0:T(128)} %home_ref.9, bf16[8,16,2048]{2,1,0:T(8,128)(2,1)} %q_ref.3, bf16[8,16,256]{2,1,0:T(8,128)(2,1)} %k_ref.3, bf16[8,16,256]{2,1,0:T(8,128)(2,1)} %v_ref.3, bf16[8,16,2048]{2,1,0:T(8,128)(2,1)} %g_ref.3, bf16[12,256]{1,0:T(8,128)(2,1)} %pk_ref.3, bf16[12,256]{1,0:T(8,128)(2,1)} %pv_ref.3), custom_call_target="tpu_custom_call" | custom-call | tf_op jit(solution)/shard_map/pallas_call | solution.py:218
  2.6 7.3 %all-to-all-start = ((bf16[8,16,2560]{2,1,0:T(8,128)(2,1)}), bf16[8,16,2560]{2,1,0:T(8,128)(2,1)S(1)}, u32[]{:S(2)}, u32[]{:S(2)}) async-start(bf16[8,16,2560]{2,1,0:T(8,128)(2,1)} %shard_map.136), calls=%async_computation | async-start | bytes 1310720 | tf_op jit(solution)/shard_map/all_to_all | solution.py:177
  9.9 1.2 %shard_map.137 = (bf16[16,2560]{1,0:T(8,128)(2,1)S(1)}, bf16[16,2560]{1,0:T(8,128)(2,1)S(1)}, bf16[16,2560]{1,0:T(8,128)(2,1)S(1)}, bf16[16,2560]{1,0:T(8,128)(2...) custom-call(s32[8]{0:T(128)} %home_ref.9, ...), custom_call_target="tpu_custom_call" | custom-call | tf_op jit(solution)/shard_map/pallas_call | solution.py:218
  11.1 2.1 %collective-permute-start = (bf16[16,2560]{1,0:T(8,128)(2,1)S(1)}, bf16[16,2560]{1,0:T(8,128)(2,1)S(1)}, u32[]{:S(2)}, u32[]{:S(2)}) collective-permute-start(bf16[16,2560]{1,0:T(8,128)(2,1)S(1)} %get-tuple-element.38), channel_id=1, source_target_pairs={{0,2},{2,0},{4,6},{6,4},{8,10},{10,8},{12,14},{14,12},{1,3},{3,1},... | collective-permute-start | bytes 245768 | tf_op jit(solution)/shard_map/ppermute | solution.py:171
  13.2 1.5 %collective-permute-start.1 = (bf16[16,2560]{1,0:T(8,128)(2,1)S(1)}, bf16[16,2560]{1,0:T(8,128)(2,1)S(1)}, u32[]{:S(2)}, u32[]{:S(2)}) collective-permute-start(bf16[16,2560]{1,0:T(8,128)(2,1)S(1)} %get-tuple-element.39), channel_id=1, source_target_pairs={{0,4},{2,6},{4,0},{6,2},{8,12},{10,14},{12,8},{14,10},{1,5},{3,7},... | collective-permute-start | bytes 245768 | tf_op jit(solution)/shard_map/ppermute | solution.py:171
  14.6 0.1 collective-permute-start.2
  14.7 2.8 %collective-permute-start.3 = (bf16[16,2560]{1,0:T(8,128)(2,1)S(1)}, bf16[16,2560]{1,0:T(8,128)(2,1)S(1)}, u32[]{:S(2)}, u32[]{:S(2)}) collective-permute-start(bf16[16,2560]{1,0:T(8,128)(2,1)S(1)} %get-tuple-element.41), channel_id=1, source_target_pairs={{0,8},{2,10},{4,12},{6,14},{8,0},{10,2},{12,4},{14,6},{1,9},{3,11}... | collective-permute-start | bytes 245768 | tf_op jit(solution)/shard_map/ppermute | solution.py:171
  17.6 1.5 %collective-permute-start.4 = (bf16[16,2560]{1,0:T(8,128)(2,1)S(1)}, bf16[16,2560]{1,0:T(8,128)(2,1)S(1)}, u32[]{:S(2)}, u32[]{:S(2)}) collective-permute-start(bf16[16,2560]{1,0:T(8,128)(2,1)S(1)} %get-tuple-element.42), channel_id=1, source_target_pairs={{0,10},{2,8},{4,14},{6,12},{8,2},{10,0},{12,6},{14,4},{1,11},{3,9}... | collective-permute-start | bytes 245768 | tf_op jit(solution)/shard_map/ppermute | solution.py:171
  19.0 0.0 collective-permute-done.rest_1_
  19.0 4.4 %collective-permute-start.5 = (bf16[16,2560]{1,0:T(8,128)(2,1)S(1)}, bf16[16,2560]{1,0:T(8,128)(2,1)S(1)}, u32[]{:S(2)}, u32[]{:S(2)}) collective-permute-start(bf16[16,2560]{1,0:T(8,128)(2,1)S(1)} %get-tuple-element.43), channel_id=1, source_target_pairs={{0,12},{2,14},{4,8},{6,10},{8,4},{10,6},{12,0},{14,2},{1,13},{3,15... | collective-permute-start | bytes 245768 | tf_op jit(solution)/shard_map/ppermute | solution.py:171
  23.5 0.0 collective-permute-done.1.rest_2_
  23.5 0.0 copy-start
  23.5 0.0 copy-start.1
  23.5 0.0 copy-start.2
  23.5 4.8 %collective-permute-start.6 = (bf16[16,2560]{1,0:T(8,128)(2,1)S(1)}, bf16[16,2560]{1,0:T(8,128)(2,1)S(1)}, u32[]{:S(2)}, u32[]{:S(2)}) collective-permute-start(bf16[16,2560]{1,0:T(8,128)(2,1)S(1)} %get-tuple-element.44), channel_id=1, source_target_pairs={{0,14},{2,12},{4,10},{6,8},{8,6},{10,4},{12,2},{14,0},{1,15},{3,13... | collective-permute-start | bytes 245768 | tf_op jit(solution)/shard_map/ppermute | solution.py:171
  28.3 0.0 collective-permute-done.2.rest_3_
  28.3 9.1 %collective-permute-done.3.rest_4_ = bf16[16,2560]{1,0:T(8,128)(2,1)S(1)} collective-permute-done((bf16[16,2560]{1,0:T(8,128)(2,1)S(1)}, bf16[16,2560]{1,0:T(8,128)(2,1)S(1)}, u32[]{:S(2)}, u32[]{:S(2)}) %collective-permute-start.3) | collective-permute-done | bytes 81952 | tf_op jit(solution)/shard_map/ppermute | solution.py:171
  37.4 2.2 %collective-permute-done.4.rest_5_ = bf16[16,2560]{1,0:T(8,128)(2,1)S(1)} collective-permute-done((bf16[16,2560]{1,0:T(8,128)(2,1)S(1)}, bf16[16,2560]{1,0:T(8,128)(2,1)S(1)}, u32[]{:S(2)}, u32[]{:S(2)}) %collective-permute-start.4) | collective-permute-done | bytes 81952 | tf_op jit(solution)/shard_map/ppermute | solution.py:171
  39.7 0.0 collective-permute-done.5.rest_6_
  39.7 0.0 collective-permute-done.6.rest_7_
  39.7 0.0 copy-done
  39.7 0.0 copy-done.1
  39.7 0.0 copy-done.2
  39.7 2.0 %shard_map.138 = (bf16[1,128,1024]{2,1,0:T(8,128)(2,1)S(1)}, bf16[16,1536]{1,0:T(8,128)(2,1)S(1)}, bf16[16,1536]{1,0:T(8,128)(2,1)S(1)}, bf16[16,1536]{1,0:T(8,1...) custom-call(s32[8]{0:T(128)S(1)} %copy-done.1, ...), custom_call_target="tpu_custom_call" | custom-call | tf_op jit(solution)/shard_map/pallas_call | solution.py:239
  41.7 1.0 %collective-permute-start.7 = (bf16[16,1536]{1,0:T(8,128)(2,1)S(1)}, bf16[16,1536]{1,0:T(8,128)(2,1)S(1)}, u32[]{:S(2)}, u32[]{:S(2)}) collective-permute-start(bf16[16,1536]{1,0:T(8,128)(2,1)S(1)} %get-tuple-element.48), channel_id=1, source_target_pairs={{0,2},{2,0},{4,6},{6,4},{8,10},{10,8},{12,14},{14,12},{1,3},{3,1},... | collective-permute-start | bytes 147464 | tf_op jit(solution)/shard_map/ppermute | solution.py:171
  42.7 2.6 %collective-permute-start.8 = (bf16[16,1536]{1,0:T(8,128)(2,1)S(1)}, bf16[16,1536]{1,0:T(8,128)(2,1)S(1)}, u32[]{:S(2)}, u32[]{:S(2)}) collective-permute-start(bf16[16,1536]{1,0:T(8,128)(2,1)S(1)} %get-tuple-element.49), channel_id=1, source_target_pairs={{0,4},{2,6},{4,0},{6,2},{8,12},{10,14},{12,8},{14,10},{1,5},{3,7},... | collective-permute-start | bytes 147464 | tf_op jit(solution)/shard_map/ppermute | solution.py:171
  45.4 0.9 %collective-permute-start.9 = (bf16[16,1536]{1,0:T(8,128)(2,1)S(1)}, bf16[16,1536]{1,0:T(8,128)(2,1)S(1)}, u32[]{:S(2)}, u32[]{:S(2)}) collective-permute-start(bf16[16,1536]{1,0:T(8,128)(2,1)S(1)} %get-tuple-element.50), channel_id=1, source_target_pairs={{0,6},{2,4},{4,2},{6,0},{8,14},{10,12},{12,10},{14,8},{1,7},{3,5},... | collective-permute-start | bytes 147464 | tf_op jit(solution)/shard_map/ppermute | solution.py:171
  46.3 2.0 %collective-permute-start.10 = (bf16[16,1536]{1,0:T(8,128)(2,1)S(1)}, bf16[16,1536]{1,0:T(8,128)(2,1)S(1)}, u32[]{:S(2)}, u32[]{:S(2)}) collective-permute-start(bf16[16,1536]{1,0:T(8,128)(2,1)S(1)} %get-tuple-element.51), channel_id=1, source_target_pairs={{0,8},{2,10},{4,12},{6,14},{8,0},{10,2},{12,4},{14,6},{1,9},{3,11}... | collective-permute-start | bytes 147464 | tf_op jit(solution)/shard_map/ppermute | solution.py:171
  48.3 0.9 %collective-permute-start.11 = (bf16[16,1536]{1,0:T(8,128)(2,1)S(1)}, bf16[16,1536]{1,0:T(8,128)(2,1)S(1)}, u32[]{:S(2)}, u32[]{:S(2)}) collective-permute-start(bf16[16,1536]{1,0:T(8,128)(2,1)S(1)} %get-tuple-element.52), channel_id=1, source_target_pairs={{0,10},{2,8},{4,14},{6,12},{8,2},{10,0},{12,6},{14,4},{1,11},{3,9}... | collective-permute-start | bytes 147464 | tf_op jit(solution)/shard_map/ppermute | solution.py:171
  49.2 0.0 all-to-all-done.rest_0_
  49.2 2.6 %shard_map.139 = (bf16[1,128,2048]{2,1,0:T(8,128)(2,1)}, bf16[16,1536]{1,0:T(8,128)(2,1)S(1)}, bf16[16,1536]{1,0:T(8,128)(2,1)S(1)}, bf16[16,1536]{1,0:T(8,128)(...) custom-call(s32[8]{0:T(128)S(1)} %copy-done.1, ...), custom_call_target="tpu_custom_call" | custom-call | tf_op jit(solution)/shard_map/pallas_call | solution.py:239
  51.8 0.0 collective-permute-done.7.rest_1_
  51.8 1.5 %collective-permute-start.12 = (bf16[16,1536]{1,0:T(8,128)(2,1)S(1)}, bf16[16,1536]{1,0:T(8,128)(2,1)S(1)}, u32[]{:S(2)}, u32[]{:S(2)}) collective-permute-start(bf16[16,1536]{1,0:T(8,128)(2,1)S(1)} %get-tuple-element.53), channel_id=1, source_target_pairs={{0,12},{2,14},{4,8},{6,10},{8,4},{10,6},{12,0},{14,2},{1,13},{3,15... | collective-permute-start | bytes 147464 | tf_op jit(solution)/shard_map/ppermute | solution.py:171
  53.3 0.0 collective-permute-done.8.rest_2_
  53.3 3.3 %collective-permute-start.13 = (bf16[16,1536]{1,0:T(8,128)(2,1)S(1)}, bf16[16,1536]{1,0:T(8,128)(2,1)S(1)}, u32[]{:S(2)}, u32[]{:S(2)}) collective-permute-start(bf16[16,1536]{1,0:T(8,128)(2,1)S(1)} %get-tuple-element.54), channel_id=1, source_target_pairs={{0,14},{2,12},{4,10},{6,8},{8,6},{10,4},{12,2},{14,0},{1,15},{3,13... | collective-permute-start | bytes 147464 | tf_op jit(solution)/shard_map/ppermute | solution.py:171
  56.6 0.0 collective-permute-done.9.rest_3_
  56.6 0.6 collective-permute-start.14
  57.1 0.0 collective-permute-done.10.rest_4_
  57.1 0.2 collective-permute-start.15
  57.3 0.0 collective-permute-done.11.rest_5_
  57.4 2.7 %collective-permute-start.16 = (bf16[16,1536]{1,0:T(8,128)(2,1)S(1)}, bf16[16,1536]{1,0:T(8,128)(2,1)S(1)}, u32[]{:S(2)}, u32[]{:S(2)}) collective-permute-start(bf16[16,1536]{1,0:T(8,128)(2,1)S(1)} %get-tuple-element.58), channel_id=1, source_target_pairs={{0,6},{2,4},{4,2},{6,0},{8,14},{10,12},{12,10},{14,8},{1,7},{3,5},... | collective-permute-start | bytes 147464 | tf_op jit(solution)/shard_map/ppermute | solution.py:171
  60.1 0.0 collective-permute-done.12.rest_6_
  60.1 0.2 collective-permute-start.17
  60.3 0.0 collective-permute-done.13.rest_7_
  60.3 2.7 %collective-permute-start.18 = (bf16[16,1536]{1,0:T(8,128)(2,1)S(1)}, bf16[16,1536]{1,0:T(8,128)(2,1)S(1)}, u32[]{:S(2)}, u32[]{:S(2)}) collective-permute-start(bf16[16,1536]{1,0:T(8,128)(2,1)S(1)} %get-tuple-element.60), channel_id=1, source_target_pairs={{0,10},{2,8},{4,14},{6,12},{8,2},{10,0},{12,6},{14,4},{1,11},{3,9}... | collective-permute-start | bytes 147464 | tf_op jit(solution)/shard_map/ppermute | solution.py:171
  63.0 0.0 collective-permute-done.14.rest_9_
  63.0 1.5 %collective-permute-start.19 = (bf16[16,1536]{1,0:T(8,128)(2,1)S(1)}, bf16[16,1536]{1,0:T(8,128)(2,1)S(1)}, u32[]{:S(2)}, u32[]{:S(2)}) collective-permute-start(bf16[16,1536]{1,0:T(8,128)(2,1)S(1)} %get-tuple-element.61), channel_id=1, source_target_pairs={{0,12},{2,14},{4,8},{6,10},{8,4},{10,6},{12,0},{14,2},{1,13},{3,15... | collective-permute-start | bytes 147464 | tf_op jit(solution)/shard_map/ppermute | solution.py:171
  64.5 0.0 collective-permute-done.15.rest_10_
  64.5 3.3 %collective-permute-start.20 = (bf16[16,1536]{1,0:T(8,128)(2,1)S(1)}, bf16[16,1536]{1,0:T(8,128)(2,1)S(1)}, u32[]{:S(2)}, u32[]{:S(2)}) collective-permute-start(bf16[16,1536]{1,0:T(8,128)(2,1)S(1)} %get-tuple-element.62), channel_id=1, source_target_pairs={{0,14},{2,12},{4,10},{6,8},{8,6},{10,4},{12,2},{14,0},{1,15},{3,13... | collective-permute-start | bytes 147464 | tf_op jit(solution)/shard_map/ppermute | solution.py:171
  67.7 0.0 collective-permute-done.16.rest_11_
  67.7 0.0 collective-permute-done.17.rest_12_
  67.7 0.1 collective-permute-done.18.rest_13_
  67.9 1.1 %collective-permute-done.19.rest_14_ = bf16[16,1536]{1,0:T(8,128)(2,1)S(1)} collective-permute-done((bf16[16,1536]{1,0:T(8,128)(2,1)S(1)}, bf16[16,1536]{1,0:T(8,128)(2,1)S(1)}, u32[]{:S(2)}, u32[]{:S(2)}) %collective-permute-start.19) | collective-permute-done | bytes 49184 | tf_op jit(solution)/shard_map/ppermute | solution.py:171
  69.0 2.3 %collective-permute-done.20.rest_15_ = bf16[16,1536]{1,0:T(8,128)(2,1)S(1)} collective-permute-done((bf16[16,1536]{1,0:T(8,128)(2,1)S(1)}, bf16[16,1536]{1,0:T(8,128)(2,1)S(1)}, u32[]{:S(2)}, u32[]{:S(2)}) %collective-permute-start.20) | collective-permute-done | bytes 49184 | tf_op jit(solution)/shard_map/ppermute | solution.py:171
  71.2 1.5 %unpack.1 = (bf16[8,16,2048]{2,1,0:T(8,128)(2,1)}, bf16[8,16,256]{2,1,0:T(8,128)(2,1)}, bf16[8,16,256]{2,1,0:T(8,128)(2,1)}, bf16[12,256]{1,0:T(8,128)(2,1)}, bf16[12,256]{1,0:T(8,128)(2,1)}) custom-call(s32[8]{0:T(128)S(1)} %copy-done, bf16[16,1536]{1,0:T(8,128)(2,1)S(1)} %get-tuple-element.47.rest_0_, bf16[16,1536]{1,0:T(8,128)(2,1)S(1)} %collective-permute-done.7.rest_1_, ...), custom_call_target="tpu_custom_call" | custom-call | tf_op jit(solution)/shard_map/unpack/pallas_call | solution.py:252
Async XLA Ops:
  2.6 46.5 %all-to-all-start = ((bf16[8,16,2560]{2,1,0:T(8,128)(2,1)}), bf16[8,16,2560]{2,1,0:T(8,128)(2,1)S(1)}, u32[]{:S(2)}, u32[]{:S(2)}) async-start(bf16[8,16,2560]{2,1,0:T(8,128)(2,1)} %shard_map.136), calls=%async_computation | async-start | bytes 1310720 | tf_op jit(solution)/shard_map/all_to_all | solution.py:177
  11.1 7.9 %collective-permute-start = (bf16[16,2560]{1,0:T(8,128)(2,1)S(1)}, bf16[16,2560]{1,0:T(8,128)(2,1)S(1)}, u32[]{:S(2)}, u32[]{:S(2)}) collective-permute-start(bf16[16,2560]{1,0:T(8,128)(2,1)S(1)} %get-tuple-element.38), channel_id=1, source_target_pairs={{0,2},{2,0},{4,6},{6,4},{8,10},{10,8},{12,14},{14,12},{1,3},{3,1},... | collective-permute-start | bytes 245768 | tf_op jit(solution)/shard_map/ppermute | solution.py:171
  13.2 10.3 %collective-permute-start.1 = (bf16[16,2560]{1,0:T(8,128)(2,1)S(1)}, bf16[16,2560]{1,0:T(8,128)(2,1)S(1)}, u32[]{:S(2)}, u32[]{:S(2)}) collective-permute-start(bf16[16,2560]{1,0:T(8,128)(2,1)S(1)} %get-tuple-element.39), channel_id=1, source_target_pairs={{0,4},{2,6},{4,0},{6,2},{8,12},{10,14},{12,8},{14,10},{1,5},{3,7},... | collective-permute-start | bytes 245768 | tf_op jit(solution)/shard_map/ppermute | solution.py:171
  14.6 13.6 %collective-permute-start.2 = (bf16[16,2560]{1,0:T(8,128)(2,1)S(1)}, bf16[16,2560]{1,0:T(8,128)(2,1)S(1)}, u32[]{:S(2)}, u32[]{:S(2)}) collective-permute-start(bf16[16,2560]{1,0:T(8,128)(2,1)S(1)} %get-tuple-element.40), channel_id=1, source_target_pairs={{0,6},{2,4},{4,2},{6,0},{8,14},{10,12},{12,10},{14,8},{1,7},{3,5},... | collective-permute-start | bytes 245768 | tf_op jit(solution)/shard_map/ppermute | solution.py:171
  14.7 22.7 %collective-permute-start.3 = (bf16[16,2560]{1,0:T(8,128)(2,1)S(1)}, bf16[16,2560]{1,0:T(8,128)(2,1)S(1)}, u32[]{:S(2)}, u32[]{:S(2)}) collective-permute-start(bf16[16,2560]{1,0:T(8,128)(2,1)S(1)} %get-tuple-element.41), channel_id=1, source_target_pairs={{0,8},{2,10},{4,12},{6,14},{8,0},{10,2},{12,4},{14,6},{1,9},{3,11}... | collective-permute-start | bytes 245768 | tf_op jit(solution)/shard_map/ppermute | solution.py:171
  17.6 22.1 %collective-permute-start.4 = (bf16[16,2560]{1,0:T(8,128)(2,1)S(1)}, bf16[16,2560]{1,0:T(8,128)(2,1)S(1)}, u32[]{:S(2)}, u32[]{:S(2)}) collective-permute-start(bf16[16,2560]{1,0:T(8,128)(2,1)S(1)} %get-tuple-element.42), channel_id=1, source_target_pairs={{0,10},{2,8},{4,14},{6,12},{8,2},{10,0},{12,6},{14,4},{1,11},{3,9}... | collective-permute-start | bytes 245768 | tf_op jit(solution)/shard_map/ppermute | solution.py:171
  19.0 20.6 %collective-permute-start.5 = (bf16[16,2560]{1,0:T(8,128)(2,1)S(1)}, bf16[16,2560]{1,0:T(8,128)(2,1)S(1)}, u32[]{:S(2)}, u32[]{:S(2)}) collective-permute-start(bf16[16,2560]{1,0:T(8,128)(2,1)S(1)} %get-tuple-element.43), channel_id=1, source_target_pairs={{0,12},{2,14},{4,8},{6,10},{8,4},{10,6},{12,0},{14,2},{1,13},{3,15... | collective-permute-start | bytes 245768 | tf_op jit(solution)/shard_map/ppermute | solution.py:171
  23.5 16.2 %copy-start = (s32[8]{0:T(128)S(1)}, s32[8]{0:T(128)}, u32[]{:S(2)}) copy-start(s32[8]{0:T(128)} %home_ref.9) | copy-start | bytes 100
  23.5 16.2 %copy-start.1 = (s32[8]{0:T(128)S(1)}, s32[8]{0:T(128)}, u32[]{:S(2)}) copy-start(s32[8]{0:T(128)} %lengths_ref.3) | copy-start | bytes 100
  23.5 16.2 %copy-start.2 = (s32[8]{0:T(128)S(1)}, s32[8]{0:T(128)}, u32[]{:S(2)}) copy-start(s32[8]{0:T(128)} %seen_ref.3) | copy-start | bytes 100
  23.5 16.2 %collective-permute-start.6 = (bf16[16,2560]{1,0:T(8,128)(2,1)S(1)}, bf16[16,2560]{1,0:T(8,128)(2,1)S(1)}, u32[]{:S(2)}, u32[]{:S(2)}) collective-permute-start(bf16[16,2560]{1,0:T(8,128)(2,1)S(1)} %get-tuple-element.44), channel_id=1, source_target_pairs={{0,14},{2,12},{4,10},{6,8},{8,6},{10,4},{12,2},{14,0},{1,15},{3,13... | collective-permute-start | bytes 245768 | tf_op jit(solution)/shard_map/ppermute | solution.py:171
  41.7 10.2 %collective-permute-start.7 = (bf16[16,1536]{1,0:T(8,128)(2,1)S(1)}, bf16[16,1536]{1,0:T(8,128)(2,1)S(1)}, u32[]{:S(2)}, u32[]{:S(2)}) collective-permute-start(bf16[16,1536]{1,0:T(8,128)(2,1)S(1)} %get-tuple-element.48), channel_id=1, source_target_pairs={{0,2},{2,0},{4,6},{6,4},{8,10},{10,8},{12,14},{14,12},{1,3},{3,1},... | collective-permute-start | bytes 147464 | tf_op jit(solution)/shard_map/ppermute | solution.py:171
  42.7 10.6 %collective-permute-start.8 = (bf16[16,1536]{1,0:T(8,128)(2,1)S(1)}, bf16[16,1536]{1,0:T(8,128)(2,1)S(1)}, u32[]{:S(2)}, u32[]{:S(2)}) collective-permute-start(bf16[16,1536]{1,0:T(8,128)(2,1)S(1)} %get-tuple-element.49), channel_id=1, source_target_pairs={{0,4},{2,6},{4,0},{6,2},{8,12},{10,14},{12,8},{14,10},{1,5},{3,7},... | collective-permute-start | bytes 147464 | tf_op jit(solution)/shard_map/ppermute | solution.py:171
  45.4 11.2 %collective-permute-start.9 = (bf16[16,1536]{1,0:T(8,128)(2,1)S(1)}, bf16[16,1536]{1,0:T(8,128)(2,1)S(1)}, u32[]{:S(2)}, u32[]{:S(2)}) collective-permute-start(bf16[16,1536]{1,0:T(8,128)(2,1)S(1)} %get-tuple-element.50), channel_id=1, source_target_pairs={{0,6},{2,4},{4,2},{6,0},{8,14},{10,12},{12,10},{14,8},{1,7},{3,5},... | collective-permute-start | bytes 147464 | tf_op jit(solution)/shard_map/ppermute | solution.py:171
  46.3 10.9 %collective-permute-start.10 = (bf16[16,1536]{1,0:T(8,128)(2,1)S(1)}, bf16[16,1536]{1,0:T(8,128)(2,1)S(1)}, u32[]{:S(2)}, u32[]{:S(2)}) collective-permute-start(bf16[16,1536]{1,0:T(8,128)(2,1)S(1)} %get-tuple-element.51), channel_id=1, source_target_pairs={{0,8},{2,10},{4,12},{6,14},{8,0},{10,2},{12,4},{14,6},{1,9},{3,11}... | collective-permute-start | bytes 147464 | tf_op jit(solution)/shard_map/ppermute | solution.py:171
  48.3 9.1 %collective-permute-start.11 = (bf16[16,1536]{1,0:T(8,128)(2,1)S(1)}, bf16[16,1536]{1,0:T(8,128)(2,1)S(1)}, u32[]{:S(2)}, u32[]{:S(2)}) collective-permute-start(bf16[16,1536]{1,0:T(8,128)(2,1)S(1)} %get-tuple-element.52), channel_id=1, source_target_pairs={{0,10},{2,8},{4,14},{6,12},{8,2},{10,0},{12,6},{14,4},{1,11},{3,9}... | collective-permute-start | bytes 147464 | tf_op jit(solution)/shard_map/ppermute | solution.py:171
  51.8 8.2 %collective-permute-start.12 = (bf16[16,1536]{1,0:T(8,128)(2,1)S(1)}, bf16[16,1536]{1,0:T(8,128)(2,1)S(1)}, u32[]{:S(2)}, u32[]{:S(2)}) collective-permute-start(bf16[16,1536]{1,0:T(8,128)(2,1)S(1)} %get-tuple-element.53), channel_id=1, source_target_pairs={{0,12},{2,14},{4,8},{6,10},{8,4},{10,6},{12,0},{14,2},{1,13},{3,15... | collective-permute-start | bytes 147464 | tf_op jit(solution)/shard_map/ppermute | solution.py:171
  53.3 7.0 %collective-permute-start.13 = (bf16[16,1536]{1,0:T(8,128)(2,1)S(1)}, bf16[16,1536]{1,0:T(8,128)(2,1)S(1)}, u32[]{:S(2)}, u32[]{:S(2)}) collective-permute-start(bf16[16,1536]{1,0:T(8,128)(2,1)S(1)} %get-tuple-element.54), channel_id=1, source_target_pairs={{0,14},{2,12},{4,10},{6,8},{8,6},{10,4},{12,2},{14,0},{1,15},{3,13... | collective-permute-start | bytes 147464 | tf_op jit(solution)/shard_map/ppermute | solution.py:171
  56.6 6.4 %collective-permute-start.14 = (bf16[16,1536]{1,0:T(8,128)(2,1)S(1)}, bf16[16,1536]{1,0:T(8,128)(2,1)S(1)}, u32[]{:S(2)}, u32[]{:S(2)}) collective-permute-start(bf16[16,1536]{1,0:T(8,128)(2,1)S(1)} %get-tuple-element.56), channel_id=1, source_target_pairs={{0,2},{2,0},{4,6},{6,4},{8,10},{10,8},{12,14},{14,12},{1,3},{3,1},... | collective-permute-start | bytes 147464 | tf_op jit(solution)/shard_map/ppermute | solution.py:171
  57.1 7.3 %collective-permute-start.15 = (bf16[16,1536]{1,0:T(8,128)(2,1)S(1)}, bf16[16,1536]{1,0:T(8,128)(2,1)S(1)}, u32[]{:S(2)}, u32[]{:S(2)}) collective-permute-start(bf16[16,1536]{1,0:T(8,128)(2,1)S(1)} %get-tuple-element.57), channel_id=1, source_target_pairs={{0,4},{2,6},{4,0},{6,2},{8,12},{10,14},{12,8},{14,10},{1,5},{3,7},... | collective-permute-start | bytes 147464 | tf_op jit(solution)/shard_map/ppermute | solution.py:171
  57.4 10.4 %collective-permute-start.16 = (bf16[16,1536]{1,0:T(8,128)(2,1)S(1)}, bf16[16,1536]{1,0:T(8,128)(2,1)S(1)}, u32[]{:S(2)}, u32[]{:S(2)}) collective-permute-start(bf16[16,1536]{1,0:T(8,128)(2,1)S(1)} %get-tuple-element.58), channel_id=1, source_target_pairs={{0,6},{2,4},{4,2},{6,0},{8,14},{10,12},{12,10},{14,8},{1,7},{3,5},... | collective-permute-start | bytes 147464 | tf_op jit(solution)/shard_map/ppermute | solution.py:171
  60.1 7.7 %collective-permute-start.17 = (bf16[16,1536]{1,0:T(8,128)(2,1)S(1)}, bf16[16,1536]{1,0:T(8,128)(2,1)S(1)}, u32[]{:S(2)}, u32[]{:S(2)}) collective-permute-start(bf16[16,1536]{1,0:T(8,128)(2,1)S(1)} %get-tuple-element.59), channel_id=1, source_target_pairs={{0,8},{2,10},{4,12},{6,14},{8,0},{10,2},{12,4},{14,6},{1,9},{3,11}... | collective-permute-start | bytes 147464 | tf_op jit(solution)/shard_map/ppermute | solution.py:171
  60.3 7.6 %collective-permute-start.18 = (bf16[16,1536]{1,0:T(8,128)(2,1)S(1)}, bf16[16,1536]{1,0:T(8,128)(2,1)S(1)}, u32[]{:S(2)}, u32[]{:S(2)}) collective-permute-start(bf16[16,1536]{1,0:T(8,128)(2,1)S(1)} %get-tuple-element.60), channel_id=1, source_target_pairs={{0,10},{2,8},{4,14},{6,12},{8,2},{10,0},{12,6},{14,4},{1,11},{3,9}... | collective-permute-start | bytes 147464 | tf_op jit(solution)/shard_map/ppermute | solution.py:171
  63.0 6.0 %collective-permute-start.19 = (bf16[16,1536]{1,0:T(8,128)(2,1)S(1)}, bf16[16,1536]{1,0:T(8,128)(2,1)S(1)}, u32[]{:S(2)}, u32[]{:S(2)}) collective-permute-start(bf16[16,1536]{1,0:T(8,128)(2,1)S(1)} %get-tuple-element.61), channel_id=1, source_target_pairs={{0,12},{2,14},{4,8},{6,10},{8,4},{10,6},{12,0},{14,2},{1,13},{3,15... | collective-permute-start | bytes 147464 | tf_op jit(solution)/shard_map/ppermute | solution.py:171
  64.5 6.8 %collective-permute-start.20 = (bf16[16,1536]{1,0:T(8,128)(2,1)S(1)}, bf16[16,1536]{1,0:T(8,128)(2,1)S(1)}, u32[]{:S(2)}, u32[]{:S(2)}) collective-permute-start(bf16[16,1536]{1,0:T(8,128)(2,1)S(1)} %get-tuple-element.62), channel_id=1, source_target_pairs={{0,14},{2,12},{4,10},{6,8},{8,6},{10,4},{12,2},{14,0},{1,15},{3,13... | collective-permute-start | bytes 147464 | tf_op jit(solution)/shard_map/ppermute | solution.py:171

commit v7 on v0

--- a/solution.py
+++ b/solution.py
@@ -1,12 +1,288 @@
+import functools
+
 import jax
 import jax.numpy as jnp
 from jax import lax
+from jax.experimental import pallas as pl
+from jax.experimental.pallas import tpu as pltpu
 from jax.sharding import PartitionSpec as P
 
 HEAD_DIM = 128
 
 
 NEG_FILL = -1e30
+BF16 = jnp.bfloat16
+F32 = jnp.float32
+
+
+def resident_of(home_ref, rank, count):
+    found = jnp.int32(0)
+    for index in range(count):
+        found = jnp.where(home_ref[index] == rank, jnp.int32(index), found)
+    return found
+
+
+def dot(left, right, contract):
+    return lax.dot_general(left, right, ((contract[0], contract[1]), ((), ())), preferred_element_type=F32)
+
+
+def padded_rows(ref, part, rows):
+    spare = jnp.zeros((rows - ref.shape[1], ref.shape[2]), BF16)
+    return jnp.concatenate([ref[part], spare], axis=0)
+
+
+def pack_kernel(home_ref, q_ref, k_ref, v_ref, g_ref, pk_ref, pv_ref, *rest, count):
+    blocks, (home, q, g, k, v, prompt, sems) = rest[:-7], rest[-7:]
+    rank = lax.axis_index("seq")
+    half = count // 2
+    rows = q.shape[1]
+    copies = [
+        pltpu.make_async_copy(source, target, sems.at[index])
+        for index, (source, target) in enumerate(
+            (
+                (home_ref, home),
+                (q_ref, q),
+                (g_ref, g),
+                (k_ref, k),
+                (v_ref, v),
+                (pk_ref, prompt.at[0]),
+                (pv_ref, prompt.at[1]),
+            )
+        )
+    ]
+    for copy in copies:
+        copy.start()
+    for copy in copies:
+        copy.wait()
+    padded = [padded_rows(prompt, part, rows) for part in range(2)]
+    for distance in range(half):
+        place = (rank ^ distance) & (half - 1)
+        for part in range(2):
+            index = resident_of(home, place + part * half, count)
+            at = slice(part * rows, (part + 1) * rows)
+            for block, refs in ((blocks[distance], (q, g, k, v)), (blocks[distance + half], (k, v))):
+                low = 0
+                for ref in refs:
+                    block[at, low : low + ref.shape[2]] = ref[index]
+                    low += ref.shape[2]
+                block[at, low:] = padded[part]
+
+
+def attend_kernel(lengths_ref, home_ref, seen_ref, *rest, count, prompt_rows, q_width, kv_width):
+    half = count // 2
+    blocks, rest = rest[:count], rest[count:]
+    kept_ref, returns, (xq, xk, xp, o, yq, yk, yp) = rest[0], rest[1 : count + 1], rest[count + 1 :]
+    rank = lax.axis_index("seq")
+    place = rank & (half - 1)
+    upper = rank // half
+    rows = xk.shape[2]
+    total = rows * count
+    own_rows = rows * half
+    heads = kv_width // HEAD_DIM
+    members = q_width // kv_width
+    scale = 1.0 / HEAD_DIM**0.5
+    for distance in range(count):
+        source = rank ^ distance
+        for part in range(2):
+            at = slice(part * rows, (part + 1) * rows)
+            low = 0
+            if distance < half:
+                low = 2 * q_width
+                xq[part, source & (half - 1)] = blocks[distance][at, :low]
+            xk[part, source] = blocks[distance][at, low : low + 2 * kv_width]
+            xp[part, source] = blocks[distance][at, low + 2 * kv_width :]
+    column = lax.broadcasted_iota(jnp.int32, (own_rows, total), 1)
+    position = lax.broadcasted_iota(jnp.int32, (own_rows, total), 0) + upper * own_rows
+    shard_row = column % rows
+    prompt_index = jnp.where(shard_row < prompt_rows, column // rows * prompt_rows + shard_row, 1 << 30)
+    causal = column <= position
+    allowed, live = [], []
+    for part in range(2):
+        index = resident_of(home_ref, place + part * half, count)
+        mask = jnp.concatenate([prompt_index < seen_ref[index], causal], axis=1)
+        allowed.append(jnp.concatenate([mask] * members, axis=0))
+        rows_live = position[:, :HEAD_DIM] < lengths_ref[index]
+        live.append(jnp.concatenate([rows_live] * members, axis=0))
+    for kv in range(heads):
+        lanes = slice(kv * HEAD_DIM, (kv + 1) * HEAD_DIM)
+        wide = slice(kv_width + kv * HEAD_DIM, kv_width + (kv + 1) * HEAD_DIM)
+        prompt_grads = [jnp.zeros((total, HEAD_DIM), F32)] * 2
+        for part in range(2):
+
+            def stacked(offset):
+                lows = [offset + (kv * members + member) * HEAD_DIM for member in range(members)]
+                return jnp.concatenate(
+                    [xq[part, :, :, low : low + HEAD_DIM].reshape(own_rows, HEAD_DIM) for low in lows], axis=0
+                )
+
+            keys = jnp.concatenate(
+                [xp[0, :, :, lanes].reshape(total, HEAD_DIM), xk[part, :, :, lanes].reshape(total, HEAD_DIM)], axis=0
+            )
+            values = jnp.concatenate(
+                [xp[1, :, :, lanes].reshape(total, HEAD_DIM), xk[part, :, :, wide].reshape(total, HEAD_DIM)], axis=0
+            )
+            query = stacked(0)
+            grad = jnp.where(live[part], stacked(q_width), jnp.zeros((), BF16))
+            logits = jnp.where(allowed[part], dot(query, keys, ((1,), (1,))) * scale, NEG_FILL)
+            spread = dot(grad, values, ((1,), (1,)))
+            raised = jnp.exp(logits - jnp.max(logits, axis=1, keepdims=True))
+            prob = raised * (1.0 / jnp.sum(raised, axis=1, keepdims=True))
+            weights = prob.astype(BF16)
+            output = jnp.where(live[part], dot(weights, values, ((1,), (0,))), 0.0).astype(BF16)
+            row_dot = jnp.sum(grad.astype(F32) * output.astype(F32), axis=1, keepdims=True)
+            dlogit = (prob * (spread - row_dot)).astype(BF16)
+            query_grad = (dot(dlogit, keys, ((1,), (0,))) * scale).astype(BF16)
+            for member in range(members):
+                low = (kv * members + member) * HEAD_DIM
+                at = slice(member * own_rows, (member + 1) * own_rows)
+                o[part, :, low : low + HEAD_DIM] = output[at]
+                yq[part, :, :, low : low + HEAD_DIM] = query_grad[at].reshape(half, rows, HEAD_DIM)
+            summed = (dot(dlogit, query, ((0,), (0,))) * scale, dot(weights, grad, ((0,), (0,))))
+            for index, to in enumerate((lanes, wide)):
+                yk[part, :, :, to] = summed[index][total:].astype(BF16).reshape(count, rows, HEAD_DIM)
+                prompt_grads[index] = prompt_grads[index] + summed[index][:total]
+        for index in range(2):
+            yp[index, :, :, lanes] = prompt_grads[index].astype(BF16).reshape(count, rows, HEAD_DIM)
+    kept_ref[...] = o[upper]
+    returns[half][:, :q_width] = o[1 - upper]
+    for distance in range(count):
+        target = rank ^ distance
+        for part in range(2):
+            at = slice(part * rows, (part + 1) * rows)
+            if distance < half:
+                returns[distance][at, :q_width] = yq[part, target & (half - 1)]
+            terms = jnp.concatenate([yk[part, target], yp[part, target]], axis=1)
+            if distance == half:
+                fold = terms.shape[1] // 2
+                returns[distance][at, q_width:] = terms[:, :fold]
+                at = slice((2 + part) * rows, (3 + part) * rows)
+                returns[distance][at, q_width:] = terms[:, fold:]
+            else:
+                returns[distance][at, q_width if distance < half else 0 :] = terms
+
+
+def unpack_kernel(home_ref, kept_ref, *rest, count, q_width):
+    half = count // 2
+    blocks, (out_ref, qg_ref, kg_ref, vg_ref, pkg_ref, pvg_ref) = rest[:count], rest[count:]
+    rank = lax.axis_index("seq")
+    upper = rank // half
+    own_rows = kept_ref.shape[0]
+    rows = qg_ref.shape[1]
+    prompt_rows, kv_width = pkg_ref.shape
+    out_ref[0, pl.ds(pl.multiple_of(upper * own_rows, own_rows), own_rows), :] = kept_ref[...]
+    other = pl.multiple_of((1 - upper) * own_rows, own_rows)
+    out_ref[0, pl.ds(other, own_rows), :] = blocks[half][:own_rows, :q_width]
+    prompt_grads = [jnp.zeros((rows, kv_width), F32)] * 2
+    for distance in range(half):
+        place = (rank ^ distance) & (half - 1)
+        for part in range(2):
+            index = resident_of(home_ref, place + part * half, count)
+            at = slice(part * rows, (part + 1) * rows)
+            qg_ref[index] = blocks[distance][at, :q_width]
+            far = blocks[distance + half]
+            if distance:
+                far = far[at, :]
+            else:
+                far = jnp.concatenate(
+                    [far[at, q_width:], far[(2 + part) * rows : (3 + part) * rows, q_width:]], axis=1
+                )
+            terms = blocks[distance][at, q_width:].astype(F32) + far.astype(F32)
+            kg_ref[index] = terms[:, :kv_width].astype(BF16)
+            vg_ref[index] = terms[:, kv_width : 2 * kv_width].astype(BF16)
+            prompt_grads[part] = prompt_grads[part] + terms[:, 2 * kv_width :]
+    pkg_ref[...] = prompt_grads[0][:prompt_rows].astype(BF16)
+    pvg_ref[...] = prompt_grads[1][:prompt_rows].astype(BF16)
+
+
+def exchange(blocks):
+    count = len(blocks)
+    arrived = list(blocks)
+    for distance in range(1, count):
+        arrived[distance] = lax.ppermute(
+            blocks[distance], "seq", [(i, i ^ distance) for i in range(count)]
+        )
+    return arrived
+
+
+SMEM = pl.BlockSpec(memory_space=pltpu.SMEM)
+VMEM = pl.BlockSpec(memory_space=pltpu.VMEM)
+HBM = pl.BlockSpec(memory_space=pltpu.HBM)
+PARAMS = pltpu.CompilerParams(vmem_limit_bytes=32 * 1024 * 1024)
+
+
+def packed_body(
+    response_query,
+    response_key,
+    response_value,
+    response_grad,
+    prompt_key,
+    prompt_value,
+    lengths,
+    home_rank,
+    prompt_seen,
+):
+    count = home_rank.shape[0]
+    half = count // 2
+    rows, q_width = response_query.shape[1:]
+    prompt_rows, kv_width = prompt_key.shape
+    own_rows = rows * half
+    terms = 3 * kv_width
+
+    def shape(*dims):
+        return jax.ShapeDtypeStruct(dims, BF16)
+
+    def scratch(*dims):
+        return pltpu.VMEM(dims, BF16)
+
+    sources = [
+        pltpu.with_memory_space_constraint(source, pltpu.HBM)
+        for source in (home_rank, response_query, response_key, response_value, response_grad, prompt_key, prompt_value)
+    ]
+    blocks = pl.pallas_call(
+        functools.partial(pack_kernel, count=count),
+        name="pack",
+        out_shape=[shape(2 * rows, 2 * q_width + terms)] * half + [shape(2 * rows, terms)] * half,
+        in_specs=[HBM] * 7,
+        out_specs=[VMEM] * count,
+        scratch_shapes=[pltpu.SMEM((count,), jnp.int32)]
+        + [scratch(count, rows, lanes) for lanes in (q_width, q_width, kv_width, kv_width)]
+        + [scratch(2, prompt_rows, kv_width), pltpu.SemaphoreType.DMA((7,))],
+        compiler_params=PARAMS,
+    )(*sources)
+    arrived = exchange(blocks)
+    far_shapes = [shape(own_rows, q_width + 2 * rows * terms // own_rows)] + [shape(2 * rows, terms)] * (half - 1)
+    kept, *returns = pl.pallas_call(
+        functools.partial(
+            attend_kernel, count=count, prompt_rows=prompt_rows, q_width=q_width, kv_width=kv_width
+        ),
+        name="attend",
+        out_shape=[shape(own_rows, q_width)] + [shape(2 * rows, q_width + terms)] * half + far_shapes,
+        in_specs=[SMEM] * 3 + [VMEM] * count,
+        out_specs=[VMEM] * (count + 1),
+        scratch_shapes=[
+            scratch(2, half, rows, 2 * q_width),
+            scratch(2, count, rows, 2 * kv_width),
+            scratch(2, count, rows, kv_width),
+            scratch(2, own_rows, q_width),
+            scratch(2, half, rows, q_width),
+            scratch(2, count, rows, 2 * kv_width),
+            scratch(2, count, rows, kv_width),
+        ],
+        compiler_params=PARAMS,
+    )(lengths, home_rank, prompt_seen, *arrived)
+    returned = exchange(returns)
+    return tuple(
+        pl.pallas_call(
+            functools.partial(unpack_kernel, count=count, q_width=q_width),
+            name="unpack",
+            out_shape=[shape(1, rows * count, q_width), shape(count, rows, q_width)]
+            + [shape(count, rows, kv_width)] * 2
+            + [shape(prompt_rows, kv_width)] * 2,
+            in_specs=[SMEM] + [VMEM] * (count + 1),
+            out_specs=[VMEM] * 6,
+            compiler_params=PARAMS,
+        )(home_rank, kept, *returned)
+    )
 
 
 def head_logits(queries, all_keys, allowed, head_index, group_size, scale_factor):
@@ -29,7 +305,7 @@
     outputs = []
     totals = []
     for head_index in range(kv_count):
-        query_head, key_head, logits = head_logits(
+        _, _, logits = head_logits(
             queries, all_keys, allowed, head_index, group_size, scale_factor
         )
         value_head = all_values[:, head_index * HEAD_DIM : (head_index + 1) * HEAD_DIM]
@@ -190,6 +466,15 @@
     )
 
 
+def choose_body(response_query, *others):
+    count, rows = response_query.shape[:2]
+    prompt_rows = others[3].shape[0]
+    fits = rows % 16 == 0 and prompt_rows <= rows and rows * count == HEAD_DIM
+    if fits and count in (4, 8):
+        return packed_body(response_query, *others)
+    return body(response_query, *others)
+
+
 def solution(mesh):
     placed = (
         P("group", "seq", "head"),
@@ -203,7 +488,7 @@
         P("group"),
     )
     return jax.shard_map(
-        body,
+        choose_body,
         mesh=mesh,
         in_specs=placed,
         out_specs=(

time: 198 us -> 64.6 us (0.33)
  the two profiles are of different devices: /device:TPU:8 before, /device:TPU:0 now
where the time goes in v7:
time: 64.6 us; the launch traced here: 64.4 us
  waiting for transfers between devices  33.5 us (52%)
  starting transfers between devices  23 us (36%)
  Pallas kernels  7.16 us (11%)
  between operations  0.71 us (1%)
    ppermute x14, waiting for transfers between devices, exchange(): lax.ppermute(blocks[distance], 'seq', [(i, i ^ distance) for i in range(c...  33.5 us
    ppermute x14, starting transfers between devices, exchange(): lax.ppermute(blocks[distance], 'seq', [(i, i ^ distance) for i in range(c...  23 us
    pallas_call x1, Pallas kernels, packed_body(): pl.pallas_call(functools.partial(attend_kernel, count=count, prompt_rows=...  4.14 us
    pallas_call x1, Pallas kernels, packed_body(): pl.pallas_call(functools.partial(unpack_kernel, count=count, q_width=q_wi...  1.65 us
    pallas_call x1, Pallas kernels, packed_body(): pl.pallas_call(functools.partial(pack_kernel, count=count), name='pack',...  1.37 us
  transfers between devices with their start and end apart: 14, of which 6 were waited for; matrix products, arithmetic and copies ran while one was open for 0% of the time, Pallas kernels for 0%

profile of v7, /device:TPU:0, one launch (start us, length us, event | category | flops | bytes accessed | tf_op | source)
XLA Modules:
  0.0 64.4 jit_solution(4493691909725619026)
XLA Ops:
  0.6 1.4 %pack.1 = (bf16[32,4864]{1,0:T(8,128)(2,1)S(1)}, bf16[32,4864]{1,0:T(8,128)(2,1)S(1)}, bf16[32,4864]{1,0:T(8,128)(2,1)S(1)}, bf16[32,4864]{1,0:T(8,128)(2,1)S(1)...) custom-call(s32[8]{0:T(128)} %home_ref.5, ...), custom_call_target="tpu_custom_call" | custom-call | tf_op jit(solution)/shard_map/pack/pallas_call | solution.py:241
  2.0 3.0 %collective-permute-start = (bf16[32,4864]{1,0:T(8,128)(2,1)S(1)}, bf16[32,4864]{1,0:T(8,128)(2,1)S(1)}, u32[]{:S(2)}, u32[]{:S(2)}) collective-permute-start(bf16[32,4864]{1,0:T(8,128)(2,1)S(1)} %get-tuple-element.24), channel_id=1, source_target_pairs={{0,2},{2,0},{4,6},{6,4},{8,10},{10,8},{12,14},{14,12},{1,3},{3,1},... | collective-permute-start | bytes 933896 | tf_op jit(solution)/shard_map/ppermute | solution.py:201
  5.0 1.6 %collective-permute-start.1 = (bf16[32,4864]{1,0:T(8,128)(2,1)S(1)}, bf16[32,4864]{1,0:T(8,128)(2,1)S(1)}, u32[]{:S(2)}, u32[]{:S(2)}) collective-permute-start(bf16[32,4864]{1,0:T(8,128)(2,1)S(1)} %get-tuple-element.25), channel_id=1, source_target_pairs={{0,4},{2,6},{4,0},{6,2},{8,12},{10,14},{12,8},{14,10},{1,5},{3,7},... | collective-permute-start | bytes 933896 | tf_op jit(solution)/shard_map/ppermute | solution.py:201
  6.6 0.0 collective-permute-start.2
  6.6 3.0 %collective-permute-start.3 = (bf16[32,768]{1,0:T(8,128)(2,1)S(1)}, bf16[32,768]{1,0:T(8,128)(2,1)S(1)}, u32[]{:S(2)}, u32[]{:S(2)}) collective-permute-start(bf16[32,768]{1,0:T(8,128)(2,1)S(1)} %get-tuple-element.27), channel_id=1, source_target_pairs={{0,8},{2,10},{4,12},{6,14},{8,0},{10,2},{12,4},{14,6},{1,9},{3,11}... | collective-permute-start | bytes 147464 | tf_op jit(solution)/shard_map/ppermute | solution.py:201
  9.6 1.3 %collective-permute-start.4 = (bf16[32,768]{1,0:T(8,128)(2,1)S(1)}, bf16[32,768]{1,0:T(8,128)(2,1)S(1)}, u32[]{:S(2)}, u32[]{:S(2)}) collective-permute-start(bf16[32,768]{1,0:T(8,128)(2,1)S(1)} %get-tuple-element.28), channel_id=1, source_target_pairs={{0,10},{2,8},{4,14},{6,12},{8,2},{10,0},{12,6},{14,4},{1,11},{3,9}... | collective-permute-start | bytes 147464 | tf_op jit(solution)/shard_map/ppermute | solution.py:201
  10.9 10.3 %collective-permute-done.3.rest_4_ = bf16[32,768]{1,0:T(8,128)(2,1)S(1)} collective-permute-done((bf16[32,768]{1,0:T(8,128)(2,1)S(1)}, bf16[32,768]{1,0:T(8,128)(2,1)S(1)}, u32[]{:S(2)}, u32[]{:S(2)}) %collective-permute-start.3) | collective-permute-done | bytes 49184 | tf_op jit(solution)/shard_map/ppermute | solution.py:201
  21.2 2.8 %collective-permute-start.5 = (bf16[32,768]{1,0:T(8,128)(2,1)S(1)}, bf16[32,768]{1,0:T(8,128)(2,1)S(1)}, u32[]{:S(2)}, u32[]{:S(2)}) collective-permute-start(bf16[32,768]{1,0:T(8,128)(2,1)S(1)} %get-tuple-element.29), channel_id=1, source_target_pairs={{0,12},{2,14},{4,8},{6,10},{8,4},{10,6},{12,0},{14,2},{1,13},{3,15... | collective-permute-start | bytes 147464 | tf_op jit(solution)/shard_map/ppermute | solution.py:201
  24.0 0.0 collective-permute-done.4.rest_5_
  24.1 0.0 copy-start
  24.1 0.0 copy-start.1
  24.1 0.0 copy-start.2
  24.1 1.0 %collective-permute-start.6 = (bf16[32,768]{1,0:T(8,128)(2,1)S(1)}, bf16[32,768]{1,0:T(8,128)(2,1)S(1)}, u32[]{:S(2)}, u32[]{:S(2)}) collective-permute-start(bf16[32,768]{1,0:T(8,128)(2,1)S(1)} %get-tuple-element.30), channel_id=1, source_target_pairs={{0,14},{2,12},{4,10},{6,8},{8,6},{10,4},{12,2},{14,0},{1,15},{3,13... | collective-permute-start | bytes 147464 | tf_op jit(solution)/shard_map/ppermute | solution.py:201
  25.1 2.1 %collective-permute-done.5.rest_6_ = bf16[32,768]{1,0:T(8,128)(2,1)S(1)} collective-permute-done((bf16[32,768]{1,0:T(8,128)(2,1)S(1)}, bf16[32,768]{1,0:T(8,128)(2,1)S(1)}, u32[]{:S(2)}, u32[]{:S(2)}) %collective-permute-start.5) | collective-permute-done | bytes 49184 | tf_op jit(solution)/shard_map/ppermute | solution.py:201
  27.2 3.7 %collective-permute-done.6.rest_7_ = bf16[32,768]{1,0:T(8,128)(2,1)S(1)} collective-permute-done((bf16[32,768]{1,0:T(8,128)(2,1)S(1)}, bf16[32,768]{1,0:T(8,128)(2,1)S(1)}, u32[]{:S(2)}, u32[]{:S(2)}) %collective-permute-start.6) | collective-permute-done | bytes 49184 | tf_op jit(solution)/shard_map/ppermute | solution.py:201
  30.9 0.0 collective-permute-done.rest_1_
  30.9 0.0 collective-permute-done.1.rest_2_
  30.9 0.0 collective-permute-done.2.rest_3_
  30.9 0.0 copy-done
  30.9 0.0 copy-done.1
  30.9 0.0 copy-done.2
  31.0 4.1 %attend.1 = (bf16[64,2048]{1,0:T(8,128)(2,1)S(1)}, bf16[32,2816]{1,0:T(8,128)(2,1)S(1)}, bf16[32,2816]{1,0:T(8,128)(2,1)S(1)}, bf16[32,2816]{1,0:T(8,128)(2,1)S(...) custom-call(s32[8]{0:T(128)S(1)} %copy-done.1, ...), custom_call_target="tpu_custom_call" | custom-call | tf_op jit(solution)/shard_map/attend/pallas_call | solution.py:254
  35.1 0.7 %collective-permute-start.10 = (bf16[64,2432]{1,0:T(8,128)(2,1)S(1)}, bf16[64,2432]{1,0:T(8,128)(2,1)S(1)}, u32[]{:S(2)}, u32[]{:S(2)}) collective-permute-start(bf16[64,2432]{1,0:T(8,128)(2,1)S(1)} %get-tuple-element.36), channel_id=1, source_target_pairs={{0,8},{2,10},{4,12},{6,14},{8,0},{10,2},{12,4},{14,6},{1,9},{3,11}... | collective-permute-start | bytes 933896 | tf_op jit(solution)/shard_map/ppermute | solution.py:201
  35.8 0.5 collective-permute-start.7
  36.4 0.9 %collective-permute-start.8 = (bf16[32,2816]{1,0:T(8,128)(2,1)S(1)}, bf16[32,2816]{1,0:T(8,128)(2,1)S(1)}, u32[]{:S(2)}, u32[]{:S(2)}) collective-permute-start(bf16[32,2816]{1,0:T(8,128)(2,1)S(1)} %get-tuple-element.34), channel_id=1, source_target_pairs={{0,4},{2,6},{4,0},{6,2},{8,12},{10,14},{12,8},{14,10},{1,5},{3,7},... | collective-permute-start | bytes 540680 | tf_op jit(solution)/shard_map/ppermute | solution.py:201
  37.3 2.0 %collective-permute-start.9 = (bf16[32,2816]{1,0:T(8,128)(2,1)S(1)}, bf16[32,2816]{1,0:T(8,128)(2,1)S(1)}, u32[]{:S(2)}, u32[]{:S(2)}) collective-permute-start(bf16[32,2816]{1,0:T(8,128)(2,1)S(1)} %get-tuple-element.35), channel_id=1, source_target_pairs={{0,6},{2,4},{4,2},{6,0},{8,14},{10,12},{12,10},{14,8},{1,7},{3,5},... | collective-permute-start | bytes 540680 | tf_op jit(solution)/shard_map/ppermute | solution.py:201
  39.3 2.2 %collective-permute-start.11 = (bf16[32,768]{1,0:T(8,128)(2,1)S(1)}, bf16[32,768]{1,0:T(8,128)(2,1)S(1)}, u32[]{:S(2)}, u32[]{:S(2)}) collective-permute-start(bf16[32,768]{1,0:T(8,128)(2,1)S(1)} %get-tuple-element.37), channel_id=1, source_target_pairs={{0,10},{2,8},{4,14},{6,12},{8,2},{10,0},{12,6},{14,4},{1,11},{3,9}... | collective-permute-start | bytes 147464 | tf_op jit(solution)/shard_map/ppermute | solution.py:201
  41.6 8.4 %collective-permute-done.11.rest_5_ = bf16[32,768]{1,0:T(8,128)(2,1)S(1)} collective-permute-done((bf16[32,768]{1,0:T(8,128)(2,1)S(1)}, bf16[32,768]{1,0:T(8,128)(2,1)S(1)}, u32[]{:S(2)}, u32[]{:S(2)}) %collective-permute-start.11) | collective-permute-done | bytes 49184 | tf_op jit(solution)/shard_map/ppermute | solution.py:201
  49.9 1.5 %collective-permute-start.12 = (bf16[32,768]{1,0:T(8,128)(2,1)S(1)}, bf16[32,768]{1,0:T(8,128)(2,1)S(1)}, u32[]{:S(2)}, u32[]{:S(2)}) collective-permute-start(bf16[32,768]{1,0:T(8,128)(2,1)S(1)} %get-tuple-element.38), channel_id=1, source_target_pairs={{0,12},{2,14},{4,8},{6,10},{8,4},{10,6},{12,0},{14,2},{1,13},{3,15... | collective-permute-start | bytes 147464 | tf_op jit(solution)/shard_map/ppermute | solution.py:201
  51.4 4.5 %collective-permute-done.12.rest_6_ = bf16[32,768]{1,0:T(8,128)(2,1)S(1)} collective-permute-done((bf16[32,768]{1,0:T(8,128)(2,1)S(1)}, bf16[32,768]{1,0:T(8,128)(2,1)S(1)}, u32[]{:S(2)}, u32[]{:S(2)}) %collective-permute-start.12) | collective-permute-done | bytes 49184 | tf_op jit(solution)/shard_map/ppermute | solution.py:201
  55.9 2.3 %collective-permute-start.13 = (bf16[32,768]{1,0:T(8,128)(2,1)S(1)}, bf16[32,768]{1,0:T(8,128)(2,1)S(1)}, u32[]{:S(2)}, u32[]{:S(2)}) collective-permute-start(bf16[32,768]{1,0:T(8,128)(2,1)S(1)} %get-tuple-element.39), channel_id=1, source_target_pairs={{0,14},{2,12},{4,10},{6,8},{8,6},{10,4},{12,2},{14,0},{1,15},{3,13... | collective-permute-start | bytes 147464 | tf_op jit(solution)/shard_map/ppermute | solution.py:201
  58.2 4.5 %collective-permute-done.13.rest_7_ = bf16[32,768]{1,0:T(8,128)(2,1)S(1)} collective-permute-done((bf16[32,768]{1,0:T(8,128)(2,1)S(1)}, bf16[32,768]{1,0:T(8,128)(2,1)S(1)}, u32[]{:S(2)}, u32[]{:S(2)}) %collective-permute-start.13) | collective-permute-done | bytes 49184 | tf_op jit(solution)/shard_map/ppermute | solution.py:201
  62.7 0.0 collective-permute-done.7.rest_1_
  62.7 0.0 collective-permute-done.8.rest_2_
  62.7 0.0 collective-permute-done.9.rest_3_
  62.7 0.0 collective-permute-done.10.rest_4_
  62.7 1.7 %unpack.1 = (bf16[1,128,2048]{2,1,0:T(8,128)(2,1)}, bf16[8,16,2048]{2,1,0:T(8,128)(2,1)}, bf16[8,16,256]{2,1,0:T(8,128)(2,1)}, bf16[8,16,256]{2,1,0:T(8,128)(2,1...) custom-call(s32[8]{0:T(128)S(1)} %copy-done, bf16[64,2048]{1,0:T(8,128)(2,1)S(1)} %get-tuple-element.31.kept_ref, ...), custom_call_target="tpu_custom_call" | custom-call | tf_op jit(solution)/shard_map/unpack/pallas_call | solution.py:275
Async XLA Ops:
  2.0 28.9 %collective-permute-start = (bf16[32,4864]{1,0:T(8,128)(2,1)S(1)}, bf16[32,4864]{1,0:T(8,128)(2,1)S(1)}, u32[]{:S(2)}, u32[]{:S(2)}) collective-permute-start(bf16[32,4864]{1,0:T(8,128)(2,1)S(1)} %get-tuple-element.24), channel_id=1, source_target_pairs={{0,2},{2,0},{4,6},{6,4},{8,10},{10,8},{12,14},{14,12},{1,3},{3,1},... | collective-permute-start | bytes 933896 | tf_op jit(solution)/shard_map/ppermute | solution.py:201
  5.0 25.9 %collective-permute-start.1 = (bf16[32,4864]{1,0:T(8,128)(2,1)S(1)}, bf16[32,4864]{1,0:T(8,128)(2,1)S(1)}, u32[]{:S(2)}, u32[]{:S(2)}) collective-permute-start(bf16[32,4864]{1,0:T(8,128)(2,1)S(1)} %get-tuple-element.25), channel_id=1, source_target_pairs={{0,4},{2,6},{4,0},{6,2},{8,12},{10,14},{12,8},{14,10},{1,5},{3,7},... | collective-permute-start | bytes 933896 | tf_op jit(solution)/shard_map/ppermute | solution.py:201
  6.6 24.3 %collective-permute-start.2 = (bf16[32,4864]{1,0:T(8,128)(2,1)S(1)}, bf16[32,4864]{1,0:T(8,128)(2,1)S(1)}, u32[]{:S(2)}, u32[]{:S(2)}) collective-permute-start(bf16[32,4864]{1,0:T(8,128)(2,1)S(1)} %get-tuple-element.26), channel_id=1, source_target_pairs={{0,6},{2,4},{4,2},{6,0},{8,14},{10,12},{12,10},{14,8},{1,7},{3,5},... | collective-permute-start | bytes 933896 | tf_op jit(solution)/shard_map/ppermute | solution.py:201
  6.6 14.6 %collective-permute-start.3 = (bf16[32,768]{1,0:T(8,128)(2,1)S(1)}, bf16[32,768]{1,0:T(8,128)(2,1)S(1)}, u32[]{:S(2)}, u32[]{:S(2)}) collective-permute-start(bf16[32,768]{1,0:T(8,128)(2,1)S(1)} %get-tuple-element.27), channel_id=1, source_target_pairs={{0,8},{2,10},{4,12},{6,14},{8,0},{10,2},{12,4},{14,6},{1,9},{3,11}... | collective-permute-start | bytes 147464 | tf_op jit(solution)/shard_map/ppermute | solution.py:201
  9.6 14.4 %collective-permute-start.4 = (bf16[32,768]{1,0:T(8,128)(2,1)S(1)}, bf16[32,768]{1,0:T(8,128)(2,1)S(1)}, u32[]{:S(2)}, u32[]{:S(2)}) collective-permute-start(bf16[32,768]{1,0:T(8,128)(2,1)S(1)} %get-tuple-element.28), channel_id=1, source_target_pairs={{0,10},{2,8},{4,14},{6,12},{8,2},{10,0},{12,6},{14,4},{1,11},{3,9}... | collective-permute-start | bytes 147464 | tf_op jit(solution)/shard_map/ppermute | solution.py:201
  21.2 6.0 %collective-permute-start.5 = (bf16[32,768]{1,0:T(8,128)(2,1)S(1)}, bf16[32,768]{1,0:T(8,128)(2,1)S(1)}, u32[]{:S(2)}, u32[]{:S(2)}) collective-permute-start(bf16[32,768]{1,0:T(8,128)(2,1)S(1)} %get-tuple-element.29), channel_id=1, source_target_pairs={{0,12},{2,14},{4,8},{6,10},{8,4},{10,6},{12,0},{14,2},{1,13},{3,15... | collective-permute-start | bytes 147464 | tf_op jit(solution)/shard_map/ppermute | solution.py:201
  24.1 6.9 %copy-start = (s32[8]{0:T(128)S(1)}, s32[8]{0:T(128)}, u32[]{:S(2)}) copy-start(s32[8]{0:T(128)} %home_ref.5) | copy-start | bytes 100
  24.1 6.9 %copy-start.1 = (s32[8]{0:T(128)S(1)}, s32[8]{0:T(128)}, u32[]{:S(2)}) copy-start(s32[8]{0:T(128)} %lengths_ref.1) | copy-start | bytes 100
  24.1 6.9 %copy-start.2 = (s32[8]{0:T(128)S(1)}, s32[8]{0:T(128)}, u32[]{:S(2)}) copy-start(s32[8]{0:T(128)} %seen_ref.1) | copy-start | bytes 100
  24.1 6.9 %collective-permute-start.6 = (bf16[32,768]{1,0:T(8,128)(2,1)S(1)}, bf16[32,768]{1,0:T(8,128)(2,1)S(1)}, u32[]{:S(2)}, u32[]{:S(2)}) collective-permute-start(bf16[32,768]{1,0:T(8,128)(2,1)S(1)} %get-tuple-element.30), channel_id=1, source_target_pairs={{0,14},{2,12},{4,10},{6,8},{8,6},{10,4},{12,2},{14,0},{1,15},{3,13... | collective-permute-start | bytes 147464 | tf_op jit(solution)/shard_map/ppermute | solution.py:201
  35.1 27.6 %collective-permute-start.10 = (bf16[64,2432]{1,0:T(8,128)(2,1)S(1)}, bf16[64,2432]{1,0:T(8,128)(2,1)S(1)}, u32[]{:S(2)}, u32[]{:S(2)}) collective-permute-start(bf16[64,2432]{1,0:T(8,128)(2,1)S(1)} %get-tuple-element.36), channel_id=1, source_target_pairs={{0,8},{2,10},{4,12},{6,14},{8,0},{10,2},{12,4},{14,6},{1,9},{3,11}... | collective-permute-start | bytes 933896 | tf_op jit(solution)/shard_map/ppermute | solution.py:201
  35.8 26.9 %collective-permute-start.7 = (bf16[32,2816]{1,0:T(8,128)(2,1)S(1)}, bf16[32,2816]{1,0:T(8,128)(2,1)S(1)}, u32[]{:S(2)}, u32[]{:S(2)}) collective-permute-start(bf16[32,2816]{1,0:T(8,128)(2,1)S(1)} %get-tuple-element.33), channel_id=1, source_target_pairs={{0,2},{2,0},{4,6},{6,4},{8,10},{10,8},{12,14},{14,12},{1,3},{3,1},... | collective-permute-start | bytes 540680 | tf_op jit(solution)/shard_map/ppermute | solution.py:201
  36.4 26.3 %collective-permute-start.8 = (bf16[32,2816]{1,0:T(8,128)(2,1)S(1)}, bf16[32,2816]{1,0:T(8,128)(2,1)S(1)}, u32[]{:S(2)}, u32[]{:S(2)}) collective-permute-start(bf16[32,2816]{1,0:T(8,128)(2,1)S(1)} %get-tuple-element.34), channel_id=1, source_target_pairs={{0,4},{2,6},{4,0},{6,2},{8,12},{10,14},{12,8},{14,10},{1,5},{3,7},... | collective-permute-start | bytes 540680 | tf_op jit(solution)/shard_map/ppermute | solution.py:201
  37.3 25.4 %collective-permute-start.9 = (bf16[32,2816]{1,0:T(8,128)(2,1)S(1)}, bf16[32,2816]{1,0:T(8,128)(2,1)S(1)}, u32[]{:S(2)}, u32[]{:S(2)}) collective-permute-start(bf16[32,2816]{1,0:T(8,128)(2,1)S(1)} %get-tuple-element.35), channel_id=1, source_target_pairs={{0,6},{2,4},{4,2},{6,0},{8,14},{10,12},{12,10},{14,8},{1,7},{3,5},... | collective-permute-start | bytes 540680 | tf_op jit(solution)/shard_map/ppermute | solution.py:201
  39.3 10.6 %collective-permute-start.11 = (bf16[32,768]{1,0:T(8,128)(2,1)S(1)}, bf16[32,768]{1,0:T(8,128)(2,1)S(1)}, u32[]{:S(2)}, u32[]{:S(2)}) collective-permute-start(bf16[32,768]{1,0:T(8,128)(2,1)S(1)} %get-tuple-element.37), channel_id=1, source_target_pairs={{0,10},{2,8},{4,14},{6,12},{8,2},{10,0},{12,6},{14,4},{1,11},{3,9}... | collective-permute-start | bytes 147464 | tf_op jit(solution)/shard_map/ppermute | solution.py:201
  49.9 6.0 %collective-permute-start.12 = (bf16[32,768]{1,0:T(8,128)(2,1)S(1)}, bf16[32,768]{1,0:T(8,128)(2,1)S(1)}, u32[]{:S(2)}, u32[]{:S(2)}) collective-permute-start(bf16[32,768]{1,0:T(8,128)(2,1)S(1)} %get-tuple-element.38), channel_id=1, source_target_pairs={{0,12},{2,14},{4,8},{6,10},{8,4},{10,6},{12,0},{14,2},{1,13},{3,15... | collective-permute-start | bytes 147464 | tf_op jit(solution)/shard_map/ppermute | solution.py:201
  55.9 6.8 %collective-permute-start.13 = (bf16[32,768]{1,0:T(8,128)(2,1)S(1)}, bf16[32,768]{1,0:T(8,128)(2,1)S(1)}, u32[]{:S(2)}, u32[]{:S(2)}) collective-permute-start(bf16[32,768]{1,0:T(8,128)(2,1)S(1)} %get-tuple-element.39), channel_id=1, source_target_pairs={{0,14},{2,12},{4,10},{6,8},{8,6},{10,4},{12,2},{14,0},{1,15},{3,13... | collective-permute-start | bytes 147464 | tf_op jit(solution)/shard_map/ppermute | solution.py:201

commit v8 on v0

--- a/solution.py
+++ b/solution.py
@@ -1,12 +1,342 @@
+import functools
+
 import jax
 import jax.numpy as jnp
 from jax import lax
+from jax.experimental import pallas as pl
+from jax.experimental.pallas import tpu as pltpu
 from jax.sharding import PartitionSpec as P
 
 HEAD_DIM = 128
 
 
 NEG_FILL = -1e30
+BF16 = jnp.bfloat16
+F32 = jnp.float32
+
+
+def resident_of(home_ref, rank, count):
+    found = jnp.int32(0)
+    for index in range(count):
+        found = jnp.where(home_ref[index] == rank, jnp.int32(index), found)
+    return found
+
+
+def dot(left, right, contract):
+    return lax.dot_general(left, right, ((contract[0], contract[1]), ((), ())), preferred_element_type=F32)
+
+
+def padded_rows(ref, part, rows):
+    spare = jnp.zeros((rows - ref.shape[1], ref.shape[2]), BF16)
+    return jnp.concatenate([ref[part], spare], axis=0)
+
+
+def pack_kernel(home_ref, q_ref, k_ref, v_ref, g_ref, pk_ref, pv_ref, *rest, count, head, with_far):
+    blocks, (home, q, g, k, v, prompt, sems) = rest[:-7], rest[-7:]
+    rank = lax.axis_index("seq")
+    half = count // 2
+    rows, q_part = q.shape[1:]
+    wide = pl.ds(head * q_part, q_part)
+    copies = [
+        pltpu.make_async_copy(source, target, sems.at[index])
+        for index, (source, target) in enumerate(
+            (
+                (home_ref, home),
+                (q_ref.at[:, :, wide], q),
+                (g_ref.at[:, :, wide], g),
+                (k_ref, k),
+                (v_ref, v),
+                (pk_ref, prompt.at[0]),
+                (pv_ref, prompt.at[1]),
+            )
+        )
+    ]
+    for copy in copies:
+        copy.start()
+    for copy in copies:
+        copy.wait()
+    padded = [padded_rows(prompt, part, rows) for part in range(2)]
+    lanes = slice(head * HEAD_DIM, (head + 1) * HEAD_DIM)
+    for distance in range(half):
+        place = (rank ^ distance) & (half - 1)
+        for part in range(2):
+            index = resident_of(home, place + part * half, count)
+            at = slice(part * rows, (part + 1) * rows)
+            near = [q[index], g[index], k[index, :, lanes], v[index, :, lanes], padded[part][:, lanes]]
+            blocks[distance][at, :] = jnp.concatenate(near, axis=1)
+            if with_far:
+                blocks[distance + half][at, :] = jnp.concatenate([k[index], v[index], padded[part]], axis=1)
+
+
+def attend_kernel(lengths_ref, home_ref, seen_ref, *rest, count, prompt_rows, head, heads):
+    half = count // 2
+    last = head == heads - 1
+    blocks, rest = rest[:count], rest[count:]
+    earlier, rest = (rest[: head * count], rest[head * count :]) if last else ((), rest)
+    kept_ref, swap_ref, returns, rest = rest[0], rest[1], list(rest[2:-6]), rest[-6:]
+    xq, xk, xp, yq, yk, yp = rest
+    rank = lax.axis_index("seq")
+    place = rank & (half - 1)
+    upper = rank // half
+    rows = xk.shape[2]
+    total = rows * count
+    own_rows = rows * half
+    q_part = yq.shape[3]
+    members = q_part // HEAD_DIM
+    scale = 1.0 / HEAD_DIM**0.5
+    for distance in range(count):
+        source = rank ^ distance
+        block = blocks[distance]
+        for part in range(2):
+            at = slice(part * rows, (part + 1) * rows)
+            if distance < half:
+                low, step = 2 * q_part, HEAD_DIM
+                xq[part, source & (half - 1)] = block[at, :low]
+            else:
+                low, step = head * HEAD_DIM, heads * HEAD_DIM
+            xk[part, source, :, :HEAD_DIM] = block[at, low : low + HEAD_DIM]
+            xk[part, source, :, HEAD_DIM:] = block[at, low + step : low + step + HEAD_DIM]
+            xp[part, source] = block[at, low + 2 * step : low + 2 * step + HEAD_DIM]
+    column = lax.broadcasted_iota(jnp.int32, (own_rows, total), 1)
+    position = lax.broadcasted_iota(jnp.int32, (own_rows, total), 0) + upper * own_rows
+    shard_row = column % rows
+    prompt_index = jnp.where(shard_row < prompt_rows, column // rows * prompt_rows + shard_row, 1 << 30)
+    causal = column <= position
+    prompt_grads = [jnp.zeros((total, HEAD_DIM), F32)] * 2
+    outputs = []
+    for part in range(2):
+        index = resident_of(home_ref, place + part * half, count)
+        mask = jnp.concatenate([prompt_index < seen_ref[index], causal], axis=1)
+        allowed = jnp.concatenate([mask] * members, axis=0)
+        live = jnp.concatenate([position[:, :HEAD_DIM] < lengths_ref[index]] * members, axis=0)
+
+        def stacked(offset):
+            return jnp.concatenate(
+                [
+                    xq[part, :, :, low : low + HEAD_DIM].reshape(own_rows, HEAD_DIM)
+                    for low in range(offset, offset + q_part, HEAD_DIM)
+                ],
+                axis=0,
+            )
+
+        keys, values = (
+            jnp.concatenate(
+                [
+                    xp[index].reshape(total, HEAD_DIM),
+                    xk[part, :, :, index * HEAD_DIM : (index + 1) * HEAD_DIM].reshape(total, HEAD_DIM),
+                ],
+                axis=0,
+            )
+            for index in range(2)
+        )
+        query = stacked(0)
+        grad = jnp.where(live, stacked(q_part), jnp.zeros((), BF16))
+        logits = jnp.where(allowed, dot(query, keys, ((1,), (1,))) * scale, NEG_FILL)
+        spread = dot(grad, values, ((1,), (1,)))
+        raised = jnp.exp(logits - jnp.max(logits, axis=1, keepdims=True))
+        prob = raised * (1.0 / jnp.sum(raised, axis=1, keepdims=True))
+        weights = prob.astype(BF16)
+        output = jnp.where(live, dot(weights, values, ((1,), (0,))), 0.0).astype(BF16)
+        row_dot = jnp.sum(grad.astype(F32) * output.astype(F32), axis=1, keepdims=True)
+        dlogit = (prob * (spread - row_dot)).astype(BF16)
+        query_grad = (dot(dlogit, keys, ((1,), (0,))) * scale).astype(BF16)
+        outputs.append(output)
+        for member in range(members):
+            at = slice(member * own_rows, (member + 1) * own_rows)
+            yq[part, :, :, member * HEAD_DIM : (member + 1) * HEAD_DIM] = query_grad[at].reshape(half, rows, HEAD_DIM)
+        summed = (dot(dlogit, query, ((0,), (0,))) * scale, dot(weights, grad, ((0,), (0,))))
+        for index in range(2):
+            to = slice(index * HEAD_DIM, (index + 1) * HEAD_DIM)
+            yk[part, :, :, to] = summed[index][total:].astype(BF16).reshape(count, rows, HEAD_DIM)
+            prompt_grads[index] = prompt_grads[index] + summed[index][:total]
+    for index in range(2):
+        yp[index] = prompt_grads[index].astype(BF16).reshape(count, rows, HEAD_DIM)
+    stays = jnp.where(upper > 0, outputs[1], outputs[0])
+    leaves = jnp.where(upper > 0, outputs[0], outputs[1])
+    for member in range(members):
+        at = slice(member * own_rows, (member + 1) * own_rows)
+        lanes = slice(member * HEAD_DIM, (member + 1) * HEAD_DIM)
+        kept_ref[:, lanes] = stays[at]
+        swap_ref[:, lanes] = leaves[at]
+    for distance in range(count):
+        target = rank ^ distance
+        near = distance < half
+        for part in range(2):
+            at = slice(part * rows, (part + 1) * rows)
+            terms = [yk[part, target], yp[part, target]]
+            if near:
+                terms = [yq[part, target & (half - 1)], *terms]
+            terms = [block[at, :] for block in earlier[distance::count]] + terms
+            terms = jnp.concatenate(terms, axis=1)
+            if last and distance == half:
+                fold = terms.shape[1] // 2
+                for index in range(2):
+                    to = slice((2 * index + part) * rows, (2 * index + part + 1) * rows)
+                    swap_ref[to, q_part:] = terms[:, index * fold : (index + 1) * fold]
+            else:
+                returns[distance - (last and distance > half)][at, :] = terms
+
+
+def join_kernel(*rest, half, heads):
+    kept, came, out_ref = rest[:heads], rest[heads:-1], rest[-1]
+    own_rows, q_part = kept[0].shape
+    upper = lax.axis_index("seq") // half
+    own = pl.multiple_of(upper * own_rows, own_rows)
+    other = pl.multiple_of((1 - upper) * own_rows, own_rows)
+    for head in range(heads):
+        lanes = slice(head * q_part, (head + 1) * q_part)
+        out_ref[0, pl.ds(own, own_rows), lanes] = kept[head][...]
+        out_ref[0, pl.ds(other, own_rows), lanes] = came[head][:, :q_part]
+
+
+def unpack_kernel(home_ref, *rest, count, heads):
+    half = count // 2
+    blocks, (qg_ref, kg_ref, vg_ref, pkg_ref, pvg_ref) = rest[:count], rest[count:]
+    rank = lax.axis_index("seq")
+    rows, q_width = qg_ref.shape[1:]
+    prompt_rows = pkg_ref.shape[0]
+    q_part = q_width // heads
+    near_size, far_size = q_part + 3 * HEAD_DIM, 3 * HEAD_DIM
+    for head in range(heads):
+        lanes = slice(head * HEAD_DIM, (head + 1) * HEAD_DIM)
+        prompt_grads = [jnp.zeros((rows, HEAD_DIM), F32)] * 2
+        for distance in range(half):
+            place = (rank ^ distance) & (half - 1)
+            for part in range(2):
+                index = resident_of(home_ref, place + part * half, count)
+                at = slice(part * rows, (part + 1) * rows)
+                low = head * near_size
+                qg_ref[index, :, head * q_part : (head + 1) * q_part] = blocks[distance][at, low : low + q_part]
+                far = blocks[distance + half]
+                if distance:
+                    far = far[at, :]
+                else:
+                    far = jnp.concatenate(
+                        [far[at, q_part:], far[(2 + part) * rows : (3 + part) * rows, q_part:]], axis=1
+                    )
+                far = far[:, head * far_size : (head + 1) * far_size]
+                terms = blocks[distance][at, low + q_part : low + near_size].astype(F32) + far.astype(F32)
+                kg_ref[index, :, lanes] = terms[:, :HEAD_DIM].astype(BF16)
+                vg_ref[index, :, lanes] = terms[:, HEAD_DIM : 2 * HEAD_DIM].astype(BF16)
+                prompt_grads[part] = prompt_grads[part] + terms[:, 2 * HEAD_DIM :]
+        pkg_ref[:, lanes] = prompt_grads[0][:prompt_rows].astype(BF16)
+        pvg_ref[:, lanes] = prompt_grads[1][:prompt_rows].astype(BF16)
+
+
+def exchange(blocks, distances, count):
+    arrived = []
+    for block, distance in zip(blocks, distances, strict=True):
+        if distance:
+            block = lax.ppermute(block, "seq", [(i, i ^ distance) for i in range(count)])
+        arrived.append(block)
+    return arrived
+
+
+SMEM = pl.BlockSpec(memory_space=pltpu.SMEM)
+VMEM = pl.BlockSpec(memory_space=pltpu.VMEM)
+HBM = pl.BlockSpec(memory_space=pltpu.HBM)
+PARAMS = pltpu.CompilerParams(vmem_limit_bytes=32 * 1024 * 1024)
+
+
+def packed_body(
+    response_query,
+    response_key,
+    response_value,
+    response_grad,
+    prompt_key,
+    prompt_value,
+    lengths,
+    home_rank,
+    prompt_seen,
+):
+    count = home_rank.shape[0]
+    half = count // 2
+    rows, q_width = response_query.shape[1:]
+    prompt_rows, kv_width = prompt_key.shape
+    heads = kv_width // HEAD_DIM
+    q_part = q_width // heads
+    own_rows = rows * half
+    near, far = range(half), range(half, count)
+    far_size = 3 * HEAD_DIM
+    near_size = q_part + far_size
+
+    def shape(*dims):
+        return jax.ShapeDtypeStruct(dims, BF16)
+
+    def scratch(*dims):
+        return pltpu.VMEM(dims, BF16)
+
+    def call(kernel, results, operands, specs, spaces):
+        made = pl.pallas_call(
+            kernel,
+            out_shape=results,
+            in_specs=specs,
+            out_specs=[VMEM] * len(results),
+            scratch_shapes=spaces,
+            compiler_params=PARAMS,
+        )(*operands)
+        return list(made)
+
+    sources = [
+        pltpu.with_memory_space_constraint(source, pltpu.HBM)
+        for source in (home_rank, response_query, response_key, response_value, response_grad, prompt_key, prompt_value)
+    ]
+    near_in = []
+    for head in range(heads):
+        blocks = call(
+            functools.partial(pack_kernel, count=count, head=head, with_far=head == 0),
+            [shape(2 * rows, q_part + near_size)] * half + [shape(2 * rows, heads * far_size)] * (0 if head else half),
+            sources,
+            [HBM] * 7,
+            [pltpu.SMEM((count,), jnp.int32)]
+            + [scratch(count, rows, lanes) for lanes in (q_part, q_part, kv_width, kv_width)]
+            + [scratch(2, prompt_rows, kv_width), pltpu.SemaphoreType.DMA((7,))],
+        )
+        near_in.append(exchange(blocks[:half], near, count))
+        if head == 0:
+            far_in = exchange(blocks[half:], far, count)
+    kept, came, returns = [], [], []
+    for head in range(heads):
+        last = head == heads - 1
+        operands = [lengths, home_rank, prompt_seen, *near_in[head], *far_in, *(returns if last else [])]
+        whole = heads if last else 1
+        fold = 2 * rows * whole * far_size // own_rows if last else 0
+        results = call(
+            functools.partial(attend_kernel, count=count, prompt_rows=prompt_rows, head=head, heads=heads),
+            [shape(own_rows, q_part), shape(own_rows, q_part + fold)]
+            + [shape(2 * rows, whole * near_size)] * half
+            + [shape(2 * rows, whole * far_size)] * (half - last),
+            operands,
+            [SMEM] * 3 + [VMEM] * (len(operands) - 3),
+            [
+                scratch(2, half, rows, 2 * q_part),
+                scratch(2, count, rows, 2 * HEAD_DIM),
+                scratch(2, count, rows, HEAD_DIM),
+                scratch(2, half, rows, q_part),
+                scratch(2, count, rows, 2 * HEAD_DIM),
+                scratch(2, count, rows, HEAD_DIM),
+            ],
+        )
+        kept.append(results[0])
+        came += exchange(results[1:2], [half], count)
+        returns = returns + results[2:] if not last else results[2:]
+    returned = exchange(returns, [*near, *far[1:]], count)
+    returned.insert(half, came[-1])
+    output = call(
+        functools.partial(join_kernel, half=half, heads=heads),
+        [shape(1, rows * count, q_width)],
+        [*kept, *came],
+        [VMEM] * (2 * heads),
+        [],
+    )
+    grads = call(
+        functools.partial(unpack_kernel, count=count, heads=heads),
+        [shape(count, rows, q_width)] + [shape(count, rows, kv_width)] * 2 + [shape(prompt_rows, kv_width)] * 2,
+        [home_rank, *returned],
+        [SMEM] + [VMEM] * count,
+        [],
+    )
+    return (*output, *grads)
 
 
 def head_logits(queries, all_keys, allowed, head_index, group_size, scale_factor):
@@ -29,7 +359,7 @@
     outputs = []
     totals = []
     for head_index in range(kv_count):
-        query_head, key_head, logits = head_logits(
+        _, _, logits = head_logits(
             queries, all_keys, allowed, head_index, group_size, scale_factor
         )
         value_head = all_values[:, head_index * HEAD_DIM : (head_index + 1) * HEAD_DIM]
@@ -190,6 +520,15 @@
     )
 
 
+def choose_body(response_query, *others):
+    count, rows = response_query.shape[:2]
+    prompt_rows = others[3].shape[0]
+    fits = rows % 16 == 0 and prompt_rows <= rows and rows * count == HEAD_DIM
+    if fits and count in (4, 8):
+        return packed_body(response_query, *others)
+    return body(response_query, *others)
+
+
 def solution(mesh):
     placed = (
         P("group", "seq", "head"),
@@ -203,7 +542,7 @@
         P("group"),
     )
     return jax.shard_map(
-        body,
+        choose_body,
         mesh=mesh,
         in_specs=placed,
         out_specs=(

time: 198 us -> 60.5 us (0.31)
  the two profiles are of different devices: /device:TPU:8 before, /device:TPU:0 now
where the time goes in v8:
time: 60.5 us; the launch traced here: 60.3 us
  starting transfers between devices  27.6 us (46%)
  waiting for transfers between devices  22.3 us (37%)
  Pallas kernels  9.66 us (16%)
  between operations  0.72 us (1%)
    ppermute x18, starting transfers between devices, exchange(): lax.ppermute(block, 'seq', [(i, i ^ distance) for i in range(count)])  27.6 us
    ppermute x18, waiting for transfers between devices, exchange(): lax.ppermute(block, 'seq', [(i, i ^ distance) for i in range(count)])  22.3 us
    pallas_call x6, Pallas kernels, call(): pl.pallas_call(kernel, out_shape=results, in_specs=specs, out_specs=[VMEM...  9.66 us
  transfers between devices with their start and end apart: 18, of which 9 were waited for; matrix products, arithmetic and copies ran while one was open for 0% of the time, Pallas kernels for 7%

profile of v8, /device:TPU:0, one launch (start us, length us, event | category | flops | bytes accessed | tf_op | source)
XLA Modules:
  0.0 60.3 jit_solution(13259916876835054886)
XLA Ops:
  0.6 1.2 %shard_map.136 = (bf16[32,2432]{1,0:T(8,128)(2,1)S(1)}, bf16[32,2432]{1,0:T(8,128)(2,1)S(1)}, bf16[32,2432]{1,0:T(8,128)(2,1)S(1)}, bf16[32,2432]{1,0:T(8,128)(2...) custom-call(s32[8]{0:T(128)} %home_ref.9, ...), custom_call_target="tpu_custom_call" | custom-call | tf_op jit(solution)/shard_map/pallas_call | solution.py:270
  1.8 3.0 %collective-permute-start = (bf16[32,2432]{1,0:T(8,128)(2,1)S(1)}, bf16[32,2432]{1,0:T(8,128)(2,1)S(1)}, u32[]{:S(2)}, u32[]{:S(2)}) collective-permute-start(bf16[32,2432]{1,0:T(8,128)(2,1)S(1)} %get-tuple-element.43), channel_id=1, source_target_pairs={{0,2},{2,0},{4,6},{6,4},{8,10},{10,8},{12,14},{14,12},{1,3},{3,1},... | collective-permute-start | bytes 466952 | tf_op jit(solution)/shard_map/ppermute | solution.py:230
  4.8 2.6 %collective-permute-start.3 = (bf16[32,768]{1,0:T(8,128)(2,1)S(1)}, bf16[32,768]{1,0:T(8,128)(2,1)S(1)}, u32[]{:S(2)}, u32[]{:S(2)}) collective-permute-start(bf16[32,768]{1,0:T(8,128)(2,1)S(1)} %get-tuple-element.46), channel_id=1, source_target_pairs={{0,8},{2,10},{4,12},{6,14},{8,0},{10,2},{12,4},{14,6},{1,9},{3,11}... | collective-permute-start | bytes 147464 | tf_op jit(solution)/shard_map/ppermute | solution.py:230
  7.4 0.0 collective-permute-start.4
  7.4 3.9 %collective-permute-start.5 = (bf16[32,768]{1,0:T(8,128)(2,1)S(1)}, bf16[32,768]{1,0:T(8,128)(2,1)S(1)}, u32[]{:S(2)}, u32[]{:S(2)}) collective-permute-start(bf16[32,768]{1,0:T(8,128)(2,1)S(1)} %get-tuple-element.48), channel_id=1, source_target_pairs={{0,12},{2,14},{4,8},{6,10},{8,4},{10,6},{12,0},{14,2},{1,13},{3,15... | collective-permute-start | bytes 147464 | tf_op jit(solution)/shard_map/ppermute | solution.py:230
  11.3 1.2 %collective-permute-start.6 = (bf16[32,768]{1,0:T(8,128)(2,1)S(1)}, bf16[32,768]{1,0:T(8,128)(2,1)S(1)}, u32[]{:S(2)}, u32[]{:S(2)}) collective-permute-start(bf16[32,768]{1,0:T(8,128)(2,1)S(1)} %get-tuple-element.49), channel_id=1, source_target_pairs={{0,14},{2,12},{4,10},{6,8},{8,6},{10,4},{12,2},{14,0},{1,15},{3,13... | collective-permute-start | bytes 147464 | tf_op jit(solution)/shard_map/ppermute | solution.py:230
  12.5 1.2 %shard_map.138 = (bf16[32,2432]{1,0:T(8,128)(2,1)S(1)}, bf16[32,2432]{1,0:T(8,128)(2,1)S(1)}, bf16[32,2432]{1,0:T(8,128)(2,1)S(1)}, bf16[32,2432]{1,0:T(8,128)(2,1)S(1)}) custom-call(s32[8]{0:T(128)} %home_ref.9, bf16[8,16,2048]{2,1,0:T(8,128)(2,1)} %q_ref.3, bf16[8,16,256]{2,1,0:T(8,128)(2,1)} %k_ref.3, bf16[8,16,256]{2,1,0:T(8,128)(2,1)} %v_ref.3, ...), custom_call_target="tpu_custom_call" | custom-call | tf_op jit(solution)/shard_map/pallas_call | solution.py:270
  13.7 0.0 collective-permute-done.3.rest_4_
  13.7 0.1 collective-permute-start.1
  13.7 1.6 %collective-permute-done.4.rest_5_ = bf16[32,768]{1,0:T(8,128)(2,1)S(1)} collective-permute-done((bf16[32,768]{1,0:T(8,128)(2,1)S(1)}, bf16[32,768]{1,0:T(8,128)(2,1)S(1)}, u32[]{:S(2)}, u32[]{:S(2)}) %collective-permute-start.4) | collective-permute-done | bytes 49184 | tf_op jit(solution)/shard_map/ppermute | solution.py:230
  15.3 0.2 collective-permute-start.2
  15.5 0.0 collective-permute-done.5.rest_6_
  15.5 1.7 %collective-permute-start.7 = (bf16[32,2432]{1,0:T(8,128)(2,1)S(1)}, bf16[32,2432]{1,0:T(8,128)(2,1)S(1)}, u32[]{:S(2)}, u32[]{:S(2)}) collective-permute-start(bf16[32,2432]{1,0:T(8,128)(2,1)S(1)} %get-tuple-element.52), channel_id=1, source_target_pairs={{0,2},{2,0},{4,6},{6,4},{8,10},{10,8},{12,14},{14,12},{1,3},{3,1},... | collective-permute-start | bytes 466952 | tf_op jit(solution)/shard_map/ppermute | solution.py:230
  17.2 1.4 %collective-permute-done.6.rest_7_ = bf16[32,768]{1,0:T(8,128)(2,1)S(1)} collective-permute-done((bf16[32,768]{1,0:T(8,128)(2,1)S(1)}, bf16[32,768]{1,0:T(8,128)(2,1)S(1)}, u32[]{:S(2)}, u32[]{:S(2)}) %collective-permute-start.6) | collective-permute-done | bytes 49184 | tf_op jit(solution)/shard_map/ppermute | solution.py:230
  18.7 0.2 collective-permute-start.8
  18.8 0.0 collective-permute-done.rest_1_
  18.8 0.0 copy-start
  18.8 0.0 copy-start.1
  18.8 0.0 copy-start.2
  18.8 2.9 %collective-permute-start.9 = (bf16[32,2432]{1,0:T(8,128)(2,1)S(1)}, bf16[32,2432]{1,0:T(8,128)(2,1)S(1)}, u32[]{:S(2)}, u32[]{:S(2)}) collective-permute-start(bf16[32,2432]{1,0:T(8,128)(2,1)S(1)} %get-tuple-element.54), channel_id=1, source_target_pairs={{0,6},{2,4},{4,2},{6,0},{8,14},{10,12},{12,10},{14,8},{1,7},{3,5},... | collective-permute-start | bytes 466952 | tf_op jit(solution)/shard_map/ppermute | solution.py:230
  21.7 0.0 collective-permute-done.1.rest_2_
  21.7 2.6 %collective-permute-done.2.rest_3_ = bf16[32,2432]{1,0:T(8,128)(2,1)S(1)} collective-permute-done((bf16[32,2432]{1,0:T(8,128)(2,1)S(1)}, bf16[32,2432]{1,0:T(8,128)(2,1)S(1)}, u32[]{:S(2)}, u32[]{:S(2)}) %collective-permute-start.2) | collective-permute-done | bytes 155680 | tf_op jit(solution)/shard_map/ppermute | solution.py:230
  24.3 0.0 copy-done
  24.3 0.0 copy-done.1
  24.3 0.0 copy-done.2
  24.3 2.5 %shard_map.137 = (bf16[64,1024]{1,0:T(8,128)(2,1)S(1)}, bf16[64,1024]{1,0:T(8,128)(2,1)S(1)}, bf16[32,1408]{1,0:T(8,128)(2,1)S(1)}, bf16[32,1408]{1,0:T(8,128)(2...) custom-call(s32[8]{0:T(128)S(1)} %copy-done.1, ...), custom_call_target="tpu_custom_call" | custom-call | tf_op jit(solution)/shard_map/pallas_call | solution.py:270
  26.8 0.0 collective-permute-done.7.rest_1_
  26.8 0.7 %collective-permute-done.8.rest_2_ = bf16[32,2432]{1,0:T(8,128)(2,1)S(1)} collective-permute-done((bf16[32,2432]{1,0:T(8,128)(2,1)S(1)}, bf16[32,2432]{1,0:T(8,128)(2,1)S(1)}, u32[]{:S(2)}, u32[]{:S(2)}) %collective-permute-start.8) | collective-permute-done | bytes 155680 | tf_op jit(solution)/shard_map/ppermute | solution.py:230
  27.5 2.0 %collective-permute-done.9.rest_3_ = bf16[32,2432]{1,0:T(8,128)(2,1)S(1)} collective-permute-done((bf16[32,2432]{1,0:T(8,128)(2,1)S(1)}, bf16[32,2432]{1,0:T(8,128)(2,1)S(1)}, u32[]{:S(2)}, u32[]{:S(2)}) %collective-permute-start.9) | collective-permute-done | bytes 155680 | tf_op jit(solution)/shard_map/ppermute | solution.py:230
  29.5 2.5 %shard_map.139 = (bf16[64,1024]{1,0:T(8,128)(2,1)S(1)}, bf16[64,1408]{1,0:T(8,128)(2,1)S(1)}, bf16[32,2816]{1,0:T(8,128)(2,1)S(1)}, bf16[32,2816]{1,0:T(8,128)(2...) custom-call(s32[8]{0:T(128)S(1)} %copy-done.1, ...), custom_call_target="tpu_custom_call" | custom-call | tf_op jit(solution)/shard_map/pallas_call | solution.py:270
  32.1 1.6 %collective-permute-start.11 = (bf16[64,1408]{1,0:T(8,128)(2,1)S(1)}, bf16[64,1408]{1,0:T(8,128)(2,1)S(1)}, u32[]{:S(2)}, u32[]{:S(2)}) collective-permute-start(bf16[64,1408]{1,0:T(8,128)(2,1)S(1)} %get-tuple-element.65), channel_id=1, source_target_pairs={{0,8},{2,10},{4,12},{6,14},{8,0},{10,2},{12,4},{14,6},{1,9},{3,11}... | collective-permute-start | bytes 540680 | tf_op jit(solution)/shard_map/ppermute | solution.py:230
  33.7 1.9 %collective-permute-start.15 = (bf16[32,768]{1,0:T(8,128)(2,1)S(1)}, bf16[32,768]{1,0:T(8,128)(2,1)S(1)}, u32[]{:S(2)}, u32[]{:S(2)}) collective-permute-start(bf16[32,768]{1,0:T(8,128)(2,1)S(1)} %get-tuple-element.70), channel_id=1, source_target_pairs={{0,10},{2,8},{4,14},{6,12},{8,2},{10,0},{12,6},{14,4},{1,11},{3,9}... | collective-permute-start | bytes 147464 | tf_op jit(solution)/shard_map/ppermute | solution.py:230
  35.6 1.8 %collective-permute-start.10 = (bf16[64,1024]{1,0:T(8,128)(2,1)S(1)}, bf16[64,1024]{1,0:T(8,128)(2,1)S(1)}, u32[]{:S(2)}, u32[]{:S(2)}) collective-permute-start(bf16[64,1024]{1,0:T(8,128)(2,1)S(1)} %get-tuple-element.64), channel_id=1, source_target_pairs={{0,8},{2,10},{4,12},{6,14},{8,0},{10,2},{12,4},{14,6},{1,9},{3,11}... | collective-permute-start | bytes 393224 | tf_op jit(solution)/shard_map/ppermute | solution.py:230
  37.5 0.6 collective-permute-start.12
  38.1 1.9 %collective-permute-start.13 = (bf16[32,2816]{1,0:T(8,128)(2,1)S(1)}, bf16[32,2816]{1,0:T(8,128)(2,1)S(1)}, u32[]{:S(2)}, u32[]{:S(2)}) collective-permute-start(bf16[32,2816]{1,0:T(8,128)(2,1)S(1)} %get-tuple-element.68), channel_id=1, source_target_pairs={{0,4},{2,6},{4,0},{6,2},{8,12},{10,14},{12,8},{14,10},{1,5},{3,7},... | collective-permute-start | bytes 540680 | tf_op jit(solution)/shard_map/ppermute | solution.py:230
  39.9 8.0 %collective-permute-done.15.rest_5_ = bf16[32,768]{1,0:T(8,128)(2,1)S(1)} collective-permute-done((bf16[32,768]{1,0:T(8,128)(2,1)S(1)}, bf16[32,768]{1,0:T(8,128)(2,1)S(1)}, u32[]{:S(2)}, u32[]{:S(2)}) %collective-permute-start.15) | collective-permute-done | bytes 49184 | tf_op jit(solution)/shard_map/ppermute | solution.py:230
  48.0 0.0 collective-permute-start.14
  48.0 1.4 %collective-permute-done.10.rest_2_ = bf16[64,1024]{1,0:T(8,128)(2,1)S(1)} collective-permute-done((bf16[64,1024]{1,0:T(8,128)(2,1)S(1)}, bf16[64,1024]{1,0:T(8,128)(2,1)S(1)}, u32[]{:S(2)}, u32[]{:S(2)}) %collective-permute-start.10) | collective-permute-done | bytes 131104 | tf_op jit(solution)/shard_map/ppermute | solution.py:230
  49.4 2.6 %collective-permute-start.16 = (bf16[32,768]{1,0:T(8,128)(2,1)S(1)}, bf16[32,768]{1,0:T(8,128)(2,1)S(1)}, u32[]{:S(2)}, u32[]{:S(2)}) collective-permute-start(bf16[32,768]{1,0:T(8,128)(2,1)S(1)} %get-tuple-element.71), channel_id=1, source_target_pairs={{0,12},{2,14},{4,8},{6,10},{8,4},{10,6},{12,0},{14,2},{1,13},{3,15... | collective-permute-start | bytes 147464 | tf_op jit(solution)/shard_map/ppermute | solution.py:230
  52.0 0.0 collective-permute-done.11.rest_3_.rest_4_
  52.0 1.4 %collective-permute-start.17 = (bf16[32,768]{1,0:T(8,128)(2,1)S(1)}, bf16[32,768]{1,0:T(8,128)(2,1)S(1)}, u32[]{:S(2)}, u32[]{:S(2)}) collective-permute-start(bf16[32,768]{1,0:T(8,128)(2,1)S(1)} %get-tuple-element.72), channel_id=1, source_target_pairs={{0,14},{2,12},{4,10},{6,8},{8,6},{10,4},{12,2},{14,0},{1,15},{3,13... | collective-permute-start | bytes 147464 | tf_op jit(solution)/shard_map/ppermute | solution.py:230
  53.4 0.9 %shard_map.140 = bf16[1,128,2048]{2,1,0:T(8,128)(2,1)} custom-call(bf16[64,1024]{1,0:T(8,128)(2,1)S(1)} %get-tuple-element.50.rest_0_, bf16[64,1024]{1,0:T(8,128)(2,1)S(1)} %get-tuple-element.63.rest_1_, bf16[64,1024]{1,0:T(8,128)(2,1)S(1)} %collective-permute-done.10.rest_2_, bf16[64,1408]{1,0:T(8,128)(2,1)S(1)} %collective-permute-done.11.rest_3_.rest_4_), custom_call_target="tpu_custom_call" | custom-call | tf_op jit(solution)/shard_map/pallas_call | solution.py:270
  54.3 1.0 %collective-permute-done.16.rest_6_ = bf16[32,768]{1,0:T(8,128)(2,1)S(1)} collective-permute-done((bf16[32,768]{1,0:T(8,128)(2,1)S(1)}, bf16[32,768]{1,0:T(8,128)(2,1)S(1)}, u32[]{:S(2)}, u32[]{:S(2)}) %collective-permute-start.16) | collective-permute-done | bytes 49184 | tf_op jit(solution)/shard_map/ppermute | solution.py:230
  55.3 3.5 %collective-permute-done.17.rest_7_ = bf16[32,768]{1,0:T(8,128)(2,1)S(1)} collective-permute-done((bf16[32,768]{1,0:T(8,128)(2,1)S(1)}, bf16[32,768]{1,0:T(8,128)(2,1)S(1)}, u32[]{:S(2)}, u32[]{:S(2)}) %collective-permute-start.17) | collective-permute-done | bytes 49184 | tf_op jit(solution)/shard_map/ppermute | solution.py:230
  58.8 0.0 collective-permute-done.12.rest_1_
  58.8 0.0 collective-permute-done.13.rest_2_
  58.8 0.0 collective-permute-done.14.rest_3_
  58.8 1.5 %shard_map.141 = (bf16[8,16,2048]{2,1,0:T(8,128)(2,1)}, bf16[8,16,256]{2,1,0:T(8,128)(2,1)}, bf16[8,16,256]{2,1,0:T(8,128)(2,1)}, bf16[12,256]{1,0:T(8,128)(2,1)}, bf16[12,256]{1,0:T(8,128)(2,1)}) custom-call(s32[8]{0:T(128)S(1)} %copy-done, bf16[32,2816]{1,0:T(8,128)(2,1)S(1)} %get-tuple-element.66.rest_0_, ...), custom_call_target="tpu_custom_call" | custom-call | tf_op jit(solution)/shard_map/pallas_call | solution.py:270
Async XLA Ops:
  1.8 17.0 %collective-permute-start = (bf16[32,2432]{1,0:T(8,128)(2,1)S(1)}, bf16[32,2432]{1,0:T(8,128)(2,1)S(1)}, u32[]{:S(2)}, u32[]{:S(2)}) collective-permute-start(bf16[32,2432]{1,0:T(8,128)(2,1)S(1)} %get-tuple-element.43), channel_id=1, source_target_pairs={{0,2},{2,0},{4,6},{6,4},{8,10},{10,8},{12,14},{14,12},{1,3},{3,1},... | collective-permute-start | bytes 466952 | tf_op jit(solution)/shard_map/ppermute | solution.py:230
  4.8 8.8 %collective-permute-start.3 = (bf16[32,768]{1,0:T(8,128)(2,1)S(1)}, bf16[32,768]{1,0:T(8,128)(2,1)S(1)}, u32[]{:S(2)}, u32[]{:S(2)}) collective-permute-start(bf16[32,768]{1,0:T(8,128)(2,1)S(1)} %get-tuple-element.46), channel_id=1, source_target_pairs={{0,8},{2,10},{4,12},{6,14},{8,0},{10,2},{12,4},{14,6},{1,9},{3,11}... | collective-permute-start | bytes 147464 | tf_op jit(solution)/shard_map/ppermute | solution.py:230
  7.4 7.9 %collective-permute-start.4 = (bf16[32,768]{1,0:T(8,128)(2,1)S(1)}, bf16[32,768]{1,0:T(8,128)(2,1)S(1)}, u32[]{:S(2)}, u32[]{:S(2)}) collective-permute-start(bf16[32,768]{1,0:T(8,128)(2,1)S(1)} %get-tuple-element.47), channel_id=1, source_target_pairs={{0,10},{2,8},{4,14},{6,12},{8,2},{10,0},{12,6},{14,4},{1,11},{3,9}... | collective-permute-start | bytes 147464 | tf_op jit(solution)/shard_map/ppermute | solution.py:230
  7.4 8.1 %collective-permute-start.5 = (bf16[32,768]{1,0:T(8,128)(2,1)S(1)}, bf16[32,768]{1,0:T(8,128)(2,1)S(1)}, u32[]{:S(2)}, u32[]{:S(2)}) collective-permute-start(bf16[32,768]{1,0:T(8,128)(2,1)S(1)} %get-tuple-element.48), channel_id=1, source_target_pairs={{0,12},{2,14},{4,8},{6,10},{8,4},{10,6},{12,0},{14,2},{1,13},{3,15... | collective-permute-start | bytes 147464 | tf_op jit(solution)/shard_map/ppermute | solution.py:230
  11.3 7.3 %collective-permute-start.6 = (bf16[32,768]{1,0:T(8,128)(2,1)S(1)}, bf16[32,768]{1,0:T(8,128)(2,1)S(1)}, u32[]{:S(2)}, u32[]{:S(2)}) collective-permute-start(bf16[32,768]{1,0:T(8,128)(2,1)S(1)} %get-tuple-element.49), channel_id=1, source_target_pairs={{0,14},{2,12},{4,10},{6,8},{8,6},{10,4},{12,2},{14,0},{1,15},{3,13... | collective-permute-start | bytes 147464 | tf_op jit(solution)/shard_map/ppermute | solution.py:230
  13.7 8.0 %collective-permute-start.1 = (bf16[32,2432]{1,0:T(8,128)(2,1)S(1)}, bf16[32,2432]{1,0:T(8,128)(2,1)S(1)}, u32[]{:S(2)}, u32[]{:S(2)}) collective-permute-start(bf16[32,2432]{1,0:T(8,128)(2,1)S(1)} %get-tuple-element.44), channel_id=1, source_target_pairs={{0,4},{2,6},{4,0},{6,2},{8,12},{10,14},{12,8},{14,10},{1,5},{3,7},... | collective-permute-start | bytes 466952 | tf_op jit(solution)/shard_map/ppermute | solution.py:230
  15.3 9.0 %collective-permute-start.2 = (bf16[32,2432]{1,0:T(8,128)(2,1)S(1)}, bf16[32,2432]{1,0:T(8,128)(2,1)S(1)}, u32[]{:S(2)}, u32[]{:S(2)}) collective-permute-start(bf16[32,2432]{1,0:T(8,128)(2,1)S(1)} %get-tuple-element.45), channel_id=1, source_target_pairs={{0,6},{2,4},{4,2},{6,0},{8,14},{10,12},{12,10},{14,8},{1,7},{3,5},... | collective-permute-start | bytes 466952 | tf_op jit(solution)/shard_map/ppermute | solution.py:230
  15.5 11.3 %collective-permute-start.7 = (bf16[32,2432]{1,0:T(8,128)(2,1)S(1)}, bf16[32,2432]{1,0:T(8,128)(2,1)S(1)}, u32[]{:S(2)}, u32[]{:S(2)}) collective-permute-start(bf16[32,2432]{1,0:T(8,128)(2,1)S(1)} %get-tuple-element.52), channel_id=1, source_target_pairs={{0,2},{2,0},{4,6},{6,4},{8,10},{10,8},{12,14},{14,12},{1,3},{3,1},... | collective-permute-start | bytes 466952 | tf_op jit(solution)/shard_map/ppermute | solution.py:230
  18.7 8.9 %collective-permute-start.8 = (bf16[32,2432]{1,0:T(8,128)(2,1)S(1)}, bf16[32,2432]{1,0:T(8,128)(2,1)S(1)}, u32[]{:S(2)}, u32[]{:S(2)}) collective-permute-start(bf16[32,2432]{1,0:T(8,128)(2,1)S(1)} %get-tuple-element.53), channel_id=1, source_target_pairs={{0,4},{2,6},{4,0},{6,2},{8,12},{10,14},{12,8},{14,10},{1,5},{3,7},... | collective-permute-start | bytes 466952 | tf_op jit(solution)/shard_map/ppermute | solution.py:230
  18.8 5.5 %copy-start = (s32[8]{0:T(128)S(1)}, s32[8]{0:T(128)}, u32[]{:S(2)}) copy-start(s32[8]{0:T(128)} %home_ref.9) | copy-start | bytes 100
  18.8 5.5 %copy-start.1 = (s32[8]{0:T(128)S(1)}, s32[8]{0:T(128)}, u32[]{:S(2)}) copy-start(s32[8]{0:T(128)} %lengths_ref.3) | copy-start | bytes 100
  18.8 5.5 %copy-start.2 = (s32[8]{0:T(128)S(1)}, s32[8]{0:T(128)}, u32[]{:S(2)}) copy-start(s32[8]{0:T(128)} %seen_ref.3) | copy-start | bytes 100
  18.8 10.7 %collective-permute-start.9 = (bf16[32,2432]{1,0:T(8,128)(2,1)S(1)}, bf16[32,2432]{1,0:T(8,128)(2,1)S(1)}, u32[]{:S(2)}, u32[]{:S(2)}) collective-permute-start(bf16[32,2432]{1,0:T(8,128)(2,1)S(1)} %get-tuple-element.54), channel_id=1, source_target_pairs={{0,6},{2,4},{4,2},{6,0},{8,14},{10,12},{12,10},{14,8},{1,7},{3,5},... | collective-permute-start | bytes 466952 | tf_op jit(solution)/shard_map/ppermute | solution.py:230
  32.1 19.9 %collective-permute-start.11 = (bf16[64,1408]{1,0:T(8,128)(2,1)S(1)}, bf16[64,1408]{1,0:T(8,128)(2,1)S(1)}, u32[]{:S(2)}, u32[]{:S(2)}) collective-permute-start(bf16[64,1408]{1,0:T(8,128)(2,1)S(1)} %get-tuple-element.65), channel_id=1, source_target_pairs={{0,8},{2,10},{4,12},{6,14},{8,0},{10,2},{12,4},{14,6},{1,9},{3,11}... | collective-permute-start | bytes 540680 | tf_op jit(solution)/shard_map/ppermute | solution.py:230
  33.7 14.3 %collective-permute-start.15 = (bf16[32,768]{1,0:T(8,128)(2,1)S(1)}, bf16[32,768]{1,0:T(8,128)(2,1)S(1)}, u32[]{:S(2)}, u32[]{:S(2)}) collective-permute-start(bf16[32,768]{1,0:T(8,128)(2,1)S(1)} %get-tuple-element.70), channel_id=1, source_target_pairs={{0,10},{2,8},{4,14},{6,12},{8,2},{10,0},{12,6},{14,4},{1,11},{3,9}... | collective-permute-start | bytes 147464 | tf_op jit(solution)/shard_map/ppermute | solution.py:230
  35.6 13.7 %collective-permute-start.10 = (bf16[64,1024]{1,0:T(8,128)(2,1)S(1)}, bf16[64,1024]{1,0:T(8,128)(2,1)S(1)}, u32[]{:S(2)}, u32[]{:S(2)}) collective-permute-start(bf16[64,1024]{1,0:T(8,128)(2,1)S(1)} %get-tuple-element.64), channel_id=1, source_target_pairs={{0,8},{2,10},{4,12},{6,14},{8,0},{10,2},{12,4},{14,6},{1,9},{3,11}... | collective-permute-start | bytes 393224 | tf_op jit(solution)/shard_map/ppermute | solution.py:230
  37.5 21.3 %collective-permute-start.12 = (bf16[32,2816]{1,0:T(8,128)(2,1)S(1)}, bf16[32,2816]{1,0:T(8,128)(2,1)S(1)}, u32[]{:S(2)}, u32[]{:S(2)}) collective-permute-start(bf16[32,2816]{1,0:T(8,128)(2,1)S(1)} %get-tuple-element.67), channel_id=1, source_target_pairs={{0,2},{2,0},{4,6},{6,4},{8,10},{10,8},{12,14},{14,12},{1,3},{3,1},... | collective-permute-start | bytes 540680 | tf_op jit(solution)/shard_map/ppermute | solution.py:230
  38.1 20.7 %collective-permute-start.13 = (bf16[32,2816]{1,0:T(8,128)(2,1)S(1)}, bf16[32,2816]{1,0:T(8,128)(2,1)S(1)}, u32[]{:S(2)}, u32[]{:S(2)}) collective-permute-start(bf16[32,2816]{1,0:T(8,128)(2,1)S(1)} %get-tuple-element.68), channel_id=1, source_target_pairs={{0,4},{2,6},{4,0},{6,2},{8,12},{10,14},{12,8},{14,10},{1,5},{3,7},... | collective-permute-start | bytes 540680 | tf_op jit(solution)/shard_map/ppermute | solution.py:230
  48.0 10.9 %collective-permute-start.14 = (bf16[32,2816]{1,0:T(8,128)(2,1)S(1)}, bf16[32,2816]{1,0:T(8,128)(2,1)S(1)}, u32[]{:S(2)}, u32[]{:S(2)}) collective-permute-start(bf16[32,2816]{1,0:T(8,128)(2,1)S(1)} %get-tuple-element.69), channel_id=1, source_target_pairs={{0,6},{2,4},{4,2},{6,0},{8,14},{10,12},{12,10},{14,8},{1,7},{3,5},... | collective-permute-start | bytes 540680 | tf_op jit(solution)/shard_map/ppermute | solution.py:230
  49.4 5.9 %collective-permute-start.16 = (bf16[32,768]{1,0:T(8,128)(2,1)S(1)}, bf16[32,768]{1,0:T(8,128)(2,1)S(1)}, u32[]{:S(2)}, u32[]{:S(2)}) collective-permute-start(bf16[32,768]{1,0:T(8,128)(2,1)S(1)} %get-tuple-element.71), channel_id=1, source_target_pairs={{0,12},{2,14},{4,8},{6,10},{8,4},{10,6},{12,0},{14,2},{1,13},{3,15... | collective-permute-start | bytes 147464 | tf_op jit(solution)/shard_map/ppermute | solution.py:230
  52.0 6.8 %collective-permute-start.17 = (bf16[32,768]{1,0:T(8,128)(2,1)S(1)}, bf16[32,768]{1,0:T(8,128)(2,1)S(1)}, u32[]{:S(2)}, u32[]{:S(2)}) collective-permute-start(bf16[32,768]{1,0:T(8,128)(2,1)S(1)} %get-tuple-element.72), channel_id=1, source_target_pairs={{0,14},{2,12},{4,10},{6,8},{8,6},{10,4},{12,2},{14,0},{1,15},{3,13... | collective-permute-start | bytes 147464 | tf_op jit(solution)/shard_map/ppermute | solution.py:230

commit v9 on v8

--- a/solution.py
+++ b/solution.py
@@ -31,19 +31,19 @@
     return jnp.concatenate([ref[part], spare], axis=0)
 
 
-def pack_kernel(home_ref, q_ref, k_ref, v_ref, g_ref, pk_ref, pv_ref, *rest, count, head, with_far):
+def pack_kernel(home_ref, q_ref, k_ref, v_ref, g_ref, pk_ref, pv_ref, *rest, count, heads):
     blocks, (home, q, g, k, v, prompt, sems) = rest[:-7], rest[-7:]
     rank = lax.axis_index("seq")
     half = count // 2
-    rows, q_part = q.shape[1:]
-    wide = pl.ds(head * q_part, q_part)
+    rows = q.shape[1]
+    q_part = q.shape[2] // heads
     copies = [
         pltpu.make_async_copy(source, target, sems.at[index])
         for index, (source, target) in enumerate(
             (
                 (home_ref, home),
-                (q_ref.at[:, :, wide], q),
-                (g_ref.at[:, :, wide], g),
+                (q_ref, q),
+                (g_ref, g),
                 (k_ref, k),
                 (v_ref, v),
                 (pk_ref, prompt.at[0]),
@@ -56,23 +56,32 @@
     for copy in copies:
         copy.wait()
     padded = [padded_rows(prompt, part, rows) for part in range(2)]
-    lanes = slice(head * HEAD_DIM, (head + 1) * HEAD_DIM)
     for distance in range(half):
         place = (rank ^ distance) & (half - 1)
         for part in range(2):
             index = resident_of(home, place + part * half, count)
             at = slice(part * rows, (part + 1) * rows)
-            near = [q[index], g[index], k[index, :, lanes], v[index, :, lanes], padded[part][:, lanes]]
-            blocks[distance][at, :] = jnp.concatenate(near, axis=1)
-            if with_far:
-                blocks[distance + half][at, :] = jnp.concatenate([k[index], v[index], padded[part]], axis=1)
+            for head in range(heads):
+                lanes = slice(head * HEAD_DIM, (head + 1) * HEAD_DIM)
+                wide = slice(head * q_part, (head + 1) * q_part)
+                near = [ref[index, :, of] for ref, of in ((q, wide), (g, wide), (k, lanes), (v, lanes))]
+                blocks[head * half + distance][at, :] = jnp.concatenate([*near, padded[part][:, lanes]], axis=1)
+            far = [k[index], v[index], padded[part]]
+            blocks[heads * half + distance][at, :] = jnp.concatenate(far, axis=1)
+
+
+def folded(part, tile, rows, half, q_part):
+    row_block, lane_block = (3 * part + tile) % half, (3 * part + tile) // half
+    low = q_part + lane_block * HEAD_DIM
+    return slice(row_block * rows, (row_block + 1) * rows), slice(low, low + HEAD_DIM)
 
 
 def attend_kernel(lengths_ref, home_ref, seen_ref, *rest, count, prompt_rows, head, heads):
     half = count // 2
     last = head == heads - 1
     blocks, rest = rest[:count], rest[count:]
-    earlier, rest = (rest[: head * count], rest[head * count :]) if last else ((), rest)
+    carried = head * (half - 1) if last else 0
+    earlier, rest = rest[:carried], rest[carried:]
     kept_ref, swap_ref, returns, rest = rest[0], rest[1], list(rest[2:-6]), rest[-6:]
     xq, xk, xp, yq, yk, yp = rest
     rank = lax.axis_index("seq")
@@ -166,15 +175,15 @@
             terms = [yk[part, target], yp[part, target]]
             if near:
                 terms = [yq[part, target & (half - 1)], *terms]
-            terms = [block[at, :] for block in earlier[distance::count]] + terms
+            elif distance > half:
+                terms = [block[at, :] for block in earlier[distance - half - 1 :: half - 1]] + terms
             terms = jnp.concatenate(terms, axis=1)
-            if last and distance == half:
-                fold = terms.shape[1] // 2
-                for index in range(2):
-                    to = slice((2 * index + part) * rows, (2 * index + part + 1) * rows)
-                    swap_ref[to, q_part:] = terms[:, index * fold : (index + 1) * fold]
+            if distance == half:
+                for tile in range(3):
+                    to_rows, to_lanes = folded(part, tile, rows, half, q_part)
+                    swap_ref[to_rows, to_lanes] = terms[:, tile * HEAD_DIM : (tile + 1) * HEAD_DIM]
             else:
-                returns[distance - (last and distance > half)][at, :] = terms
+                returns[distance - (distance > half)][at, :] = terms
 
 
 def join_kernel(*rest, half, heads):
@@ -191,31 +200,29 @@
 
 def unpack_kernel(home_ref, *rest, count, heads):
     half = count // 2
-    blocks, (qg_ref, kg_ref, vg_ref, pkg_ref, pvg_ref) = rest[:count], rest[count:]
+    blocks, (qg_ref, kg_ref, vg_ref, pkg_ref, pvg_ref) = rest[:-5], rest[-5:]
+    near, came, far = blocks[: heads * half], blocks[heads * half : heads * (half + 1)], blocks[heads * (half + 1) :]
     rank = lax.axis_index("seq")
     rows, q_width = qg_ref.shape[1:]
     prompt_rows = pkg_ref.shape[0]
     q_part = q_width // heads
-    near_size, far_size = q_part + 3 * HEAD_DIM, 3 * HEAD_DIM
+    far_size = 3 * HEAD_DIM
     for head in range(heads):
         lanes = slice(head * HEAD_DIM, (head + 1) * HEAD_DIM)
         prompt_grads = [jnp.zeros((rows, HEAD_DIM), F32)] * 2
         for distance in range(half):
             place = (rank ^ distance) & (half - 1)
+            block = near[head * half + distance]
             for part in range(2):
                 index = resident_of(home_ref, place + part * half, count)
                 at = slice(part * rows, (part + 1) * rows)
-                low = head * near_size
-                qg_ref[index, :, head * q_part : (head + 1) * q_part] = blocks[distance][at, low : low + q_part]
-                far = blocks[distance + half]
+                qg_ref[index, :, head * q_part : (head + 1) * q_part] = block[at, :q_part]
                 if distance:
-                    far = far[at, :]
+                    other = far[distance - 1][at, head * far_size : (head + 1) * far_size]
                 else:
-                    far = jnp.concatenate(
-                        [far[at, q_part:], far[(2 + part) * rows : (3 + part) * rows, q_part:]], axis=1
-                    )
-                far = far[:, head * far_size : (head + 1) * far_size]
-                terms = blocks[distance][at, low + q_part : low + near_size].astype(F32) + far.astype(F32)
+                    spots = [folded(part, tile, rows, half, q_part) for tile in range(3)]
+                    other = jnp.concatenate([came[head][spot] for spot in spots], axis=1)
+                terms = block[at, q_part:].astype(F32) + other.astype(F32)
                 kg_ref[index, :, lanes] = terms[:, :HEAD_DIM].astype(BF16)
                 vg_ref[index, :, lanes] = terms[:, HEAD_DIM : 2 * HEAD_DIM].astype(BF16)
                 prompt_grads[part] = prompt_grads[part] + terms[:, 2 * HEAD_DIM :]
@@ -281,31 +288,28 @@
         pltpu.with_memory_space_constraint(source, pltpu.HBM)
         for source in (home_rank, response_query, response_key, response_value, response_grad, prompt_key, prompt_value)
     ]
-    near_in = []
-    for head in range(heads):
-        blocks = call(
-            functools.partial(pack_kernel, count=count, head=head, with_far=head == 0),
-            [shape(2 * rows, q_part + near_size)] * half + [shape(2 * rows, heads * far_size)] * (0 if head else half),
-            sources,
-            [HBM] * 7,
-            [pltpu.SMEM((count,), jnp.int32)]
-            + [scratch(count, rows, lanes) for lanes in (q_part, q_part, kv_width, kv_width)]
-            + [scratch(2, prompt_rows, kv_width), pltpu.SemaphoreType.DMA((7,))],
-        )
-        near_in.append(exchange(blocks[:half], near, count))
-        if head == 0:
-            far_in = exchange(blocks[half:], far, count)
-    kept, came, returns = [], [], []
+    blocks = call(
+        functools.partial(pack_kernel, count=count, heads=heads),
+        [shape(2 * rows, q_part + near_size)] * (heads * half) + [shape(2 * rows, heads * far_size)] * half,
+        sources,
+        [HBM] * 7,
+        [pltpu.SMEM((count,), jnp.int32)]
+        + [scratch(count, rows, lanes) for lanes in (q_width, q_width, kv_width, kv_width)]
+        + [scratch(2, prompt_rows, kv_width), pltpu.SemaphoreType.DMA((7,))],
+    )
+    near_in = [exchange(blocks[head * half : (head + 1) * half], near, count) for head in range(heads)]
+    far_in = exchange(blocks[heads * half :], far, count)
+    kept, came, near_back, far_back = [], [], [], []
+    beside = -(-6 // half) * HEAD_DIM
     for head in range(heads):
         last = head == heads - 1
-        operands = [lengths, home_rank, prompt_seen, *near_in[head], *far_in, *(returns if last else [])]
+        operands = [lengths, home_rank, prompt_seen, *near_in[head], *far_in, *(far_back if last else [])]
         whole = heads if last else 1
-        fold = 2 * rows * whole * far_size // own_rows if last else 0
         results = call(
             functools.partial(attend_kernel, count=count, prompt_rows=prompt_rows, head=head, heads=heads),
-            [shape(own_rows, q_part), shape(own_rows, q_part + fold)]
-            + [shape(2 * rows, whole * near_size)] * half
-            + [shape(2 * rows, whole * far_size)] * (half - last),
+            [shape(own_rows, q_part), shape(own_rows, q_part + beside)]
+            + [shape(2 * rows, near_size)] * half
+            + [shape(2 * rows, whole * far_size)] * (half - 1),
             operands,
             [SMEM] * 3 + [VMEM] * (len(operands) - 3),
             [
@@ -319,9 +323,9 @@
         )
         kept.append(results[0])
         came += exchange(results[1:2], [half], count)
-        returns = returns + results[2:] if not last else results[2:]
-    returned = exchange(returns, [*near, *far[1:]], count)
-    returned.insert(half, came[-1])
+        near_back += exchange(results[2 : 2 + half], near, count)
+        far_back = [*([] if last else far_back), *results[2 + half :]]
+    returned = [*near_back, *came, *exchange(far_back, far[1:], count)]
     output = call(
         functools.partial(join_kernel, half=half, heads=heads),
         [shape(1, rows * count, q_width)],
@@ -333,7 +337,7 @@
         functools.partial(unpack_kernel, count=count, heads=heads),
         [shape(count, rows, q_width)] + [shape(count, rows, kv_width)] * 2 + [shape(prompt_rows, kv_width)] * 2,
         [home_rank, *returned],
-        [SMEM] + [VMEM] * count,
+        [SMEM] + [VMEM] * len(returned),
         [],
     )
     return (*output, *grads)

time: 60.5 us -> 69.5 us (1.15)
  waiting for transfers between devices: 22.3 us -> 31.3 us
  starting transfers between devices: 27.6 us -> 28.6 us
  Pallas kernels: 9.66 us -> 8.7 us
    ppermute x18 -> x21, waiting for transfers between devices: 22.3 us -> 31.3 us  [exchange(): lax.ppermute(block, 'seq', [(i, i ^ distance) for i in range(count)])]
    ppermute x18 -> x21, starting transfers between devices: 27.6 us -> 28.6 us  [exchange(): lax.ppermute(block, 'seq', [(i, i ^ distance) for i in range(count)])]
    pallas_call x6 -> x5, Pallas kernels: 9.66 us -> 8.7 us  [call(): pl.pallas_call(kernel, out_shape=results, in_specs=specs, out_specs=[VMEM...]
  transfers between devices with their start and end apart: 18 -> 21, of which waited for: 9 -> 9; matrix products, arithmetic and copies ran while one was open for 0% -> 0% of each run, Pallas kernels for 7% -> 5%
where the time goes in v9:
time: 69.5 us; the launch traced here: 69.3 us
  waiting for transfers between devices  31.3 us (45%)
  starting transfers between devices  28.6 us (41%)
  Pallas kernels  8.7 us (13%)
  between operations  0.7 us (1%)
    ppermute x21, waiting for transfers between devices, exchange(): lax.ppermute(block, 'seq', [(i, i ^ distance) for i in range(count)])  31.3 us
    ppermute x21, starting transfers between devices, exchange(): lax.ppermute(block, 'seq', [(i, i ^ distance) for i in range(count)])  28.6 us
    pallas_call x5, Pallas kernels, call(): pl.pallas_call(kernel, out_shape=results, in_specs=specs, out_specs=[VMEM...  8.7 us
  transfers between devices with their start and end apart: 21, of which 9 were waited for; matrix products, arithmetic and copies ran while one was open for 0% of the time, Pallas kernels for 5%

profile of v9, /device:TPU:0, one launch (start us, length us, event | category | flops | bytes accessed | tf_op | source)
XLA Modules:
  0.0 69.3 jit_solution(12729836387887946761)
XLA Ops:
  0.6 1.4 %shard_map.136 = (bf16[32,2432]{1,0:T(8,128)(2,1)S(1)}, bf16[32,2432]{1,0:T(8,128)(2,1)S(1)}, bf16[32,2432]{1,0:T(8,128)(2,1)S(1)}, bf16[32,2432]{1,0:T(8,128)(2...) custom-call(s32[8]{0:T(128)} %home_ref.7, ...), custom_call_target="tpu_custom_call" | custom-call | tf_op jit(solution)/shard_map/pallas_call | solution.py:277
  2.0 3.0 %collective-permute-start = (bf16[32,2432]{1,0:T(8,128)(2,1)S(1)}, bf16[32,2432]{1,0:T(8,128)(2,1)S(1)}, u32[]{:S(2)}, u32[]{:S(2)}) collective-permute-start(bf16[32,2432]{1,0:T(8,128)(2,1)S(1)} %get-tuple-element.42), channel_id=1, source_target_pairs={{0,2},{2,0},{4,6},{6,4},{8,10},{10,8},{12,14},{14,12},{1,3},{3,1},... | collective-permute-start | bytes 466952 | tf_op jit(solution)/shard_map/ppermute | solution.py:237
  5.1 2.6 %collective-permute-start.3 = (bf16[32,768]{1,0:T(8,128)(2,1)S(1)}, bf16[32,768]{1,0:T(8,128)(2,1)S(1)}, u32[]{:S(2)}, u32[]{:S(2)}) collective-permute-start(bf16[32,768]{1,0:T(8,128)(2,1)S(1)} %get-tuple-element.45), channel_id=1, source_target_pairs={{0,8},{2,10},{4,12},{6,14},{8,0},{10,2},{12,4},{14,6},{1,9},{3,11}... | collective-permute-start | bytes 147464 | tf_op jit(solution)/shard_map/ppermute | solution.py:237
  7.7 0.0 collective-permute-start.4
  7.7 3.9 %collective-permute-start.5 = (bf16[32,768]{1,0:T(8,128)(2,1)S(1)}, bf16[32,768]{1,0:T(8,128)(2,1)S(1)}, u32[]{:S(2)}, u32[]{:S(2)}) collective-permute-start(bf16[32,768]{1,0:T(8,128)(2,1)S(1)} %get-tuple-element.47), channel_id=1, source_target_pairs={{0,12},{2,14},{4,8},{6,10},{8,4},{10,6},{12,0},{14,2},{1,13},{3,15... | collective-permute-start | bytes 147464 | tf_op jit(solution)/shard_map/ppermute | solution.py:237
  11.6 1.2 %collective-permute-start.6 = (bf16[32,768]{1,0:T(8,128)(2,1)S(1)}, bf16[32,768]{1,0:T(8,128)(2,1)S(1)}, u32[]{:S(2)}, u32[]{:S(2)}) collective-permute-start(bf16[32,768]{1,0:T(8,128)(2,1)S(1)} %get-tuple-element.48), channel_id=1, source_target_pairs={{0,14},{2,12},{4,10},{6,8},{8,6},{10,4},{12,2},{14,0},{1,15},{3,13... | collective-permute-start | bytes 147464 | tf_op jit(solution)/shard_map/ppermute | solution.py:237
  12.7 0.0 collective-permute-done.3.rest_4_
  12.7 0.0 collective-permute-start.1
  12.7 2.8 %collective-permute-done.4.rest_5_ = bf16[32,768]{1,0:T(8,128)(2,1)S(1)} collective-permute-done((bf16[32,768]{1,0:T(8,128)(2,1)S(1)}, bf16[32,768]{1,0:T(8,128)(2,1)S(1)}, u32[]{:S(2)}, u32[]{:S(2)}) %collective-permute-start.4) | collective-permute-done | bytes 49184 | tf_op jit(solution)/shard_map/ppermute | solution.py:237
  15.5 0.0 collective-permute-start.2
  15.5 0.0 collective-permute-done.5.rest_6_
  15.5 1.1 %collective-permute-start.7 = (bf16[32,2432]{1,0:T(8,128)(2,1)S(1)}, bf16[32,2432]{1,0:T(8,128)(2,1)S(1)}, u32[]{:S(2)}, u32[]{:S(2)}) collective-permute-start(bf16[32,2432]{1,0:T(8,128)(2,1)S(1)} %get-tuple-element.51), channel_id=1, source_target_pairs={{0,2},{2,0},{4,6},{6,4},{8,10},{10,8},{12,14},{14,12},{1,3},{3,1},... | collective-permute-start | bytes 466952 | tf_op jit(solution)/shard_map/ppermute | solution.py:237
  16.7 1.8 %collective-permute-done.6.rest_7_ = bf16[32,768]{1,0:T(8,128)(2,1)S(1)} collective-permute-done((bf16[32,768]{1,0:T(8,128)(2,1)S(1)}, bf16[32,768]{1,0:T(8,128)(2,1)S(1)}, u32[]{:S(2)}, u32[]{:S(2)}) %collective-permute-start.6) | collective-permute-done | bytes 49184 | tf_op jit(solution)/shard_map/ppermute | solution.py:237
  18.5 0.6 collective-permute-start.8
  19.0 0.0 collective-permute-done.rest_1_
  19.0 0.0 copy-start
  19.0 0.0 copy-start.1
  19.0 0.0 copy-start.2
  19.0 2.9 %collective-permute-start.9 = (bf16[32,2432]{1,0:T(8,128)(2,1)S(1)}, bf16[32,2432]{1,0:T(8,128)(2,1)S(1)}, u32[]{:S(2)}, u32[]{:S(2)}) collective-permute-start(bf16[32,2432]{1,0:T(8,128)(2,1)S(1)} %get-tuple-element.53), channel_id=1, source_target_pairs={{0,6},{2,4},{4,2},{6,0},{8,14},{10,12},{12,10},{14,8},{1,7},{3,5},... | collective-permute-start | bytes 466952 | tf_op jit(solution)/shard_map/ppermute | solution.py:237
  21.9 0.0 collective-permute-done.1.rest_2_
  21.9 1.5 %collective-permute-done.2.rest_3_ = bf16[32,2432]{1,0:T(8,128)(2,1)S(1)} collective-permute-done((bf16[32,2432]{1,0:T(8,128)(2,1)S(1)}, bf16[32,2432]{1,0:T(8,128)(2,1)S(1)}, u32[]{:S(2)}, u32[]{:S(2)}) %collective-permute-start.2) | collective-permute-done | bytes 155680 | tf_op jit(solution)/shard_map/ppermute | solution.py:237
  23.4 0.0 copy-done
  23.4 0.0 copy-done.1
  23.4 0.0 copy-done.2
  23.4 2.5 %shard_map.137 = (bf16[64,1024]{1,0:T(8,128)(2,1)S(1)}, bf16[64,1280]{1,0:T(8,128)(2,1)S(1)}, bf16[32,1408]{1,0:T(8,128)(2,1)S(1)}, bf16[32,1408]{1,0:T(8,128)(2...) custom-call(s32[8]{0:T(128)S(1)} %copy-done.1, ...), custom_call_target="tpu_custom_call" | custom-call | tf_op jit(solution)/shard_map/pallas_call | solution.py:277
  25.9 0.0 collective-permute-done.7.rest_1_
  25.9 0.9 %collective-permute-done.8.rest_2_ = bf16[32,2432]{1,0:T(8,128)(2,1)S(1)} collective-permute-done((bf16[32,2432]{1,0:T(8,128)(2,1)S(1)}, bf16[32,2432]{1,0:T(8,128)(2,1)S(1)}, u32[]{:S(2)}, u32[]{:S(2)}) %collective-permute-start.8) | collective-permute-done | bytes 155680 | tf_op jit(solution)/shard_map/ppermute | solution.py:237
  26.8 2.3 %collective-permute-done.9.rest_3_ = bf16[32,2432]{1,0:T(8,128)(2,1)S(1)} collective-permute-done((bf16[32,2432]{1,0:T(8,128)(2,1)S(1)}, bf16[32,2432]{1,0:T(8,128)(2,1)S(1)}, u32[]{:S(2)}, u32[]{:S(2)}) %collective-permute-start.9) | collective-permute-done | bytes 155680 | tf_op jit(solution)/shard_map/ppermute | solution.py:237
  29.1 2.5 %shard_map.138 = (bf16[64,1024]{1,0:T(8,128)(2,1)S(1)}, bf16[64,1280]{1,0:T(8,128)(2,1)S(1)}, bf16[32,1408]{1,0:T(8,128)(2,1)S(1)}, bf16[32,1408]{1,0:T(8,128)(2...) custom-call(s32[8]{0:T(128)S(1)} %copy-done.1, ...), custom_call_target="tpu_custom_call" | custom-call | tf_op jit(solution)/shard_map/pallas_call | solution.py:277
  31.6 1.5 %collective-permute-start.11 = (bf16[64,1280]{1,0:T(8,128)(2,1)S(1)}, bf16[64,1280]{1,0:T(8,128)(2,1)S(1)}, u32[]{:S(2)}, u32[]{:S(2)}) collective-permute-start(bf16[64,1280]{1,0:T(8,128)(2,1)S(1)} %get-tuple-element.59), channel_id=1, source_target_pairs={{0,8},{2,10},{4,12},{6,14},{8,0},{10,2},{12,4},{14,6},{1,9},{3,11}... | collective-permute-start | bytes 491528 | tf_op jit(solution)/shard_map/ppermute | solution.py:237
  33.2 1.5 %collective-permute-start.10 = (bf16[64,1280]{1,0:T(8,128)(2,1)S(1)}, bf16[64,1280]{1,0:T(8,128)(2,1)S(1)}, u32[]{:S(2)}, u32[]{:S(2)}) collective-permute-start(bf16[64,1280]{1,0:T(8,128)(2,1)S(1)} %get-tuple-element.58), channel_id=1, source_target_pairs={{0,8},{2,10},{4,12},{6,14},{8,0},{10,2},{12,4},{14,6},{1,9},{3,11}... | collective-permute-start | bytes 491528 | tf_op jit(solution)/shard_map/ppermute | solution.py:237
  34.6 2.4 %collective-permute-start.18 = (bf16[32,768]{1,0:T(8,128)(2,1)S(1)}, bf16[32,768]{1,0:T(8,128)(2,1)S(1)}, u32[]{:S(2)}, u32[]{:S(2)}) collective-permute-start(bf16[32,768]{1,0:T(8,128)(2,1)S(1)} %get-tuple-element.68), channel_id=1, source_target_pairs={{0,10},{2,8},{4,14},{6,12},{8,2},{10,0},{12,6},{14,4},{1,11},{3,9}... | collective-permute-start | bytes 147464 | tf_op jit(solution)/shard_map/ppermute | solution.py:237
  37.0 0.5 collective-permute-start.12
  37.5 1.4 %collective-permute-start.19 = (bf16[32,768]{1,0:T(8,128)(2,1)S(1)}, bf16[32,768]{1,0:T(8,128)(2,1)S(1)}, u32[]{:S(2)}, u32[]{:S(2)}) collective-permute-start(bf16[32,768]{1,0:T(8,128)(2,1)S(1)} %get-tuple-element.69), channel_id=1, source_target_pairs={{0,12},{2,14},{4,8},{6,10},{8,4},{10,6},{12,0},{14,2},{1,13},{3,15... | collective-permute-start | bytes 147464 | tf_op jit(solution)/shard_map/ppermute | solution.py:237
  38.9 13.2 %collective-permute-done.18.rest_10_ = bf16[32,768]{1,0:T(8,128)(2,1)S(1)} collective-permute-done((bf16[32,768]{1,0:T(8,128)(2,1)S(1)}, bf16[32,768]{1,0:T(8,128)(2,1)S(1)}, u32[]{:S(2)}, u32[]{:S(2)}) %collective-permute-start.18) | collective-permute-done | bytes 49184 | tf_op jit(solution)/shard_map/ppermute | solution.py:237
  52.1 2.3 %collective-permute-start.20 = (bf16[32,768]{1,0:T(8,128)(2,1)S(1)}, bf16[32,768]{1,0:T(8,128)(2,1)S(1)}, u32[]{:S(2)}, u32[]{:S(2)}) collective-permute-start(bf16[32,768]{1,0:T(8,128)(2,1)S(1)} %get-tuple-element.70), channel_id=1, source_target_pairs={{0,14},{2,12},{4,10},{6,8},{8,6},{10,4},{12,2},{14,0},{1,15},{3,13... | collective-permute-start | bytes 147464 | tf_op jit(solution)/shard_map/ppermute | solution.py:237
  54.3 0.0 collective-permute-done.19.rest_11_
  54.3 0.0 collective-permute-start.13
  54.3 4.6 %collective-permute-done.20.rest_12_ = bf16[32,768]{1,0:T(8,128)(2,1)S(1)} collective-permute-done((bf16[32,768]{1,0:T(8,128)(2,1)S(1)}, bf16[32,768]{1,0:T(8,128)(2,1)S(1)}, u32[]{:S(2)}, u32[]{:S(2)}) %collective-permute-start.20) | collective-permute-done | bytes 49184 | tf_op jit(solution)/shard_map/ppermute | solution.py:237
  59.0 0.0 collective-permute-start.14
  59.0 0.0 collective-permute-done.12.rest_1_
  59.0 0.8 %collective-permute-start.15 = (bf16[32,1408]{1,0:T(8,128)(2,1)S(1)}, bf16[32,1408]{1,0:T(8,128)(2,1)S(1)}, u32[]{:S(2)}, u32[]{:S(2)}) collective-permute-start(bf16[32,1408]{1,0:T(8,128)(2,1)S(1)} %get-tuple-element.65), channel_id=1, source_target_pairs={{0,2},{2,0},{4,6},{6,4},{8,10},{10,8},{12,14},{14,12},{1,3},{3,1},... | collective-permute-start | bytes 270344 | tf_op jit(solution)/shard_map/ppermute | solution.py:237
  59.8 0.0 collective-permute-done.11.rest_3_.rest_9_
  59.8 2.7 %collective-permute-start.16 = (bf16[32,1408]{1,0:T(8,128)(2,1)S(1)}, bf16[32,1408]{1,0:T(8,128)(2,1)S(1)}, u32[]{:S(2)}, u32[]{:S(2)}) collective-permute-start(bf16[32,1408]{1,0:T(8,128)(2,1)S(1)} %get-tuple-element.66), channel_id=1, source_target_pairs={{0,4},{2,6},{4,0},{6,2},{8,12},{10,14},{12,8},{14,10},{1,5},{3,7},... | collective-permute-start | bytes 270344 | tf_op jit(solution)/shard_map/ppermute | solution.py:237
  62.4 0.0 collective-permute-done.10.rest_2_.rest_8_
  62.5 0.3 collective-permute-start.17
  62.8 0.9 %shard_map.139 = bf16[1,128,2048]{2,1,0:T(8,128)(2,1)} custom-call(bf16[64,1024]{1,0:T(8,128)(2,1)S(1)} %get-tuple-element.49.rest_0_, bf16[64,1024]{1,0:T(8,128)(2,1)S(1)} %get-tuple-element.57.rest_1_, bf16[64,1280]{1,0:T(8,128)(2,1)S(1)} %collective-permute-done.10.rest_2_.rest_8_, bf16[64,1280]{1,0:T(8,128)(2,1)S(1)} %collective-permute-done.11.rest_3_.rest_9_), custom_call_target="tpu_custom_call" | custom-call | tf_op jit(solution)/shard_map/pallas_call | solution.py:277
  63.6 0.0 collective-permute-done.13.rest_2_
  63.6 1.8 %collective-permute-done.14.rest_3_ = bf16[32,1408]{1,0:T(8,128)(2,1)S(1)} collective-permute-done((bf16[32,1408]{1,0:T(8,128)(2,1)S(1)}, bf16[32,1408]{1,0:T(8,128)(2,1)S(1)}, u32[]{:S(2)}, u32[]{:S(2)}) %collective-permute-start.14) | collective-permute-done | bytes 90144 | tf_op jit(solution)/shard_map/ppermute | solution.py:237
  65.4 0.0 collective-permute-done.15.rest_5_
  65.4 0.0 collective-permute-done.16.rest_6_
  65.4 2.5 %collective-permute-done.17.rest_7_ = bf16[32,1408]{1,0:T(8,128)(2,1)S(1)} collective-permute-done((bf16[32,1408]{1,0:T(8,128)(2,1)S(1)}, bf16[32,1408]{1,0:T(8,128)(2,1)S(1)}, u32[]{:S(2)}, u32[]{:S(2)}) %collective-permute-start.17) | collective-permute-done | bytes 90144 | tf_op jit(solution)/shard_map/ppermute | solution.py:237
  67.9 1.5 %shard_map.140 = (bf16[8,16,2048]{2,1,0:T(8,128)(2,1)}, bf16[8,16,256]{2,1,0:T(8,128)(2,1)}, bf16[8,16,256]{2,1,0:T(8,128)(2,1)}, bf16[12,256]{1,0:T(8,128)(2,1)}, bf16[12,256]{1,0:T(8,128)(2,1)}) custom-call(s32[8]{0:T(128)S(1)} %copy-done, bf16[32,1408]{1,0:T(8,128)(2,1)S(1)} %get-tuple-element.60.rest_0_, ...), custom_call_target="tpu_custom_call" | custom-call | tf_op jit(solution)/shard_map/pallas_call | solution.py:277
Async XLA Ops:
  2.0 17.0 %collective-permute-start = (bf16[32,2432]{1,0:T(8,128)(2,1)S(1)}, bf16[32,2432]{1,0:T(8,128)(2,1)S(1)}, u32[]{:S(2)}, u32[]{:S(2)}) collective-permute-start(bf16[32,2432]{1,0:T(8,128)(2,1)S(1)} %get-tuple-element.42), channel_id=1, source_target_pairs={{0,2},{2,0},{4,6},{6,4},{8,10},{10,8},{12,14},{14,12},{1,3},{3,1},... | collective-permute-start | bytes 466952 | tf_op jit(solution)/shard_map/ppermute | solution.py:237
  5.1 7.7 %collective-permute-start.3 = (bf16[32,768]{1,0:T(8,128)(2,1)S(1)}, bf16[32,768]{1,0:T(8,128)(2,1)S(1)}, u32[]{:S(2)}, u32[]{:S(2)}) collective-permute-start(bf16[32,768]{1,0:T(8,128)(2,1)S(1)} %get-tuple-element.45), channel_id=1, source_target_pairs={{0,8},{2,10},{4,12},{6,14},{8,0},{10,2},{12,4},{14,6},{1,9},{3,11}... | collective-permute-start | bytes 147464 | tf_op jit(solution)/shard_map/ppermute | solution.py:237
  7.7 7.9 %collective-permute-start.4 = (bf16[32,768]{1,0:T(8,128)(2,1)S(1)}, bf16[32,768]{1,0:T(8,128)(2,1)S(1)}, u32[]{:S(2)}, u32[]{:S(2)}) collective-permute-start(bf16[32,768]{1,0:T(8,128)(2,1)S(1)} %get-tuple-element.46), channel_id=1, source_target_pairs={{0,10},{2,8},{4,14},{6,12},{8,2},{10,0},{12,6},{14,4},{1,11},{3,9}... | collective-permute-start | bytes 147464 | tf_op jit(solution)/shard_map/ppermute | solution.py:237
  7.7 7.9 %collective-permute-start.5 = (bf16[32,768]{1,0:T(8,128)(2,1)S(1)}, bf16[32,768]{1,0:T(8,128)(2,1)S(1)}, u32[]{:S(2)}, u32[]{:S(2)}) collective-permute-start(bf16[32,768]{1,0:T(8,128)(2,1)S(1)} %get-tuple-element.47), channel_id=1, source_target_pairs={{0,12},{2,14},{4,8},{6,10},{8,4},{10,6},{12,0},{14,2},{1,13},{3,15... | collective-permute-start | bytes 147464 | tf_op jit(solution)/shard_map/ppermute | solution.py:237
  11.6 6.9 %collective-permute-start.6 = (bf16[32,768]{1,0:T(8,128)(2,1)S(1)}, bf16[32,768]{1,0:T(8,128)(2,1)S(1)}, u32[]{:S(2)}, u32[]{:S(2)}) collective-permute-start(bf16[32,768]{1,0:T(8,128)(2,1)S(1)} %get-tuple-element.48), channel_id=1, source_target_pairs={{0,14},{2,12},{4,10},{6,8},{8,6},{10,4},{12,2},{14,0},{1,15},{3,13... | collective-permute-start | bytes 147464 | tf_op jit(solution)/shard_map/ppermute | solution.py:237
  12.7 9.2 %collective-permute-start.1 = (bf16[32,2432]{1,0:T(8,128)(2,1)S(1)}, bf16[32,2432]{1,0:T(8,128)(2,1)S(1)}, u32[]{:S(2)}, u32[]{:S(2)}) collective-permute-start(bf16[32,2432]{1,0:T(8,128)(2,1)S(1)} %get-tuple-element.43), channel_id=1, source_target_pairs={{0,4},{2,6},{4,0},{6,2},{8,12},{10,14},{12,8},{14,10},{1,5},{3,7},... | collective-permute-start | bytes 466952 | tf_op jit(solution)/shard_map/ppermute | solution.py:237
  15.5 7.8 %collective-permute-start.2 = (bf16[32,2432]{1,0:T(8,128)(2,1)S(1)}, bf16[32,2432]{1,0:T(8,128)(2,1)S(1)}, u32[]{:S(2)}, u32[]{:S(2)}) collective-permute-start(bf16[32,2432]{1,0:T(8,128)(2,1)S(1)} %get-tuple-element.44), channel_id=1, source_target_pairs={{0,6},{2,4},{4,2},{6,0},{8,14},{10,12},{12,10},{14,8},{1,7},{3,5},... | collective-permute-start | bytes 466952 | tf_op jit(solution)/shard_map/ppermute | solution.py:237
  15.5 10.4 %collective-permute-start.7 = (bf16[32,2432]{1,0:T(8,128)(2,1)S(1)}, bf16[32,2432]{1,0:T(8,128)(2,1)S(1)}, u32[]{:S(2)}, u32[]{:S(2)}) collective-permute-start(bf16[32,2432]{1,0:T(8,128)(2,1)S(1)} %get-tuple-element.51), channel_id=1, source_target_pairs={{0,2},{2,0},{4,6},{6,4},{8,10},{10,8},{12,14},{14,12},{1,3},{3,1},... | collective-permute-start | bytes 466952 | tf_op jit(solution)/shard_map/ppermute | solution.py:237
  18.5 8.4 %collective-permute-start.8 = (bf16[32,2432]{1,0:T(8,128)(2,1)S(1)}, bf16[32,2432]{1,0:T(8,128)(2,1)S(1)}, u32[]{:S(2)}, u32[]{:S(2)}) collective-permute-start(bf16[32,2432]{1,0:T(8,128)(2,1)S(1)} %get-tuple-element.52), channel_id=1, source_target_pairs={{0,4},{2,6},{4,0},{6,2},{8,12},{10,14},{12,8},{14,10},{1,5},{3,7},... | collective-permute-start | bytes 466952 | tf_op jit(solution)/shard_map/ppermute | solution.py:237
  19.0 4.3 %copy-start = (s32[8]{0:T(128)S(1)}, s32[8]{0:T(128)}, u32[]{:S(2)}) copy-start(s32[8]{0:T(128)} %home_ref.7) | copy-start | bytes 100
  19.0 4.3 %copy-start.1 = (s32[8]{0:T(128)S(1)}, s32[8]{0:T(128)}, u32[]{:S(2)}) copy-start(s32[8]{0:T(128)} %lengths_ref.3) | copy-start | bytes 100
  19.0 4.3 %copy-start.2 = (s32[8]{0:T(128)S(1)}, s32[8]{0:T(128)}, u32[]{:S(2)}) copy-start(s32[8]{0:T(128)} %seen_ref.3) | copy-start | bytes 100
  19.0 10.1 %collective-permute-start.9 = (bf16[32,2432]{1,0:T(8,128)(2,1)S(1)}, bf16[32,2432]{1,0:T(8,128)(2,1)S(1)}, u32[]{:S(2)}, u32[]{:S(2)}) collective-permute-start(bf16[32,2432]{1,0:T(8,128)(2,1)S(1)} %get-tuple-element.53), channel_id=1, source_target_pairs={{0,6},{2,4},{4,2},{6,0},{8,14},{10,12},{12,10},{14,8},{1,7},{3,5},... | collective-permute-start | bytes 466952 | tf_op jit(solution)/shard_map/ppermute | solution.py:237
  31.6 28.1 %collective-permute-start.11 = (bf16[64,1280]{1,0:T(8,128)(2,1)S(1)}, bf16[64,1280]{1,0:T(8,128)(2,1)S(1)}, u32[]{:S(2)}, u32[]{:S(2)}) collective-permute-start(bf16[64,1280]{1,0:T(8,128)(2,1)S(1)} %get-tuple-element.59), channel_id=1, source_target_pairs={{0,8},{2,10},{4,12},{6,14},{8,0},{10,2},{12,4},{14,6},{1,9},{3,11}... | collective-permute-start | bytes 491528 | tf_op jit(solution)/shard_map/ppermute | solution.py:237
  33.2 29.3 %collective-permute-start.10 = (bf16[64,1280]{1,0:T(8,128)(2,1)S(1)}, bf16[64,1280]{1,0:T(8,128)(2,1)S(1)}, u32[]{:S(2)}, u32[]{:S(2)}) collective-permute-start(bf16[64,1280]{1,0:T(8,128)(2,1)S(1)} %get-tuple-element.58), channel_id=1, source_target_pairs={{0,8},{2,10},{4,12},{6,14},{8,0},{10,2},{12,4},{14,6},{1,9},{3,11}... | collective-permute-start | bytes 491528 | tf_op jit(solution)/shard_map/ppermute | solution.py:237
  34.6 17.4 %collective-permute-start.18 = (bf16[32,768]{1,0:T(8,128)(2,1)S(1)}, bf16[32,768]{1,0:T(8,128)(2,1)S(1)}, u32[]{:S(2)}, u32[]{:S(2)}) collective-permute-start(bf16[32,768]{1,0:T(8,128)(2,1)S(1)} %get-tuple-element.68), channel_id=1, source_target_pairs={{0,10},{2,8},{4,14},{6,12},{8,2},{10,0},{12,6},{14,4},{1,11},{3,9}... | collective-permute-start | bytes 147464 | tf_op jit(solution)/shard_map/ppermute | solution.py:237
  37.0 22.0 %collective-permute-start.12 = (bf16[32,1408]{1,0:T(8,128)(2,1)S(1)}, bf16[32,1408]{1,0:T(8,128)(2,1)S(1)}, u32[]{:S(2)}, u32[]{:S(2)}) collective-permute-start(bf16[32,1408]{1,0:T(8,128)(2,1)S(1)} %get-tuple-element.61), channel_id=1, source_target_pairs={{0,2},{2,0},{4,6},{6,4},{8,10},{10,8},{12,14},{14,12},{1,3},{3,1},... | collective-permute-start | bytes 270344 | tf_op jit(solution)/shard_map/ppermute | solution.py:237
  37.5 16.8 %collective-permute-start.19 = (bf16[32,768]{1,0:T(8,128)(2,1)S(1)}, bf16[32,768]{1,0:T(8,128)(2,1)S(1)}, u32[]{:S(2)}, u32[]{:S(2)}) collective-permute-start(bf16[32,768]{1,0:T(8,128)(2,1)S(1)} %get-tuple-element.69), channel_id=1, source_target_pairs={{0,12},{2,14},{4,8},{6,10},{8,4},{10,6},{12,0},{14,2},{1,13},{3,15... | collective-permute-start | bytes 147464 | tf_op jit(solution)/shard_map/ppermute | solution.py:237
  52.1 6.9 %collective-permute-start.20 = (bf16[32,768]{1,0:T(8,128)(2,1)S(1)}, bf16[32,768]{1,0:T(8,128)(2,1)S(1)}, u32[]{:S(2)}, u32[]{:S(2)}) collective-permute-start(bf16[32,768]{1,0:T(8,128)(2,1)S(1)} %get-tuple-element.70), channel_id=1, source_target_pairs={{0,14},{2,12},{4,10},{6,8},{8,6},{10,4},{12,2},{14,0},{1,15},{3,13... | collective-permute-start | bytes 147464 | tf_op jit(solution)/shard_map/ppermute | solution.py:237
  54.3 9.3 %collective-permute-start.13 = (bf16[32,1408]{1,0:T(8,128)(2,1)S(1)}, bf16[32,1408]{1,0:T(8,128)(2,1)S(1)}, u32[]{:S(2)}, u32[]{:S(2)}) collective-permute-start(bf16[32,1408]{1,0:T(8,128)(2,1)S(1)} %get-tuple-element.62), channel_id=1, source_target_pairs={{0,4},{2,6},{4,0},{6,2},{8,12},{10,14},{12,8},{14,10},{1,5},{3,7},... | collective-permute-start | bytes 270344 | tf_op jit(solution)/shard_map/ppermute | solution.py:237
  59.0 6.5 %collective-permute-start.14 = (bf16[32,1408]{1,0:T(8,128)(2,1)S(1)}, bf16[32,1408]{1,0:T(8,128)(2,1)S(1)}, u32[]{:S(2)}, u32[]{:S(2)}) collective-permute-start(bf16[32,1408]{1,0:T(8,128)(2,1)S(1)} %get-tuple-element.63), channel_id=1, source_target_pairs={{0,6},{2,4},{4,2},{6,0},{8,14},{10,12},{12,10},{14,8},{1,7},{3,5},... | collective-permute-start | bytes 270344 | tf_op jit(solution)/shard_map/ppermute | solution.py:237
  59.0 6.5 %collective-permute-start.15 = (bf16[32,1408]{1,0:T(8,128)(2,1)S(1)}, bf16[32,1408]{1,0:T(8,128)(2,1)S(1)}, u32[]{:S(2)}, u32[]{:S(2)}) collective-permute-start(bf16[32,1408]{1,0:T(8,128)(2,1)S(1)} %get-tuple-element.65), channel_id=1, source_target_pairs={{0,2},{2,0},{4,6},{6,4},{8,10},{10,8},{12,14},{14,12},{1,3},{3,1},... | collective-permute-start | bytes 270344 | tf_op jit(solution)/shard_map/ppermute | solution.py:237
  59.8 5.7 %collective-permute-start.16 = (bf16[32,1408]{1,0:T(8,128)(2,1)S(1)}, bf16[32,1408]{1,0:T(8,128)(2,1)S(1)}, u32[]{:S(2)}, u32[]{:S(2)}) collective-permute-start(bf16[32,1408]{1,0:T(8,128)(2,1)S(1)} %get-tuple-element.66), channel_id=1, source_target_pairs={{0,4},{2,6},{4,0},{6,2},{8,12},{10,14},{12,8},{14,10},{1,5},{3,7},... | collective-permute-start | bytes 270344 | tf_op jit(solution)/shard_map/ppermute | solution.py:237
  62.5 5.4 %collective-permute-start.17 = (bf16[32,1408]{1,0:T(8,128)(2,1)S(1)}, bf16[32,1408]{1,0:T(8,128)(2,1)S(1)}, u32[]{:S(2)}, u32[]{:S(2)}) collective-permute-start(bf16[32,1408]{1,0:T(8,128)(2,1)S(1)} %get-tuple-element.67), channel_id=1, source_target_pairs={{0,6},{2,4},{4,2},{6,0},{8,14},{10,12},{12,10},{14,8},{1,7},{3,5},... | collective-permute-start | bytes 270344 | tf_op jit(solution)/shard_map/ppermute | solution.py:237
